TPU v7x, 32 devices: a whole 2x2x4 slice. The times are simulated.
32 devices in a mesh: sweep: 2 (over y), expert: 4 (over z), dp: 4 (over x, core).
Axes of the slice: x: 2, y: 2, z: 4, core: 2. Of those that a mesh axis runs over, the one named last changes fastest.
Arguments:
- tokens: bfloat16 [4096, 1536], P(('sweep', 'expert', 'dp')), parts along dimension 0, may hold values from -6 to 6
- expert_ids: int32 [4096, 8], P(('sweep', 'expert', 'dp')), parts along dimension 0, may hold values from 0 to 63, all different within a row; in each aligned block of 128 rows (0 to 127, 128 to 255, ...) at most 20 rows name the same one
- gate_weights: float32 [4096, 8], P(('sweep', 'expert', 'dp')), parts along dimension 0, may hold values from 0.1 to 0.6
- expert_in: bfloat16 [128, 1536, 768], P(('sweep', 'expert'), 'dp'), parts along dimension 0, may hold values from -0.15625 to 0.15625
- expert_out: bfloat16 [128, 768, 1536], P(('sweep', 'expert'), None, 'dp'), parts along dimension 0, may hold values from -0.21875 to 0.21875
- shared_in: bfloat16 [3072, 768], P(('sweep', 'dp')), parts along dimension 0, may hold values from -0.15625 to 0.15625
- shared_out: bfloat16 [1536, 1536], P('sweep', 'dp'), parts along dimension 0, may hold values from -0.21875 to 0.21875
Outputs:
- block_out: bfloat16 [4096, 1536], P(('sweep', 'expert', 'dp')), parts along dimension 0
There are 2 independent parts, one for each index of `sweep`. A program takes and returns all parts, laid end to end along the dimension named above; each array names one. Nothing has to cross between parts.
Inputs may be any that keep to these rules, and one draw needn't show every extreme that they name: `expert_ids`: each token names 8 different experts. In each aligned block of 128 tokens (the tokens of one device) no expert is named by more than 20 tokens; some blocks have an expert named by exactly 20.
All inputs are finite; a program needn't handle non-finite values.
Results may differ from a plain program's by a relative error of at most 0.0051.
Values may be sent and summed in bfloat16 or wider, within the bound.
No kernel may reach another device: no remote copies, remote signals or barrier semaphores. Data moves between devices by JAX's collectives and lax.ppermute only.
A program may use at most 192 MiB of HBM per device.

v0:
```python
import jax
import jax.numpy as jnp
from jax import lax
from jax.sharding import PartitionSpec as P

CAP = 20


def layer_norm(tokens):
    values = tokens.astype(jnp.float32)
    center = values - jnp.mean(values, axis=-1, keepdims=True)
    spread = jnp.mean(center * center, axis=-1, keepdims=True)
    return (center * lax.rsqrt(spread + 1e-06)).astype(jnp.bfloat16)


def copy_slots(expert_ids, expert_count):
    expert_iota = jnp.arange(expert_count, dtype=jnp.int32)
    matches = (expert_ids[..., None] == expert_iota).astype(jnp.int32)
    per_token = jnp.sum(matches, axis=-2, dtype=jnp.int32)
    earlier = jnp.cumsum(per_token, axis=-2, dtype=jnp.int32) - per_token
    return jnp.sum(matches * earlier[..., None, :], axis=-1, dtype=jnp.int32)


def run_experts(shard_piece, weight_in, weight_out):
    pre_act = jnp.einsum(
        "gesd,edf->gesf", shard_piece, weight_in, preferred_element_type=jnp.float32
    )
    hidden = jax.nn.gelu(pre_act).astype(jnp.bfloat16)
    return jnp.einsum(
        "gesf,efd->gesd", hidden, weight_out, preferred_element_type=jnp.float32
    ).astype(jnp.bfloat16)


def per_device(tokens, expert_ids, gate_weights, expert_in, expert_out, shared_in, shared_out):
    row_count, model_width = tokens.shape
    pick_count = expert_ids.shape[1]
    local_count = expert_in.shape[0]
    group_count = lax.axis_size("expert")
    expert_total = local_count * group_count
    normed = layer_norm(tokens)
    full_in, full_out = (
        lax.all_gather(expert_in, "dp", axis=1, tiled=True),
        lax.all_gather(expert_out, "dp", axis=2, tiled=True),
    )
    slot_of = copy_slots(expert_ids, expert_total)
    positions = (expert_ids * CAP + slot_of).reshape(-1)
    copies = jnp.repeat(normed, pick_count, axis=0)
    outgoing = jnp.zeros((expert_total * CAP, model_width), jnp.bfloat16).at[positions].set(copies)
    outgoing = outgoing.reshape(group_count, local_count, CAP, model_width)
    received = lax.all_to_all(outgoing, "expert", split_axis=0, concat_axis=0, tiled=True)
    returned = lax.all_to_all(
        run_experts(received, full_in, full_out), "expert", split_axis=0, concat_axis=0, tiled=True
    )
    results = returned.reshape(expert_total * CAP, model_width)[positions].reshape(
        row_count, pick_count, model_width
    )
    routed = jnp.sum(results.astype(jnp.float32) * gate_weights[:, :, None], axis=1)
    shared_pre = jnp.dot(
        normed,
        lax.all_gather(shared_in, "dp", axis=0, tiled=True),
        preferred_element_type=jnp.float32,
    )
    shared_hidden = jax.nn.gelu(shared_pre).astype(jnp.bfloat16)
    shared_result = jnp.dot(
        shared_hidden,
        lax.all_gather(shared_out, "dp", axis=1, tiled=True),
        preferred_element_type=jnp.float32,
    )
    return (tokens.astype(jnp.float32) + shared_result + routed).astype(jnp.bfloat16)


def solution(mesh):
    placed = (
        P(("sweep", "expert", "dp"), None),
        P(("sweep", "expert", "dp"), None),
        P(("sweep", "expert", "dp"), None),
        P(("sweep", "expert"), "dp", None),
        P(("sweep", "expert"), None, "dp"),
        P(("sweep", "dp"), None),
        P("sweep", "dp"),
    )
    return jax.shard_map(
        per_device,
        mesh=mesh,
        in_specs=placed,
        out_specs=P(("sweep", "expert", "dp"), None),
        check_vma=False,
    )
```

profile of v0, /device:TPU:0, one launch (start us, length us, event | category | flops | bytes accessed | tf_op | source)
XLA Modules:
  0.0 624.6 jit_solution(13773395586247064220)
XLA Ops:
  6.5 0.7 all-gather.9.cloned.1.call-update
  7.3 0.7 all-gather.11.cloned.1.call-update
  8.1 0.1 copy.22
  8.2 0.2 reduce_window_sum.11
  8.4 0.1 copy.24
  8.4 0.1 select_reduce_fusion
  8.5 0.1 copy.25
  8.6 0.1 reshape.66
  8.7 0.1 convert_reduce_fusion
  8.9 0.3 fusion.29
  9.1 0.2 fusion.30
  9.4 8.1 %scatter_custom_fusion = bf16[1280,1536]{1,0:T(8,128)(2,1)} fusion(s32[1024]{0:T(1024)S(1)} %bitcast.27, bf16[]{:T(256)} %constant.6.clone.1, bf16[128,1536]{1,0:T(8,128)(2,1)S(1)} %fusion.30), kind=kCustom, calls=%fused_computation.19 | custom fusion | bytes 4325378 | tf_op jit(solution)/shard_map/scatter | solution.py:48
  17.5 7.5 %reshape.68 = bf16[4,16,20,1536]{3,2,1,0:T(8,128)(2,1)} reshape(bf16[1280,1536]{1,0:T(8,128)(2,1)} %scatter_custom_fusion) | data formatting | bytes 7864320 | tf_op jit(solution)/shard_map/reshape | solution.py:49
  24.9 6.8 %copy.26 = bf16[4,16,20,1536]{3,1,2,0:T(8,128)(2,1)} copy(bf16[4,16,20,1536]{3,2,1,0:T(8,128)(2,1)} %reshape.68) | data formatting | bytes 7864320 | tf_op jit(solution)/shard_map/reshape | solution.py:49
  31.7 7.1 %all-to-all-start = ((bf16[4,16,20,1536]{3,1,2,0:T(8,128)(2,1)}), bf16[4,16,20,1536]{3,1,2,0:T(8,128)(2,1)}, u32[]{:S(2)}, u32[]{:S(2)}) async-start(bf16[4,16,20,1536]{3,1,2,0:T(8,128)(2,1)} %copy.26), calls=%async_computation | async-start | bytes 7864320 | tf_op jit(solution)/shard_map/all_to_all | solution.py:50
  38.8 0.7 all-gather.5.cloned.1.call-update
  39.5 87.2 %all-to-all-done = bf16[4,16,20,1536]{3,1,2,0:T(8,128)(2,1)} async-done(((bf16[4,16,20,1536]{3,1,2,0:T(8,128)(2,1)}), bf16[4,16,20,1536]{3,1,2,0:T(8,128)(2,1)}, u32[]{:S(2)}, u32[]{:S(2)}) %all-to-all-start) | async-done | bytes 3932192 | tf_op jit(solution)/shard_map/all_to_all | solution.py:50
  126.8 112.0 %all-gather.9.cloned.1.call-done = bf16[16,1536,768]{2,1,0:T(8,128)(2,1)} async-done(((bf16[16,384,768]{2,1,0:T(8,128)(2,1)}), bf16[16,1536,768]{2,1,0:T(8,128)(2,1)}) %all-gather.9.cloned.1.call-update) | async-done | bytes 37748752 | tf_op jit(solution)/shard_map/all_gather | solution.py:42
  238.7 28.0 %fusion.2 = f32[16,4,20,768]{3,2,1,0:T(8,128)} fusion(bf16[16,1536,768]{2,1,0:T(8,128)(2,1)} %all-gather.9.cloned.1.call-done, bf16[4,16,20,1536]{3,1,2,0:T(8,128)(2,1)} %all-to-all-done), kind=kOutput, calls=%fused_computation.4 | convolution fusion | flops 3019898880 | bytes 45613056 | tf_op jit(solution)/shard_map/gesd,edf->gesf/dot_general | solution.py:25
  266.7 200.2 %all-gather.11.cloned.1.call-done = bf16[16,768,1536]{2,1,0:T(8,128)(2,1)} async-done(((bf16[16,768,384]{2,1,0:T(8,128)(2,1)}), bf16[16,768,1536]{2,1,0:T(8,128)(2,1)}) %all-gather.11.cloned.1.call-update) | async-done | bytes 37748752 | tf_op jit(solution)/shard_map/all_gather | solution.py:43
  466.9 19.8 %convert_bitcast_fusion = bf16[4,16,20,1536]{3,2,0,1:T(8,128)(2,1)} fusion(bf16[16,768,1536]{2,1,0:T(8,128)(2,1)} %all-gather.11.cloned.1.call-done, f32[16,4,20,768]{3,2,1,0:T(8,128)} %fusion.2), kind=kOutput, calls=%fused_computation.18 | convolution fusion | flops 3030712320 | bytes 45613056 | tf_op jit(solution)/shard_map/gesf,efd->gesd/dot_general | solution.py:29
  486.7 6.4 %copy.28 = bf16[4,16,20,1536]{3,1,2,0:T(8,128)(2,1)} copy(bf16[4,16,20,1536]{3,2,0,1:T(8,128)(2,1)} %convert_bitcast_fusion) | data formatting | bytes 7864320 | tf_op jit(solution)/shard_map/convert_element_type | solution.py:31
  493.1 5.0 all-to-all-start.1
  498.1 0.0 all-gather.7.cloned.1.call-start
  498.1 0.5 all-gather.7.cloned.1.call-update
  498.7 0.7 copy.30
  499.4 87.0 %all-to-all-done.1 = bf16[4,16,20,1536]{3,1,2,0:T(8,128)(2,1)} async-done(((bf16[4,16,20,1536]{3,1,2,0:T(8,128)(2,1)}), bf16[4,16,20,1536]{3,1,2,0:T(8,128)(2,1)}, u32[]{:S(2)}, u32[]{:S(2)}) %all-to-all-start.1) | async-done | bytes 3932192 | tf_op jit(solution)/shard_map/all_to_all | solution.py:51
  586.4 6.5 %copy.29 = bf16[4,16,20,1536]{3,2,1,0:T(8,128)(2,1)} copy(bf16[4,16,20,1536]{3,1,2,0:T(8,128)(2,1)} %all-to-all-done.1) | data formatting | bytes 7864320 | tf_op jit(solution)/shard_map/all_to_all | solution.py:51
  592.9 6.9 %reshape.69 = bf16[1280,1536]{1,0:T(8,128)(2,1)} reshape(bf16[4,16,20,1536]{3,2,1,0:T(8,128)(2,1)} %copy.29) | data formatting | bytes 7864320 | tf_op jit(solution)/shard_map/reshape | solution.py:54
  599.8 9.3 %gather_fusion = bf16[1024,1536]{1,0:T(8,128)(2,1)S(1)} fusion(bf16[1280,1536]{1,0:T(8,128)(2,1)} %reshape.69, s32[1024]{0:T(1024)S(1)} %broadcast_clamp_fusion), kind=kCustom, calls=%fused_computation | custom fusion | bytes 6295552 | tf_op jit(solution)/shard_map/gather | solution.py:54
  609.1 4.5 fusion.4
  613.6 4.4 fusion.19
  (18 shorter events, 0.1 us)
Async XLA Ops:
  6.5 232.2 %all-gather.9.cloned.1.call-start = ((), (), s32[]{:S(2)}) async-start(), calls=%async_computation.4 | async-start | bytes 47185920 | tf_op jit(solution)/shard_map/all_gather | solution.py:42
  7.3 0.8 copy-start.1
  7.3 1.4 copy-start
  7.3 459.7 %all-gather.11.cloned.1.call-start = ((), (), s32[]{:S(2)}) async-start(), calls=%async_computation.5 | async-start | bytes 47185920 | tf_op jit(solution)/shard_map/all_gather | solution.py:43
  31.7 95.1 %all-to-all-start = ((bf16[4,16,20,1536]{3,1,2,0:T(8,128)(2,1)}), bf16[4,16,20,1536]{3,1,2,0:T(8,128)(2,1)}, u32[]{:S(2)}, u32[]{:S(2)}) async-start(bf16[4,16,20,1536]{3,1,2,0:T(8,128)(2,1)} %copy.26), calls=%async_computation | async-start | bytes 7864320 | tf_op jit(solution)/shard_map/all_to_all | solution.py:50
  38.8 574.8 %all-gather.5.cloned.1.call-start = ((), (), s32[]{:S(2)}) async-start(), calls=%async_computation.2 | async-start | bytes 2949120 | tf_op jit(solution)/shard_map/all_gather | solution.py:60
  493.1 5.5 copy-start.2
  493.1 93.3 %all-to-all-start.1 = ((bf16[4,16,20,1536]{3,1,2,0:T(8,128)(2,1)}), bf16[4,16,20,1536]{3,1,2,0:T(8,128)(2,1)}, u32[]{:S(2)}, u32[]{:S(2)}) async-start(bf16[4,16,20,1536]{3,1,2,0:T(8,128)(2,1)} %copy.28), calls=%async_computation.1 | async-start | bytes 7864320 | tf_op jit(solution)/shard_map/all_to_all | solution.py:51
  498.1 115.5 %all-gather.7.cloned.1.call-start = ((), (), s32[]{:S(2)}) async-start(), calls=%async_computation.3 | async-start | bytes 2949120 | tf_op jit(solution)/shard_map/all_gather | solution.py:66
Sparse Core Ops, SparseCore 0:
  8.9 229.7 all-gather.8
  240.3 226.6 all-gather.10
  468.5 24.0 all-gather.4
  500.2 24.4 all-gather.6
where the time goes:
time: 625 us
  waiting for transfers between devices  489 us (78%)
  local copies, waits for them, and re-layouts  52.5 us (8%)
  matrix products  52.2 us (8%)
  between operations  13.2 us (2%)
  starting transfers between devices  12.1 us (2%)
    all_gather x1, waiting for transfers between devices, per_device(): lax.all_gather(expert_out, 'dp', axis=2, tiled=True)  200 us
    all_gather x1, waiting for transfers between devices, per_device(): lax.all_gather(expert_in, 'dp', axis=1, tiled=True)  112 us
    all_to_all x1, waiting for transfers between devices, per_device(): lax.all_to_all(outgoing, 'expert', split_axis=0, concat_axis=0, tiled=True)  87.2 us
    all_to_all x1, waiting for transfers between devices, per_device(): lax.all_to_all(run_experts(received, full_in, full_out), 'expert', split_...  87 us
    dot_general x1, matrix products, run_experts(): jnp.einsum('gesd,edf->gesf', shard_piece, weight_in, preferred_element_ty...  28 us
    dot_general x1, matrix products, run_experts(): jnp.einsum('gesf,efd->gesd', hidden, weight_out, preferred_element_type=j...  19.8 us
    reshape x2, local copies, waits for them, and re-layouts, per_device(): outgoing = outgoing.reshape(group_count, local_count, CAP, model_width)  14.2 us
  transfers between devices with their start and end apart: 6, of which 4 were waited for; matrix products, arithmetic and copies ran while one was open for 17% of the time, Pallas kernels for 0%

commit v1 on v0

v1 whole, which is shorter than its diff:
```python
import functools

import jax
import jax.numpy as jnp
from jax import lax
from jax.experimental import pallas as pl
from jax.experimental.pallas import tpu as pltpu
from jax.sharding import PartitionSpec as P

CAP = 20
F32 = jnp.float32
BF16 = jnp.bfloat16
META = 16


def layer_norm(tokens):
    values = tokens.astype(F32)
    center = values - jnp.mean(values, axis=-1, keepdims=True)
    spread = jnp.mean(center * center, axis=-1, keepdims=True)
    return (center * lax.rsqrt(spread + 1e-06)).astype(BF16)


def copy_slots(expert_ids, expert_count):
    expert_iota = jnp.arange(expert_count, dtype=jnp.int32)
    matches = (expert_ids[..., None] == expert_iota).astype(jnp.int32)
    per_token = jnp.sum(matches, axis=-2, dtype=jnp.int32)
    earlier = jnp.cumsum(per_token, axis=-2, dtype=jnp.int32) - per_token
    return jnp.sum(matches * earlier[..., None, :], axis=-1, dtype=jnp.int32)


def run_experts(shard_piece, weight_in, weight_out):
    pre_act = jnp.einsum("gesd,edf->gesf", shard_piece, weight_in, preferred_element_type=F32)
    hidden = jax.nn.gelu(pre_act).astype(BF16)
    return jnp.einsum("gesf,efd->gesd", hidden, weight_out, preferred_element_type=F32).astype(BF16)


def gathered_weights(tokens, expert_ids, gate_weights, expert_in, expert_out, shared_in, shared_out):
    row_count, model_width = tokens.shape
    pick_count = expert_ids.shape[1]
    local_count = expert_in.shape[0]
    group_count = lax.axis_size("expert")
    expert_total = local_count * group_count
    normed = layer_norm(tokens)
    full_in = lax.all_gather(expert_in, "dp", axis=1, tiled=True)
    full_out = lax.all_gather(expert_out, "dp", axis=2, tiled=True)
    slot_of = copy_slots(expert_ids, expert_total)
    positions = (expert_ids * CAP + slot_of).reshape(-1)
    copies = jnp.repeat(normed, pick_count, axis=0)
    outgoing = jnp.zeros((expert_total * CAP, model_width), BF16).at[positions].set(copies)
    outgoing = outgoing.reshape(group_count, local_count, CAP, model_width)
    received = lax.all_to_all(outgoing, "expert", split_axis=0, concat_axis=0, tiled=True)
    returned = lax.all_to_all(
        run_experts(received, full_in, full_out), "expert", split_axis=0, concat_axis=0, tiled=True
    )
    results = returned.reshape(expert_total * CAP, model_width)[positions].reshape(
        row_count, pick_count, model_width
    )
    routed = jnp.sum(results.astype(F32) * gate_weights[:, :, None], axis=1)
    shared_pre = jnp.dot(
        normed, lax.all_gather(shared_in, "dp", axis=0, tiled=True), preferred_element_type=F32
    )
    shared_hidden = jax.nn.gelu(shared_pre).astype(BF16)
    shared_result = jnp.dot(
        shared_hidden,
        lax.all_gather(shared_out, "dp", axis=1, tiled=True),
        preferred_element_type=F32,
    )
    return (tokens.astype(F32) + shared_result + routed).astype(BF16)


def dot(a, b):
    return jnp.dot(a, b, preferred_element_type=F32)


def swap(value, axis, mask):
    size = lax.axis_size(axis)
    return lax.ppermute(value, axis, [(i, i ^ mask) for i in range(size)])


def cost(flops, moved):
    return pl.CostEstimate(flops=int(flops), bytes_accessed=int(moved), transcendentals=0)


def norm_kernel(place, tokens, ids, gates, mine, theirs):
    rows, width = tokens.shape
    half = width // 2
    values = tokens[...].astype(F32)
    center = values - jnp.mean(values, axis=-1, keepdims=True)
    spread = jnp.mean(center * center, axis=-1, keepdims=True)
    normed = (center * lax.rsqrt(spread + 1e-06)).astype(BF16)
    low = place[1] == 0
    mine[0:rows, :] = jnp.where(low, normed[:, :half], normed[:, half:])
    theirs[0:rows, :] = jnp.where(low, normed[:, half:], normed[:, :half])
    gate = gates[...]
    high = gate.astype(BF16).astype(F32)
    rest = gate - high
    picks = ids.shape[0]
    spare = jnp.zeros((picks, half - 3 * rows), F32)
    table = jnp.concatenate([ids[...].astype(F32), high, rest, spare], axis=1)
    table = jnp.concatenate([table, jnp.zeros((META - picks, half), F32)], axis=0).astype(BF16)
    mine[rows : rows + META, :] = table
    theirs[rows : rows + META, :] = table


def selection(codes, rows):
    count, tokens = codes.shape
    wanted = lax.broadcasted_iota(jnp.int32, (rows, tokens), 0).astype(F32)
    return [(wanted == codes[e : e + 1, :]).astype(F32) for e in range(count)]


def first_kernel(units, picks, place, *refs):
    feeds, (own, other, part, code, gate, packed) = refs[:units], refs[units:]
    local, rows, half = packed.shape
    slots = rows // (2 * units)
    tokens = feeds[0].shape[0] // 2 - META
    step = pl.program_id(0)

    @pl.when(step == 0)
    def _():
        lead = place[2]
        before = (
            lax.broadcasted_iota(jnp.int32, (tokens, tokens), 0)
            < lax.broadcasted_iota(jnp.int32, (tokens, tokens), 1)
        ).astype(F32).astype(BF16)
        expert = (lax.broadcasted_iota(jnp.int32, (local, tokens), 0) + lead).astype(F32)
        for u in range(units):
            for b in range(2):
                at = 2 * tokens + b * META
                table = feeds[u][at : at + META, 0 : 3 * tokens].astype(F32)
                named = jnp.zeros((local, tokens), F32)
                weight = jnp.zeros((local, tokens), F32)
                for k in range(picks):
                    same = table[k : k + 1, 0:tokens] == expert
                    value = table[k : k + 1, tokens : 2 * tokens] + table[k : k + 1, 2 * tokens :]
                    named = jnp.where(same, 1.0, named)
                    weight = jnp.where(same, value, weight)
                rank = dot(named.astype(BF16), before)
                turn = place[1] if b == 0 else 1 - place[1]
                base = ((2 * u + turn) * slots).astype(F32)
                column = (2 * u + b) * tokens
                code[:, column : column + tokens] = jnp.where(named > 0, rank + base, -1.0)
                gate[:, column : column + tokens] = weight
        pick = jnp.concatenate(selection(code[...], rows), axis=0).astype(BF16)
        wide = half // 3 if half % 384 == 0 else half
        for n in range(half // wide):
            columns = slice(n * wide, (n + 1) * wide)
            chosen = sum(
                dot(pick[:, 2 * u * tokens : 2 * (u + 1) * tokens], feeds[u][0 : 2 * tokens, columns])
                for u in range(units)
            )
            for e in range(local):
                packed[e, :, columns] = chosen[e * rows : (e + 1) * rows].astype(BF16)

    quarter = half // 2
    here = pl.multiple_of(place[0] * quarter, quarter)
    there = pl.multiple_of((1 - place[0]) * quarter, quarter)
    total = dot(packed[step, :, pl.ds(here, quarter)], own[0])
    total += dot(packed[step, :, pl.ds(there, quarter)], other[0])
    part[0] = total.astype(BF16)


def second_kernel(units, keep, send, place, *refs):
    code, gate, near, far, own, other = refs[:6]
    outs, total = refs[6:-1], refs[-1]
    local = code.shape[0]
    rows, hidden_width = near.shape[1:]
    half = total.shape[1]
    step = pl.program_id(0)
    wanted = lax.broadcasted_iota(jnp.int32, (rows, code.shape[1]), 0).astype(F32)
    same = wanted == code[pl.ds(step, 1), :]
    scale = jnp.sum(jnp.where(same, gate[pl.ds(step, 1), :], 0.0), axis=1, keepdims=True)
    hidden = jax.nn.gelu(near[0].astype(F32) + far[0].astype(F32)).astype(BF16)
    quarter = half // 2
    here = pl.multiple_of(place[0] * quarter, quarter)
    there = pl.multiple_of((1 - place[0]) * quarter, quarter)
    at = pl.ds(pl.multiple_of(step * rows, rows), rows)
    total[at, pl.ds(here, quarter)] = dot(hidden, own[0]) * scale
    total[at, pl.ds(there, quarter)] = dot(hidden, other[0]) * scale

    @pl.when(step == local - 1)
    def _():
        pick = jnp.concatenate(selection(code[...], rows), axis=0).astype(BF16)
        wide = half // 3 if half % 384 == 0 else half
        count = code.shape[1] // units
        for n in range(half // wide):
            columns = slice(n * wide, (n + 1) * wide)
            summed = lax.dot_general(
                pick,
                total[:, columns].astype(BF16),
                (((0,), (0,)), ((), ())),
                preferred_element_type=F32,
            )
            slot = 0
            if keep:
                outs[slot][:, columns] = summed[0:count]
                slot += 1
            if send:
                outs[slot][:, columns] = summed[(units - 1) * count :].astype(BF16)


def first_stage(feeds, place, own, other, picks):
    units = len(feeds)
    local, quarter, hidden = other.shape
    half = 2 * quarter
    tokens = feeds[0].shape[0] // 2 - META
    rows = 2 * units * CAP
    whole = lambda e, s: (0, 0)
    return pl.pallas_call(
        functools.partial(first_kernel, units, picks),
        grid_spec=pltpu.PrefetchScalarGridSpec(
            num_scalar_prefetch=1,
            grid=(local,),
            in_specs=[pl.BlockSpec(f.shape, whole) for f in feeds]
            + [
                pl.BlockSpec((1, quarter, hidden), lambda e, s: (s[0] * local + e, 0, 0)),
                pl.BlockSpec((1, quarter, hidden), lambda e, s: (e, 0, 0)),
            ],
            out_specs=[
                pl.BlockSpec((1, rows, hidden), lambda e, s: (e, 0, 0)),
                pl.BlockSpec((local, 2 * units * tokens), whole),
                pl.BlockSpec((local, 2 * units * tokens), whole),
            ],
            scratch_shapes=[pltpu.VMEM((local, rows, half), BF16)],
        ),
        out_shape=[
            jax.ShapeDtypeStruct((local, rows, hidden), BF16),
            jax.ShapeDtypeStruct((local, 2 * units * tokens), F32),
            jax.ShapeDtypeStruct((local, 2 * units * tokens), F32),
        ],
        cost_estimate=cost(2 * local * rows * half * hidden, 2 * local * half * hidden),
        name=f"first_{units}",
    )(place, *feeds, own, other)


def second_stage(units, code, gate, near, far, place, own, other, keep, send):
    local, hidden, quarter = other.shape
    half = 2 * quarter
    rows = near.shape[1]
    count = code.shape[1] // units
    whole = lambda e, s: (0, 0)
    shapes = []
    if keep:
        shapes.append(jax.ShapeDtypeStruct((count, half), F32))
    if send:
        shapes.append(jax.ShapeDtypeStruct((count, half), BF16))
    return pl.pallas_call(
        functools.partial(second_kernel, units, keep, send),
        grid_spec=pltpu.PrefetchScalarGridSpec(
            num_scalar_prefetch=1,
            grid=(local,),
            in_specs=[
                pl.BlockSpec(code.shape, whole),
                pl.BlockSpec(gate.shape, whole),
                pl.BlockSpec((1, rows, hidden), lambda e, s: (e, 0, 0)),
                pl.BlockSpec((1, rows, hidden), lambda e, s: (e, 0, 0)),
                pl.BlockSpec((1, hidden, quarter), lambda e, s: (s[0] * local + e, 0, 0)),
                pl.BlockSpec((1, hidden, quarter), lambda e, s: (e, 0, 0)),
            ],
            out_specs=[pl.BlockSpec(s.shape, whole) for s in shapes],
            scratch_shapes=[pltpu.VMEM((local * rows, half), F32)],
        ),
        out_shape=shapes,
        cost_estimate=cost(2 * local * rows * half * hidden, 2 * local * half * hidden),
        name=f"second_{units}",
    )(place, code, gate, near, far, own, other)


def shared_first_kernel(place, feed, own, other, part):
    quarter = own.shape[0]
    rows = part.shape[0] // 2
    here = pl.multiple_of(place[0] * quarter, quarter)
    there = pl.multiple_of((1 - place[0]) * quarter, quarter)
    total = dot(feed[0 : 2 * rows, pl.ds(here, quarter)], own[...])
    total += dot(feed[0 : 2 * rows, pl.ds(there, quarter)], other[...])
    for b in range(2):
        turn = place[1] if b == 0 else 1 - place[1]
        at = pl.ds(pl.multiple_of(turn * rows, rows), rows)
        part[at, :] = total[b * rows : (b + 1) * rows].astype(BF16)


def shared_second_kernel(place, near, far, own, other, out):
    quarter = own.shape[1]
    rows = near.shape[0] // 2
    here = pl.multiple_of(place[0] * quarter, quarter)
    there = pl.multiple_of((1 - place[0]) * quarter, quarter)
    hidden = jax.nn.gelu(near[...].astype(F32) + far[...].astype(F32)).astype(BF16)
    left, right = dot(hidden, own[...]), dot(hidden, other[...])
    for b in range(2):
        turn = place[1] if b == 0 else 1 - place[1]
        at = pl.ds(pl.multiple_of(turn * rows, rows), rows)
        out[at, pl.ds(here, quarter)] = left[b * rows : (b + 1) * rows]
        out[at, pl.ds(there, quarter)] = right[b * rows : (b + 1) * rows]


SMEM = pl.BlockSpec(memory_space=pltpu.SMEM)
VMEM = pl.BlockSpec(memory_space=pltpu.VMEM)


def exchanged_partials(tokens, expert_ids, gate_weights, expert_in, expert_out, shared_in, shared_out):
    rows, width = tokens.shape
    half = width // 2
    picks = expert_ids.shape[1]
    group = expert_in.shape[0]
    local = group // 2
    hidden = expert_in.shape[2]
    groups = lax.axis_size("expert")
    spot = lax.axis_index("dp")
    side, core = spot // 2, spot % 2
    lead = lax.axis_index("expert") * group + core * local
    place = jnp.stack([core, side, lead]).astype(jnp.int32)

    give_in = lax.dynamic_slice_in_dim(expert_in, (1 - core) * local, local, 0)
    other_in = swap(give_in, "dp", 1)
    mine, theirs = pl.pallas_call(
        norm_kernel,
        in_specs=[SMEM, VMEM, VMEM, VMEM],
        out_specs=[VMEM, VMEM],
        out_shape=[jax.ShapeDtypeStruct((rows + META, half), BF16)] * 2,
        cost_estimate=cost(20 * rows * width, 4 * rows * width),
        name="norm",
    )(place, tokens, expert_ids.T, gate_weights.T)
    peer = swap(theirs, "dp", 2)
    other_shared_in = swap(shared_in, "dp", 1)
    give_out = lax.dynamic_slice_in_dim(expert_out, (1 - core) * local, local, 0)
    other_out = swap(give_out, "dp", 1)
    other_shared_out = swap(shared_out, "dp", 1)

    unit = jnp.concatenate([mine[:rows], peer[:rows], mine[rows:], peer[rows:]], axis=0)
    away = [(g, swap(unit, "expert", g)) for g in range(1, groups)]
    beside = swap(unit, "dp", 1)

    chunks = [([unit], True, False)]
    for _, got in away:
        chunks.append(([got, swap(got, "dp", 1)], True, True))
    chunks.append(([beside], False, True))

    firsts = []
    for feeds, _, _ in chunks:
        part, code, gate = first_stage(feeds, place, expert_in, other_in, picks)
        firsts.append((part, code, gate, swap(part, "dp", 2)))
    shared_part = pl.pallas_call(
        shared_first_kernel,
        in_specs=[SMEM, VMEM, VMEM, VMEM],
        out_specs=VMEM,
        out_shape=jax.ShapeDtypeStruct((2 * rows, hidden), BF16),
        cost_estimate=cost(4 * rows * half * hidden, 2 * half * hidden),
        name="shared_first",
    )(place, unit, shared_in, other_shared_in)
    shared_far = swap(shared_part, "dp", 2)

    total = None
    for i, ((feeds, keep, send), (part, code, gate, far)) in enumerate(zip(chunks, firsts)):
        outs = second_stage(
            len(feeds), code, gate, part, far, place, expert_out, other_out, keep, send
        )
        if keep and not send:
            piece = outs[0]
        elif keep:
            joined = (outs[0] + swap(outs[1], "dp", 1).astype(F32)).astype(BF16)
            piece = swap(joined, "expert", away[i - 1][0]).astype(F32)
        else:
            piece = swap(outs[0], "dp", 1).astype(F32)
        total = piece if total is None else total + piece
    shared = pl.pallas_call(
        shared_second_kernel,
        in_specs=[SMEM, VMEM, VMEM, VMEM, VMEM],
        out_specs=VMEM,
        out_shape=jax.ShapeDtypeStruct((2 * rows, half), F32),
        cost_estimate=cost(4 * rows * half * hidden, 2 * half * hidden),
        name="shared_second",
    )(place, shared_part, shared_far, shared_out, other_shared_out)
    total = total + shared
    cross = swap(total[rows:].astype(BF16), "dp", 2).astype(F32)
    kept = total[:rows]
    low = side == 0
    added = jnp.concatenate([jnp.where(low, kept, cross), jnp.where(low, cross, kept)], axis=1)
    return (tokens.astype(F32) + added).astype(BF16)


def per_device(*args):
    tokens, expert_ids, expert_in = args[0], args[1], args[3]
    groups = lax.axis_size("expert")
    fits = (
        lax.axis_size("dp") == 4
        and expert_in.shape[0] % 16 == 0
        and groups & (groups - 1) == 0
        and groups <= 8
        and tokens.shape[0] % 128 == 0
        and tokens.shape[1] % 512 == 0
        and tokens.shape[1] // 2 >= 3 * tokens.shape[0]
        and expert_ids.shape[1] <= 8
        and expert_in.shape[2] % 128 == 0
    )
    return exchanged_partials(*args) if fits else gathered_weights(*args)


def solution(mesh):
    placed = (
        P(("sweep", "expert", "dp"), None),
        P(("sweep", "expert", "dp"), None),
        P(("sweep", "expert", "dp"), None),
        P(("sweep", "expert"), "dp", None),
        P(("sweep", "expert"), None, "dp"),
        P(("sweep", "dp"), None),
        P("sweep", "dp"),
    )
    return jax.shard_map(
        per_device,
        mesh=mesh,
        in_specs=placed,
        out_specs=P(("sweep", "expert", "dp"), None),
        check_vma=False,
    )
```

time: 625 us -> 224 us (0.36)
  waiting for transfers between devices: 489 us -> 72.7 us
  Pallas kernels: 0 us -> 104 us
  matrix products: 52.2 us -> 0 us
  local copies, waits for them, and re-layouts: 52.5 us -> 15.3 us
  between operations: 13.2 us -> 0.21 us
  starting transfers between devices: 12.1 us -> 21.8 us
    all_gather x4 -> x0, waiting for transfers between devices: 312 us -> none  [the longest x1 200 us: per_device(): lax.all_gather(expert_out, 'dp', axis=2, tiled=True)]
    all_to_all x2 -> x0, waiting for transfers between devices: 174 us -> none  [the longest x1 87.2 us: per_device(): lax.all_to_all(outgoing, 'expert', split_axis=0, concat_axis=0, tiled=True)]
    pallas_call x0 -> x13, Pallas kernels: none -> 104 us  [the longest x5 48.9 us: second_stage(): pl.pallas_call(functools.partial(second_kernel, units, keep, send), grid_...]
    ppermute x0 -> x26, waiting for transfers between devices: none -> 72.7 us  [swap(): return lax.ppermute(value, axis, [(i, i ^ mask) for i in range(size)])]
    dot_general x3 -> x0, matrix products: 52.2 us -> none  [the longest x1 28 us: run_experts(): jnp.einsum('gesd,edf->gesf', shard_piece, weight_in, preferred_element_ty...]
    ppermute x0 -> x26, starting transfers between devices: none -> 21.8 us  [swap(): return lax.ppermute(value, axis, [(i, i ^ mask) for i in range(size)])]
    reshape x4 -> x0, local copies, waits for them, and re-layouts: 21.3 us -> none  [the longest x2 14.2 us: per_device(): outgoing = outgoing.reshape(group_count, local_count, CAP, model_width)]
    all_to_all x2 -> x0, starting transfers between devices: 12.1 us -> none  [the longest x1 7.11 us: per_device(): lax.all_to_all(outgoing, 'expert', split_axis=0, concat_axis=0, tiled=True)]
  transfers between devices with their start and end apart: 6 -> 26, of which waited for: 4 -> 6; matrix products, arithmetic and copies ran while one was open for 17% -> 4% of each run, Pallas kernels for 0% -> 47%
where the time goes in v1:
time: 224 us; the launch traced here: 222 us
  Pallas kernels  104 us (46%)
  waiting for transfers between devices  72.7 us (32%)
  starting transfers between devices  21.8 us (10%)
  local copies, waits for them, and re-layouts  15.3 us (7%)
  other arithmetic  7.45 us (3%)
    ppermute x26, waiting for transfers between devices, swap(): return lax.ppermute(value, axis, [(i, i ^ mask) for i in range(size)])  72.7 us
    pallas_call x5, Pallas kernels, second_stage(): pl.pallas_call(functools.partial(second_kernel, units, keep, send), grid_...  48.9 us
    pallas_call x5, Pallas kernels, first_stage(): pl.pallas_call(functools.partial(first_kernel, units, picks), grid_spec=p...  47.3 us
    ppermute x26, starting transfers between devices, swap(): return lax.ppermute(value, axis, [(i, i ^ mask) for i in range(size)])  21.8 us
    unnamed x36, local copies, waits for them, and re-layouts  5.68 us
    dynamic_slice x1, local copies, waits for them, and re-layouts, exchanged_partials(): give_in = lax.dynamic_slice_in_dim(expert_in, (1 - core) * local, local, 0)  5.19 us
  transfers between devices with their start and end apart: 26, of which 6 were waited for; matrix products, arithmetic and copies ran while one was open for 4% of the time, Pallas kernels for 47%

profile of v1, /device:TPU:0, one launch (start us, length us, event | category | flops | bytes accessed | tf_op | source)
XLA Modules:
  0.0 221.6 jit_solution(297421637455334314)
XLA Ops:
  0.0 5.2 %constant_dynamic-slice_fusion.1 = bf16[8,384,768]{2,1,0:T(8,128)(2,1)} fusion(bf16[16,384,768]{2,1,0:T(8,128)(2,1)} %refs_1_.3, s32[]{:T(128)S(6)} %select_n.30), kind=kLoop, calls=%fused_computation.12 | loop fusion | bytes 9437188 | tf_op jit(solution)/shard_map/dynamic_slice | solution.py:312
  6.8 2.8 %constant_dynamic-slice_fusion = bf16[8,768,384]{2,1,0:T(8,128)(2,1)} fusion(bf16[16,768,384]{2,1,0:T(8,128)(2,1)S(1)} %copy-done, s32[]{:T(128)S(6)} %select_n.30), kind=kLoop, calls=%fused_computation.11 | loop fusion | bytes 9437188 | tf_op jit(solution)/shard_map/dynamic_slice | solution.py:324
  10.7 2.1 norm.1
  12.8 2.5 %collective-permute-start = (bf16[144,768]{1,0:T(8,128)(2,1)}, bf16[144,768]{1,0:T(8,128)(2,1)S(1)}, u32[]{:S(2)}, u32[]{:S(2)}) collective-permute-start(bf16[144,768]{1,0:T(8,128)(2,1)} %get-tuple-element.29), channel_id=1, source_target_pairs={{0,2},{1,3},{2,0},{3,1},{4,6},{5,7},{6,4},{7,5},{8,10},{9,11},{10,... | collective-permute-start | bytes 663560 | tf_op jit(solution)/shard_map/ppermute | solution.py:77
  17.0 4.6 %collective-permute-done = bf16[144,768]{1,0:T(8,128)(2,1)S(1)} collective-permute-done((bf16[144,768]{1,0:T(8,128)(2,1)}, bf16[144,768]{1,0:T(8,128)(2,1)S(1)}, u32[]{:S(2)}, u32[]{:S(2)}) %collective-permute-start) | collective-permute-done | bytes 221216 | tf_op jit(solution)/shard_map/ppermute | solution.py:77
  21.7 3.9 %collective-permute-start.14 = (bf16[288,768]{1,0:T(8,128)(2,1)S(1)}, bf16[288,768]{1,0:T(8,128)(2,1)S(1)}, u32[]{:S(2)}, u32[]{:S(2)}) collective-permute-start(bf16[288,768]{1,0:T(8,128)(2,1)S(1)} %pad_maximum_fusion.refs_0_.feed), channel_id=1, source_target_pairs={{0,12},{4,8},{8,4},{12,0},{1,13},{5,9},{9,5},{13,1},{2,14},{6,10},... | collective-permute-start | bytes 1327112 | tf_op jit(solution)/shard_map/ppermute | solution.py:77
  26.2 10.5 %collective-permute-done.14.refs_0_ = bf16[288,768]{1,0:T(8,128)(2,1)S(1)} collective-permute-done((bf16[288,768]{1,0:T(8,128)(2,1)S(1)}, bf16[288,768]{1,0:T(8,128)(2,1)S(1)}, u32[]{:S(2)}, u32[]{:S(2)}) %collective-permute-start.14) | collective-permute-done | bytes 442400 | tf_op jit(solution)/shard_map/ppermute | solution.py:77
  36.7 26.4 %collective-permute-done.9.refs_0_ = bf16[288,768]{1,0:T(8,128)(2,1)S(1)} collective-permute-done((bf16[288,768]{1,0:T(8,128)(2,1)S(1)}, bf16[288,768]{1,0:T(8,128)(2,1)S(1)}, u32[]{:S(2)}, u32[]{:S(2)}) %collective-permute-start.9) | collective-permute-done | bytes 442400 | tf_op jit(solution)/shard_map/ppermute | solution.py:77
  64.4 9.7 %first_2.5 = (bf16[8,80,768]{2,1,0:T(8,128)(2,1)}, f32[8,512]{1,0:T(8,128)}, f32[8,512]{1,0:T(8,128)}) custom-call(s32[3]{0:T(128)} %pad_add_fusion.place, bf16[288,768]{1,0:T(8,128)(2,1)} %copy-done.13, bf16[288,768]{1,0:T(8,128)(2,1)} %copy-done.15, bf16[16,384,768]{2,1,0:T(8,128)(2,1)} %refs_1_.3, bf16[8,384,768]{2,1,0:T(8,128)(2,1)} %collective-permute-done.1.refs_2_.refs_3_), custom_call_target="tpu_custom_call" | custom-call | flops 754974720 | bytes 9437184 | tf_op jit(solution)/shard_map/first_2/pallas_call | solution.py:208
  74.2 1.6 collective-permute-start.16
  76.5 9.8 %first_2.4 = (bf16[8,80,768]{2,1,0:T(8,128)(2,1)}, f32[8,512]{1,0:T(8,128)}, f32[8,512]{1,0:T(8,128)}) custom-call(s32[3]{0:T(128)} %pad_add_fusion.place, bf16[288,768]{1,0:T(8,128)(2,1)} %copy-done.12, bf16[288,768]{1,0:T(8,128)(2,1)} %copy-done.14, bf16[16,384,768]{2,1,0:T(8,128)(2,1)} %refs_1_.3, bf16[8,384,768]{2,1,0:T(8,128)(2,1)} %collective-permute-done.1.refs_2_.refs_3_), custom_call_target="tpu_custom_call" | custom-call | flops 754974720 | bytes 9437184 | tf_op jit(solution)/shard_map/first_2/pallas_call | solution.py:208
  86.8 9.7 %first_2.3 = (bf16[8,80,768]{2,1,0:T(8,128)(2,1)}, f32[8,512]{1,0:T(8,128)}, f32[8,512]{1,0:T(8,128)}) custom-call(s32[3]{0:T(128)} %pad_add_fusion.place, bf16[288,768]{1,0:T(8,128)(2,1)} %copy-done.11, bf16[288,768]{1,0:T(8,128)(2,1)} %collective-permute-done.5.refs_1_, bf16[16,384,768]{2,1,0:T(8,128)(2,1)} %refs_1_.3, ...), custom_call_target="tpu_custom_call" | custom-call | flops 754974720 | bytes 9437184 | tf_op jit(solution)/shard_map/first_2/pallas_call | solution.py:208
  96.6 1.5 collective-permute-start.6
  98.1 9.0 %first_1.3 = (bf16[8,40,768]{2,1,0:T(8,128)(2,1)}, f32[8,256]{1,0:T(8,128)}, f32[8,256]{1,0:T(8,128)}) custom-call(s32[3]{0:T(128)} %pad_add_fusion.place, bf16[288,768]{1,0:T(8,128)(2,1)} %collective-permute-done.19.refs_0_, bf16[16,384,768]{2,1,0:T(8,128)(2,1)} %refs_1_.3, bf16[8,384,768]{2,1,0:T(8,128)(2,1)} %collective-permute-done.1.refs_2_.refs_3_), custom_call_target="tpu_custom_call" | custom-call | flops 377487360 | bytes 9437184 | tf_op jit(solution)/shard_map/first_1/pallas_call | solution.py:208
  108.6 10.1 %second_2.5 = (f32[256,768]{1,0:T(8,128)}, bf16[256,768]{1,0:T(8,128)(2,1)}) custom-call(s32[3]{0:T(128)} %pad_add_fusion.place, f32[8,512]{1,0:T(8,128)} %get-tuple-element.43.refs_0_, f32[8,512]{1,0:T(8,128)} %get-tuple-element.44.refs_1_, bf16[8,80,768]{2,1,0:T(8,128)(2,1)} %get-tuple-element.45.refs_2_, bf16[8,80,768]{2,1,0:T(8,128)(2,1)} %copy-done.7, ...), custom_call_target="tpu_custom_call" | custom-call | flops 754974720 | bytes 9437184 | tf_op jit(solution)/shard_map/second_2/pallas_call | solution.py:246
  119.3 2.7 %shared_first.1.near = bf16[256,768]{1,0:T(8,128)(2,1)} custom-call(s32[3]{0:T(128)} %pad_add_fusion.place, bf16[288,768]{1,0:T(8,128)(2,1)} %copy-done.1, bf16[384,768]{1,0:T(8,128)(2,1)} %own.2, bf16[384,768]{1,0:T(8,128)(2,1)} %collective-permute-done.22.other), custom_call_target="tpu_custom_call" | custom-call | flops 301989888 | bytes 1179648 | tf_op jit(solution)/shard_map/shared_first/pallas_call | solution.py:341
  122.9 10.1 %second_2.4 = (f32[256,768]{1,0:T(8,128)}, bf16[256,768]{1,0:T(8,128)(2,1)}) custom-call(s32[3]{0:T(128)} %pad_add_fusion.place, f32[8,512]{1,0:T(8,128)} %get-tuple-element.38.refs_0_, f32[8,512]{1,0:T(8,128)} %get-tuple-element.39.refs_1_, bf16[8,80,768]{2,1,0:T(8,128)(2,1)} %get-tuple-element.40.refs_2_, bf16[8,80,768]{2,1,0:T(8,128)(2,1)} %copy-done.6, ...), custom_call_target="tpu_custom_call" | custom-call | flops 754974720 | bytes 9437184 | tf_op jit(solution)/shard_map/second_2/pallas_call | solution.py:246
  133.3 9.0 %first_1.2 = (bf16[8,40,768]{2,1,0:T(8,128)(2,1)}, f32[8,256]{1,0:T(8,128)}, f32[8,256]{1,0:T(8,128)}) custom-call(s32[3]{0:T(128)} %pad_add_fusion.place, bf16[288,768]{1,0:T(8,128)(2,1)} %copy-done.1, bf16[16,384,768]{2,1,0:T(8,128)(2,1)} %refs_1_.3, bf16[8,384,768]{2,1,0:T(8,128)(2,1)} %collective-permute-done.1.refs_2_.refs_3_), custom_call_target="tpu_custom_call" | custom-call | flops 377487360 | bytes 9437184 | tf_op jit(solution)/shard_map/first_1/pallas_call | solution.py:208
  142.3 8.8 %collective-permute-done.20.refs_3_ = bf16[8,40,768]{2,1,0:T(8,128)(2,1)} collective-permute-done((bf16[8,40,768]{2,1,0:T(8,128)(2,1)}, bf16[8,40,768]{2,1,0:T(8,128)(2,1)}, u32[]{:S(2)}, u32[]{:S(2)}) %collective-permute-start.20) | collective-permute-done | bytes 491552 | tf_op jit(solution)/shard_map/ppermute | solution.py:77
  151.1 1.5 collective-permute-start.23
  152.6 9.0 %second_1.3 = bf16[256,768]{1,0:T(8,128)(2,1)} custom-call(s32[3]{0:T(128)} %pad_add_fusion.place, f32[8,256]{1,0:T(8,128)} %get-tuple-element.48.refs_0_, f32[8,256]{1,0:T(8,128)} %get-tuple-element.49.refs_1_, bf16[8,40,768]{2,1,0:T(8,128)(2,1)} %get-tuple-element.50.refs_2_, bf16[8,40,768]{2,1,0:T(8,128)(2,1)} %collective-permute-done.20.refs_3_, ...), custom_call_target="tpu_custom_call" | custom-call | flops 377487360 | bytes 9437184 | tf_op jit(solution)/shard_map/second_1/pallas_call | solution.py:246
  162.6 10.3 %second_2.3 = (f32[256,768]{1,0:T(8,128)}, bf16[256,768]{1,0:T(8,128)(2,1)}) custom-call(s32[3]{0:T(128)} %pad_add_fusion.place, f32[8,512]{1,0:T(8,128)} %get-tuple-element.33.refs_0_, f32[8,512]{1,0:T(8,128)} %get-tuple-element.34.refs_1_, bf16[8,80,768]{2,1,0:T(8,128)(2,1)} %get-tuple-element.35.refs_2_, bf16[8,80,768]{2,1,0:T(8,128)(2,1)} %copy-done.5, ...), custom_call_target="tpu_custom_call" | custom-call | flops 754974720 | bytes 9437184 | tf_op jit(solution)/shard_map/second_2/pallas_call | solution.py:246
  173.0 1.8 add_convert_fusion
  176.3 2.5 %collective-permute-start.18 = (bf16[256,768]{1,0:T(8,128)(2,1)}, bf16[256,768]{1,0:T(8,128)(2,1)S(1)}, u32[]{:S(2)}, u32[]{:S(2)}) collective-permute-start(bf16[256,768]{1,0:T(8,128)(2,1)} %add_convert_fusion), channel_id=1, source_target_pairs={{0,12},{4,8},{8,4},{12,0},{1,13},{5,9},{9,5},{13,1},{2,14},{6,10},... | collective-permute-start | bytes 1179656 | tf_op jit(solution)/shard_map/ppermute | solution.py:77
  178.9 1.2 add_convert_fusion.2
  180.2 1.9 collective-permute-start.8
  182.1 3.1 %shared_second.1 = f32[256,768]{1,0:T(8,128)} custom-call(s32[3]{0:T(128)} %pad_add_fusion.place, bf16[256,768]{1,0:T(8,128)(2,1)} %shared_first.1.near, bf16[256,768]{1,0:T(8,128)(2,1)} %collective-permute-done.23.far, bf16[768,384]{1,0:T(8,128)(2,1)} %own.3, bf16[768,384]{1,0:T(8,128)(2,1)} %copy-done.10), custom_call_target="tpu_custom_call" | custom-call | flops 301989888 | bytes 1179648 | tf_op jit(solution)/shard_map/shared_second/pallas_call | solution.py:364
  185.2 9.3 %second_1.2 = f32[256,768]{1,0:T(8,128)} custom-call(s32[3]{0:T(128)} %pad_add_fusion.place, f32[8,256]{1,0:T(8,128)} %get-tuple-element.30.refs_0_, f32[8,256]{1,0:T(8,128)} %get-tuple-element.31.refs_1_, bf16[8,40,768]{2,1,0:T(8,128)(2,1)} %get-tuple-element.32.refs_2_, bf16[8,40,768]{2,1,0:T(8,128)(2,1)} %collective-permute-done.2.refs_3_, ...), custom_call_target="tpu_custom_call" | custom-call | flops 377487360 | bytes 9437184 | tf_op jit(solution)/shard_map/second_1/pallas_call | solution.py:246
  194.5 17.5 %collective-permute-done.13 = bf16[256,768]{1,0:T(8,128)(2,1)S(1)} collective-permute-done((bf16[256,768]{1,0:T(8,128)(2,1)S(1)}, bf16[256,768]{1,0:T(8,128)(2,1)S(1)}, u32[]{:S(2)}, u32[]{:S(2)}) %collective-permute-start.13) | collective-permute-done | bytes 393248 | tf_op jit(solution)/shard_map/ppermute | solution.py:77
  212.8 1.8 add_add_fusion
  214.6 1.2 collective-permute-start.25
  215.8 4.8 %collective-permute-done.25 = bf16[128,768]{1,0:T(8,128)(2,1)S(1)} collective-permute-done((bf16[128,768]{1,0:T(8,128)(2,1)S(1)}, bf16[128,768]{1,0:T(8,128)(2,1)S(1)}, u32[]{:S(2)}, u32[]{:S(2)}) %collective-permute-start.25) | collective-permute-done | bytes 196640 | tf_op jit(solution)/shard_map/ppermute | solution.py:77
  (84 shorter events, 15.2 us)
Async XLA Ops:
  5.2 58.5 %collective-permute-start.1 = (bf16[8,384,768]{2,1,0:T(8,128)(2,1)}, bf16[8,384,768]{2,1,0:T(8,128)(2,1)}, u32[]{:S(2)}, u32[]{:S(2)}) collective-permute-start(bf16[8,384,768]{2,1,0:T(8,128)(2,1)} %constant_dynamic-slice_fusion.1), channel_id=1, source_target_pairs={{0,1},{1,0},{2,3},{3,2},{4,5},{5,4},{6,7},{7,6},{8,9},{9,8},{10,11... | collective-permute-start | bytes 14155784 | tf_op jit(solution)/shard_map/ppermute | solution.py:77
  9.6 97.6 %collective-permute-start.3 = (bf16[8,768,384]{2,1,0:T(8,128)(2,1)}, bf16[8,768,384]{2,1,0:T(8,128)(2,1)}, u32[]{:S(2)}, u32[]{:S(2)}) collective-permute-start(bf16[8,768,384]{2,1,0:T(8,128)(2,1)} %constant_dynamic-slice_fusion), channel_id=1, source_target_pairs={{0,1},{1,0},{2,3},{3,2},{4,5},{5,4},{6,7},{7,6},{8,9},{9,8},{10,11... | collective-permute-start | bytes 14155784 | tf_op jit(solution)/shard_map/ppermute | solution.py:77
  12.8 8.8 %collective-permute-start = (bf16[144,768]{1,0:T(8,128)(2,1)}, bf16[144,768]{1,0:T(8,128)(2,1)S(1)}, u32[]{:S(2)}, u32[]{:S(2)}) collective-permute-start(bf16[144,768]{1,0:T(8,128)(2,1)} %get-tuple-element.29), channel_id=1, source_target_pairs={{0,2},{1,3},{2,0},{3,1},{4,6},{5,7},{6,4},{7,5},{8,10},{9,11},{10,... | collective-permute-start | bytes 663560 | tf_op jit(solution)/shard_map/ppermute | solution.py:77
  21.7 54.1 %copy-start.1 = (bf16[288,768]{1,0:T(8,128)(2,1)}, bf16[288,768]{1,0:T(8,128)(2,1)S(1)}, u32[]{:S(2)}) copy-start(bf16[288,768]{1,0:T(8,128)(2,1)S(1)} %pad_maximum_fusion.refs_0_.feed) | copy-start | bytes 1327108
  21.7 15.0 %collective-permute-start.14 = (bf16[288,768]{1,0:T(8,128)(2,1)S(1)}, bf16[288,768]{1,0:T(8,128)(2,1)S(1)}, u32[]{:S(2)}, u32[]{:S(2)}) collective-permute-start(bf16[288,768]{1,0:T(8,128)(2,1)S(1)} %pad_maximum_fusion.refs_0_.feed), channel_id=1, source_target_pairs={{0,12},{4,8},{8,4},{12,0},{1,13},{5,9},{9,5},{13,1},{2,14},{6,10},... | collective-permute-start | bytes 1327112 | tf_op jit(solution)/shard_map/ppermute | solution.py:77
  25.6 37.6 %collective-permute-start.9 = (bf16[288,768]{1,0:T(8,128)(2,1)S(1)}, bf16[288,768]{1,0:T(8,128)(2,1)S(1)}, u32[]{:S(2)}, u32[]{:S(2)}) collective-permute-start(bf16[288,768]{1,0:T(8,128)(2,1)S(1)} %pad_maximum_fusion.refs_0_.feed), channel_id=1, source_target_pairs={{0,8},{4,12},{8,0},{12,4},{1,9},{5,13},{9,1},{13,5},{2,10},{6,14},... | collective-permute-start | bytes 1327112 | tf_op jit(solution)/shard_map/ppermute | solution.py:77
  25.6 37.6 %collective-permute-start.4 = (bf16[288,768]{1,0:T(8,128)(2,1)S(1)}, bf16[288,768]{1,0:T(8,128)(2,1)S(1)}, u32[]{:S(2)}, u32[]{:S(2)}) collective-permute-start(bf16[288,768]{1,0:T(8,128)(2,1)S(1)} %pad_maximum_fusion.refs_0_.feed), channel_id=1, source_target_pairs={{0,4},{4,0},{8,12},{12,8},{1,5},{5,1},{9,13},{13,9},{2,6},{6,2},{1... | collective-permute-start | bytes 1327112 | tf_op jit(solution)/shard_map/ppermute | solution.py:77
  36.7 27.0 %copy-start.13 = (bf16[288,768]{1,0:T(8,128)(2,1)}, bf16[288,768]{1,0:T(8,128)(2,1)S(1)}, u32[]{:S(2)}) copy-start(bf16[288,768]{1,0:T(8,128)(2,1)S(1)} %collective-permute-done.14.refs_0_) | copy-start | bytes 1327108
  36.7 27.0 %collective-permute-start.15 = (bf16[288,768]{1,0:T(8,128)(2,1)S(1)}, bf16[288,768]{1,0:T(8,128)(2,1)S(1)}, u32[]{:S(2)}, u32[]{:S(2)}) collective-permute-start(bf16[288,768]{1,0:T(8,128)(2,1)S(1)} %collective-permute-done.14.refs_0_), channel_id=1, source_target_pairs={{0,1},{1,0},{2,3},{3,2},{4,5},{5,4},{6,7},{7,6},{8,9},{9,8},{10,11... | collective-permute-start | bytes 1327112 | tf_op jit(solution)/shard_map/ppermute | solution.py:77
  63.2 12.6 %collective-permute-start.10 = (bf16[288,768]{1,0:T(8,128)(2,1)S(1)}, bf16[288,768]{1,0:T(8,128)(2,1)S(1)}, u32[]{:S(2)}, u32[]{:S(2)}) collective-permute-start(bf16[288,768]{1,0:T(8,128)(2,1)S(1)} %collective-permute-done.9.refs_0_), channel_id=1, source_target_pairs={{0,1},{1,0},{2,3},{3,2},{4,5},{5,4},{6,7},{7,6},{8,9},{9,8},{10,11... | collective-permute-start | bytes 1327112 | tf_op jit(solution)/shard_map/ppermute | solution.py:77
  63.2 23.6 %collective-permute-start.5 = (bf16[288,768]{1,0:T(8,128)(2,1)S(1)}, bf16[288,768]{1,0:T(8,128)(2,1)}, u32[]{:S(2)}, u32[]{:S(2)}) collective-permute-start(bf16[288,768]{1,0:T(8,128)(2,1)S(1)} %collective-permute-done.4.refs_0_), channel_id=1, source_target_pairs={{0,1},{1,0},{2,3},{3,2},{4,5},{5,4},{6,7},{7,6},{8,9},{9,8},{10,11... | collective-permute-start | bytes 1327112 | tf_op jit(solution)/shard_map/ppermute | solution.py:77
  74.2 33.5 %collective-permute-start.16 = (bf16[8,80,768]{2,1,0:T(8,128)(2,1)}, bf16[8,80,768]{2,1,0:T(8,128)(2,1)S(1)}, u32[]{:S(2)}, u32[]{:S(2)}) collective-permute-start(bf16[8,80,768]{2,1,0:T(8,128)(2,1)} %get-tuple-element.45.refs_2_), channel_id=1, source_target_pairs={{0,2},{1,3},{2,0},{3,1},{4,6},{5,7},{6,4},{7,5},{8,10},{9,11},{10,... | collective-permute-start | bytes 2949128 | tf_op jit(solution)/shard_map/ppermute | solution.py:77
  75.8 22.3 %collective-permute-start.19 = (bf16[288,768]{1,0:T(8,128)(2,1)S(1)}, bf16[288,768]{1,0:T(8,128)(2,1)}, u32[]{:S(2)}, u32[]{:S(2)}) collective-permute-start(bf16[288,768]{1,0:T(8,128)(2,1)S(1)} %pad_maximum_fusion.refs_0_.feed), channel_id=1, source_target_pairs={{0,1},{1,0},{2,3},{3,2},{4,5},{5,4},{6,7},{7,6},{8,9},{9,8},{10,11... | collective-permute-start | bytes 1327112 | tf_op jit(solution)/shard_map/ppermute | solution.py:77
  86.3 35.7 %collective-permute-start.11 = (bf16[8,80,768]{2,1,0:T(8,128)(2,1)}, bf16[8,80,768]{2,1,0:T(8,128)(2,1)S(1)}, u32[]{:S(2)}, u32[]{:S(2)}) collective-permute-start(bf16[8,80,768]{2,1,0:T(8,128)(2,1)} %get-tuple-element.40.refs_2_), channel_id=1, source_target_pairs={{0,2},{1,3},{2,0},{3,1},{4,6},{5,7},{6,4},{7,5},{8,10},{9,11},{10,... | collective-permute-start | bytes 2949128 | tf_op jit(solution)/shard_map/ppermute | solution.py:77
  96.6 65.0 %collective-permute-start.6 = (bf16[8,80,768]{2,1,0:T(8,128)(2,1)}, bf16[8,80,768]{2,1,0:T(8,128)(2,1)S(1)}, u32[]{:S(2)}, u32[]{:S(2)}) collective-permute-start(bf16[8,80,768]{2,1,0:T(8,128)(2,1)} %get-tuple-element.35.refs_2_), channel_id=1, source_target_pairs={{0,2},{1,3},{2,0},{3,1},{4,6},{5,7},{6,4},{7,5},{8,10},{9,11},{10,... | collective-permute-start | bytes 2949128 | tf_op jit(solution)/shard_map/ppermute | solution.py:77
  98.1 20.9 %collective-permute-start.22 = (bf16[384,768]{1,0:T(8,128)(2,1)}, bf16[384,768]{1,0:T(8,128)(2,1)}, u32[]{:S(2)}, u32[]{:S(2)}) collective-permute-start(bf16[384,768]{1,0:T(8,128)(2,1)} %own.2), channel_id=1, source_target_pairs={{0,1},{1,0},{2,3},{3,2},{4,5},{5,4},{6,7},{7,6},{8,9},{9,8},{10,11... | collective-permute-start | bytes 1769480 | tf_op jit(solution)/shard_map/ppermute | solution.py:77
  107.1 43.9 %collective-permute-start.20 = (bf16[8,40,768]{2,1,0:T(8,128)(2,1)}, bf16[8,40,768]{2,1,0:T(8,128)(2,1)}, u32[]{:S(2)}, u32[]{:S(2)}) collective-permute-start(bf16[8,40,768]{2,1,0:T(8,128)(2,1)} %get-tuple-element.50.refs_2_), channel_id=1, source_target_pairs={{0,2},{1,3},{2,0},{3,1},{4,6},{5,7},{6,4},{7,5},{8,10},{9,11},{10,... | collective-permute-start | bytes 1474568 | tf_op jit(solution)/shard_map/ppermute | solution.py:77
  118.8 54.1 %collective-permute-start.17 = (bf16[256,768]{1,0:T(8,128)(2,1)}, bf16[256,768]{1,0:T(8,128)(2,1)}, u32[]{:S(2)}, u32[]{:S(2)}) collective-permute-start(bf16[256,768]{1,0:T(8,128)(2,1)} %get-tuple-element.47), channel_id=1, source_target_pairs={{0,1},{1,0},{2,3},{3,2},{4,5},{5,4},{6,7},{7,6},{8,9},{9,8},{10,11... | collective-permute-start | bytes 1179656 | tf_op jit(solution)/shard_map/ppermute | solution.py:77
  119.0 61.1 %collective-permute-start.24 = (bf16[768,384]{1,0:T(8,128)(2,1)}, bf16[768,384]{1,0:T(8,128)(2,1)S(1)}, u32[]{:S(2)}, u32[]{:S(2)}) collective-permute-start(bf16[768,384]{1,0:T(8,128)(2,1)} %own.3), channel_id=1, source_target_pairs={{0,1},{1,0},{2,3},{3,2},{4,5},{5,4},{6,7},{7,6},{8,9},{9,8},{10,11... | collective-permute-start | bytes 1769480 | tf_op jit(solution)/shard_map/ppermute | solution.py:77
  133.1 18.0 %copy-start.4 = (bf16[256,768]{1,0:T(8,128)(2,1)S(1)}, bf16[256,768]{1,0:T(8,128)(2,1)}, u32[]{:S(2)}) copy-start(bf16[256,768]{1,0:T(8,128)(2,1)} %shared_first.1.near) | copy-start | bytes 1179652
  133.1 41.7 %collective-permute-start.12 = (bf16[256,768]{1,0:T(8,128)(2,1)}, bf16[256,768]{1,0:T(8,128)(2,1)}, u32[]{:S(2)}, u32[]{:S(2)}) collective-permute-start(bf16[256,768]{1,0:T(8,128)(2,1)} %get-tuple-element.42), channel_id=1, source_target_pairs={{0,1},{1,0},{2,3},{3,2},{4,5},{5,4},{6,7},{7,6},{8,9},{9,8},{10,11... | collective-permute-start | bytes 1179656 | tf_op jit(solution)/shard_map/ppermute | solution.py:77
  151.1 29.1 %collective-permute-start.23 = (bf16[256,768]{1,0:T(8,128)(2,1)S(1)}, bf16[256,768]{1,0:T(8,128)(2,1)}, u32[]{:S(2)}, u32[]{:S(2)}) collective-permute-start(bf16[256,768]{1,0:T(8,128)(2,1)S(1)} %copy-done.4), channel_id=1, source_target_pairs={{0,2},{1,3},{2,0},{3,1},{4,6},{5,7},{6,4},{7,5},{8,10},{9,11},{10,... | collective-permute-start | bytes 1179656 | tf_op jit(solution)/shard_map/ppermute | solution.py:77
  161.6 23.6 %collective-permute-start.2 = (bf16[8,40,768]{2,1,0:T(8,128)(2,1)}, bf16[8,40,768]{2,1,0:T(8,128)(2,1)}, u32[]{:S(2)}, u32[]{:S(2)}) collective-permute-start(bf16[8,40,768]{2,1,0:T(8,128)(2,1)} %get-tuple-element.32.refs_2_), channel_id=1, source_target_pairs={{0,2},{1,3},{2,0},{3,1},{4,6},{5,7},{6,4},{7,5},{8,10},{9,11},{10,... | collective-permute-start | bytes 1474568 | tf_op jit(solution)/shard_map/ppermute | solution.py:77
  172.9 3.5 %collective-permute-start.7 = (bf16[256,768]{1,0:T(8,128)(2,1)}, bf16[256,768]{1,0:T(8,128)(2,1)S(1)}, u32[]{:S(2)}, u32[]{:S(2)}) collective-permute-start(bf16[256,768]{1,0:T(8,128)(2,1)} %get-tuple-element.37), channel_id=1, source_target_pairs={{0,1},{1,0},{2,3},{3,2},{4,5},{5,4},{6,7},{7,6},{8,9},{9,8},{10,11... | collective-permute-start | bytes 1179656 | tf_op jit(solution)/shard_map/ppermute | solution.py:77
  174.8 19.7 %collective-permute-start.21 = (bf16[256,768]{1,0:T(8,128)(2,1)}, bf16[256,768]{1,0:T(8,128)(2,1)}, u32[]{:S(2)}, u32[]{:S(2)}) collective-permute-start(bf16[256,768]{1,0:T(8,128)(2,1)} %second_1.3), channel_id=1, source_target_pairs={{0,1},{1,0},{2,3},{3,2},{4,5},{5,4},{6,7},{7,6},{8,9},{9,8},{10,11... | collective-permute-start | bytes 1179656 | tf_op jit(solution)/shard_map/ppermute | solution.py:77
  176.3 18.1 %collective-permute-start.18 = (bf16[256,768]{1,0:T(8,128)(2,1)}, bf16[256,768]{1,0:T(8,128)(2,1)S(1)}, u32[]{:S(2)}, u32[]{:S(2)}) collective-permute-start(bf16[256,768]{1,0:T(8,128)(2,1)} %add_convert_fusion), channel_id=1, source_target_pairs={{0,12},{4,8},{8,4},{12,0},{1,13},{5,9},{9,5},{13,1},{2,14},{6,10},... | collective-permute-start | bytes 1179656 | tf_op jit(solution)/shard_map/ppermute | solution.py:77
  180.1 31.9 %collective-permute-start.13 = (bf16[256,768]{1,0:T(8,128)(2,1)S(1)}, bf16[256,768]{1,0:T(8,128)(2,1)S(1)}, u32[]{:S(2)}, u32[]{:S(2)}) collective-permute-start(bf16[256,768]{1,0:T(8,128)(2,1)S(1)} %add_convert_fusion.1), channel_id=1, source_target_pairs={{0,8},{4,12},{8,0},{12,4},{1,9},{5,13},{9,1},{13,5},{2,10},{6,14},... | collective-permute-start | bytes 1179656 | tf_op jit(solution)/shard_map/ppermute | solution.py:77
  180.2 32.6 %collective-permute-start.8 = (bf16[256,768]{1,0:T(8,128)(2,1)S(1)}, bf16[256,768]{1,0:T(8,128)(2,1)}, u32[]{:S(2)}, u32[]{:S(2)}) collective-permute-start(bf16[256,768]{1,0:T(8,128)(2,1)S(1)} %add_convert_fusion.2), channel_id=1, source_target_pairs={{0,4},{4,0},{8,12},{12,8},{1,5},{5,1},{9,13},{13,9},{2,6},{6,2},{1... | collective-permute-start | bytes 1179656 | tf_op jit(solution)/shard_map/ppermute | solution.py:77
  185.2 27.6 %copy-start.2 = (f32[256,768]{1,0:T(8,128)S(1)}, f32[256,768]{1,0:T(8,128)}, u32[]{:S(2)}) copy-start(f32[256,768]{1,0:T(8,128)} %shared_second.1) | copy-start | bytes 2359300
  194.5 26.3 %copy-start.3 = (bf16[128,1536]{1,0:T(8,128)(2,1)S(1)}, bf16[128,1536]{1,0:T(8,128)(2,1)}, u32[]{:S(2)}) copy-start(bf16[128,1536]{1,0:T(8,128)(2,1)} %tokens.1) | copy-start | bytes 1179652
  194.5 17.6 %copy-start.16 = (bf16[256,768]{1,0:T(8,128)(2,1)}, bf16[256,768]{1,0:T(8,128)(2,1)S(1)}, u32[]{:S(2)}) copy-start(bf16[256,768]{1,0:T(8,128)(2,1)S(1)} %collective-permute-done.18) | copy-start | bytes 1179652
  214.6 6.0 %collective-permute-start.25 = (bf16[128,768]{1,0:T(8,128)(2,1)S(1)}, bf16[128,768]{1,0:T(8,128)(2,1)S(1)}, u32[]{:S(2)}, u32[]{:S(2)}) collective-permute-start(bf16[128,768]{1,0:T(8,128)(2,1)S(1)} %slice.32), channel_id=1, source_target_pairs={{0,2},{1,3},{2,0},{3,1},{4,6},{5,7},{6,4},{7,5},{8,10},{9,11},{10,... | collective-permute-start | bytes 589832 | tf_op jit(solution)/shard_map/ppermute | solution.py:77
  (12 other events, 59.1 us)

commit v2 on v0

v2 whole, which is shorter than its diff:
```python
import functools

import jax
import jax.numpy as jnp
from jax import lax
from jax.experimental import pallas as pl
from jax.experimental.pallas import tpu as pltpu
from jax.sharding import PartitionSpec as P


CAP = 20
F32 = jnp.float32
BF16 = jnp.bfloat16
KERNEL_FLOPS = 10_000_000
META = 16


def layer_norm(tokens):
    values = tokens.astype(F32)
    center = values - jnp.mean(values, axis=-1, keepdims=True)
    spread = jnp.mean(center * center, axis=-1, keepdims=True)
    return (center * lax.rsqrt(spread + 1e-06)).astype(BF16)


def copy_slots(expert_ids, expert_count):
    expert_iota = jnp.arange(expert_count, dtype=jnp.int32)
    matches = (expert_ids[..., None] == expert_iota).astype(jnp.int32)
    per_token = jnp.sum(matches, axis=-2, dtype=jnp.int32)
    earlier = jnp.cumsum(per_token, axis=-2, dtype=jnp.int32) - per_token
    return jnp.sum(matches * earlier[..., None, :], axis=-1, dtype=jnp.int32)


def run_experts(shard_piece, weight_in, weight_out):
    pre_act = jnp.einsum("gesd,edf->gesf", shard_piece, weight_in, preferred_element_type=F32)
    hidden = jax.nn.gelu(pre_act).astype(BF16)
    return jnp.einsum("gesf,efd->gesd", hidden, weight_out, preferred_element_type=F32).astype(BF16)


def gathered_weights(tokens, expert_ids, gate_weights, expert_in, expert_out, shared_in, shared_out):
    row_count, model_width = tokens.shape
    pick_count = expert_ids.shape[1]
    local_count = expert_in.shape[0]
    group_count = lax.axis_size("expert")
    expert_total = local_count * group_count
    normed = layer_norm(tokens)
    full_in = lax.all_gather(expert_in, "dp", axis=1, tiled=True)
    full_out = lax.all_gather(expert_out, "dp", axis=2, tiled=True)
    slot_of = copy_slots(expert_ids, expert_total)
    positions = (expert_ids * CAP + slot_of).reshape(-1)
    copies = jnp.repeat(normed, pick_count, axis=0)
    outgoing = jnp.zeros((expert_total * CAP, model_width), BF16).at[positions].set(copies)
    outgoing = outgoing.reshape(group_count, local_count, CAP, model_width)
    received = lax.all_to_all(outgoing, "expert", split_axis=0, concat_axis=0, tiled=True)
    returned = lax.all_to_all(
        run_experts(received, full_in, full_out), "expert", split_axis=0, concat_axis=0, tiled=True
    )
    results = returned.reshape(expert_total * CAP, model_width)[positions].reshape(
        row_count, pick_count, model_width
    )
    routed = jnp.sum(results.astype(F32) * gate_weights[:, :, None], axis=1)
    shared_pre = jnp.dot(
        normed, lax.all_gather(shared_in, "dp", axis=0, tiled=True), preferred_element_type=F32
    )
    shared_hidden = jax.nn.gelu(shared_pre).astype(BF16)
    shared_result = jnp.dot(
        shared_hidden,
        lax.all_gather(shared_out, "dp", axis=1, tiled=True),
        preferred_element_type=F32,
    )
    return (tokens.astype(F32) + shared_result + routed).astype(BF16)


def dot(a, b):
    return jnp.dot(a, b, preferred_element_type=F32)


def swap(value, axis, mask):
    size = lax.axis_size(axis)
    return lax.ppermute(value, axis, [(i, i ^ mask) for i in range(size)])


def cost(flops, moved):
    return pl.CostEstimate(flops=int(flops), bytes_accessed=int(moved), transcendentals=0)


def norm_kernel(place, tokens, ids, gates, source, mine, theirs, given, held, came, left):
    local = held.shape[0]
    base = (1 - place[0]) * local

    def fetch(e):
        return pltpu.make_async_copy(source.at[base + e], held.at[e], came.at[e])

    def put(e):
        return pltpu.make_async_copy(held.at[e], given.at[e], left.at[e])

    for e in range(local):
        fetch(e).start()
    rows, width = tokens.shape
    half = width // 2
    values = tokens[...].astype(F32)
    center = values - jnp.mean(values, axis=-1, keepdims=True)
    spread = jnp.mean(center * center, axis=-1, keepdims=True)
    normed = (center * lax.rsqrt(spread + 1e-06)).astype(BF16)
    low = place[1] == 0
    mine[0:rows, :] = jnp.where(low, normed[:, :half], normed[:, half:])
    theirs[0:rows, :] = jnp.where(low, normed[:, half:], normed[:, :half])
    gate = gates[...]
    high = gate.astype(BF16).astype(F32)
    rest = gate - high
    picks = ids.shape[0]
    spare = jnp.zeros((picks, half - 3 * rows), F32)
    table = jnp.concatenate([ids[...].astype(F32), high, rest, spare], axis=1)
    table = jnp.concatenate([table, jnp.zeros((META - picks, half), F32)], axis=0).astype(BF16)
    mine[rows : rows + META, :] = table
    theirs[rows : rows + META, :] = table
    for e in range(local):
        fetch(e).wait()
        put(e).start()
    for e in range(local):
        put(e).wait()


def give_kernel(place, source, after, given, held, came, left):
    local = held.shape[0]
    base = (1 - place[0]) * local

    def fetch(e):
        return pltpu.make_async_copy(source.at[base + e], held.at[e], came.at[e])

    def put(e):
        return pltpu.make_async_copy(held.at[e], given.at[e], left.at[e])

    for e in range(local):
        fetch(e).start()
    for e in range(local):
        fetch(e).wait()
        put(e).start()
    for e in range(local):
        put(e).wait()


def selection(codes, rows):
    count, tokens = codes.shape
    wanted = lax.broadcasted_iota(jnp.int32, (rows, tokens), 0).astype(F32)
    return [(wanted == codes[e : e + 1, :]).astype(F32) for e in range(count)]


def weight_copies(place, own, other, held_own, held_other, came):
    local = held_own.shape[0]

    def copies(e):
        return (
            pltpu.make_async_copy(own.at[place[0] * local + e], held_own.at[e], came.at[0, e]),
            pltpu.make_async_copy(other.at[e], held_other.at[e], came.at[1, e]),
        )

    return copies


def first_kernel(units, picks, place, *refs):
    feeds, refs = refs[:units], refs[units:]
    own, other, _, part, code, gate, packed, held_own, held_other, made, came, left = refs
    local, rows, half = packed.shape
    slots = rows // (2 * units)
    tokens = feeds[0].shape[0] // 2 - META
    copies = weight_copies(place, own, other, held_own, held_other, came)
    for e in range(local):
        for c in copies(e):
            c.start()

    before = (
        lax.broadcasted_iota(jnp.int32, (tokens, tokens), 0)
        < lax.broadcasted_iota(jnp.int32, (tokens, tokens), 1)
    ).astype(F32).astype(BF16)
    expert = (lax.broadcasted_iota(jnp.int32, (local, tokens), 0) + place[2]).astype(F32)
    for u in range(units):
        for b in range(2):
            at = 2 * tokens + b * META
            table = feeds[u][at : at + META, 0 : 3 * tokens].astype(F32)
            named = jnp.zeros((local, tokens), F32)
            weight = jnp.zeros((local, tokens), F32)
            for k in range(picks):
                same = table[k : k + 1, 0:tokens] == expert
                value = table[k : k + 1, tokens : 2 * tokens] + table[k : k + 1, 2 * tokens :]
                named = jnp.where(same, 1.0, named)
                weight = jnp.where(same, value, weight)
            rank = dot(named.astype(BF16), before)
            turn = place[1] if b == 0 else 1 - place[1]
            base = ((2 * u + turn) * slots).astype(F32)
            column = (2 * u + b) * tokens
            code[:, column : column + tokens] = jnp.where(named > 0, rank + base, -1.0)
            gate[:, column : column + tokens] = weight
    pick = jnp.concatenate(selection(code[...], rows), axis=0).astype(BF16)
    wide = half // 3 if half % 384 == 0 else half
    for n in range(half // wide):
        columns = slice(n * wide, (n + 1) * wide)
        chosen = sum(
            dot(pick[:, 2 * u * tokens : 2 * (u + 1) * tokens], feeds[u][0 : 2 * tokens, columns])
            for u in range(units)
        )
        for e in range(local):
            packed[e, :, columns] = chosen[e * rows : (e + 1) * rows].astype(BF16)

    quarter = half // 2
    here = pl.multiple_of(place[0] * quarter, quarter)
    there = pl.multiple_of((1 - place[0]) * quarter, quarter)

    def put(e):
        return pltpu.make_async_copy(made.at[e], part.at[e], left.at[e])

    @pl.loop(0, local // 2)
    def _(pair):
        for e in (2 * pair, 2 * pair + 1):
            for c in copies(e):
                c.wait()
            total = dot(packed[e, :, pl.ds(here, quarter)], held_own[e])
            total += dot(packed[e, :, pl.ds(there, quarter)], held_other[e])
            made[e] = total.astype(BF16)
        for e in (2 * pair, 2 * pair + 1):
            put(e).start()

    @pl.loop(0, local)
    def _(e):
        put(e).wait()


def second_kernel(units, keep, send, place, *refs):
    code, gate, near, far, own, other, _ = refs[:7]
    outs, (total, held_own, held_other, came) = refs[7:-4], refs[-4:]
    local = code.shape[0]
    rows = near.shape[1]
    half = total.shape[1]
    copies = weight_copies(place, own, other, held_own, held_other, came)
    for e in range(local):
        for c in copies(e):
            c.start()
    quarter = half // 2
    here = pl.multiple_of(place[0] * quarter, quarter)
    there = pl.multiple_of((1 - place[0]) * quarter, quarter)
    wanted = lax.broadcasted_iota(jnp.int32, (rows, code.shape[1]), 0).astype(F32)

    @pl.loop(0, local // 2)
    def _(pair):
        for e in (2 * pair, 2 * pair + 1):
            same = wanted == code[pl.ds(e, 1), :]
            scale = jnp.sum(jnp.where(same, gate[pl.ds(e, 1), :], 0.0), axis=1, keepdims=True)
            hidden = jax.nn.gelu(near[e].astype(F32) + far[e].astype(F32)).astype(BF16)
            for c in copies(e):
                c.wait()
            at = pl.ds(pl.multiple_of(e * rows, rows), rows)
            total[at, pl.ds(here, quarter)] = dot(hidden, held_own[e]) * scale
            total[at, pl.ds(there, quarter)] = dot(hidden, held_other[e]) * scale

    pick = jnp.concatenate(selection(code[...], rows), axis=0).astype(BF16)
    wide = half // 3 if half % 384 == 0 else half
    count = code.shape[1] // units
    for n in range(half // wide):
        columns = slice(n * wide, (n + 1) * wide)
        summed = lax.dot_general(
            pick,
            total[:, columns].astype(BF16),
            (((0,), (0,)), ((), ())),
            preferred_element_type=F32,
        )
        slot = 0
        if keep:
            outs[slot][:, columns] = summed[0:count]
            slot += 1
        if send:
            outs[slot][:, columns] = summed[(units - 1) * count :].astype(BF16)


SMEM = pl.BlockSpec(memory_space=pltpu.SMEM)
VMEM = pl.BlockSpec(memory_space=pltpu.VMEM)
ANY = pl.BlockSpec(memory_space=pl.ANY)
HBM = pl.BlockSpec(memory_space=pltpu.HBM)
GRANT = 55 << 20


def give_scratch(local, shape):
    return [
        pltpu.VMEM((local, *shape), BF16),
        pltpu.SemaphoreType.DMA((local,)),
        pltpu.SemaphoreType.DMA((local,)),
    ]


def first_stage(feeds, place, own, other, after, picks):
    units = len(feeds)
    local, quarter, hidden = other.shape
    half = 2 * quarter
    tokens = feeds[0].shape[0] // 2 - META
    rows = 2 * units * CAP
    table = jax.ShapeDtypeStruct((local, 2 * units * tokens), F32)
    return pl.pallas_call(
        functools.partial(first_kernel, units, picks),
        in_specs=[SMEM] + [VMEM] * units + [HBM, HBM, ANY],
        out_specs=[ANY, VMEM, VMEM],
        scratch_shapes=[
            pltpu.VMEM((local, rows, half), BF16),
            pltpu.VMEM((local, quarter, hidden), BF16),
            pltpu.VMEM((local, quarter, hidden), BF16),
            pltpu.VMEM((local, rows, hidden), BF16),
            pltpu.SemaphoreType.DMA((2, local)),
            pltpu.SemaphoreType.DMA((local,)),
        ],
        out_shape=[jax.ShapeDtypeStruct((local, rows, hidden), BF16), table, table],
        compiler_params=pltpu.CompilerParams(vmem_limit_bytes=GRANT),
        cost_estimate=cost(KERNEL_FLOPS, 2 * local * half * hidden),
    )(place, *feeds, own, other, after)


def second_stage(units, code, gate, near, far, place, own, other, after, keep, send):
    local, hidden, quarter = other.shape
    half = 2 * quarter
    rows = near.shape[1]
    count = code.shape[1] // units
    shapes = []
    if keep:
        shapes.append(jax.ShapeDtypeStruct((count, half), F32))
    if send:
        shapes.append(jax.ShapeDtypeStruct((count, half), BF16))
    return pl.pallas_call(
        functools.partial(second_kernel, units, keep, send),
        in_specs=[SMEM] + [VMEM] * 4 + [HBM, HBM, ANY],
        out_specs=[VMEM] * len(shapes),
        scratch_shapes=[
            pltpu.VMEM((local * rows, half), F32),
            pltpu.VMEM((local, hidden, quarter), BF16),
            pltpu.VMEM((local, hidden, quarter), BF16),
            pltpu.SemaphoreType.DMA((2, local)),
        ],
        out_shape=shapes,
        compiler_params=pltpu.CompilerParams(vmem_limit_bytes=GRANT),
        cost_estimate=cost(KERNEL_FLOPS, 2 * local * half * hidden),
    )(place, code, gate, near, far, own, other, after)


def shared_first_kernel(place, feed, own, other, _, part):
    quarter = own.shape[0]
    rows = part.shape[0] // 2
    here = pl.multiple_of(place[0] * quarter, quarter)
    there = pl.multiple_of((1 - place[0]) * quarter, quarter)
    total = dot(feed[0 : 2 * rows, pl.ds(here, quarter)], own[...])
    total += dot(feed[0 : 2 * rows, pl.ds(there, quarter)], other[...])
    for b in range(2):
        turn = place[1] if b == 0 else 1 - place[1]
        at = pl.ds(pl.multiple_of(turn * rows, rows), rows)
        part[at, :] = total[b * rows : (b + 1) * rows].astype(BF16)


def shared_second_kernel(place, near, far, own, other, _, out):
    quarter = own.shape[1]
    rows = near.shape[0] // 2
    here = pl.multiple_of(place[0] * quarter, quarter)
    there = pl.multiple_of((1 - place[0]) * quarter, quarter)
    hidden = jax.nn.gelu(near[...].astype(F32) + far[...].astype(F32)).astype(BF16)
    left, right = dot(hidden, own[...]), dot(hidden, other[...])
    for b in range(2):
        turn = place[1] if b == 0 else 1 - place[1]
        at = pl.ds(pl.multiple_of(turn * rows, rows), rows)
        out[at, pl.ds(here, quarter)] = left[b * rows : (b + 1) * rows]
        out[at, pl.ds(there, quarter)] = right[b * rows : (b + 1) * rows]


def exchanged_partials(tokens, expert_ids, gate_weights, expert_in, expert_out, shared_in, shared_out):
    rows, width = tokens.shape
    half = width // 2
    quarter = half // 2
    picks = expert_ids.shape[1]
    group = expert_in.shape[0]
    local = group // 2
    hidden = expert_in.shape[2]
    groups = lax.axis_size("expert")
    spot = lax.axis_index("dp")
    side, core = spot // 2, spot % 2
    lead = lax.axis_index("expert") * group + core * local
    place = jnp.stack([core, side, lead]).astype(jnp.int32)
    grant = pltpu.CompilerParams(vmem_limit_bytes=GRANT)

    mine, theirs, give_in = pl.pallas_call(
        norm_kernel,
        in_specs=[SMEM, VMEM, VMEM, VMEM, HBM],
        out_specs=[VMEM, VMEM, HBM],
        out_shape=[jax.ShapeDtypeStruct((rows + META, half), BF16)] * 2
        + [jax.ShapeDtypeStruct((local, quarter, hidden), BF16)],
        scratch_shapes=give_scratch(local, (quarter, hidden)),
        compiler_params=grant,
        cost_estimate=cost(KERNEL_FLOPS, 4 * rows * width),
        name="norm",
    )(place, tokens, expert_ids.T, gate_weights.T, expert_in)
    peer = swap(theirs, "dp", 2)
    other_in = swap(give_in, "dp", 1)
    give_out = pl.pallas_call(
        give_kernel,
        in_specs=[SMEM, HBM, ANY],
        out_specs=HBM,
        out_shape=jax.ShapeDtypeStruct((local, hidden, quarter), BF16),
        scratch_shapes=give_scratch(local, (hidden, quarter)),
        compiler_params=grant,
        cost_estimate=cost(KERNEL_FLOPS, 4 * local * hidden * quarter),
        name="give_out",
    )(place, expert_out, mine)
    other_shared_in = swap(shared_in, "dp", 1)
    other_out = swap(give_out, "dp", 1)
    other_shared_out = swap(shared_out, "dp", 1)

    unit = jnp.concatenate([mine[:rows], peer[:rows], mine[rows:], peer[rows:]], axis=0)
    feeds = {0: [unit]}
    far_groups = list(range(groups - 1, 0, -1))
    for g in far_groups:
        got = swap(unit, "expert", g)
        feeds[g] = [got, swap(got, "dp", 1)]
    feeds[groups] = [swap(unit, "dp", 1)]

    firsts = {}
    shared_part = shared_far = None
    sums = []
    last = give_out

    def first(g):
        nonlocal last
        part, code, gate = first_stage(feeds[g], place, expert_in, other_in, last, picks)
        firsts[g] = (part, code, gate, swap(part, "dp", 2))
        last = code

    def second(g):
        nonlocal last
        part, code, gate, far = firsts[g]
        keep, send = g != groups, g != 0
        outs = second_stage(
            len(feeds[g]), code, gate, part, far, place, expert_out, other_out, last,
            keep, send,
        )
        last = outs[0]
        if not send:
            sums.append(outs[0])
            return
        came = swap(outs[-1], "dp", 1).astype(F32)
        if keep:
            joined = (outs[0] + came).astype(BF16)
            came = swap(joined, "expert", g).astype(F32)
            last = joined
        sums.append(came)

    first(0)
    shared_part = pl.pallas_call(
        shared_first_kernel,
        in_specs=[SMEM, VMEM, VMEM, VMEM, ANY],
        out_specs=VMEM,
        out_shape=jax.ShapeDtypeStruct((2 * rows, hidden), BF16),
        cost_estimate=cost(KERNEL_FLOPS, 2 * half * hidden),
        compiler_params=grant,
        name="shared_first",
    )(place, unit, shared_in, other_shared_in, last)
    last = shared_part
    shared_far = swap(shared_part, "dp", 2)
    second(0)
    first(far_groups[0])
    shared = pl.pallas_call(
        shared_second_kernel,
        in_specs=[SMEM, VMEM, VMEM, VMEM, VMEM, ANY],
        out_specs=VMEM,
        out_shape=jax.ShapeDtypeStruct((2 * rows, half), F32),
        cost_estimate=cost(KERNEL_FLOPS, 2 * half * hidden),
        compiler_params=grant,
        name="shared_second",
    )(place, shared_part, shared_far, shared_out, other_shared_out, last)
    last = shared
    sums.append(shared)
    for g in far_groups[1:]:
        first(g)
    first(groups)
    for g in far_groups:
        second(g)
    second(groups)

    total = sum(sums[1:], sums[0])
    cross = swap(total[rows:].astype(BF16), "dp", 2).astype(F32)
    kept = total[:rows]
    low = side == 0
    added = jnp.concatenate([jnp.where(low, kept, cross), jnp.where(low, cross, kept)], axis=1)
    return (tokens.astype(F32) + added).astype(BF16)


def exchange_fits(mesh, tokens, expert_ids, expert_in):
    groups, sides = mesh.shape["expert"], mesh.shape["dp"]
    blocks = mesh.shape["sweep"] * groups
    rows, width = tokens.shape[0] // (blocks * sides), tokens.shape[1]
    return (
        sides == 4
        and expert_in.shape[0] % (blocks * 16) == 0
        and groups in (2, 4, 8)
        and rows % 128 == 0
        and width % 512 == 0
        and width // 2 >= 3 * rows
        and expert_ids.shape[1] <= 8
        and expert_in.shape[2] % 128 == 0
    )


def solution(mesh):
    rows = P(("sweep", "expert", "dp"), None)
    placed = (
        rows,
        rows,
        rows,
        P(("sweep", "expert"), "dp", None),
        P(("sweep", "expert"), None, "dp"),
        P(("sweep", "dp"), None),
        P("sweep", "dp"),
    )
    spread = functools.partial(
        jax.shard_map, mesh=mesh, in_specs=placed, out_specs=rows, check_vma=False
    )

    def program(*args):
        if not exchange_fits(mesh, args[0], args[1], args[3]):
            return spread(gathered_weights)(*args)
        step = spread(exchanged_partials)
        return step(*args)

    return program
```

time: 625 us -> 219 us (0.35)
  waiting for transfers between devices: 489 us -> 82.4 us
  Pallas kernels: 0 us -> 89.9 us
  matrix products: 52.2 us -> 0 us
  local copies, waits for them, and re-layouts: 52.5 us -> 10.5 us
  starting transfers between devices: 12.1 us -> 27.5 us
  between operations: 13.2 us -> 0.42 us
    all_gather x4 -> x0, waiting for transfers between devices: 312 us -> none  [the longest x1 200 us: per_device(): lax.all_gather(expert_out, 'dp', axis=2, tiled=True)]
    all_to_all x2 -> x0, waiting for transfers between devices: 174 us -> none  [the longest x1 87.2 us: per_device(): lax.all_to_all(outgoing, 'expert', split_axis=0, concat_axis=0, tiled=True)]
    pallas_call x0 -> x14, Pallas kernels: none -> 89.9 us  [the longest x5 38.7 us: second_stage(): pl.pallas_call(functools.partial(second_kernel, units, keep, send), in_sp...]
    ppermute x0 -> x26, waiting for transfers between devices: none -> 82.4 us  [swap(): return lax.ppermute(value, axis, [(i, i ^ mask) for i in range(size)])]
    dot_general x3 -> x0, matrix products: 52.2 us -> none  [the longest x1 28 us: run_experts(): jnp.einsum('gesd,edf->gesf', shard_piece, weight_in, preferred_element_ty...]
    ppermute x0 -> x26, starting transfers between devices: none -> 27.5 us  [swap(): return lax.ppermute(value, axis, [(i, i ^ mask) for i in range(size)])]
    reshape x4 -> x0, local copies, waits for them, and re-layouts: 21.3 us -> none  [the longest x2 14.2 us: per_device(): outgoing = outgoing.reshape(group_count, local_count, CAP, model_width)]
    all_to_all x2 -> x0, starting transfers between devices: 12.1 us -> none  [the longest x1 7.11 us: per_device(): lax.all_to_all(outgoing, 'expert', split_axis=0, concat_axis=0, tiled=True)]
  transfers between devices with their start and end apart: 6 -> 26, of which waited for: 4 -> 11; matrix products, arithmetic and copies ran while one was open for 17% -> 3% of each run, Pallas kernels for 0% -> 34%
where the time goes in v2:
time: 219 us; the launch traced here: 218 us
  Pallas kernels  89.9 us (41%)
  waiting for transfers between devices  82.4 us (38%)
  starting transfers between devices  27.5 us (13%)
  local copies, waits for them, and re-layouts  10.5 us (5%)
  other arithmetic  7.56 us (3%)
    ppermute x26, waiting for transfers between devices, swap(): return lax.ppermute(value, axis, [(i, i ^ mask) for i in range(size)])  82.4 us
    pallas_call x5, Pallas kernels, second_stage(): pl.pallas_call(functools.partial(second_kernel, units, keep, send), in_sp...  38.7 us
    pallas_call x5, Pallas kernels, first_stage(): pl.pallas_call(functools.partial(first_kernel, units, picks), in_specs=[S...  34.4 us
    ppermute x26, starting transfers between devices, swap(): return lax.ppermute(value, axis, [(i, i ^ mask) for i in range(size)])  27.5 us
    unnamed x62, local copies, waits for them, and re-layouts  10.5 us
    pallas_call x1, Pallas kernels, exchanged_partials(): pl.pallas_call(norm_kernel, in_specs=[SMEM, VMEM, VMEM, VMEM, HBM], out_s...  5.98 us
    convert_element_type x3, other arithmetic, second(): joined = (outs[0] + came).astype(BF16)  5.84 us
    pallas_call x1, Pallas kernels, exchanged_partials(): pl.pallas_call(give_kernel, in_specs=[SMEM, HBM, ANY], out_specs=HBM, out...  4.94 us
  transfers between devices with their start and end apart: 26, of which 11 were waited for; matrix products, arithmetic and copies ran while one was open for 3% of the time, Pallas kernels for 34%

profile of v2, /device:TPU:0, one launch (start us, length us, event | category | flops | bytes accessed | tf_op | source)
XLA Modules:
  0.0 218.3 jit_solution(4085127734728251343)
XLA Ops:
  0.6 6.0 %norm.1 = (bf16[144,768]{1,0:T(8,128)(2,1)}, bf16[144,768]{1,0:T(8,128)(2,1)}, bf16[8,384,768]{2,1,0:T(8,128)(2,1)}) custom-call(s32[3]{0:T(128)} %pad_add_fusion.place, bf16[128,1536]{1,0:T(8,128)(2,1)} %tokens.1, s32[8,128]{1,0:T(8,128)} %bitcast.5, f32[8,128]{1,0:T(8,128)} %bitcast.6, bf16[16,384,768]{2,1,0:T(8,128)(2,1)} %refs_1_.3), custom_call_target="tpu_custom_call" | custom-call | flops 10000000 | bytes 786432 | tf_op jit(solution)/shard_map/norm/pallas_call | solution.py:381
  7.1 4.9 %give_out.1.refs_3_ = bf16[8,768,384]{2,1,0:T(8,128)(2,1)} custom-call(s32[3]{0:T(128)} %pad_add_fusion.place, bf16[16,768,384]{2,1,0:T(8,128)(2,1)} %refs_4_.9, bf16[144,768]{1,0:T(8,128)(2,1)} %get-tuple-element.29.after), custom_call_target="tpu_custom_call" | custom-call | flops 10000000 | bytes 9437184 | tf_op jit(solution)/shard_map/give_out/pallas_call | solution.py:394
  12.2 2.9 %collective-permute-start = (bf16[144,768]{1,0:T(8,128)(2,1)S(1)}, bf16[144,768]{1,0:T(8,128)(2,1)S(1)}, u32[]{:S(2)}, u32[]{:S(2)}) collective-permute-start(bf16[144,768]{1,0:T(8,128)(2,1)S(1)} %copy-done.30), channel_id=1, source_target_pairs={{0,2},{1,3},{2,0},{3,1},{4,6},{5,7},{6,4},{7,5},{8,10},{9,11},{10,... | collective-permute-start | bytes 663560 | tf_op jit(solution)/shard_map/ppermute | solution.py:79
  15.2 5.6 %collective-permute-done = bf16[144,768]{1,0:T(8,128)(2,1)S(1)} collective-permute-done((bf16[144,768]{1,0:T(8,128)(2,1)S(1)}, bf16[144,768]{1,0:T(8,128)(2,1)S(1)}, u32[]{:S(2)}, u32[]{:S(2)}) %collective-permute-start) | collective-permute-done | bytes 221216 | tf_op jit(solution)/shard_map/ppermute | solution.py:79
  20.9 3.9 %collective-permute-start.7 = (bf16[288,768]{1,0:T(8,128)(2,1)S(1)}, bf16[288,768]{1,0:T(8,128)(2,1)S(1)}, u32[]{:S(2)}, u32[]{:S(2)}) collective-permute-start(bf16[288,768]{1,0:T(8,128)(2,1)S(1)} %pad_maximum_fusion.refs_0_.feed), channel_id=1, source_target_pairs={{0,12},{4,8},{8,4},{12,0},{1,13},{5,9},{9,5},{13,1},{2,14},{6,10},... | collective-permute-start | bytes 1327112 | tf_op jit(solution)/shard_map/ppermute | solution.py:79
  24.8 6.6 %shard_map.73 = (bf16[8,40,768]{2,1,0:T(8,128)(2,1)}, f32[8,256]{1,0:T(8,128)}, f32[8,256]{1,0:T(8,128)}) custom-call(s32[3]{0:T(128)} %pad_add_fusion.place, bf16[288,768]{1,0:T(8,128)(2,1)} %copy-done.3, bf16[16,384,768]{2,1,0:T(8,128)(2,1)} %refs_1_.3, bf16[8,384,768]{2,1,0:T(8,128)(2,1)} %collective-permute-done.1.refs_2_.refs_3_, ...), custom_call_target="tpu_custom_call" | custom-call | flops 10000000 | bytes 9437184 | tf_op jit(solution)/shard_map/pallas_call | solution.py:295
  31.5 1.6 collective-permute-start.2
  34.5 10.1 %collective-permute-start.13 = (bf16[288,768]{1,0:T(8,128)(2,1)}, bf16[288,768]{1,0:T(8,128)(2,1)S(1)}, u32[]{:S(2)}, u32[]{:S(2)}) collective-permute-start(bf16[288,768]{1,0:T(8,128)(2,1)} %copy-done.3), channel_id=1, source_target_pairs={{0,8},{4,12},{8,0},{12,4},{1,9},{5,13},{9,1},{13,5},{2,10},{6,14},... | collective-permute-start | bytes 1327112 | tf_op jit(solution)/shard_map/ppermute | solution.py:79
  45.4 2.7 %shared_first.1.refs_6_.near = bf16[256,768]{1,0:T(8,128)(2,1)} custom-call(s32[3]{0:T(128)} %pad_add_fusion.place, bf16[288,768]{1,0:T(8,128)(2,1)} %copy-done.3, bf16[384,768]{1,0:T(8,128)(2,1)} %own.2, bf16[384,768]{1,0:T(8,128)(2,1)} %copy-done.16, f32[8,256]{1,0:T(8,128)} %get-tuple-element.32._.refs_0_), custom_call_target="tpu_custom_call" | custom-call | flops 10000000 | bytes 1179648 | tf_op jit(solution)/shard_map/shared_first/pallas_call | solution.py:447
  48.2 2.2 copy-done
  50.5 6.7 %shard_map.74.refs_4_ = f32[256,768]{1,0:T(8,128)} custom-call(s32[3]{0:T(128)} %pad_add_fusion.place, f32[8,256]{1,0:T(8,128)} %get-tuple-element.32._.refs_0_, f32[8,256]{1,0:T(8,128)} %get-tuple-element.33.refs_1_, bf16[8,40,768]{2,1,0:T(8,128)(2,1)} %get-tuple-element.34.refs_2_, bf16[8,40,768]{2,1,0:T(8,128)(2,1)} %copy-done.20, ...), custom_call_target="tpu_custom_call" | custom-call | flops 10000000 | bytes 9437184 | tf_op jit(solution)/shard_map/pallas_call | solution.py:323
  58.0 7.0 %shard_map.75 = (bf16[8,80,768]{2,1,0:T(8,128)(2,1)}, f32[8,512]{1,0:T(8,128)}, f32[8,512]{1,0:T(8,128)}) custom-call(s32[3]{0:T(128)} %pad_add_fusion.place, bf16[288,768]{1,0:T(8,128)(2,1)} %copy-done.23, bf16[288,768]{1,0:T(8,128)(2,1)} %copy-done.24, bf16[16,384,768]{2,1,0:T(8,128)(2,1)} %refs_1_.3, ...), custom_call_target="tpu_custom_call" | custom-call | flops 10000000 | bytes 9437184 | tf_op jit(solution)/shard_map/pallas_call | solution.py:295
  65.1 1.6 collective-permute-start.9
  67.3 11.3 %collective-permute-done.11.refs_0_ = bf16[288,768]{1,0:T(8,128)(2,1)S(1)} collective-permute-done((bf16[288,768]{1,0:T(8,128)(2,1)S(1)}, bf16[288,768]{1,0:T(8,128)(2,1)S(1)}, u32[]{:S(2)}, u32[]{:S(2)}) %collective-permute-start.11) | collective-permute-done | bytes 442400 | tf_op jit(solution)/shard_map/ppermute | solution.py:79
  79.1 18.5 %collective-permute-done.5.far = bf16[256,768]{1,0:T(8,128)(2,1)S(1)} collective-permute-done((bf16[256,768]{1,0:T(8,128)(2,1)S(1)}, bf16[256,768]{1,0:T(8,128)(2,1)S(1)}, u32[]{:S(2)}, u32[]{:S(2)}) %collective-permute-start.5) | collective-permute-done | bytes 393248 | tf_op jit(solution)/shard_map/ppermute | solution.py:79
  98.4 3.1 %shared_second.1.refs_4_ = f32[256,768]{1,0:T(8,128)} custom-call(s32[3]{0:T(128)} %pad_add_fusion.place, bf16[256,768]{1,0:T(8,128)(2,1)} %shared_first.1.refs_6_.near, bf16[256,768]{1,0:T(8,128)(2,1)} %copy-done.29, bf16[768,384]{1,0:T(8,128)(2,1)} %own.3, bf16[768,384]{1,0:T(8,128)(2,1)} %copy-done.18, f32[8,512]{1,0:T(8,128)} %get-tuple-element.35._.refs_0_), custom_call_target="tpu_custom_call" | custom-call | flops 10000000 | bytes 1179648 | tf_op jit(solution)/shard_map/shared_second/pallas_call | solution.py:460
  102.3 7.1 %shard_map.76 = (bf16[8,80,768]{2,1,0:T(8,128)(2,1)}, f32[8,512]{1,0:T(8,128)}, f32[8,512]{1,0:T(8,128)}) custom-call(s32[3]{0:T(128)} %pad_add_fusion.place, bf16[288,768]{1,0:T(8,128)(2,1)} %copy-done.22, bf16[288,768]{1,0:T(8,128)(2,1)} %copy-done.25, bf16[16,384,768]{2,1,0:T(8,128)(2,1)} %refs_1_.3, ...), custom_call_target="tpu_custom_call" | custom-call | flops 10000000 | bytes 9437184 | tf_op jit(solution)/shard_map/pallas_call | solution.py:295
  111.7 7.1 %shard_map.77 = (bf16[8,80,768]{2,1,0:T(8,128)(2,1)}, f32[8,512]{1,0:T(8,128)}, f32[8,512]{1,0:T(8,128)}) custom-call(s32[3]{0:T(128)} %pad_add_fusion.place, bf16[288,768]{1,0:T(8,128)(2,1)} %copy-done.26, bf16[288,768]{1,0:T(8,128)(2,1)} %copy-done.28, bf16[16,384,768]{2,1,0:T(8,128)(2,1)} %refs_1_.3, ...), custom_call_target="tpu_custom_call" | custom-call | flops 10000000 | bytes 9437184 | tf_op jit(solution)/shard_map/pallas_call | solution.py:295
  119.6 6.6 %shard_map.78 = (bf16[8,40,768]{2,1,0:T(8,128)(2,1)}, f32[8,256]{1,0:T(8,128)}, f32[8,256]{1,0:T(8,128)}) custom-call(s32[3]{0:T(128)} %pad_add_fusion.place, bf16[288,768]{1,0:T(8,128)(2,1)} %copy-done.27, bf16[16,384,768]{2,1,0:T(8,128)(2,1)} %refs_1_.3, bf16[8,384,768]{2,1,0:T(8,128)(2,1)} %collective-permute-done.1.refs_2_.refs_3_, ...), custom_call_target="tpu_custom_call" | custom-call | flops 10000000 | bytes 9437184 | tf_op jit(solution)/shard_map/pallas_call | solution.py:295
  127.2 8.4 %shard_map.79 = (f32[256,768]{1,0:T(8,128)}, bf16[256,768]{1,0:T(8,128)(2,1)}) custom-call(s32[3]{0:T(128)} %pad_add_fusion.place, f32[8,512]{1,0:T(8,128)} %get-tuple-element.35._.refs_0_, f32[8,512]{1,0:T(8,128)} %get-tuple-element.36.refs_1_, bf16[8,80,768]{2,1,0:T(8,128)(2,1)} %get-tuple-element.37.refs_2_, bf16[8,80,768]{2,1,0:T(8,128)(2,1)} %copy-done.10, ...), custom_call_target="tpu_custom_call" | custom-call | flops 10000000 | bytes 9437184 | tf_op jit(solution)/shard_map/pallas_call | solution.py:323
  137.6 1.9 add_convert_fusion.2.refs_6_
  140.5 8.3 %shard_map.80 = (f32[256,768]{1,0:T(8,128)}, bf16[256,768]{1,0:T(8,128)(2,1)}) custom-call(s32[3]{0:T(128)} %pad_add_fusion.place, f32[8,512]{1,0:T(8,128)} %get-tuple-element.38.refs_4_.refs_0_, f32[8,512]{1,0:T(8,128)} %get-tuple-element.43.refs_1_, bf16[8,80,768]{2,1,0:T(8,128)(2,1)} %get-tuple-element.44.refs_2_, bf16[8,80,768]{2,1,0:T(8,128)(2,1)} %copy-done.12, ...), custom_call_target="tpu_custom_call" | custom-call | flops 10000000 | bytes 9437184 | tf_op jit(solution)/shard_map/pallas_call | solution.py:323
  149.0 1.8 collective-permute-done.18
  150.8 1.9 add_convert_fusion.1.refs_6_
  152.7 7.1 %collective-permute-done.20.refs_3_ = bf16[8,80,768]{2,1,0:T(8,128)(2,1)S(1)} collective-permute-done((bf16[8,80,768]{2,1,0:T(8,128)(2,1)S(1)}, bf16[8,80,768]{2,1,0:T(8,128)(2,1)S(1)}, u32[]{:S(2)}, u32[]{:S(2)}) %collective-permute-start.20) | collective-permute-done | bytes 983072 | tf_op jit(solution)/shard_map/ppermute | solution.py:79
  160.8 8.7 %shard_map.81 = (f32[256,768]{1,0:T(8,128)}, bf16[256,768]{1,0:T(8,128)(2,1)}) custom-call(s32[3]{0:T(128)} %pad_add_fusion.place, f32[8,512]{1,0:T(8,128)} %get-tuple-element.39.refs_3_.refs_0_, f32[8,512]{1,0:T(8,128)} %get-tuple-element.47.refs_1_, bf16[8,80,768]{2,1,0:T(8,128)(2,1)} %get-tuple-element.48.refs_2_, bf16[8,80,768]{2,1,0:T(8,128)(2,1)} %copy-done.13, ...), custom_call_target="tpu_custom_call" | custom-call | flops 10000000 | bytes 9437184 | tf_op jit(solution)/shard_map/pallas_call | solution.py:323
  171.5 1.9 add_convert_fusion.refs_6_
  173.5 9.7 %collective-permute-done.23.refs_3_ = bf16[8,40,768]{2,1,0:T(8,128)(2,1)S(1)} collective-permute-done((bf16[8,40,768]{2,1,0:T(8,128)(2,1)S(1)}, bf16[8,40,768]{2,1,0:T(8,128)(2,1)S(1)}, u32[]{:S(2)}, u32[]{:S(2)}) %collective-permute-start.23) | collective-permute-done | bytes 491552 | tf_op jit(solution)/shard_map/ppermute | solution.py:79
  183.9 6.7 %shard_map.82 = bf16[256,768]{1,0:T(8,128)(2,1)} custom-call(s32[3]{0:T(128)} %pad_add_fusion.place, f32[8,256]{1,0:T(8,128)} %get-tuple-element.40.refs_6_.refs_0_, f32[8,256]{1,0:T(8,128)} %get-tuple-element.51.refs_1_, bf16[8,40,768]{2,1,0:T(8,128)(2,1)} %get-tuple-element.52.refs_2_, bf16[8,40,768]{2,1,0:T(8,128)(2,1)} %copy-done.21, ...), custom_call_target="tpu_custom_call" | custom-call | flops 10000000 | bytes 9437184 | tf_op jit(solution)/shard_map/pallas_call | solution.py:323
  190.8 14.5 %collective-permute-done.19 = bf16[256,768]{1,0:T(8,128)(2,1)S(1)} collective-permute-done((bf16[256,768]{1,0:T(8,128)(2,1)S(1)}, bf16[256,768]{1,0:T(8,128)(2,1)S(1)}, u32[]{:S(2)}, u32[]{:S(2)}) %collective-permute-start.19) | collective-permute-done | bytes 393248 | tf_op jit(solution)/shard_map/ppermute | solution.py:79
  205.4 5.3 %collective-permute-done.22 = bf16[256,768]{1,0:T(8,128)(2,1)S(1)} collective-permute-done((bf16[256,768]{1,0:T(8,128)(2,1)S(1)}, bf16[256,768]{1,0:T(8,128)(2,1)S(1)}, u32[]{:S(2)}, u32[]{:S(2)}) %collective-permute-start.22) | collective-permute-done | bytes 393248 | tf_op jit(solution)/shard_map/ppermute | solution.py:79
  211.6 5.8 %collective-permute-done.25 = bf16[128,768]{1,0:T(8,128)(2,1)S(1)} collective-permute-done((bf16[128,768]{1,0:T(8,128)(2,1)S(1)}, bf16[128,768]{1,0:T(8,128)(2,1)S(1)}, u32[]{:S(2)}, u32[]{:S(2)}) %collective-permute-start.25) | collective-permute-done | bytes 196640 | tf_op jit(solution)/shard_map/ppermute | solution.py:79
  (109 shorter events, 20.3 us)
Async XLA Ops:
  6.6 18.3 %collective-permute-start.1 = (bf16[8,384,768]{2,1,0:T(8,128)(2,1)}, bf16[8,384,768]{2,1,0:T(8,128)(2,1)}, u32[]{:S(2)}, u32[]{:S(2)}) collective-permute-start(bf16[8,384,768]{2,1,0:T(8,128)(2,1)} %get-tuple-element.31), channel_id=1, source_target_pairs={{0,1},{1,0},{2,3},{3,2},{4,5},{5,4},{6,7},{7,6},{8,9},{9,8},{10,11... | collective-permute-start | bytes 14155784 | tf_op jit(solution)/shard_map/ppermute | solution.py:79
  12.1 36.1 %collective-permute-start.3 = (bf16[8,768,384]{2,1,0:T(8,128)(2,1)}, bf16[8,768,384]{2,1,0:T(8,128)(2,1)S(1)}, u32[]{:S(2)}, u32[]{:S(2)}) collective-permute-start(bf16[8,768,384]{2,1,0:T(8,128)(2,1)} %give_out.1.refs_3_), channel_id=1, source_target_pairs={{0,1},{1,0},{2,3},{3,2},{4,5},{5,4},{6,7},{7,6},{8,9},{9,8},{10,11... | collective-permute-start | bytes 14155784 | tf_op jit(solution)/shard_map/ppermute | solution.py:79
  12.2 8.6 %collective-permute-start = (bf16[144,768]{1,0:T(8,128)(2,1)S(1)}, bf16[144,768]{1,0:T(8,128)(2,1)S(1)}, u32[]{:S(2)}, u32[]{:S(2)}) collective-permute-start(bf16[144,768]{1,0:T(8,128)(2,1)S(1)} %copy-done.30), channel_id=1, source_target_pairs={{0,2},{1,3},{2,0},{3,1},{4,6},{5,7},{6,4},{7,5},{8,10},{9,11},{10,... | collective-permute-start | bytes 663560 | tf_op jit(solution)/shard_map/ppermute | solution.py:79
  20.9 23.7 %copy-start.17 = (bf16[768,384]{1,0:T(8,128)(2,1)S(1)}, bf16[768,384]{1,0:T(8,128)(2,1)}, u32[]{:S(2)}) copy-start(bf16[768,384]{1,0:T(8,128)(2,1)} %own.3) | copy-start | bytes 1769476
  20.9 13.6 %collective-permute-start.7 = (bf16[288,768]{1,0:T(8,128)(2,1)S(1)}, bf16[288,768]{1,0:T(8,128)(2,1)S(1)}, u32[]{:S(2)}, u32[]{:S(2)}) collective-permute-start(bf16[288,768]{1,0:T(8,128)(2,1)S(1)} %pad_maximum_fusion.refs_0_.feed), channel_id=1, source_target_pairs={{0,12},{4,8},{8,4},{12,0},{1,13},{5,9},{9,5},{13,1},{2,14},{6,10},... | collective-permute-start | bytes 1327112 | tf_op jit(solution)/shard_map/ppermute | solution.py:79
  24.8 19.8 %collective-permute-start.4 = (bf16[384,768]{1,0:T(8,128)(2,1)S(1)}, bf16[384,768]{1,0:T(8,128)(2,1)S(1)}, u32[]{:S(2)}, u32[]{:S(2)}) collective-permute-start(bf16[384,768]{1,0:T(8,128)(2,1)S(1)} %copy-done.15), channel_id=1, source_target_pairs={{0,1},{1,0},{2,3},{3,2},{4,5},{5,4},{6,7},{7,6},{8,9},{9,8},{10,11... | collective-permute-start | bytes 1769480 | tf_op jit(solution)/shard_map/ppermute | solution.py:79
  31.5 16.7 %collective-permute-start.2 = (bf16[8,40,768]{2,1,0:T(8,128)(2,1)}, bf16[8,40,768]{2,1,0:T(8,128)(2,1)S(1)}, u32[]{:S(2)}, u32[]{:S(2)}) collective-permute-start(bf16[8,40,768]{2,1,0:T(8,128)(2,1)} %get-tuple-element.34.refs_2_), channel_id=1, source_target_pairs={{0,2},{1,3},{2,0},{3,1},{4,6},{5,7},{6,4},{7,5},{8,10},{9,11},{10,... | collective-permute-start | bytes 1474568 | tf_op jit(solution)/shard_map/ppermute | solution.py:79
  34.5 22.7 %collective-permute-start.8 = (bf16[288,768]{1,0:T(8,128)(2,1)S(1)}, bf16[288,768]{1,0:T(8,128)(2,1)S(1)}, u32[]{:S(2)}, u32[]{:S(2)}) collective-permute-start(bf16[288,768]{1,0:T(8,128)(2,1)S(1)} %collective-permute-done.7.refs_0_), channel_id=1, source_target_pairs={{0,1},{1,0},{2,3},{3,2},{4,5},{5,4},{6,7},{7,6},{8,9},{9,8},{10,11... | collective-permute-start | bytes 1327112 | tf_op jit(solution)/shard_map/ppermute | solution.py:79
  34.5 32.2 %collective-permute-start.13 = (bf16[288,768]{1,0:T(8,128)(2,1)}, bf16[288,768]{1,0:T(8,128)(2,1)S(1)}, u32[]{:S(2)}, u32[]{:S(2)}) collective-permute-start(bf16[288,768]{1,0:T(8,128)(2,1)} %copy-done.3), channel_id=1, source_target_pairs={{0,8},{4,12},{8,0},{12,4},{1,9},{5,13},{9,1},{13,5},{2,10},{6,14},... | collective-permute-start | bytes 1327112 | tf_op jit(solution)/shard_map/ppermute | solution.py:79
  44.6 34.0 %collective-permute-start.6 = (bf16[768,384]{1,0:T(8,128)(2,1)S(1)}, bf16[768,384]{1,0:T(8,128)(2,1)S(1)}, u32[]{:S(2)}, u32[]{:S(2)}) collective-permute-start(bf16[768,384]{1,0:T(8,128)(2,1)S(1)} %copy-done.17), channel_id=1, source_target_pairs={{0,1},{1,0},{2,3},{3,2},{4,5},{5,4},{6,7},{7,6},{8,9},{9,8},{10,11... | collective-permute-start | bytes 1769480 | tf_op jit(solution)/shard_map/ppermute | solution.py:79
  65.1 61.1 %collective-permute-start.9 = (bf16[8,80,768]{2,1,0:T(8,128)(2,1)}, bf16[8,80,768]{2,1,0:T(8,128)(2,1)S(1)}, u32[]{:S(2)}, u32[]{:S(2)}) collective-permute-start(bf16[8,80,768]{2,1,0:T(8,128)(2,1)} %get-tuple-element.37.refs_2_), channel_id=1, source_target_pairs={{0,2},{1,3},{2,0},{3,1},{4,6},{5,7},{6,4},{7,5},{8,10},{9,11},{10,... | collective-permute-start | bytes 2949128 | tf_op jit(solution)/shard_map/ppermute | solution.py:79
  66.6 12.0 %collective-permute-start.11 = (bf16[288,768]{1,0:T(8,128)(2,1)S(1)}, bf16[288,768]{1,0:T(8,128)(2,1)S(1)}, u32[]{:S(2)}, u32[]{:S(2)}) collective-permute-start(bf16[288,768]{1,0:T(8,128)(2,1)S(1)} %copy-done.4), channel_id=1, source_target_pairs={{0,4},{4,0},{8,12},{12,8},{1,5},{5,1},{9,13},{13,9},{2,6},{6,2},{1... | collective-permute-start | bytes 1327112 | tf_op jit(solution)/shard_map/ppermute | solution.py:79
  66.6 34.9 %copy-start.22 = (bf16[288,768]{1,0:T(8,128)(2,1)}, bf16[288,768]{1,0:T(8,128)(2,1)S(1)}, u32[]{:S(2)}) copy-start(bf16[288,768]{1,0:T(8,128)(2,1)S(1)} %collective-permute-done.13.refs_0_) | copy-start | bytes 1327108
  66.7 34.9 %collective-permute-start.14 = (bf16[288,768]{1,0:T(8,128)(2,1)S(1)}, bf16[288,768]{1,0:T(8,128)(2,1)S(1)}, u32[]{:S(2)}, u32[]{:S(2)}) collective-permute-start(bf16[288,768]{1,0:T(8,128)(2,1)S(1)} %collective-permute-done.13.refs_0_), channel_id=1, source_target_pairs={{0,1},{1,0},{2,3},{3,2},{4,5},{5,4},{6,7},{7,6},{8,9},{9,8},{10,11... | collective-permute-start | bytes 1327112 | tf_op jit(solution)/shard_map/ppermute | solution.py:79
  66.7 30.9 %collective-permute-start.5 = (bf16[256,768]{1,0:T(8,128)(2,1)S(1)}, bf16[256,768]{1,0:T(8,128)(2,1)S(1)}, u32[]{:S(2)}, u32[]{:S(2)}) collective-permute-start(bf16[256,768]{1,0:T(8,128)(2,1)S(1)} %copy-done.5), channel_id=1, source_target_pairs={{0,2},{1,3},{2,0},{3,1},{4,6},{5,7},{6,4},{7,5},{8,10},{9,11},{10,... | collective-permute-start | bytes 1179656 | tf_op jit(solution)/shard_map/ppermute | solution.py:79
  78.6 32.3 %copy-start.26 = (bf16[288,768]{1,0:T(8,128)(2,1)}, bf16[288,768]{1,0:T(8,128)(2,1)S(1)}, u32[]{:S(2)}) copy-start(bf16[288,768]{1,0:T(8,128)(2,1)S(1)} %collective-permute-done.11.refs_0_) | copy-start | bytes 1327108
  78.6 32.3 %collective-permute-start.12 = (bf16[288,768]{1,0:T(8,128)(2,1)S(1)}, bf16[288,768]{1,0:T(8,128)(2,1)S(1)}, u32[]{:S(2)}, u32[]{:S(2)}) collective-permute-start(bf16[288,768]{1,0:T(8,128)(2,1)S(1)} %collective-permute-done.11.refs_0_), channel_id=1, source_target_pairs={{0,1},{1,0},{2,3},{3,2},{4,5},{5,4},{6,7},{7,6},{8,9},{9,8},{10,11... | collective-permute-start | bytes 1327112 | tf_op jit(solution)/shard_map/ppermute | solution.py:79
  78.7 40.1 %collective-permute-start.10 = (bf16[288,768]{1,0:T(8,128)(2,1)S(1)}, bf16[288,768]{1,0:T(8,128)(2,1)S(1)}, u32[]{:S(2)}, u32[]{:S(2)}) collective-permute-start(bf16[288,768]{1,0:T(8,128)(2,1)S(1)} %copy-done.4), channel_id=1, source_target_pairs={{0,1},{1,0},{2,3},{3,2},{4,5},{5,4},{6,7},{7,6},{8,9},{9,8},{10,11... | collective-permute-start | bytes 1327112 | tf_op jit(solution)/shard_map/ppermute | solution.py:79
  109.4 30.1 %collective-permute-start.17 = (bf16[8,80,768]{2,1,0:T(8,128)(2,1)}, bf16[8,80,768]{2,1,0:T(8,128)(2,1)S(1)}, u32[]{:S(2)}, u32[]{:S(2)}) collective-permute-start(bf16[8,80,768]{2,1,0:T(8,128)(2,1)} %get-tuple-element.44.refs_2_), channel_id=1, source_target_pairs={{0,2},{1,3},{2,0},{3,1},{4,6},{5,7},{6,4},{7,5},{8,10},{9,11},{10,... | collective-permute-start | bytes 2949128 | tf_op jit(solution)/shard_map/ppermute | solution.py:79
  135.6 2.0 collective-permute-start.15
  135.6 24.1 %collective-permute-start.20 = (bf16[8,80,768]{2,1,0:T(8,128)(2,1)S(1)}, bf16[8,80,768]{2,1,0:T(8,128)(2,1)S(1)}, u32[]{:S(2)}, u32[]{:S(2)}) collective-permute-start(bf16[8,80,768]{2,1,0:T(8,128)(2,1)S(1)} %copy-done.11), channel_id=1, source_target_pairs={{0,2},{1,3},{2,0},{3,1},{4,6},{5,7},{6,4},{7,5},{8,10},{9,11},{10,... | collective-permute-start | bytes 2949128 | tf_op jit(solution)/shard_map/ppermute | solution.py:79
  148.8 2.0 collective-permute-start.18
  169.4 2.1 collective-permute-start.21
  169.5 13.6 %collective-permute-start.23 = (bf16[8,40,768]{2,1,0:T(8,128)(2,1)S(1)}, bf16[8,40,768]{2,1,0:T(8,128)(2,1)S(1)}, u32[]{:S(2)}, u32[]{:S(2)}) collective-permute-start(bf16[8,40,768]{2,1,0:T(8,128)(2,1)S(1)} %copy-done.19), channel_id=1, source_target_pairs={{0,2},{1,3},{2,0},{3,1},{4,6},{5,7},{6,4},{7,5},{8,10},{9,11},{10,... | collective-permute-start | bytes 1474568 | tf_op jit(solution)/shard_map/ppermute | solution.py:79
  170.1 20.7 %collective-permute-start.16 = (bf16[256,768]{1,0:T(8,128)(2,1)S(1)}, bf16[256,768]{1,0:T(8,128)(2,1)S(1)}, u32[]{:S(2)}, u32[]{:S(2)}) collective-permute-start(bf16[256,768]{1,0:T(8,128)(2,1)S(1)} %copy-done.7), channel_id=1, source_target_pairs={{0,12},{4,8},{8,4},{12,0},{1,13},{5,9},{9,5},{13,1},{2,14},{6,10},... | collective-permute-start | bytes 1179656 | tf_op jit(solution)/shard_map/ppermute | solution.py:79
  171.5 33.9 %collective-permute-start.19 = (bf16[256,768]{1,0:T(8,128)(2,1)S(1)}, bf16[256,768]{1,0:T(8,128)(2,1)S(1)}, u32[]{:S(2)}, u32[]{:S(2)}) collective-permute-start(bf16[256,768]{1,0:T(8,128)(2,1)S(1)} %copy-done.8), channel_id=1, source_target_pairs={{0,8},{4,12},{8,0},{12,4},{1,9},{5,13},{9,1},{13,5},{2,10},{6,14},... | collective-permute-start | bytes 1179656 | tf_op jit(solution)/shard_map/ppermute | solution.py:79
  183.9 26.8 %copy-start.1 = (f32[256,768]{1,0:T(8,128)S(1)}, f32[256,768]{1,0:T(8,128)}, u32[]{:S(2)}) copy-start(f32[256,768]{1,0:T(8,128)} %shard_map.74.refs_4_) | copy-start | bytes 2359300
  183.9 26.8 %copy-start.2 = (f32[256,768]{1,0:T(8,128)S(1)}, f32[256,768]{1,0:T(8,128)}, u32[]{:S(2)}) copy-start(f32[256,768]{1,0:T(8,128)} %shared_second.1.refs_4_) | copy-start | bytes 2359300
  190.7 26.8 %copy-start.6 = (bf16[128,1536]{1,0:T(8,128)(2,1)S(1)}, bf16[128,1536]{1,0:T(8,128)(2,1)}, u32[]{:S(2)}) copy-start(bf16[128,1536]{1,0:T(8,128)(2,1)} %tokens.1) | copy-start | bytes 1179652
  190.7 14.7 %collective-permute-start.24 = (bf16[256,768]{1,0:T(8,128)(2,1)}, bf16[256,768]{1,0:T(8,128)(2,1)S(1)}, u32[]{:S(2)}, u32[]{:S(2)}) collective-permute-start(bf16[256,768]{1,0:T(8,128)(2,1)} %shard_map.82), channel_id=1, source_target_pairs={{0,1},{1,0},{2,3},{3,2},{4,5},{5,4},{6,7},{7,6},{8,9},{9,8},{10,11... | collective-permute-start | bytes 1179656 | tf_op jit(solution)/shard_map/ppermute | solution.py:79
  190.8 19.9 %collective-permute-start.22 = (bf16[256,768]{1,0:T(8,128)(2,1)S(1)}, bf16[256,768]{1,0:T(8,128)(2,1)S(1)}, u32[]{:S(2)}, u32[]{:S(2)}) collective-permute-start(bf16[256,768]{1,0:T(8,128)(2,1)S(1)} %copy-done.9), channel_id=1, source_target_pairs={{0,4},{4,0},{8,12},{12,8},{1,5},{5,1},{9,13},{13,9},{2,6},{6,2},{1... | collective-permute-start | bytes 1179656 | tf_op jit(solution)/shard_map/ppermute | solution.py:79
  211.0 6.4 %collective-permute-start.25 = (bf16[128,768]{1,0:T(8,128)(2,1)S(1)}, bf16[128,768]{1,0:T(8,128)(2,1)S(1)}, u32[]{:S(2)}, u32[]{:S(2)}) collective-permute-start(bf16[128,768]{1,0:T(8,128)(2,1)S(1)} %slice.32), channel_id=1, source_target_pairs={{0,2},{1,3},{2,0},{3,1},{4,6},{5,7},{6,4},{7,5},{8,10},{9,11},{10,... | collective-permute-start | bytes 589832 | tf_op jit(solution)/shard_map/ppermute | solution.py:79
  (25 other events, 152.5 us)

commit v3 on v2

--- a/solution.py
+++ b/solution.py
@@ -83,18 +83,18 @@
     return pl.CostEstimate(flops=int(flops), bytes_accessed=int(moved), transcendentals=0)
 
 
-def norm_kernel(place, tokens, ids, gates, source, mine, theirs, given, held, came, left):
-    local = held.shape[0]
-    base = (1 - place[0]) * local
-
-    def fetch(e):
-        return pltpu.make_async_copy(source.at[base + e], held.at[e], came.at[e])
-
-    def put(e):
-        return pltpu.make_async_copy(held.at[e], given.at[e], left.at[e])
-
-    for e in range(local):
-        fetch(e).start()
+def half_copies(source, held, base, came):
+    return [
+        pltpu.make_async_copy(source.at[base + e], held.at[e], came.at[e])
+        for e in range(held.shape[0])
+    ]
+
+
+def norm_kernel(place, tokens, ids, gates, source, mine, theirs, given, came):
+    local = given.shape[0]
+    copies = half_copies(source, given, (1 - place[0]) * local, came)
+    for c in copies:
+        c.start()
     rows, width = tokens.shape
     half = width // 2
     values = tokens[...].astype(F32)
@@ -113,30 +113,17 @@
     table = jnp.concatenate([table, jnp.zeros((META - picks, half), F32)], axis=0).astype(BF16)
     mine[rows : rows + META, :] = table
     theirs[rows : rows + META, :] = table
-    for e in range(local):
-        fetch(e).wait()
-        put(e).start()
-    for e in range(local):
-        put(e).wait()
-
-
-def give_kernel(place, source, after, given, held, came, left):
-    local = held.shape[0]
-    base = (1 - place[0]) * local
-
-    def fetch(e):
-        return pltpu.make_async_copy(source.at[base + e], held.at[e], came.at[e])
-
-    def put(e):
-        return pltpu.make_async_copy(held.at[e], given.at[e], left.at[e])
-
-    for e in range(local):
-        fetch(e).start()
-    for e in range(local):
-        fetch(e).wait()
-        put(e).start()
-    for e in range(local):
-        put(e).wait()
+    for c in copies:
+        c.wait()
+
+
+def give_kernel(place, source, after, given, came):
+    local = given.shape[0]
+    copies = half_copies(source, given, (1 - place[0]) * local, came)
+    for c in copies:
+        c.start()
+    for c in copies:
+        c.wait()
 
 
 def selection(codes, rows):
@@ -145,27 +132,15 @@
     return [(wanted == codes[e : e + 1, :]).astype(F32) for e in range(count)]
 
 
-def weight_copies(place, own, other, held_own, held_other, came):
-    local = held_own.shape[0]
-
-    def copies(e):
-        return (
-            pltpu.make_async_copy(own.at[place[0] * local + e], held_own.at[e], came.at[0, e]),
-            pltpu.make_async_copy(other.at[e], held_other.at[e], came.at[1, e]),
-        )
-
-    return copies
-
-
-def first_kernel(units, picks, place, *refs):
+def first_kernel(units, picks, load, place, *refs):
     feeds, refs = refs[:units], refs[units:]
-    own, other, _, part, code, gate, packed, held_own, held_other, made, came, left = refs
+    source, other, _, part, code, gate = refs[:6]
+    own, (packed, made, left, *came) = (refs[6], refs[7:]) if load else (source, refs[6:])
     local, rows, half = packed.shape
     slots = rows // (2 * units)
     tokens = feeds[0].shape[0] // 2 - META
-    copies = weight_copies(place, own, other, held_own, held_other, came)
-    for e in range(local):
-        for c in copies(e):
+    if load:
+        for c in half_copies(source, own, place[0] * local, came[0]):
             c.start()
 
     before = (
@@ -211,10 +186,11 @@
     @pl.loop(0, local // 2)
     def _(pair):
         for e in (2 * pair, 2 * pair + 1):
-            for c in copies(e):
-                c.wait()
-            total = dot(packed[e, :, pl.ds(here, quarter)], held_own[e])
-            total += dot(packed[e, :, pl.ds(there, quarter)], held_other[e])
+            total = dot(packed[e, :, pl.ds(there, quarter)], other[e])
+            if load:
+                base = place[0] * local
+                pltpu.make_async_copy(source.at[base + e], own.at[e], came[0].at[e]).wait()
+            total += dot(packed[e, :, pl.ds(here, quarter)], own[e])
             made[e] = total.astype(BF16)
         for e in (2 * pair, 2 * pair + 1):
             put(e).start()
@@ -224,15 +200,16 @@
         put(e).wait()
 
 
-def second_kernel(units, keep, send, place, *refs):
-    code, gate, near, far, own, other, _ = refs[:7]
-    outs, (total, held_own, held_other, came) = refs[7:-4], refs[-4:]
+def second_kernel(units, keep, send, load, place, *refs):
+    code, gate, near, far, source, other, _ = refs[:7]
+    shown = keep + send
+    outs, refs = refs[7 : 7 + shown], refs[7 + shown :]
+    own, (total, *came) = (refs[0], refs[1:]) if load else (source, refs)
     local = code.shape[0]
     rows = near.shape[1]
     half = total.shape[1]
-    copies = weight_copies(place, own, other, held_own, held_other, came)
-    for e in range(local):
-        for c in copies(e):
+    if load:
+        for c in half_copies(source, own, place[0] * local, came[0]):
             c.start()
     quarter = half // 2
     here = pl.multiple_of(place[0] * quarter, quarter)
@@ -245,11 +222,12 @@
             same = wanted == code[pl.ds(e, 1), :]
             scale = jnp.sum(jnp.where(same, gate[pl.ds(e, 1), :], 0.0), axis=1, keepdims=True)
             hidden = jax.nn.gelu(near[e].astype(F32) + far[e].astype(F32)).astype(BF16)
-            for c in copies(e):
-                c.wait()
             at = pl.ds(pl.multiple_of(e * rows, rows), rows)
-            total[at, pl.ds(here, quarter)] = dot(hidden, held_own[e]) * scale
-            total[at, pl.ds(there, quarter)] = dot(hidden, held_other[e]) * scale
+            total[at, pl.ds(there, quarter)] = dot(hidden, other[e]) * scale
+            if load:
+                base = place[0] * local
+                pltpu.make_async_copy(source.at[base + e], own.at[e], came[0].at[e]).wait()
+            total[at, pl.ds(here, quarter)] = dot(hidden, own[e]) * scale
 
     pick = jnp.concatenate(selection(code[...], rows), axis=0).astype(BF16)
     wide = half // 3 if half % 384 == 0 else half
@@ -274,18 +252,15 @@
 VMEM = pl.BlockSpec(memory_space=pltpu.VMEM)
 ANY = pl.BlockSpec(memory_space=pl.ANY)
 HBM = pl.BlockSpec(memory_space=pltpu.HBM)
-GRANT = 55 << 20
-
-
-def give_scratch(local, shape):
-    return [
-        pltpu.VMEM((local, *shape), BF16),
-        pltpu.SemaphoreType.DMA((local,)),
-        pltpu.SemaphoreType.DMA((local,)),
-    ]
-
-
-def first_stage(feeds, place, own, other, after, picks):
+GRANT = 24 << 20
+WEIGHT_GRANTS = {"norm": 46 << 20, "give": 42 << 20, "first": 40 << 20, "second": 36 << 20}
+
+
+def granted(size=GRANT):
+    return pltpu.CompilerParams(vmem_limit_bytes=size)
+
+
+def first_stage(feeds, place, own, other, after, picks, load):
     units = len(feeds)
     local, quarter, hidden = other.shape
     half = 2 * quarter
@@ -293,24 +268,23 @@
     rows = 2 * units * CAP
     table = jax.ShapeDtypeStruct((local, 2 * units * tokens), F32)
     return pl.pallas_call(
-        functools.partial(first_kernel, units, picks),
-        in_specs=[SMEM] + [VMEM] * units + [HBM, HBM, ANY],
-        out_specs=[ANY, VMEM, VMEM],
+        functools.partial(first_kernel, units, picks, load),
+        in_specs=[SMEM] + [VMEM] * units + [HBM if load else VMEM, VMEM, ANY],
+        out_specs=[ANY, VMEM, VMEM] + [VMEM] * load,
         scratch_shapes=[
             pltpu.VMEM((local, rows, half), BF16),
-            pltpu.VMEM((local, quarter, hidden), BF16),
-            pltpu.VMEM((local, quarter, hidden), BF16),
             pltpu.VMEM((local, rows, hidden), BF16),
-            pltpu.SemaphoreType.DMA((2, local)),
             pltpu.SemaphoreType.DMA((local,)),
-        ],
-        out_shape=[jax.ShapeDtypeStruct((local, rows, hidden), BF16), table, table],
-        compiler_params=pltpu.CompilerParams(vmem_limit_bytes=GRANT),
+        ]
+        + [pltpu.SemaphoreType.DMA((local,))] * load,
+        out_shape=[jax.ShapeDtypeStruct((local, rows, hidden), BF16), table, table]
+        + [jax.ShapeDtypeStruct(other.shape, BF16)] * load,
+        compiler_params=granted(WEIGHT_GRANTS["first"] if load else GRANT),
         cost_estimate=cost(KERNEL_FLOPS, 2 * local * half * hidden),
     )(place, *feeds, own, other, after)
 
 
-def second_stage(units, code, gate, near, far, place, own, other, after, keep, send):
+def second_stage(units, code, gate, near, far, place, own, other, after, keep, send, load):
     local, hidden, quarter = other.shape
     half = 2 * quarter
     rows = near.shape[1]
@@ -320,18 +294,16 @@
         shapes.append(jax.ShapeDtypeStruct((count, half), F32))
     if send:
         shapes.append(jax.ShapeDtypeStruct((count, half), BF16))
+    if load:
+        shapes.append(jax.ShapeDtypeStruct(other.shape, BF16))
     return pl.pallas_call(
-        functools.partial(second_kernel, units, keep, send),
-        in_specs=[SMEM] + [VMEM] * 4 + [HBM, HBM, ANY],
+        functools.partial(second_kernel, units, keep, send, load),
+        in_specs=[SMEM] + [VMEM] * 4 + [HBM if load else VMEM, VMEM, ANY],
         out_specs=[VMEM] * len(shapes),
-        scratch_shapes=[
-            pltpu.VMEM((local * rows, half), F32),
-            pltpu.VMEM((local, hidden, quarter), BF16),
-            pltpu.VMEM((local, hidden, quarter), BF16),
-            pltpu.SemaphoreType.DMA((2, local)),
-        ],
+        scratch_shapes=[pltpu.VMEM((local * rows, half), F32)]
+        + [pltpu.SemaphoreType.DMA((local,))] * load,
         out_shape=shapes,
-        compiler_params=pltpu.CompilerParams(vmem_limit_bytes=GRANT),
+        compiler_params=granted(WEIGHT_GRANTS["second"] if load else GRANT),
         cost_estimate=cost(KERNEL_FLOPS, 2 * local * half * hidden),
     )(place, code, gate, near, far, own, other, after)
 
@@ -376,16 +348,15 @@
     side, core = spot // 2, spot % 2
     lead = lax.axis_index("expert") * group + core * local
     place = jnp.stack([core, side, lead]).astype(jnp.int32)
-    grant = pltpu.CompilerParams(vmem_limit_bytes=GRANT)
 
     mine, theirs, give_in = pl.pallas_call(
         norm_kernel,
         in_specs=[SMEM, VMEM, VMEM, VMEM, HBM],
-        out_specs=[VMEM, VMEM, HBM],
+        out_specs=[VMEM, VMEM, VMEM],
         out_shape=[jax.ShapeDtypeStruct((rows + META, half), BF16)] * 2
         + [jax.ShapeDtypeStruct((local, quarter, hidden), BF16)],
-        scratch_shapes=give_scratch(local, (quarter, hidden)),
-        compiler_params=grant,
+        scratch_shapes=[pltpu.SemaphoreType.DMA((local,))],
+        compiler_params=granted(WEIGHT_GRANTS["norm"]),
         cost_estimate=cost(KERNEL_FLOPS, 4 * rows * width),
         name="norm",
     )(place, tokens, expert_ids.T, gate_weights.T, expert_in)
@@ -394,10 +365,10 @@
     give_out = pl.pallas_call(
         give_kernel,
         in_specs=[SMEM, HBM, ANY],
-        out_specs=HBM,
+        out_specs=VMEM,
         out_shape=jax.ShapeDtypeStruct((local, hidden, quarter), BF16),
-        scratch_shapes=give_scratch(local, (hidden, quarter)),
-        compiler_params=grant,
+        scratch_shapes=[pltpu.SemaphoreType.DMA((local,))],
+        compiler_params=granted(WEIGHT_GRANTS["give"]),
         cost_estimate=cost(KERNEL_FLOPS, 4 * local * hidden * quarter),
         name="give_out",
     )(place, expert_out, mine)
@@ -406,75 +377,85 @@
     other_shared_out = swap(shared_out, "dp", 1)
 
     unit = jnp.concatenate([mine[:rows], peer[:rows], mine[rows:], peer[rows:]], axis=0)
-    feeds = {0: [unit]}
-    far_groups = list(range(groups - 1, 0, -1))
+    far_groups = list(range(groups - 1, 1, -1))
+    got = swap(unit, "expert", 1)
+    feeds = {"own": [unit], "near": [got]}
+    feeds["late"] = [swap(got, "dp", 1)]
     for g in far_groups:
         got = swap(unit, "expert", g)
         feeds[g] = [got, swap(got, "dp", 1)]
-    feeds[groups] = [swap(unit, "dp", 1)]
-
-    firsts = {}
-    shared_part = shared_far = None
-    sums = []
-    last = give_out
+    feeds["twin"] = [swap(unit, "dp", 1)]
+
+    firsts, kept, sums = {}, {}, []
+    last, own_in, own_out = give_out, None, None
 
     def first(g):
-        nonlocal last
-        part, code, gate = first_stage(feeds[g], place, expert_in, other_in, last, picks)
+        nonlocal last, own_in
+        load = own_in is None
+        part, code, gate, *held = first_stage(
+            feeds[g], place, expert_in if load else own_in, other_in, last, picks,
+            load,
+        )
         firsts[g] = (part, code, gate, swap(part, "dp", 2))
         last = code
+        own_in = held[0] if load else own_in
 
     def second(g):
-        nonlocal last
+        nonlocal last, own_out
         part, code, gate, far = firsts[g]
-        keep, send = g != groups, g != 0
+        load = own_out is None
+        keep, send = g not in ("late", "twin"), g not in ("own", "near")
         outs = second_stage(
-            len(feeds[g]), code, gate, part, far, place, expert_out, other_out, last,
-            keep, send,
+            len(feeds[g]), code, gate, part, far, place, expert_out if load else own_out,
+            other_out, last, keep, send, load,
         )
         last = outs[0]
+        own_out = outs[-1] if load else own_out
+        if keep:
+            kept[g] = outs[0]
         if not send:
-            sums.append(outs[0])
             return
-        came = swap(outs[-1], "dp", 1).astype(F32)
-        if keep:
-            joined = (outs[0] + came).astype(BF16)
-            came = swap(joined, "expert", g).astype(F32)
-            last = joined
+        came = swap(outs[keep], "dp", 1).astype(F32)
+        if g != "twin":
+            last = (kept.pop("near" if g == "late" else g) + came).astype(BF16)
+            came = swap(last, "expert", 1 if g == "late" else g).astype(F32)
         sums.append(came)
 
-    first(0)
+    first("own")
     shared_part = pl.pallas_call(
         shared_first_kernel,
         in_specs=[SMEM, VMEM, VMEM, VMEM, ANY],
         out_specs=VMEM,
         out_shape=jax.ShapeDtypeStruct((2 * rows, hidden), BF16),
         cost_estimate=cost(KERNEL_FLOPS, 2 * half * hidden),
-        compiler_params=grant,
+        compiler_params=granted(),
         name="shared_first",
     )(place, unit, shared_in, other_shared_in, last)
     last = shared_part
     shared_far = swap(shared_part, "dp", 2)
-    second(0)
-    first(far_groups[0])
+    first("near")
+    second("own")
+    for g in far_groups[:1]:
+        first(g)
     shared = pl.pallas_call(
         shared_second_kernel,
         in_specs=[SMEM, VMEM, VMEM, VMEM, VMEM, ANY],
         out_specs=VMEM,
         out_shape=jax.ShapeDtypeStruct((2 * rows, half), F32),
         cost_estimate=cost(KERNEL_FLOPS, 2 * half * hidden),
-        compiler_params=grant,
+        compiler_params=granted(),
         name="shared_second",
     )(place, shared_part, shared_far, shared_out, other_shared_out, last)
     last = shared
-    sums.append(shared)
+    second("near")
     for g in far_groups[1:]:
         first(g)
-    first(groups)
-    for g in far_groups:
+    first("late")
+    first("twin")
+    for g in far_groups + ["late", "twin"]:
         second(g)
-    second(groups)
-
+
+    sums += [shared, kept["own"]]
     total = sum(sums[1:], sums[0])
     cross = swap(total[rows:].astype(BF16), "dp", 2).astype(F32)
     kept = total[:rows]

time: 219 us -> 198 us (0.904)
  Pallas kernels: 89.9 us -> 57.6 us
  waiting for transfers between devices: 82.4 us -> 104 us
  local copies, waits for them, and re-layouts: 10.5 us -> 2.46 us
  other arithmetic: 7.56 us -> 1.57 us
  starting transfers between devices: 27.5 us -> 31.5 us
    pallas_call x11 -> x13, Pallas kernels: 78.1 us -> 51.7 us  [the longest x6 27.8 us: first_stage(): pl.pallas_call(functools.partial(first_kernel, units, picks, load), in_sp...]
    ppermute x26 -> x27, waiting for transfers between devices: 82.4 us -> 104 us  [swap(): return lax.ppermute(value, axis, [(i, i ^ mask) for i in range(size)])]
    unnamed x62 -> x18, local copies, waits for them, and re-layouts: 10.5 us -> 2.4 us
    convert_element_type x3, other arithmetic: 5.84 us -> 0.27 us  [second(): last = (kept.pop('near' if g == 'late' else g) + came).astype(BF16)]
    ppermute x26 -> x27, starting transfers between devices: 27.5 us -> 31.5 us  [swap(): return lax.ppermute(value, axis, [(i, i ^ mask) for i in range(size)])]
    pallas_call x1, Pallas kernels: 5.98 us -> 3.01 us  [exchanged_partials(): pl.pallas_call(norm_kernel, in_specs=[SMEM, VMEM, VMEM, VMEM, HBM], out_s...]
  transfers between devices with their start and end apart: 26 -> 27, of which waited for: 11 -> 12; matrix products, arithmetic and copies ran while one was open for 3% -> 0% of each run, Pallas kernels for 34% -> 24%
where the time goes in v3:
time: 198 us
  waiting for transfers between devices  104 us (53%)
  Pallas kernels  57.6 us (29%)
  starting transfers between devices  31.5 us (16%)
  local copies, waits for them, and re-layouts  2.46 us (1%)
    ppermute x27, waiting for transfers between devices, swap(): return lax.ppermute(value, axis, [(i, i ^ mask) for i in range(size)])  104 us
    ppermute x27, starting transfers between devices, swap(): return lax.ppermute(value, axis, [(i, i ^ mask) for i in range(size)])  31.5 us
    pallas_call x6, Pallas kernels, first_stage(): pl.pallas_call(functools.partial(first_kernel, units, picks, load), in_sp...  27.8 us
    pallas_call x6, Pallas kernels, second_stage(): pl.pallas_call(functools.partial(second_kernel, units, keep, send, load),...  21 us
  transfers between devices with their start and end apart: 27, of which 12 were waited for; matrix products, arithmetic and copies ran while one was open for 0% of the time, Pallas kernels for 24%

profile of v3, /device:TPU:0, one launch (start us, length us, event | category | flops | bytes accessed | tf_op | source)
XLA Modules:
  0.0 197.7 jit_solution(17444004605843874067)
XLA Ops:
  2.4 3.0 %norm.1 = (bf16[144,768]{1,0:T(8,128)(2,1)S(1)}, bf16[144,768]{1,0:T(8,128)(2,1)S(1)}, bf16[8,384,768]{2,1,0:T(8,128)(2,1)S(1)}) custom-call(s32[3]{0:T(128)S(1)} %pad_add_fusion.place, bf16[128,1536]{1,0:T(8,128)(2,1)S(1)} %copy-done.1, s32[8,128]{1,0:T(8,128)S(1)} %bitcast.5, f32[8,128]{1,0:T(8,128)S(1)} %bitcast.6, bf16[16,384,768]{2,1,0:T(8,128)(2,1)} %refs_1_.1), custom_call_target="tpu_custom_call" | custom-call | flops 10000000 | bytes 786432 | tf_op jit(solution)/shard_map/norm/pallas_call | solution.py:352
  6.0 2.9 %give_out.1.refs_3_ = bf16[8,768,384]{2,1,0:T(8,128)(2,1)S(1)} custom-call(s32[3]{0:T(128)S(1)} %pad_add_fusion.place, bf16[16,768,384]{2,1,0:T(8,128)(2,1)} %refs_4_.1, bf16[144,768]{1,0:T(8,128)(2,1)S(1)} %get-tuple-element.33.after), custom_call_target="tpu_custom_call" | custom-call | flops 10000000 | bytes 9437184 | tf_op jit(solution)/shard_map/give_out/pallas_call | solution.py:365
  9.1 3.0 %collective-permute-start = (bf16[144,768]{1,0:T(8,128)(2,1)S(1)}, bf16[144,768]{1,0:T(8,128)(2,1)S(1)}, u32[]{:S(2)}, u32[]{:S(2)}) collective-permute-start(bf16[144,768]{1,0:T(8,128)(2,1)S(1)} %get-tuple-element.34), channel_id=1, source_target_pairs={{0,2},{1,3},{2,0},{3,1},{4,6},{5,7},{6,4},{7,5},{8,10},{9,11},{10,... | collective-permute-start | bytes 663560 | tf_op jit(solution)/shard_map/ppermute | solution.py:79
  12.0 5.6 %collective-permute-done = bf16[144,768]{1,0:T(8,128)(2,1)S(1)} collective-permute-done((bf16[144,768]{1,0:T(8,128)(2,1)S(1)}, bf16[144,768]{1,0:T(8,128)(2,1)S(1)}, u32[]{:S(2)}, u32[]{:S(2)}) %collective-permute-start) | collective-permute-done | bytes 221216 | tf_op jit(solution)/shard_map/ppermute | solution.py:79
  17.8 3.9 %collective-permute-start.1 = (bf16[288,768]{1,0:T(8,128)(2,1)S(1)}, bf16[288,768]{1,0:T(8,128)(2,1)}, u32[]{:S(2)}, u32[]{:S(2)}) collective-permute-start(bf16[288,768]{1,0:T(8,128)(2,1)S(1)} %pad_maximum_fusion.refs_0_.feed), channel_id=1, source_target_pairs={{0,12},{4,8},{8,4},{12,0},{1,13},{5,9},{9,5},{13,1},{2,14},{6,10},... | collective-permute-start | bytes 1327112 | tf_op jit(solution)/shard_map/ppermute | solution.py:79
  21.7 5.6 %shard_map.73 = (bf16[8,40,768]{2,1,0:T(8,128)(2,1)S(1)}, f32[8,256]{1,0:T(8,128)S(1)}, f32[8,256]{1,0:T(8,128)S(1)}, bf16[8,384,768]{2,1,0:T(8,128)(2,1)S(1)}) custom-call(s32[3]{0:T(128)S(1)} %pad_add_fusion.place, bf16[288,768]{1,0:T(8,128)(2,1)S(1)} %pad_maximum_fusion.refs_0_.feed, bf16[16,384,768]{2,1,0:T(8,128)(2,1)} %refs_1_.1, ...), custom_call_target="tpu_custom_call" | custom-call | flops 10000000 | bytes 9437184 | tf_op jit(solution)/shard_map/pallas_call | solution.py:270
  27.4 1.6 collective-permute-start.4
  28.9 3.9 %collective-permute-done.1.refs_0_ = bf16[288,768]{1,0:T(8,128)(2,1)} collective-permute-done((bf16[288,768]{1,0:T(8,128)(2,1)S(1)}, bf16[288,768]{1,0:T(8,128)(2,1)}, u32[]{:S(2)}, u32[]{:S(2)}) %collective-permute-start.1) | collective-permute-done | bytes 442400 | tf_op jit(solution)/shard_map/ppermute | solution.py:79
  32.9 8.7 %collective-permute-start.11 = (bf16[288,768]{1,0:T(8,128)(2,1)S(1)}, bf16[288,768]{1,0:T(8,128)(2,1)S(1)}, u32[]{:S(2)}, u32[]{:S(2)}) collective-permute-start(bf16[288,768]{1,0:T(8,128)(2,1)S(1)} %pad_maximum_fusion.refs_0_.feed), channel_id=1, source_target_pairs={{0,8},{4,12},{8,0},{12,4},{1,9},{5,13},{9,1},{13,5},{2,10},{6,14},... | collective-permute-start | bytes 1327112 | tf_op jit(solution)/shard_map/ppermute | solution.py:79
  43.0 3.8 %shard_map.74 = (bf16[8,40,768]{2,1,0:T(8,128)(2,1)S(1)}, f32[8,256]{1,0:T(8,128)S(1)}, f32[8,256]{1,0:T(8,128)S(1)}) custom-call(s32[3]{0:T(128)S(1)} %pad_add_fusion.place, bf16[288,768]{1,0:T(8,128)(2,1)S(1)} %collective-permute-done.6.refs_0_, bf16[8,384,768]{2,1,0:T(8,128)(2,1)S(1)} %get-tuple-element.36.refs_1_.refs_2_, ...), custom_call_target="tpu_custom_call" | custom-call | flops 10000000 | bytes 9437184 | tf_op jit(solution)/shard_map/pallas_call | solution.py:270
  46.8 4.9 %shard_map.75 = (f32[256,768]{1,0:T(8,128)S(1)}, bf16[8,768,384]{2,1,0:T(8,128)(2,1)S(1)}) custom-call(s32[3]{0:T(128)S(1)} %pad_add_fusion.place, f32[8,256]{1,0:T(8,128)S(1)} %get-tuple-element.37._.refs_0_, f32[8,256]{1,0:T(8,128)S(1)} %get-tuple-element.38.refs_1_, bf16[8,40,768]{2,1,0:T(8,128)(2,1)S(1)} %get-tuple-element.39.refs_2_, ...), custom_call_target="tpu_custom_call" | custom-call | flops 10000000 | bytes 9437184 | tf_op jit(solution)/shard_map/pallas_call | solution.py:299
  51.8 5.7 %shard_map.76 = (bf16[8,80,768]{2,1,0:T(8,128)(2,1)S(1)}, f32[8,512]{1,0:T(8,128)S(1)}, f32[8,512]{1,0:T(8,128)S(1)}) custom-call(s32[3]{0:T(128)S(1)} %pad_add_fusion.place, bf16[288,768]{1,0:T(8,128)(2,1)} %collective-permute-done.1.refs_0_, bf16[288,768]{1,0:T(8,128)(2,1)} %collective-permute-done.2.refs_1_, ...), custom_call_target="tpu_custom_call" | custom-call | flops 10000000 | bytes 9437184 | tf_op jit(solution)/shard_map/pallas_call | solution.py:270
  57.4 1.6 collective-permute-start.8
  62.4 28.2 %collective-permute-done.14.far = bf16[256,768]{1,0:T(8,128)(2,1)S(1)} collective-permute-done((bf16[256,768]{1,0:T(8,128)(2,1)S(1)}, bf16[256,768]{1,0:T(8,128)(2,1)S(1)}, u32[]{:S(2)}, u32[]{:S(2)}) %collective-permute-start.14) | collective-permute-done | bytes 393248 | tf_op jit(solution)/shard_map/ppermute | solution.py:79
  90.6 1.8 shared_second.1.refs_6_
  92.3 8.0 %collective-permute-done.13.refs_3_ = bf16[8,40,768]{2,1,0:T(8,128)(2,1)S(1)} collective-permute-done((bf16[8,40,768]{2,1,0:T(8,128)(2,1)S(1)}, bf16[8,40,768]{2,1,0:T(8,128)(2,1)S(1)}, u32[]{:S(2)}, u32[]{:S(2)}) %collective-permute-start.13) | collective-permute-done | bytes 491552 | tf_op jit(solution)/shard_map/ppermute | solution.py:79
  100.4 2.9 %shard_map.77.refs_4_ = f32[256,768]{1,0:T(8,128)S(1)} custom-call(s32[3]{0:T(128)S(1)} %pad_add_fusion.place, f32[8,256]{1,0:T(8,128)S(1)} %get-tuple-element.40.refs_6_.refs_0_, f32[8,256]{1,0:T(8,128)S(1)} %get-tuple-element.46.refs_1_, bf16[8,40,768]{2,1,0:T(8,128)(2,1)S(1)} %get-tuple-element.47.refs_2_, ...), custom_call_target="tpu_custom_call" | custom-call | flops 10000000 | bytes 9437184 | tf_op jit(solution)/shard_map/pallas_call | solution.py:299
  103.3 5.0 %shard_map.78 = (bf16[8,80,768]{2,1,0:T(8,128)(2,1)S(1)}, f32[8,512]{1,0:T(8,128)S(1)}, f32[8,512]{1,0:T(8,128)S(1)}) custom-call(s32[3]{0:T(128)S(1)} %pad_add_fusion.place, bf16[288,768]{1,0:T(8,128)(2,1)S(1)} %collective-permute-done.11.refs_0_, bf16[288,768]{1,0:T(8,128)(2,1)S(1)} %collective-permute-done.12.refs_1_, ...), custom_call_target="tpu_custom_call" | custom-call | flops 10000000 | bytes 9437184 | tf_op jit(solution)/shard_map/pallas_call | solution.py:270
  109.9 3.8 %shard_map.79 = (bf16[8,40,768]{2,1,0:T(8,128)(2,1)S(1)}, f32[8,256]{1,0:T(8,128)S(1)}, f32[8,256]{1,0:T(8,128)S(1)}) custom-call(s32[3]{0:T(128)S(1)} %pad_add_fusion.place, bf16[288,768]{1,0:T(8,128)(2,1)S(1)} %collective-permute-done.10.refs_0_, bf16[8,384,768]{2,1,0:T(8,128)(2,1)S(1)} %get-tuple-element.36.refs_1_.refs_2_, ...), custom_call_target="tpu_custom_call" | custom-call | flops 10000000 | bytes 9437184 | tf_op jit(solution)/shard_map/pallas_call | solution.py:270
  113.7 3.8 %shard_map.80 = (bf16[8,40,768]{2,1,0:T(8,128)(2,1)S(1)}, f32[8,256]{1,0:T(8,128)S(1)}, f32[8,256]{1,0:T(8,128)S(1)}) custom-call(s32[3]{0:T(128)S(1)} %pad_add_fusion.place, bf16[288,768]{1,0:T(8,128)(2,1)S(1)} %collective-permute-done.9.refs_0_, bf16[8,384,768]{2,1,0:T(8,128)(2,1)S(1)} %get-tuple-element.36.refs_1_.refs_2_, ...), custom_call_target="tpu_custom_call" | custom-call | flops 10000000 | bytes 9437184 | tf_op jit(solution)/shard_map/pallas_call | solution.py:270
  117.6 3.7 %shard_map.81 = (f32[256,768]{1,0:T(8,128)S(1)}, bf16[256,768]{1,0:T(8,128)(2,1)S(1)}) custom-call(s32[3]{0:T(128)S(1)} %pad_add_fusion.place, f32[8,512]{1,0:T(8,128)S(1)} %get-tuple-element.42._.refs_0_, f32[8,512]{1,0:T(8,128)S(1)} %get-tuple-element.43.refs_1_, bf16[8,80,768]{2,1,0:T(8,128)(2,1)S(1)} %get-tuple-element.44.refs_2_, ...), custom_call_target="tpu_custom_call" | custom-call | flops 10000000 | bytes 9437184 | tf_op jit(solution)/shard_map/pallas_call | solution.py:299
  121.3 1.7 collective-permute-done.16
  123.1 8.3 %collective-permute-done.18.refs_3_ = bf16[8,80,768]{2,1,0:T(8,128)(2,1)S(1)} collective-permute-done((bf16[8,80,768]{2,1,0:T(8,128)(2,1)S(1)}, bf16[8,80,768]{2,1,0:T(8,128)(2,1)S(1)}, u32[]{:S(2)}, u32[]{:S(2)}) %collective-permute-start.18) | collective-permute-done | bytes 983072 | tf_op jit(solution)/shard_map/ppermute | solution.py:79
  131.4 3.6 %shard_map.82 = (f32[256,768]{1,0:T(8,128)S(1)}, bf16[256,768]{1,0:T(8,128)(2,1)S(1)}) custom-call(s32[3]{0:T(128)S(1)} %pad_add_fusion.place, f32[8,512]{1,0:T(8,128)S(1)} %get-tuple-element.48.refs_3_.refs_0_, f32[8,512]{1,0:T(8,128)S(1)} %get-tuple-element.53.refs_1_, bf16[8,80,768]{2,1,0:T(8,128)(2,1)S(1)} %get-tuple-element.54.refs_2_, ...), custom_call_target="tpu_custom_call" | custom-call | flops 10000000 | bytes 9437184 | tf_op jit(solution)/shard_map/pallas_call | solution.py:299
  136.9 11.8 %collective-permute-done.21.refs_3_ = bf16[8,40,768]{2,1,0:T(8,128)(2,1)S(1)} collective-permute-done((bf16[8,40,768]{2,1,0:T(8,128)(2,1)S(1)}, bf16[8,40,768]{2,1,0:T(8,128)(2,1)S(1)}, u32[]{:S(2)}, u32[]{:S(2)}) %collective-permute-start.21) | collective-permute-done | bytes 491552 | tf_op jit(solution)/shard_map/ppermute | solution.py:79
  148.7 2.9 %shard_map.83 = bf16[256,768]{1,0:T(8,128)(2,1)S(1)} custom-call(s32[3]{0:T(128)S(1)} %pad_add_fusion.place, f32[8,256]{1,0:T(8,128)S(1)} %get-tuple-element.49.refs_3_.refs_0_, f32[8,256]{1,0:T(8,128)S(1)} %get-tuple-element.57.refs_1_, bf16[8,40,768]{2,1,0:T(8,128)(2,1)S(1)} %get-tuple-element.58.refs_2_, ...), custom_call_target="tpu_custom_call" | custom-call | flops 10000000 | bytes 9437184 | tf_op jit(solution)/shard_map/pallas_call | solution.py:299
  151.7 1.5 collective-permute-start.24
  153.3 2.6 %collective-permute-start.17 = (bf16[256,768]{1,0:T(8,128)(2,1)S(1)}, bf16[256,768]{1,0:T(8,128)(2,1)S(1)}, u32[]{:S(2)}, u32[]{:S(2)}) collective-permute-start(bf16[256,768]{1,0:T(8,128)(2,1)S(1)} %add_convert_fusion.2.refs_6_), channel_id=1, source_target_pairs={{0,12},{4,8},{8,4},{12,0},{1,13},{5,9},{9,5},{13,1},{2,14},{6,10},... | collective-permute-start | bytes 1179656 | tf_op jit(solution)/shard_map/ppermute | solution.py:79
  156.0 9.4 %collective-permute-done.24.refs_3_ = bf16[8,40,768]{2,1,0:T(8,128)(2,1)S(1)} collective-permute-done((bf16[8,40,768]{2,1,0:T(8,128)(2,1)S(1)}, bf16[8,40,768]{2,1,0:T(8,128)(2,1)S(1)}, u32[]{:S(2)}, u32[]{:S(2)}) %collective-permute-start.24) | collective-permute-done | bytes 491552 | tf_op jit(solution)/shard_map/ppermute | solution.py:79
  165.4 2.9 %shard_map.84 = bf16[256,768]{1,0:T(8,128)(2,1)S(1)} custom-call(s32[3]{0:T(128)S(1)} %pad_add_fusion.place, f32[8,256]{1,0:T(8,128)S(1)} %get-tuple-element.50.refs_6_.refs_0_, f32[8,256]{1,0:T(8,128)S(1)} %get-tuple-element.59.refs_1_, bf16[8,40,768]{2,1,0:T(8,128)(2,1)S(1)} %get-tuple-element.60.refs_2_, ...), custom_call_target="tpu_custom_call" | custom-call | flops 10000000 | bytes 9437184 | tf_op jit(solution)/shard_map/pallas_call | solution.py:299
  169.6 20.7 %collective-permute-done.20 = bf16[256,768]{1,0:T(8,128)(2,1)S(1)} collective-permute-done((bf16[256,768]{1,0:T(8,128)(2,1)S(1)}, bf16[256,768]{1,0:T(8,128)(2,1)S(1)}, u32[]{:S(2)}, u32[]{:S(2)}) %collective-permute-start.20) | collective-permute-done | bytes 393248 | tf_op jit(solution)/shard_map/ppermute | solution.py:79
  191.3 5.6 %collective-permute-done.26 = bf16[128,768]{1,0:T(8,128)(2,1)S(1)} collective-permute-done((bf16[128,768]{1,0:T(8,128)(2,1)S(1)}, bf16[128,768]{1,0:T(8,128)(2,1)S(1)}, u32[]{:S(2)}, u32[]{:S(2)}) %collective-permute-start.26) | collective-permute-done | bytes 196640 | tf_op jit(solution)/shard_map/ppermute | solution.py:79
  (69 shorter events, 14.8 us)
Async XLA Ops:
  5.5 16.2 %collective-permute-start.3 = (bf16[8,384,768]{2,1,0:T(8,128)(2,1)S(1)}, bf16[8,384,768]{2,1,0:T(8,128)(2,1)S(1)}, u32[]{:S(2)}, u32[]{:S(2)}) collective-permute-start(bf16[8,384,768]{2,1,0:T(8,128)(2,1)S(1)} %get-tuple-element.35), channel_id=1, source_target_pairs={{0,1},{1,0},{2,3},{3,2},{4,5},{5,4},{6,7},{7,6},{8,9},{9,8},{10,11... | collective-permute-start | bytes 14155784 | tf_op jit(solution)/shard_map/ppermute | solution.py:79
  6.0 15.7 %copy-start.3 = (bf16[384,768]{1,0:T(8,128)(2,1)S(1)}, bf16[384,768]{1,0:T(8,128)(2,1)}, u32[]{:S(2)}) copy-start(bf16[384,768]{1,0:T(8,128)(2,1)} %own.2) | copy-start | bytes 1769476
  9.0 12.8 %copy-start = (bf16[8,768,384]{2,1,0:T(8,128)(2,1)}, bf16[8,768,384]{2,1,0:T(8,128)(2,1)S(1)}, u32[]{:S(2)}) copy-start(bf16[8,768,384]{2,1,0:T(8,128)(2,1)S(1)} %give_out.1.refs_3_) | copy-start | bytes 14155780
  9.0 37.9 %collective-permute-start.5 = (bf16[8,768,384]{2,1,0:T(8,128)(2,1)S(1)}, bf16[8,768,384]{2,1,0:T(8,128)(2,1)S(1)}, u32[]{:S(2)}, u32[]{:S(2)}) collective-permute-start(bf16[8,768,384]{2,1,0:T(8,128)(2,1)S(1)} %give_out.1.refs_3_), channel_id=1, source_target_pairs={{0,1},{1,0},{2,3},{3,2},{4,5},{5,4},{6,7},{7,6},{8,9},{9,8},{10,11... | collective-permute-start | bytes 14155784 | tf_op jit(solution)/shard_map/ppermute | solution.py:79
  9.1 8.6 %collective-permute-start = (bf16[144,768]{1,0:T(8,128)(2,1)S(1)}, bf16[144,768]{1,0:T(8,128)(2,1)S(1)}, u32[]{:S(2)}, u32[]{:S(2)}) collective-permute-start(bf16[144,768]{1,0:T(8,128)(2,1)S(1)} %get-tuple-element.34), channel_id=1, source_target_pairs={{0,2},{1,3},{2,0},{3,1},{4,6},{5,7},{6,4},{7,5},{8,10},{9,11},{10,... | collective-permute-start | bytes 663560 | tf_op jit(solution)/shard_map/ppermute | solution.py:79
  17.8 23.8 %copy-start.4 = (bf16[768,384]{1,0:T(8,128)(2,1)S(1)}, bf16[768,384]{1,0:T(8,128)(2,1)}, u32[]{:S(2)}) copy-start(bf16[768,384]{1,0:T(8,128)(2,1)} %own.3) | copy-start | bytes 1769476
  17.8 15.1 %collective-permute-start.1 = (bf16[288,768]{1,0:T(8,128)(2,1)S(1)}, bf16[288,768]{1,0:T(8,128)(2,1)}, u32[]{:S(2)}, u32[]{:S(2)}) collective-permute-start(bf16[288,768]{1,0:T(8,128)(2,1)S(1)} %pad_maximum_fusion.refs_0_.feed), channel_id=1, source_target_pairs={{0,12},{4,8},{8,4},{12,0},{1,13},{5,9},{9,5},{13,1},{2,14},{6,10},... | collective-permute-start | bytes 1327112 | tf_op jit(solution)/shard_map/ppermute | solution.py:79
  21.7 11.2 %collective-permute-start.7 = (bf16[384,768]{1,0:T(8,128)(2,1)S(1)}, bf16[384,768]{1,0:T(8,128)(2,1)S(1)}, u32[]{:S(2)}, u32[]{:S(2)}) collective-permute-start(bf16[384,768]{1,0:T(8,128)(2,1)S(1)} %copy-done.3), channel_id=1, source_target_pairs={{0,1},{1,0},{2,3},{3,2},{4,5},{5,4},{6,7},{7,6},{8,9},{9,8},{10,11... | collective-permute-start | bytes 1769480 | tf_op jit(solution)/shard_map/ppermute | solution.py:79
  21.7 19.9 %collective-permute-start.6 = (bf16[288,768]{1,0:T(8,128)(2,1)S(1)}, bf16[288,768]{1,0:T(8,128)(2,1)S(1)}, u32[]{:S(2)}, u32[]{:S(2)}) collective-permute-start(bf16[288,768]{1,0:T(8,128)(2,1)S(1)} %pad_maximum_fusion.refs_0_.feed), channel_id=1, source_target_pairs={{0,4},{4,0},{8,12},{12,8},{1,5},{5,1},{9,13},{13,9},{2,6},{6,2},{1... | collective-permute-start | bytes 1327112 | tf_op jit(solution)/shard_map/ppermute | solution.py:79
  27.4 19.5 %collective-permute-start.4 = (bf16[8,40,768]{2,1,0:T(8,128)(2,1)S(1)}, bf16[8,40,768]{2,1,0:T(8,128)(2,1)S(1)}, u32[]{:S(2)}, u32[]{:S(2)}) collective-permute-start(bf16[8,40,768]{2,1,0:T(8,128)(2,1)S(1)} %get-tuple-element.39.refs_2_), channel_id=1, source_target_pairs={{0,2},{1,3},{2,0},{3,1},{4,6},{5,7},{6,4},{7,5},{8,10},{9,11},{10,... | collective-permute-start | bytes 1474568 | tf_op jit(solution)/shard_map/ppermute | solution.py:79
  32.9 18.9 %collective-permute-start.2 = (bf16[288,768]{1,0:T(8,128)(2,1)}, bf16[288,768]{1,0:T(8,128)(2,1)}, u32[]{:S(2)}, u32[]{:S(2)}) collective-permute-start(bf16[288,768]{1,0:T(8,128)(2,1)} %collective-permute-done.1.refs_0_), channel_id=1, source_target_pairs={{0,1},{1,0},{2,3},{3,2},{4,5},{5,4},{6,7},{7,6},{8,9},{9,8},{10,11... | collective-permute-start | bytes 1327112 | tf_op jit(solution)/shard_map/ppermute | solution.py:79
  32.9 29.0 %collective-permute-start.11 = (bf16[288,768]{1,0:T(8,128)(2,1)S(1)}, bf16[288,768]{1,0:T(8,128)(2,1)S(1)}, u32[]{:S(2)}, u32[]{:S(2)}) collective-permute-start(bf16[288,768]{1,0:T(8,128)(2,1)S(1)} %pad_maximum_fusion.refs_0_.feed), channel_id=1, source_target_pairs={{0,8},{4,12},{8,0},{12,4},{1,9},{5,13},{9,1},{13,5},{2,10},{6,14},... | collective-permute-start | bytes 1327112 | tf_op jit(solution)/shard_map/ppermute | solution.py:79
  41.6 20.3 %collective-permute-start.15 = (bf16[768,384]{1,0:T(8,128)(2,1)S(1)}, bf16[768,384]{1,0:T(8,128)(2,1)}, u32[]{:S(2)}, u32[]{:S(2)}) collective-permute-start(bf16[768,384]{1,0:T(8,128)(2,1)S(1)} %copy-done.4), channel_id=1, source_target_pairs={{0,1},{1,0},{2,3},{3,2},{4,5},{5,4},{6,7},{7,6},{8,9},{9,8},{10,11... | collective-permute-start | bytes 1769480 | tf_op jit(solution)/shard_map/ppermute | solution.py:79
  51.8 10.1 %copy-start.6 = (bf16[288,768]{1,0:T(8,128)(2,1)S(1)}, bf16[288,768]{1,0:T(8,128)(2,1)}, u32[]{:S(2)}) copy-start(bf16[288,768]{1,0:T(8,128)(2,1)} %copy-done.5) | copy-start | bytes 1327108
  57.4 60.1 %collective-permute-start.8 = (bf16[8,80,768]{2,1,0:T(8,128)(2,1)S(1)}, bf16[8,80,768]{2,1,0:T(8,128)(2,1)S(1)}, u32[]{:S(2)}, u32[]{:S(2)}) collective-permute-start(bf16[8,80,768]{2,1,0:T(8,128)(2,1)S(1)} %get-tuple-element.44.refs_2_), channel_id=1, source_target_pairs={{0,2},{1,3},{2,0},{3,1},{4,6},{5,7},{6,4},{7,5},{8,10},{9,11},{10,... | collective-permute-start | bytes 2949128 | tf_op jit(solution)/shard_map/ppermute | solution.py:79
  59.0 31.6 %collective-permute-start.14 = (bf16[256,768]{1,0:T(8,128)(2,1)S(1)}, bf16[256,768]{1,0:T(8,128)(2,1)S(1)}, u32[]{:S(2)}, u32[]{:S(2)}) collective-permute-start(bf16[256,768]{1,0:T(8,128)(2,1)S(1)} %shared_first.1.refs_3_.near), channel_id=1, source_target_pairs={{0,2},{1,3},{2,0},{3,1},{4,6},{5,7},{6,4},{7,5},{8,10},{9,11},{10,... | collective-permute-start | bytes 1179656 | tf_op jit(solution)/shard_map/ppermute | solution.py:79
  59.5 40.8 %collective-permute-start.13 = (bf16[8,40,768]{2,1,0:T(8,128)(2,1)S(1)}, bf16[8,40,768]{2,1,0:T(8,128)(2,1)S(1)}, u32[]{:S(2)}, u32[]{:S(2)}) collective-permute-start(bf16[8,40,768]{2,1,0:T(8,128)(2,1)S(1)} %get-tuple-element.47.refs_2_), channel_id=1, source_target_pairs={{0,2},{1,3},{2,0},{3,1},{4,6},{5,7},{6,4},{7,5},{8,10},{9,11},{10,... | collective-permute-start | bytes 1474568 | tf_op jit(solution)/shard_map/ppermute | solution.py:79
  61.9 41.4 %collective-permute-start.12 = (bf16[288,768]{1,0:T(8,128)(2,1)S(1)}, bf16[288,768]{1,0:T(8,128)(2,1)S(1)}, u32[]{:S(2)}, u32[]{:S(2)}) collective-permute-start(bf16[288,768]{1,0:T(8,128)(2,1)S(1)} %collective-permute-done.11.refs_0_), channel_id=1, source_target_pairs={{0,1},{1,0},{2,3},{3,2},{4,5},{5,4},{6,7},{7,6},{8,9},{9,8},{10,11... | collective-permute-start | bytes 1327112 | tf_op jit(solution)/shard_map/ppermute | solution.py:79
  61.9 48.0 %collective-permute-start.10 = (bf16[288,768]{1,0:T(8,128)(2,1)S(1)}, bf16[288,768]{1,0:T(8,128)(2,1)S(1)}, u32[]{:S(2)}, u32[]{:S(2)}) collective-permute-start(bf16[288,768]{1,0:T(8,128)(2,1)S(1)} %copy-done.6), channel_id=1, source_target_pairs={{0,1},{1,0},{2,3},{3,2},{4,5},{5,4},{6,7},{7,6},{8,9},{9,8},{10,11... | collective-permute-start | bytes 1327112 | tf_op jit(solution)/shard_map/ppermute | solution.py:79
  90.6 23.1 %collective-permute-start.9 = (bf16[288,768]{1,0:T(8,128)(2,1)S(1)}, bf16[288,768]{1,0:T(8,128)(2,1)S(1)}, u32[]{:S(2)}, u32[]{:S(2)}) collective-permute-start(bf16[288,768]{1,0:T(8,128)(2,1)S(1)} %pad_maximum_fusion.refs_0_.feed), channel_id=1, source_target_pairs={{0,1},{1,0},{2,3},{3,2},{4,5},{5,4},{6,7},{7,6},{8,9},{9,8},{10,11... | collective-permute-start | bytes 1327112 | tf_op jit(solution)/shard_map/ppermute | solution.py:79
  108.3 23.1 %collective-permute-start.18 = (bf16[8,80,768]{2,1,0:T(8,128)(2,1)S(1)}, bf16[8,80,768]{2,1,0:T(8,128)(2,1)S(1)}, u32[]{:S(2)}, u32[]{:S(2)}) collective-permute-start(bf16[8,80,768]{2,1,0:T(8,128)(2,1)S(1)} %get-tuple-element.54.refs_2_), channel_id=1, source_target_pairs={{0,2},{1,3},{2,0},{3,1},{4,6},{5,7},{6,4},{7,5},{8,10},{9,11},{10,... | collective-permute-start | bytes 2949128 | tf_op jit(solution)/shard_map/ppermute | solution.py:79
  121.2 1.8 collective-permute-start.16
  135.0 1.8 collective-permute-start.19
  135.1 13.6 %collective-permute-start.21 = (bf16[8,40,768]{2,1,0:T(8,128)(2,1)S(1)}, bf16[8,40,768]{2,1,0:T(8,128)(2,1)S(1)}, u32[]{:S(2)}, u32[]{:S(2)}) collective-permute-start(bf16[8,40,768]{2,1,0:T(8,128)(2,1)S(1)} %get-tuple-element.58.refs_2_), channel_id=1, source_target_pairs={{0,2},{1,3},{2,0},{3,1},{4,6},{5,7},{6,4},{7,5},{8,10},{9,11},{10,... | collective-permute-start | bytes 1474568 | tf_op jit(solution)/shard_map/ppermute | solution.py:79
  151.7 4.2 %collective-permute-start.22 = (bf16[256,768]{1,0:T(8,128)(2,1)S(1)}, bf16[256,768]{1,0:T(8,128)(2,1)S(1)}, u32[]{:S(2)}, u32[]{:S(2)}) collective-permute-start(bf16[256,768]{1,0:T(8,128)(2,1)S(1)} %shard_map.83), channel_id=1, source_target_pairs={{0,1},{1,0},{2,3},{3,2},{4,5},{5,4},{6,7},{7,6},{8,9},{9,8},{10,11... | collective-permute-start | bytes 1179656 | tf_op jit(solution)/shard_map/ppermute | solution.py:79
  151.7 13.6 %collective-permute-start.24 = (bf16[8,40,768]{2,1,0:T(8,128)(2,1)S(1)}, bf16[8,40,768]{2,1,0:T(8,128)(2,1)S(1)}, u32[]{:S(2)}, u32[]{:S(2)}) collective-permute-start(bf16[8,40,768]{2,1,0:T(8,128)(2,1)S(1)} %get-tuple-element.60.refs_2_), channel_id=1, source_target_pairs={{0,2},{1,3},{2,0},{3,1},{4,6},{5,7},{6,4},{7,5},{8,10},{9,11},{10,... | collective-permute-start | bytes 1474568 | tf_op jit(solution)/shard_map/ppermute | solution.py:79
  153.3 16.3 %collective-permute-start.17 = (bf16[256,768]{1,0:T(8,128)(2,1)S(1)}, bf16[256,768]{1,0:T(8,128)(2,1)S(1)}, u32[]{:S(2)}, u32[]{:S(2)}) collective-permute-start(bf16[256,768]{1,0:T(8,128)(2,1)S(1)} %add_convert_fusion.2.refs_6_), channel_id=1, source_target_pairs={{0,12},{4,8},{8,4},{12,0},{1,13},{5,9},{9,5},{13,1},{2,14},{6,10},... | collective-permute-start | bytes 1179656 | tf_op jit(solution)/shard_map/ppermute | solution.py:79
  155.9 34.4 %collective-permute-start.20 = (bf16[256,768]{1,0:T(8,128)(2,1)S(1)}, bf16[256,768]{1,0:T(8,128)(2,1)S(1)}, u32[]{:S(2)}, u32[]{:S(2)}) collective-permute-start(bf16[256,768]{1,0:T(8,128)(2,1)S(1)} %add_convert_fusion.1.refs_6_), channel_id=1, source_target_pairs={{0,8},{4,12},{8,0},{12,4},{1,9},{5,13},{9,1},{13,5},{2,10},{6,14},... | collective-permute-start | bytes 1179656 | tf_op jit(solution)/shard_map/ppermute | solution.py:79
  168.3 28.6 %copy-start.2 = (bf16[128,1536]{1,0:T(8,128)(2,1)S(1)}, bf16[128,1536]{1,0:T(8,128)(2,1)}, u32[]{:S(2)}) copy-start(bf16[128,1536]{1,0:T(8,128)(2,1)} %tokens.1) | copy-start | bytes 1179652
  168.3 22.0 %collective-permute-start.25 = (bf16[256,768]{1,0:T(8,128)(2,1)S(1)}, bf16[256,768]{1,0:T(8,128)(2,1)S(1)}, u32[]{:S(2)}, u32[]{:S(2)}) collective-permute-start(bf16[256,768]{1,0:T(8,128)(2,1)S(1)} %shard_map.84), channel_id=1, source_target_pairs={{0,1},{1,0},{2,3},{3,2},{4,5},{5,4},{6,7},{7,6},{8,9},{9,8},{10,11... | collective-permute-start | bytes 1179656 | tf_op jit(solution)/shard_map/ppermute | solution.py:79
  168.4 21.9 %collective-permute-start.23 = (bf16[256,768]{1,0:T(8,128)(2,1)S(1)}, bf16[256,768]{1,0:T(8,128)(2,1)S(1)}, u32[]{:S(2)}, u32[]{:S(2)}) collective-permute-start(bf16[256,768]{1,0:T(8,128)(2,1)S(1)} %add_convert_fusion.refs_6_), channel_id=1, source_target_pairs={{0,4},{4,0},{8,12},{12,8},{1,5},{5,1},{9,13},{13,9},{2,6},{6,2},{1... | collective-permute-start | bytes 1179656 | tf_op jit(solution)/shard_map/ppermute | solution.py:79
  190.7 6.2 %collective-permute-start.26 = (bf16[128,768]{1,0:T(8,128)(2,1)S(1)}, bf16[128,768]{1,0:T(8,128)(2,1)S(1)}, u32[]{:S(2)}, u32[]{:S(2)}) collective-permute-start(bf16[128,768]{1,0:T(8,128)(2,1)S(1)} %slice.32), channel_id=1, source_target_pairs={{0,2},{1,3},{2,0},{3,1},{4,6},{5,7},{6,4},{7,5},{8,10},{9,11},{10,... | collective-permute-start | bytes 589832 | tf_op jit(solution)/shard_map/ppermute | solution.py:79
  (4 other events, 7.6 us)

commit v4 on v3

--- a/solution.py
+++ b/solution.py
@@ -9,6 +9,7 @@
 
 
 CAP = 20
+SWEEP, GROUP, SIDE = "sweep", "expert", "dp"
 F32 = jnp.float32
 BF16 = jnp.bfloat16
 KERNEL_FLOPS = 10_000_000
@@ -40,31 +41,31 @@
     row_count, model_width = tokens.shape
     pick_count = expert_ids.shape[1]
     local_count = expert_in.shape[0]
-    group_count = lax.axis_size("expert")
+    group_count = lax.axis_size(GROUP)
     expert_total = local_count * group_count
     normed = layer_norm(tokens)
-    full_in = lax.all_gather(expert_in, "dp", axis=1, tiled=True)
-    full_out = lax.all_gather(expert_out, "dp", axis=2, tiled=True)
+    full_in = lax.all_gather(expert_in, SIDE, axis=1, tiled=True)
+    full_out = lax.all_gather(expert_out, SIDE, axis=2, tiled=True)
     slot_of = copy_slots(expert_ids, expert_total)
     positions = (expert_ids * CAP + slot_of).reshape(-1)
     copies = jnp.repeat(normed, pick_count, axis=0)
     outgoing = jnp.zeros((expert_total * CAP, model_width), BF16).at[positions].set(copies)
     outgoing = outgoing.reshape(group_count, local_count, CAP, model_width)
-    received = lax.all_to_all(outgoing, "expert", split_axis=0, concat_axis=0, tiled=True)
+    received = lax.all_to_all(outgoing, GROUP, split_axis=0, concat_axis=0, tiled=True)
     returned = lax.all_to_all(
-        run_experts(received, full_in, full_out), "expert", split_axis=0, concat_axis=0, tiled=True
+        run_experts(received, full_in, full_out), GROUP, split_axis=0, concat_axis=0, tiled=True
     )
     results = returned.reshape(expert_total * CAP, model_width)[positions].reshape(
         row_count, pick_count, model_width
     )
     routed = jnp.sum(results.astype(F32) * gate_weights[:, :, None], axis=1)
     shared_pre = jnp.dot(
-        normed, lax.all_gather(shared_in, "dp", axis=0, tiled=True), preferred_element_type=F32
+        normed, lax.all_gather(shared_in, SIDE, axis=0, tiled=True), preferred_element_type=F32
     )
     shared_hidden = jax.nn.gelu(shared_pre).astype(BF16)
     shared_result = jnp.dot(
         shared_hidden,
-        lax.all_gather(shared_out, "dp", axis=1, tiled=True),
+        lax.all_gather(shared_out, SIDE, axis=1, tiled=True),
         preferred_element_type=F32,
     )
     return (tokens.astype(F32) + shared_result + routed).astype(BF16)
@@ -72,11 +73,6 @@
 
 def dot(a, b):
     return jnp.dot(a, b, preferred_element_type=F32)
-
-
-def swap(value, axis, mask):
-    size = lax.axis_size(axis)
-    return lax.ppermute(value, axis, [(i, i ^ mask) for i in range(size)])
 
 
 def cost(flops, moved):
@@ -90,11 +86,7 @@
     ]
 
 
-def norm_kernel(place, tokens, ids, gates, source, mine, theirs, given, came):
-    local = given.shape[0]
-    copies = half_copies(source, given, (1 - place[0]) * local, came)
-    for c in copies:
-        c.start()
+def norm_kernel(place, tokens, ids, gates, _, mine, theirs):
     rows, width = tokens.shape
     half = width // 2
     values = tokens[...].astype(F32)
@@ -113,8 +105,6 @@
     table = jnp.concatenate([table, jnp.zeros((META - picks, half), F32)], axis=0).astype(BF16)
     mine[rows : rows + META, :] = table
     theirs[rows : rows + META, :] = table
-    for c in copies:
-        c.wait()
 
 
 def give_kernel(place, source, after, given, came):
@@ -135,7 +125,7 @@
 def first_kernel(units, picks, load, place, *refs):
     feeds, refs = refs[:units], refs[units:]
     source, other, _, part, code, gate = refs[:6]
-    own, (packed, made, left, *came) = (refs[6], refs[7:]) if load else (source, refs[6:])
+    own, (packed, *came) = (refs[6], refs[7:]) if load else (source, refs[6:])
     local, rows, half = packed.shape
     slots = rows // (2 * units)
     tokens = feeds[0].shape[0] // 2 - META
@@ -180,9 +170,6 @@
     here = pl.multiple_of(place[0] * quarter, quarter)
     there = pl.multiple_of((1 - place[0]) * quarter, quarter)
 
-    def put(e):
-        return pltpu.make_async_copy(made.at[e], part.at[e], left.at[e])
-
     @pl.loop(0, local // 2)
     def _(pair):
         for e in (2 * pair, 2 * pair + 1):
@@ -191,13 +178,7 @@
                 base = place[0] * local
                 pltpu.make_async_copy(source.at[base + e], own.at[e], came[0].at[e]).wait()
             total += dot(packed[e, :, pl.ds(here, quarter)], own[e])
-            made[e] = total.astype(BF16)
-        for e in (2 * pair, 2 * pair + 1):
-            put(e).start()
-
-    @pl.loop(0, local)
-    def _(e):
-        put(e).wait()
+            part[e] = total.astype(BF16)
 
 
 def second_kernel(units, keep, send, load, place, *refs):
@@ -253,7 +234,9 @@
 ANY = pl.BlockSpec(memory_space=pl.ANY)
 HBM = pl.BlockSpec(memory_space=pltpu.HBM)
 GRANT = 24 << 20
-WEIGHT_GRANTS = {"norm": 46 << 20, "give": 42 << 20, "first": 40 << 20, "second": 36 << 20}
+GIVE_GRANTS = (46 << 20, 42 << 20)
+FIRST_GRANT = 40 << 20
+SECOND_GRANT = 36 << 20
 
 
 def granted(size=GRANT):
@@ -270,16 +253,12 @@
     return pl.pallas_call(
         functools.partial(first_kernel, units, picks, load),
         in_specs=[SMEM] + [VMEM] * units + [HBM if load else VMEM, VMEM, ANY],
-        out_specs=[ANY, VMEM, VMEM] + [VMEM] * load,
-        scratch_shapes=[
-            pltpu.VMEM((local, rows, half), BF16),
-            pltpu.VMEM((local, rows, hidden), BF16),
-            pltpu.SemaphoreType.DMA((local,)),
-        ]
+        out_specs=[VMEM] * (3 + load),
+        scratch_shapes=[pltpu.VMEM((local, rows, half), BF16)]
         + [pltpu.SemaphoreType.DMA((local,))] * load,
         out_shape=[jax.ShapeDtypeStruct((local, rows, hidden), BF16), table, table]
         + [jax.ShapeDtypeStruct(other.shape, BF16)] * load,
-        compiler_params=granted(WEIGHT_GRANTS["first"] if load else GRANT),
+        compiler_params=granted(FIRST_GRANT if load else GRANT),
         cost_estimate=cost(KERNEL_FLOPS, 2 * local * half * hidden),
     )(place, *feeds, own, other, after)
 
@@ -303,7 +282,7 @@
         scratch_shapes=[pltpu.VMEM((local * rows, half), F32)]
         + [pltpu.SemaphoreType.DMA((local,))] * load,
         out_shape=shapes,
-        compiler_params=granted(WEIGHT_GRANTS["second"] if load else GRANT),
+        compiler_params=granted(SECOND_GRANT if load else GRANT),
         cost_estimate=cost(KERNEL_FLOPS, 2 * local * half * hidden),
     )(place, code, gate, near, far, own, other, after)
 
@@ -335,56 +314,75 @@
         out[at, pl.ds(there, quarter)] = right[b * rows : (b + 1) * rows]
 
 
+def give_stage(place, source, after, grant):
+    shape = (source.shape[0] // 2, *source.shape[1:])
+    return pl.pallas_call(
+        give_kernel,
+        in_specs=[SMEM, HBM, ANY],
+        out_specs=VMEM,
+        out_shape=jax.ShapeDtypeStruct(shape, BF16),
+        scratch_shapes=[pltpu.SemaphoreType.DMA(shape[:1])],
+        compiler_params=granted(grant),
+        cost_estimate=cost(KERNEL_FLOPS, 4 * shape[0] * shape[1] * shape[2]),
+    )(place, source, after)
+
+
+def kernel(body, after, shapes, place, *args):
+    return pl.pallas_call(
+        body,
+        in_specs=[SMEM] + [VMEM] * len(args) + [ANY],
+        out_specs=[VMEM] * len(shapes),
+        out_shape=shapes,
+        compiler_params=granted(),
+        cost_estimate=cost(KERNEL_FLOPS, 1 << 20),
+    )(place, *args, after)
+
+
 def exchanged_partials(tokens, expert_ids, gate_weights, expert_in, expert_out, shared_in, shared_out):
     rows, width = tokens.shape
     half = width // 2
-    quarter = half // 2
     picks = expert_ids.shape[1]
     group = expert_in.shape[0]
     local = group // 2
     hidden = expert_in.shape[2]
-    groups = lax.axis_size("expert")
-    spot = lax.axis_index("dp")
+    groups = lax.axis_size(GROUP)
+    spot = lax.axis_index(SIDE)
     side, core = spot // 2, spot % 2
-    lead = lax.axis_index("expert") * group + core * local
+    lead = lax.axis_index(GROUP) * group + core * local
     place = jnp.stack([core, side, lead]).astype(jnp.int32)
 
-    mine, theirs, give_in = pl.pallas_call(
-        norm_kernel,
-        in_specs=[SMEM, VMEM, VMEM, VMEM, HBM],
-        out_specs=[VMEM, VMEM, VMEM],
-        out_shape=[jax.ShapeDtypeStruct((rows + META, half), BF16)] * 2
-        + [jax.ShapeDtypeStruct((local, quarter, hidden), BF16)],
-        scratch_shapes=[pltpu.SemaphoreType.DMA((local,))],
-        compiler_params=granted(WEIGHT_GRANTS["norm"]),
-        cost_estimate=cost(KERNEL_FLOPS, 4 * rows * width),
-        name="norm",
-    )(place, tokens, expert_ids.T, gate_weights.T, expert_in)
-    peer = swap(theirs, "dp", 2)
-    other_in = swap(give_in, "dp", 1)
-    give_out = pl.pallas_call(
-        give_kernel,
-        in_specs=[SMEM, HBM, ANY],
-        out_specs=VMEM,
-        out_shape=jax.ShapeDtypeStruct((local, hidden, quarter), BF16),
-        scratch_shapes=[pltpu.SemaphoreType.DMA((local,))],
-        compiler_params=granted(WEIGHT_GRANTS["give"]),
-        cost_estimate=cost(KERNEL_FLOPS, 4 * local * hidden * quarter),
-        name="give_out",
-    )(place, expert_out, mine)
-    other_shared_in = swap(shared_in, "dp", 1)
-    other_out = swap(give_out, "dp", 1)
-    other_shared_out = swap(shared_out, "dp", 1)
+    def swap(value, axis, mask):
+        return lax.ppermute(value, axis, [(i, i ^ mask) for i in range(lax.axis_size(axis))])
+
+    def cross(value):
+        return swap(value, SIDE, 2)
+
+    def share(value):
+        return swap(value, SIDE, 1)
+
+    give_in = give_stage(place, expert_in, place, GIVE_GRANTS[0])
+    other_in = share(give_in)
+    block = jax.ShapeDtypeStruct((rows + META, half), BF16)
+    mine, theirs = kernel(
+        norm_kernel, give_in, [block] * 2,
+        place, tokens, expert_ids.T, gate_weights.T,
+    )
+    peer = cross(theirs)
+    give_out = give_stage(place, expert_out, mine, GIVE_GRANTS[1])
+    other_shared_in = share(shared_in)
+    other_out = share(give_out)
+    other_shared_out = share(shared_out)
 
     unit = jnp.concatenate([mine[:rows], peer[:rows], mine[rows:], peer[rows:]], axis=0)
-    far_groups = list(range(groups - 1, 1, -1))
-    got = swap(unit, "expert", 1)
-    feeds = {"own": [unit], "near": [got]}
-    feeds["late"] = [swap(got, "dp", 1)]
-    for g in far_groups:
-        got = swap(unit, "expert", g)
-        feeds[g] = [got, swap(got, "dp", 1)]
-    feeds["twin"] = [swap(unit, "dp", 1)]
+    far = far_groups(groups)
+    near = swap(unit, GROUP, 1)
+    feeds = {"o": [unit], "n": [near], "l": [share(near)], "t": [share(unit)]}
+    for g in far:
+        if g % 2:
+            got = swap(unit, GROUP, g)
+        else:
+            got = swap(feeds[str(g + 1)][0], GROUP, 1)
+        feeds[str(g)] = [got, share(got)]
 
     firsts, kept, sums = {}, {}, []
     last, own_in, own_out = give_out, None, None
@@ -396,17 +394,17 @@
             feeds[g], place, expert_in if load else own_in, other_in, last, picks,
             load,
         )
-        firsts[g] = (part, code, gate, swap(part, "dp", 2))
+        firsts[g] = (part, code, gate, cross(part))
         last = code
         own_in = held[0] if load else own_in
 
     def second(g):
         nonlocal last, own_out
-        part, code, gate, far = firsts[g]
+        part, code, gate, across = firsts[g]
         load = own_out is None
-        keep, send = g not in ("late", "twin"), g not in ("own", "near")
+        keep, send = g not in "lt", g not in "on"
         outs = second_stage(
-            len(feeds[g]), code, gate, part, far, place, expert_out if load else own_out,
+            len(feeds[g]), code, gate, part, across, place, expert_out if load else own_out,
             other_out, last, keep, send, load,
         )
         last = outs[0]
@@ -415,58 +413,49 @@
             kept[g] = outs[0]
         if not send:
             return
-        came = swap(outs[keep], "dp", 1).astype(F32)
-        if g != "twin":
-            last = (kept.pop("near" if g == "late" else g) + came).astype(BF16)
-            came = swap(last, "expert", 1 if g == "late" else g).astype(F32)
+        came = share(outs[keep]).astype(F32)
+        if g != "t":
+            last = (kept.pop("n" if g == "l" else g) + came).astype(BF16)
+            came = swap(last, GROUP, 1 if g == "l" else int(g)).astype(F32)
         sums.append(came)
 
-    first("own")
-    shared_part = pl.pallas_call(
-        shared_first_kernel,
-        in_specs=[SMEM, VMEM, VMEM, VMEM, ANY],
-        out_specs=VMEM,
-        out_shape=jax.ShapeDtypeStruct((2 * rows, hidden), BF16),
-        cost_estimate=cost(KERNEL_FLOPS, 2 * half * hidden),
-        compiler_params=granted(),
-        name="shared_first",
-    )(place, unit, shared_in, other_shared_in, last)
+    first("o")
+    (shared_part,) = kernel(
+        shared_first_kernel, last,
+        [jax.ShapeDtypeStruct((2 * rows, hidden), BF16)],
+        place, unit, shared_in, other_shared_in,
+    )
     last = shared_part
-    shared_far = swap(shared_part, "dp", 2)
-    first("near")
-    second("own")
-    for g in far_groups[:1]:
-        first(g)
-    shared = pl.pallas_call(
-        shared_second_kernel,
-        in_specs=[SMEM, VMEM, VMEM, VMEM, VMEM, ANY],
-        out_specs=VMEM,
-        out_shape=jax.ShapeDtypeStruct((2 * rows, half), F32),
-        cost_estimate=cost(KERNEL_FLOPS, 2 * half * hidden),
-        compiler_params=granted(),
-        name="shared_second",
-    )(place, shared_part, shared_far, shared_out, other_shared_out, last)
+    shared_far = cross(shared_part)
+    first("n")
+    second("o")
+    for g in far[:1]:
+        first(str(g))
+    (shared,) = kernel(
+        shared_second_kernel, last,
+        [jax.ShapeDtypeStruct((2 * rows, half), F32)],
+        place, shared_part, shared_far, shared_out, other_shared_out,
+    )
     last = shared
-    second("near")
-    for g in far_groups[1:]:
-        first(g)
-    first("late")
-    first("twin")
-    for g in far_groups + ["late", "twin"]:
+    second("n")
+    for g in far[1:]:
+        first(str(g))
+    first("l")
+    first("t")
+    for g in [*map(str, far), "l", "t"]:
         second(g)
 
-    sums += [shared, kept["own"]]
-    total = sum(sums[1:], sums[0])
-    cross = swap(total[rows:].astype(BF16), "dp", 2).astype(F32)
-    kept = total[:rows]
+    total = sum(sums, shared + kept["o"])
+    crossed = cross(total[rows:].astype(BF16)).astype(F32)
+    stay = total[:rows]
     low = side == 0
-    added = jnp.concatenate([jnp.where(low, kept, cross), jnp.where(low, cross, kept)], axis=1)
+    added = jnp.concatenate([jnp.where(low, stay, crossed), jnp.where(low, crossed, stay)], axis=1)
     return (tokens.astype(F32) + added).astype(BF16)
 
 
 def exchange_fits(mesh, tokens, expert_ids, expert_in):
-    groups, sides = mesh.shape["expert"], mesh.shape["dp"]
-    blocks = mesh.shape["sweep"] * groups
+    groups, sides = mesh.shape[GROUP], mesh.shape[SIDE]
+    blocks = mesh.shape[SWEEP] * groups
     rows, width = tokens.shape[0] // (blocks * sides), tokens.shape[1]
     return (
         sides == 4
@@ -480,16 +469,20 @@
     )
 
 
+def far_groups(groups):
+    return list(range(groups - 1, 1, -1))
+
+
 def solution(mesh):
-    rows = P(("sweep", "expert", "dp"), None)
+    rows = P((SWEEP, GROUP, SIDE), None)
     placed = (
         rows,
         rows,
         rows,
-        P(("sweep", "expert"), "dp", None),
-        P(("sweep", "expert"), None, "dp"),
-        P(("sweep", "dp"), None),
-        P("sweep", "dp"),
+        P((SWEEP, GROUP), SIDE, None),
+        P((SWEEP, GROUP), None, SIDE),
+        P((SWEEP, SIDE), None),
+        P(SWEEP, SIDE),
     )
     spread = functools.partial(
         jax.shard_map, mesh=mesh, in_specs=placed, out_specs=rows, check_vma=False

time: 198 us -> 194 us (0.980)
  Pallas kernels: 57.6 us -> 52.6 us
  waiting for transfers between devices: 104 us -> 107 us
    pallas_call x6, Pallas kernels: 27.8 us -> 22 us  [first_stage(): pl.pallas_call(functools.partial(first_kernel, units, picks, load), in_sp...]
    ppermute x27, waiting for transfers between devices: 104 us -> 107 us  [swap(): lax.ppermute(value, axis, [(i, i ^ mask) for i in range(lax.axis_size(axi...]
    pallas_call x4 -> x5, Pallas kernels: 8.82 us -> 9.6 us  [the longest x2 5.85 us: give_stage(): pl.pallas_call(give_kernel, in_specs=[SMEM, HBM, ANY], out_specs=VMEM, ou...]
  transfers between devices with their start and end apart: 27 -> 27, of which waited for: 12 -> 12; matrix products, arithmetic and copies ran while one was open for 0% -> 0% of each run, Pallas kernels for 24% -> 22%
where the time goes in v4:
time: 194 us
  waiting for transfers between devices  107 us (55%)
  Pallas kernels  52.6 us (27%)
  starting transfers between devices  31.5 us (16%)
    ppermute x27, waiting for transfers between devices, swap(): lax.ppermute(value, axis, [(i, i ^ mask) for i in range(lax.axis_size(axi...  107 us
    ppermute x27, starting transfers between devices, swap(): lax.ppermute(value, axis, [(i, i ^ mask) for i in range(lax.axis_size(axi...  31.5 us
    pallas_call x6, Pallas kernels, first_stage(): pl.pallas_call(functools.partial(first_kernel, units, picks, load), in_sp...  22 us
    pallas_call x6, Pallas kernels, second_stage(): pl.pallas_call(functools.partial(second_kernel, units, keep, send, load),...  21 us
    pallas_call x2, Pallas kernels, give_stage(): pl.pallas_call(give_kernel, in_specs=[SMEM, HBM, ANY], out_specs=VMEM, ou...  5.85 us
  transfers between devices with their start and end apart: 27, of which 12 were waited for; matrix products, arithmetic and copies ran while one was open for 0% of the time, Pallas kernels for 22%

profile of v4, /device:TPU:0, one launch (start us, length us, event | category | flops | bytes accessed | tf_op | source)
XLA Modules:
  0.0 193.5 jit_solution(17721287062914956404)
XLA Ops:
  0.1 2.9 %shard_map.73._ = bf16[8,384,768]{2,1,0:T(8,128)(2,1)S(1)} custom-call(s32[3]{0:T(128)S(1)} %pad_add_fusion.place.after, bf16[16,384,768]{2,1,0:T(8,128)(2,1)} %refs_1_.1, s32[3]{0:T(128)S(1)} %pad_add_fusion.place.after), custom_call_target="tpu_custom_call" | custom-call | flops 10000000 | bytes 9437184 | tf_op jit(solution)/shard_map/pallas_call | solution.py:319
  4.4 2.9 %shard_map.75.refs_3_ = bf16[8,768,384]{2,1,0:T(8,128)(2,1)S(1)} custom-call(s32[3]{0:T(128)S(1)} %pad_add_fusion.place.after, bf16[16,768,384]{2,1,0:T(8,128)(2,1)} %refs_4_.1, bf16[144,768]{1,0:T(8,128)(2,1)S(1)} %get-tuple-element.32.after), custom_call_target="tpu_custom_call" | custom-call | flops 10000000 | bytes 9437184 | tf_op jit(solution)/shard_map/pallas_call | solution.py:319
  7.5 2.9 %collective-permute-start = (bf16[144,768]{1,0:T(8,128)(2,1)S(1)}, bf16[144,768]{1,0:T(8,128)(2,1)S(1)}, u32[]{:S(2)}, u32[]{:S(2)}) collective-permute-start(bf16[144,768]{1,0:T(8,128)(2,1)S(1)} %get-tuple-element.33), channel_id=1, source_target_pairs={{0,2},{1,3},{2,0},{3,1},{4,6},{5,7},{6,4},{7,5},{8,10},{9,11},{10,... | collective-permute-start | bytes 663560 | tf_op jit(solution)/shard_map/ppermute | solution.py:355
  10.5 5.6 %collective-permute-done = bf16[144,768]{1,0:T(8,128)(2,1)S(1)} collective-permute-done((bf16[144,768]{1,0:T(8,128)(2,1)S(1)}, bf16[144,768]{1,0:T(8,128)(2,1)S(1)}, u32[]{:S(2)}, u32[]{:S(2)}) %collective-permute-start) | collective-permute-done | bytes 221216 | tf_op jit(solution)/shard_map/ppermute | solution.py:355
  16.2 3.9 %collective-permute-start.5 = (bf16[288,768]{1,0:T(8,128)(2,1)S(1)}, bf16[288,768]{1,0:T(8,128)(2,1)}, u32[]{:S(2)}, u32[]{:S(2)}) collective-permute-start(bf16[288,768]{1,0:T(8,128)(2,1)S(1)} %pad_maximum_fusion.refs_0_.feed), channel_id=1, source_target_pairs={{0,12},{4,8},{8,4},{12,0},{1,13},{5,9},{9,5},{13,1},{2,14},{6,10},... | collective-permute-start | bytes 1327112 | tf_op jit(solution)/shard_map/ppermute | solution.py:355
  20.1 4.9 %shard_map.76 = (bf16[8,40,768]{2,1,0:T(8,128)(2,1)S(1)}, f32[8,256]{1,0:T(8,128)S(1)}, f32[8,256]{1,0:T(8,128)S(1)}, bf16[8,384,768]{2,1,0:T(8,128)(2,1)S(1)}) custom-call(s32[3]{0:T(128)S(1)} %pad_add_fusion.place.after, bf16[288,768]{1,0:T(8,128)(2,1)S(1)} %pad_maximum_fusion.refs_0_.feed, bf16[16,384,768]{2,1,0:T(8,128)(2,1)} %refs_1_.1, ...), custom_call_target="tpu_custom_call" | custom-call | flops 10000000 | bytes 9437184 | tf_op jit(solution)/shard_map/pallas_call | solution.py:253
  25.0 1.6 collective-permute-start.7
  26.6 4.7 %collective-permute-done.5.refs_0_ = bf16[288,768]{1,0:T(8,128)(2,1)} collective-permute-done((bf16[288,768]{1,0:T(8,128)(2,1)S(1)}, bf16[288,768]{1,0:T(8,128)(2,1)}, u32[]{:S(2)}, u32[]{:S(2)}) %collective-permute-start.5) | collective-permute-done | bytes 442400 | tf_op jit(solution)/shard_map/ppermute | solution.py:355
  31.3 7.7 %collective-permute-start.13 = (bf16[288,768]{1,0:T(8,128)(2,1)}, bf16[288,768]{1,0:T(8,128)(2,1)S(1)}, u32[]{:S(2)}, u32[]{:S(2)}) collective-permute-start(bf16[288,768]{1,0:T(8,128)(2,1)} %collective-permute-done.5.refs_0_), channel_id=1, source_target_pairs={{0,4},{4,0},{8,12},{12,8},{1,5},{5,1},{9,13},{13,9},{2,6},{6,2},{1... | collective-permute-start | bytes 1327112 | tf_op jit(solution)/shard_map/ppermute | solution.py:355
  40.4 3.1 %shard_map.78 = (bf16[8,40,768]{2,1,0:T(8,128)(2,1)S(1)}, f32[8,256]{1,0:T(8,128)S(1)}, f32[8,256]{1,0:T(8,128)S(1)}) custom-call(s32[3]{0:T(128)S(1)} %pad_add_fusion.place.after, bf16[288,768]{1,0:T(8,128)(2,1)S(1)} %collective-permute-done.9.refs_0_, bf16[8,384,768]{2,1,0:T(8,128)(2,1)S(1)} %get-tuple-element.35.refs_1_.refs_2_, ...), custom_call_target="tpu_custom_call" | custom-call | flops 10000000 | bytes 9437184 | tf_op jit(solution)/shard_map/pallas_call | solution.py:253
  44.3 4.9 %shard_map.79 = (f32[256,768]{1,0:T(8,128)S(1)}, bf16[8,768,384]{2,1,0:T(8,128)(2,1)S(1)}) custom-call(s32[3]{0:T(128)S(1)} %pad_add_fusion.place.after, f32[8,256]{1,0:T(8,128)S(1)} %get-tuple-element.34._.refs_0_, f32[8,256]{1,0:T(8,128)S(1)} %get-tuple-element.36.refs_1_, bf16[8,40,768]{2,1,0:T(8,128)(2,1)S(1)} %get-tuple-element.37.refs_2_, ...), custom_call_target="tpu_custom_call" | custom-call | flops 10000000 | bytes 9437184 | tf_op jit(solution)/shard_map/pallas_call | solution.py:278
  49.3 4.3 %shard_map.80 = (bf16[8,80,768]{2,1,0:T(8,128)(2,1)S(1)}, f32[8,512]{1,0:T(8,128)S(1)}, f32[8,512]{1,0:T(8,128)S(1)}) custom-call(s32[3]{0:T(128)S(1)} %pad_add_fusion.place.after, bf16[288,768]{1,0:T(8,128)(2,1)} %collective-permute-done.5.refs_0_, bf16[288,768]{1,0:T(8,128)(2,1)} %collective-permute-done.6.refs_1_, ...), custom_call_target="tpu_custom_call" | custom-call | flops 10000000 | bytes 9437184 | tf_op jit(solution)/shard_map/pallas_call | solution.py:253
  57.7 29.0 %collective-permute-done.3.far = bf16[256,768]{1,0:T(8,128)(2,1)S(1)} collective-permute-done((bf16[256,768]{1,0:T(8,128)(2,1)S(1)}, bf16[256,768]{1,0:T(8,128)(2,1)S(1)}, u32[]{:S(2)}, u32[]{:S(2)}) %collective-permute-start.3) | collective-permute-done | bytes 393248 | tf_op jit(solution)/shard_map/ppermute | solution.py:355
  86.7 1.8 shard_map.81.refs_6_
  88.5 8.2 %collective-permute-done.15.refs_3_ = bf16[8,40,768]{2,1,0:T(8,128)(2,1)S(1)} collective-permute-done((bf16[8,40,768]{2,1,0:T(8,128)(2,1)S(1)}, bf16[8,40,768]{2,1,0:T(8,128)(2,1)S(1)}, u32[]{:S(2)}, u32[]{:S(2)}) %collective-permute-start.15) | collective-permute-done | bytes 491552 | tf_op jit(solution)/shard_map/ppermute | solution.py:355
  96.7 2.9 %shard_map.82.refs_4_ = f32[256,768]{1,0:T(8,128)S(1)} custom-call(s32[3]{0:T(128)S(1)} %pad_add_fusion.place.after, f32[8,256]{1,0:T(8,128)S(1)} %get-tuple-element.38.refs_6_.refs_0_, f32[8,256]{1,0:T(8,128)S(1)} %get-tuple-element.44.refs_1_, bf16[8,40,768]{2,1,0:T(8,128)(2,1)S(1)} %copy-done.5, bf16[8,40,768]{2,1,0:T(8,128)(2,1)S(1)} %collective-permute-done.15.refs_3_, ...), custom_call_target="tpu_custom_call" | custom-call | flops 10000000 | bytes 9437184 | tf_op jit(solution)/shard_map/pallas_call | solution.py:278
  99.6 3.6 %shard_map.83 = (bf16[8,80,768]{2,1,0:T(8,128)(2,1)S(1)}, f32[8,512]{1,0:T(8,128)S(1)}, f32[8,512]{1,0:T(8,128)S(1)}) custom-call(s32[3]{0:T(128)S(1)} %pad_add_fusion.place.after, bf16[288,768]{1,0:T(8,128)(2,1)S(1)} %collective-permute-done.13.refs_0_, bf16[288,768]{1,0:T(8,128)(2,1)S(1)} %collective-permute-done.14.refs_1_, ...), custom_call_target="tpu_custom_call" | custom-call | flops 10000000 | bytes 9437184 | tf_op jit(solution)/shard_map/pallas_call | solution.py:253
  104.8 3.1 %shard_map.84 = (bf16[8,40,768]{2,1,0:T(8,128)(2,1)S(1)}, f32[8,256]{1,0:T(8,128)S(1)}, f32[8,256]{1,0:T(8,128)S(1)}) custom-call(s32[3]{0:T(128)S(1)} %pad_add_fusion.place.after, bf16[288,768]{1,0:T(8,128)(2,1)S(1)} %collective-permute-done.12.refs_0_, bf16[8,384,768]{2,1,0:T(8,128)(2,1)S(1)} %get-tuple-element.35.refs_1_.refs_2_, ...), custom_call_target="tpu_custom_call" | custom-call | flops 10000000 | bytes 9437184 | tf_op jit(solution)/shard_map/pallas_call | solution.py:253
  107.9 3.1 %shard_map.85 = (bf16[8,40,768]{2,1,0:T(8,128)(2,1)S(1)}, f32[8,256]{1,0:T(8,128)S(1)}, f32[8,256]{1,0:T(8,128)S(1)}) custom-call(s32[3]{0:T(128)S(1)} %pad_add_fusion.place.after, bf16[288,768]{1,0:T(8,128)(2,1)S(1)} %collective-permute-done.11.refs_0_, bf16[8,384,768]{2,1,0:T(8,128)(2,1)S(1)} %get-tuple-element.35.refs_1_.refs_2_, ...), custom_call_target="tpu_custom_call" | custom-call | flops 10000000 | bytes 9437184 | tf_op jit(solution)/shard_map/pallas_call | solution.py:253
  111.0 3.7 %shard_map.86 = (f32[256,768]{1,0:T(8,128)S(1)}, bf16[256,768]{1,0:T(8,128)(2,1)S(1)}) custom-call(s32[3]{0:T(128)S(1)} %pad_add_fusion.place.after, f32[8,512]{1,0:T(8,128)S(1)} %get-tuple-element.40._.refs_0_, f32[8,512]{1,0:T(8,128)S(1)} %get-tuple-element.41.refs_1_, bf16[8,80,768]{2,1,0:T(8,128)(2,1)S(1)} %get-tuple-element.42.refs_2_, ...), custom_call_target="tpu_custom_call" | custom-call | flops 10000000 | bytes 9437184 | tf_op jit(solution)/shard_map/pallas_call | solution.py:278
  114.7 1.7 collective-permute-done.16
  116.5 10.0 %collective-permute-done.18.refs_3_ = bf16[8,80,768]{2,1,0:T(8,128)(2,1)S(1)} collective-permute-done((bf16[8,80,768]{2,1,0:T(8,128)(2,1)S(1)}, bf16[8,80,768]{2,1,0:T(8,128)(2,1)S(1)}, u32[]{:S(2)}, u32[]{:S(2)}) %collective-permute-start.18) | collective-permute-done | bytes 983072 | tf_op jit(solution)/shard_map/ppermute | solution.py:355
  126.5 3.6 %shard_map.87 = (f32[256,768]{1,0:T(8,128)S(1)}, bf16[256,768]{1,0:T(8,128)(2,1)S(1)}) custom-call(s32[3]{0:T(128)S(1)} %pad_add_fusion.place.after, f32[8,512]{1,0:T(8,128)S(1)} %get-tuple-element.46.refs_3_.refs_0_, f32[8,512]{1,0:T(8,128)S(1)} %get-tuple-element.51.refs_1_, bf16[8,80,768]{2,1,0:T(8,128)(2,1)S(1)} %get-tuple-element.52.refs_2_, ...), custom_call_target="tpu_custom_call" | custom-call | flops 10000000 | bytes 9437184 | tf_op jit(solution)/shard_map/pallas_call | solution.py:278
  130.2 1.6 collective-permute-start.21
  132.0 11.8 %collective-permute-done.21.refs_3_ = bf16[8,40,768]{2,1,0:T(8,128)(2,1)S(1)} collective-permute-done((bf16[8,40,768]{2,1,0:T(8,128)(2,1)S(1)}, bf16[8,40,768]{2,1,0:T(8,128)(2,1)S(1)}, u32[]{:S(2)}, u32[]{:S(2)}) %collective-permute-start.21) | collective-permute-done | bytes 491552 | tf_op jit(solution)/shard_map/ppermute | solution.py:355
  143.8 2.9 %shard_map.88 = bf16[256,768]{1,0:T(8,128)(2,1)S(1)} custom-call(s32[3]{0:T(128)S(1)} %pad_add_fusion.place.after, f32[8,256]{1,0:T(8,128)S(1)} %get-tuple-element.47.refs_3_.refs_0_, f32[8,256]{1,0:T(8,128)S(1)} %get-tuple-element.55.refs_1_, bf16[8,40,768]{2,1,0:T(8,128)(2,1)S(1)} %get-tuple-element.56.refs_2_, ...), custom_call_target="tpu_custom_call" | custom-call | flops 10000000 | bytes 9437184 | tf_op jit(solution)/shard_map/pallas_call | solution.py:278
  148.4 3.2 %collective-permute-start.17 = (bf16[256,768]{1,0:T(8,128)(2,1)S(1)}, bf16[256,768]{1,0:T(8,128)(2,1)S(1)}, u32[]{:S(2)}, u32[]{:S(2)}) collective-permute-start(bf16[256,768]{1,0:T(8,128)(2,1)S(1)} %add_convert_fusion.2.refs_6_), channel_id=1, source_target_pairs={{0,12},{4,8},{8,4},{12,0},{1,13},{5,9},{9,5},{13,1},{2,14},{6,10},... | collective-permute-start | bytes 1179656 | tf_op jit(solution)/shard_map/ppermute | solution.py:355
  151.7 8.8 %collective-permute-done.24.refs_3_ = bf16[8,40,768]{2,1,0:T(8,128)(2,1)S(1)} collective-permute-done((bf16[8,40,768]{2,1,0:T(8,128)(2,1)S(1)}, bf16[8,40,768]{2,1,0:T(8,128)(2,1)S(1)}, u32[]{:S(2)}, u32[]{:S(2)}) %collective-permute-start.24) | collective-permute-done | bytes 491552 | tf_op jit(solution)/shard_map/ppermute | solution.py:355
  160.5 2.9 %shard_map.89 = bf16[256,768]{1,0:T(8,128)(2,1)S(1)} custom-call(s32[3]{0:T(128)S(1)} %pad_add_fusion.place.after, f32[8,256]{1,0:T(8,128)S(1)} %get-tuple-element.48.refs_6_.refs_0_, f32[8,256]{1,0:T(8,128)S(1)} %get-tuple-element.57.refs_1_, bf16[8,40,768]{2,1,0:T(8,128)(2,1)S(1)} %get-tuple-element.58.refs_2_, ...), custom_call_target="tpu_custom_call" | custom-call | flops 10000000 | bytes 9437184 | tf_op jit(solution)/shard_map/pallas_call | solution.py:278
  163.5 1.8 collective-permute-start.23
  165.3 20.7 %collective-permute-done.20 = bf16[256,768]{1,0:T(8,128)(2,1)S(1)} collective-permute-done((bf16[256,768]{1,0:T(8,128)(2,1)S(1)}, bf16[256,768]{1,0:T(8,128)(2,1)S(1)}, u32[]{:S(2)}, u32[]{:S(2)}) %collective-permute-start.20) | collective-permute-done | bytes 393248 | tf_op jit(solution)/shard_map/ppermute | solution.py:355
  187.0 5.6 %collective-permute-done.26 = bf16[128,768]{1,0:T(8,128)(2,1)S(1)} collective-permute-done((bf16[128,768]{1,0:T(8,128)(2,1)S(1)}, bf16[128,768]{1,0:T(8,128)(2,1)S(1)}, u32[]{:S(2)}, u32[]{:S(2)}) %collective-permute-start.26) | collective-permute-done | bytes 196640 | tf_op jit(solution)/shard_map/ppermute | solution.py:355
  (72 shorter events, 13.7 us)
Async XLA Ops:
  3.0 17.1 %collective-permute-start.2 = (bf16[8,384,768]{2,1,0:T(8,128)(2,1)S(1)}, bf16[8,384,768]{2,1,0:T(8,128)(2,1)S(1)}, u32[]{:S(2)}, u32[]{:S(2)}) collective-permute-start(bf16[8,384,768]{2,1,0:T(8,128)(2,1)S(1)} %shard_map.73._), channel_id=1, source_target_pairs={{0,1},{1,0},{2,3},{3,2},{4,5},{5,4},{6,7},{7,6},{8,9},{9,8},{10,11... | collective-permute-start | bytes 14155784 | tf_op jit(solution)/shard_map/ppermute | solution.py:355
  4.4 15.7 %copy-start.2 = (bf16[384,768]{1,0:T(8,128)(2,1)S(1)}, bf16[384,768]{1,0:T(8,128)(2,1)}, u32[]{:S(2)}) copy-start(bf16[384,768]{1,0:T(8,128)(2,1)} %own.2) | copy-start | bytes 1769476
  7.4 12.8 %copy-start = (bf16[8,768,384]{2,1,0:T(8,128)(2,1)}, bf16[8,768,384]{2,1,0:T(8,128)(2,1)S(1)}, u32[]{:S(2)}) copy-start(bf16[8,768,384]{2,1,0:T(8,128)(2,1)S(1)} %shard_map.75.refs_3_) | copy-start | bytes 14155780
  7.4 36.9 %collective-permute-start.8 = (bf16[8,768,384]{2,1,0:T(8,128)(2,1)S(1)}, bf16[8,768,384]{2,1,0:T(8,128)(2,1)S(1)}, u32[]{:S(2)}, u32[]{:S(2)}) collective-permute-start(bf16[8,768,384]{2,1,0:T(8,128)(2,1)S(1)} %shard_map.75.refs_3_), channel_id=1, source_target_pairs={{0,1},{1,0},{2,3},{3,2},{4,5},{5,4},{6,7},{7,6},{8,9},{9,8},{10,11... | collective-permute-start | bytes 14155784 | tf_op jit(solution)/shard_map/ppermute | solution.py:355
  7.5 8.6 %collective-permute-start = (bf16[144,768]{1,0:T(8,128)(2,1)S(1)}, bf16[144,768]{1,0:T(8,128)(2,1)S(1)}, u32[]{:S(2)}, u32[]{:S(2)}) collective-permute-start(bf16[144,768]{1,0:T(8,128)(2,1)S(1)} %get-tuple-element.33), channel_id=1, source_target_pairs={{0,2},{1,3},{2,0},{3,1},{4,6},{5,7},{6,4},{7,5},{8,10},{9,11},{10,... | collective-permute-start | bytes 663560 | tf_op jit(solution)/shard_map/ppermute | solution.py:355
  16.2 23.1 %copy-start.3 = (bf16[768,384]{1,0:T(8,128)(2,1)S(1)}, bf16[768,384]{1,0:T(8,128)(2,1)}, u32[]{:S(2)}) copy-start(bf16[768,384]{1,0:T(8,128)(2,1)} %own.3) | copy-start | bytes 1769476
  16.2 15.1 %collective-permute-start.5 = (bf16[288,768]{1,0:T(8,128)(2,1)S(1)}, bf16[288,768]{1,0:T(8,128)(2,1)}, u32[]{:S(2)}, u32[]{:S(2)}) collective-permute-start(bf16[288,768]{1,0:T(8,128)(2,1)S(1)} %pad_maximum_fusion.refs_0_.feed), channel_id=1, source_target_pairs={{0,12},{4,8},{8,4},{12,0},{1,13},{5,9},{9,5},{13,1},{2,14},{6,10},... | collective-permute-start | bytes 1327112 | tf_op jit(solution)/shard_map/ppermute | solution.py:355
  20.1 11.2 %collective-permute-start.1 = (bf16[384,768]{1,0:T(8,128)(2,1)S(1)}, bf16[384,768]{1,0:T(8,128)(2,1)S(1)}, u32[]{:S(2)}, u32[]{:S(2)}) collective-permute-start(bf16[384,768]{1,0:T(8,128)(2,1)S(1)} %copy-done.2), channel_id=1, source_target_pairs={{0,1},{1,0},{2,3},{3,2},{4,5},{5,4},{6,7},{7,6},{8,9},{9,8},{10,11... | collective-permute-start | bytes 1769480 | tf_op jit(solution)/shard_map/ppermute | solution.py:355
  20.1 19.1 %collective-permute-start.9 = (bf16[288,768]{1,0:T(8,128)(2,1)S(1)}, bf16[288,768]{1,0:T(8,128)(2,1)S(1)}, u32[]{:S(2)}, u32[]{:S(2)}) collective-permute-start(bf16[288,768]{1,0:T(8,128)(2,1)S(1)} %pad_maximum_fusion.refs_0_.feed), channel_id=1, source_target_pairs={{0,4},{4,0},{8,12},{12,8},{1,5},{5,1},{9,13},{13,9},{2,6},{6,2},{1... | collective-permute-start | bytes 1327112 | tf_op jit(solution)/shard_map/ppermute | solution.py:355
  25.0 19.3 %collective-permute-start.7 = (bf16[8,40,768]{2,1,0:T(8,128)(2,1)S(1)}, bf16[8,40,768]{2,1,0:T(8,128)(2,1)S(1)}, u32[]{:S(2)}, u32[]{:S(2)}) collective-permute-start(bf16[8,40,768]{2,1,0:T(8,128)(2,1)S(1)} %get-tuple-element.37.refs_2_), channel_id=1, source_target_pairs={{0,2},{1,3},{2,0},{3,1},{4,6},{5,7},{6,4},{7,5},{8,10},{9,11},{10,... | collective-permute-start | bytes 1474568 | tf_op jit(solution)/shard_map/ppermute | solution.py:355
  31.3 18.0 %collective-permute-start.6 = (bf16[288,768]{1,0:T(8,128)(2,1)}, bf16[288,768]{1,0:T(8,128)(2,1)}, u32[]{:S(2)}, u32[]{:S(2)}) collective-permute-start(bf16[288,768]{1,0:T(8,128)(2,1)} %collective-permute-done.5.refs_0_), channel_id=1, source_target_pairs={{0,1},{1,0},{2,3},{3,2},{4,5},{5,4},{6,7},{7,6},{8,9},{9,8},{10,11... | collective-permute-start | bytes 1327112 | tf_op jit(solution)/shard_map/ppermute | solution.py:355
  31.3 25.9 %collective-permute-start.13 = (bf16[288,768]{1,0:T(8,128)(2,1)}, bf16[288,768]{1,0:T(8,128)(2,1)S(1)}, u32[]{:S(2)}, u32[]{:S(2)}) collective-permute-start(bf16[288,768]{1,0:T(8,128)(2,1)} %collective-permute-done.5.refs_0_), channel_id=1, source_target_pairs={{0,4},{4,0},{8,12},{12,8},{1,5},{5,1},{9,13},{13,9},{2,6},{6,2},{1... | collective-permute-start | bytes 1327112 | tf_op jit(solution)/shard_map/ppermute | solution.py:355
  39.2 17.9 %collective-permute-start.4 = (bf16[768,384]{1,0:T(8,128)(2,1)S(1)}, bf16[768,384]{1,0:T(8,128)(2,1)}, u32[]{:S(2)}, u32[]{:S(2)}) collective-permute-start(bf16[768,384]{1,0:T(8,128)(2,1)S(1)} %copy-done.3), channel_id=1, source_target_pairs={{0,1},{1,0},{2,3},{3,2},{4,5},{5,4},{6,7},{7,6},{8,9},{9,8},{10,11... | collective-permute-start | bytes 1769480 | tf_op jit(solution)/shard_map/ppermute | solution.py:355
  49.3 6.4 %copy-start.5 = (bf16[8,40,768]{2,1,0:T(8,128)(2,1)S(1)}, bf16[8,40,768]{2,1,0:T(8,128)(2,1)}, u32[]{:S(2)}) copy-start(bf16[8,40,768]{2,1,0:T(8,128)(2,1)} %copy-done.4) | copy-start | bytes 1474564
  49.3 7.9 %copy-start.7 = (bf16[288,768]{1,0:T(8,128)(2,1)S(1)}, bf16[288,768]{1,0:T(8,128)(2,1)}, u32[]{:S(2)}) copy-start(bf16[288,768]{1,0:T(8,128)(2,1)} %copy-done.6) | copy-start | bytes 1327108
  53.6 57.3 %collective-permute-start.10 = (bf16[8,80,768]{2,1,0:T(8,128)(2,1)S(1)}, bf16[8,80,768]{2,1,0:T(8,128)(2,1)S(1)}, u32[]{:S(2)}, u32[]{:S(2)}) collective-permute-start(bf16[8,80,768]{2,1,0:T(8,128)(2,1)S(1)} %get-tuple-element.42.refs_2_), channel_id=1, source_target_pairs={{0,2},{1,3},{2,0},{3,1},{4,6},{5,7},{6,4},{7,5},{8,10},{9,11},{10,... | collective-permute-start | bytes 2949128 | tf_op jit(solution)/shard_map/ppermute | solution.py:355
  55.1 31.6 %collective-permute-start.3 = (bf16[256,768]{1,0:T(8,128)(2,1)S(1)}, bf16[256,768]{1,0:T(8,128)(2,1)S(1)}, u32[]{:S(2)}, u32[]{:S(2)}) collective-permute-start(bf16[256,768]{1,0:T(8,128)(2,1)S(1)} %shard_map.77.refs_3_.near), channel_id=1, source_target_pairs={{0,2},{1,3},{2,0},{3,1},{4,6},{5,7},{6,4},{7,5},{8,10},{9,11},{10,... | collective-permute-start | bytes 1179656 | tf_op jit(solution)/shard_map/ppermute | solution.py:355
  55.7 41.0 %collective-permute-start.15 = (bf16[8,40,768]{2,1,0:T(8,128)(2,1)S(1)}, bf16[8,40,768]{2,1,0:T(8,128)(2,1)S(1)}, u32[]{:S(2)}, u32[]{:S(2)}) collective-permute-start(bf16[8,40,768]{2,1,0:T(8,128)(2,1)S(1)} %copy-done.5), channel_id=1, source_target_pairs={{0,2},{1,3},{2,0},{3,1},{4,6},{5,7},{6,4},{7,5},{8,10},{9,11},{10,... | collective-permute-start | bytes 1474568 | tf_op jit(solution)/shard_map/ppermute | solution.py:355
  57.2 42.4 %collective-permute-start.14 = (bf16[288,768]{1,0:T(8,128)(2,1)S(1)}, bf16[288,768]{1,0:T(8,128)(2,1)S(1)}, u32[]{:S(2)}, u32[]{:S(2)}) collective-permute-start(bf16[288,768]{1,0:T(8,128)(2,1)S(1)} %collective-permute-done.13.refs_0_), channel_id=1, source_target_pairs={{0,1},{1,0},{2,3},{3,2},{4,5},{5,4},{6,7},{7,6},{8,9},{9,8},{10,11... | collective-permute-start | bytes 1327112 | tf_op jit(solution)/shard_map/ppermute | solution.py:355
  57.2 47.6 %collective-permute-start.12 = (bf16[288,768]{1,0:T(8,128)(2,1)S(1)}, bf16[288,768]{1,0:T(8,128)(2,1)S(1)}, u32[]{:S(2)}, u32[]{:S(2)}) collective-permute-start(bf16[288,768]{1,0:T(8,128)(2,1)S(1)} %copy-done.7), channel_id=1, source_target_pairs={{0,1},{1,0},{2,3},{3,2},{4,5},{5,4},{6,7},{7,6},{8,9},{9,8},{10,11... | collective-permute-start | bytes 1327112 | tf_op jit(solution)/shard_map/ppermute | solution.py:355
  86.7 21.1 %collective-permute-start.11 = (bf16[288,768]{1,0:T(8,128)(2,1)S(1)}, bf16[288,768]{1,0:T(8,128)(2,1)S(1)}, u32[]{:S(2)}, u32[]{:S(2)}) collective-permute-start(bf16[288,768]{1,0:T(8,128)(2,1)S(1)} %pad_maximum_fusion.refs_0_.feed), channel_id=1, source_target_pairs={{0,1},{1,0},{2,3},{3,2},{4,5},{5,4},{6,7},{7,6},{8,9},{9,8},{10,11... | collective-permute-start | bytes 1327112 | tf_op jit(solution)/shard_map/ppermute | solution.py:355
  103.2 23.2 %collective-permute-start.18 = (bf16[8,80,768]{2,1,0:T(8,128)(2,1)S(1)}, bf16[8,80,768]{2,1,0:T(8,128)(2,1)S(1)}, u32[]{:S(2)}, u32[]{:S(2)}) collective-permute-start(bf16[8,80,768]{2,1,0:T(8,128)(2,1)S(1)} %get-tuple-element.52.refs_2_), channel_id=1, source_target_pairs={{0,2},{1,3},{2,0},{3,1},{4,6},{5,7},{6,4},{7,5},{8,10},{9,11},{10,... | collective-permute-start | bytes 2949128 | tf_op jit(solution)/shard_map/ppermute | solution.py:355
  114.6 1.8 collective-permute-start.16
  130.1 1.8 collective-permute-start.19
  130.2 13.6 %collective-permute-start.21 = (bf16[8,40,768]{2,1,0:T(8,128)(2,1)S(1)}, bf16[8,40,768]{2,1,0:T(8,128)(2,1)S(1)}, u32[]{:S(2)}, u32[]{:S(2)}) collective-permute-start(bf16[8,40,768]{2,1,0:T(8,128)(2,1)S(1)} %get-tuple-element.56.refs_2_), channel_id=1, source_target_pairs={{0,2},{1,3},{2,0},{3,1},{4,6},{5,7},{6,4},{7,5},{8,10},{9,11},{10,... | collective-permute-start | bytes 1474568 | tf_op jit(solution)/shard_map/ppermute | solution.py:355
  146.8 4.8 %collective-permute-start.22 = (bf16[256,768]{1,0:T(8,128)(2,1)S(1)}, bf16[256,768]{1,0:T(8,128)(2,1)S(1)}, u32[]{:S(2)}, u32[]{:S(2)}) collective-permute-start(bf16[256,768]{1,0:T(8,128)(2,1)S(1)} %shard_map.88), channel_id=1, source_target_pairs={{0,1},{1,0},{2,3},{3,2},{4,5},{5,4},{6,7},{7,6},{8,9},{9,8},{10,11... | collective-permute-start | bytes 1179656 | tf_op jit(solution)/shard_map/ppermute | solution.py:355
  146.8 13.6 %collective-permute-start.24 = (bf16[8,40,768]{2,1,0:T(8,128)(2,1)S(1)}, bf16[8,40,768]{2,1,0:T(8,128)(2,1)S(1)}, u32[]{:S(2)}, u32[]{:S(2)}) collective-permute-start(bf16[8,40,768]{2,1,0:T(8,128)(2,1)S(1)} %get-tuple-element.58.refs_2_), channel_id=1, source_target_pairs={{0,2},{1,3},{2,0},{3,1},{4,6},{5,7},{6,4},{7,5},{8,10},{9,11},{10,... | collective-permute-start | bytes 1474568 | tf_op jit(solution)/shard_map/ppermute | solution.py:355
  148.4 16.9 %collective-permute-start.17 = (bf16[256,768]{1,0:T(8,128)(2,1)S(1)}, bf16[256,768]{1,0:T(8,128)(2,1)S(1)}, u32[]{:S(2)}, u32[]{:S(2)}) collective-permute-start(bf16[256,768]{1,0:T(8,128)(2,1)S(1)} %add_convert_fusion.2.refs_6_), channel_id=1, source_target_pairs={{0,12},{4,8},{8,4},{12,0},{1,13},{5,9},{9,5},{13,1},{2,14},{6,10},... | collective-permute-start | bytes 1179656 | tf_op jit(solution)/shard_map/ppermute | solution.py:355
  151.6 34.4 %collective-permute-start.20 = (bf16[256,768]{1,0:T(8,128)(2,1)S(1)}, bf16[256,768]{1,0:T(8,128)(2,1)S(1)}, u32[]{:S(2)}, u32[]{:S(2)}) collective-permute-start(bf16[256,768]{1,0:T(8,128)(2,1)S(1)} %add_convert_fusion.1.refs_6_), channel_id=1, source_target_pairs={{0,8},{4,12},{8,0},{12,4},{1,9},{5,13},{9,1},{13,5},{2,10},{6,14},... | collective-permute-start | bytes 1179656 | tf_op jit(solution)/shard_map/ppermute | solution.py:355
  163.4 22.6 %collective-permute-start.25 = (bf16[256,768]{1,0:T(8,128)(2,1)S(1)}, bf16[256,768]{1,0:T(8,128)(2,1)S(1)}, u32[]{:S(2)}, u32[]{:S(2)}) collective-permute-start(bf16[256,768]{1,0:T(8,128)(2,1)S(1)} %shard_map.89), channel_id=1, source_target_pairs={{0,1},{1,0},{2,3},{3,2},{4,5},{5,4},{6,7},{7,6},{8,9},{9,8},{10,11... | collective-permute-start | bytes 1179656 | tf_op jit(solution)/shard_map/ppermute | solution.py:355
  163.5 22.5 %collective-permute-start.23 = (bf16[256,768]{1,0:T(8,128)(2,1)S(1)}, bf16[256,768]{1,0:T(8,128)(2,1)S(1)}, u32[]{:S(2)}, u32[]{:S(2)}) collective-permute-start(bf16[256,768]{1,0:T(8,128)(2,1)S(1)} %add_convert_fusion.refs_6_), channel_id=1, source_target_pairs={{0,4},{4,0},{8,12},{12,8},{1,5},{5,1},{9,13},{13,9},{2,6},{6,2},{1... | collective-permute-start | bytes 1179656 | tf_op jit(solution)/shard_map/ppermute | solution.py:355
  186.4 6.3 %collective-permute-start.26 = (bf16[128,768]{1,0:T(8,128)(2,1)S(1)}, bf16[128,768]{1,0:T(8,128)(2,1)S(1)}, u32[]{:S(2)}, u32[]{:S(2)}) collective-permute-start(bf16[128,768]{1,0:T(8,128)(2,1)S(1)} %slice.32), channel_id=1, source_target_pairs={{0,2},{1,3},{2,0},{3,1},{4,6},{5,7},{6,4},{7,5},{8,10},{9,11},{10,... | collective-permute-start | bytes 589832 | tf_op jit(solution)/shard_map/ppermute | solution.py:355
  (5 other events, 15.6 us)

commit v5 on v4

--- a/solution.py
+++ b/solution.py
@@ -107,9 +107,9 @@
     theirs[rows : rows + META, :] = table
 
 
-def give_kernel(place, source, after, given, came):
-    local = given.shape[0]
-    copies = half_copies(source, given, (1 - place[0]) * local, came)
+def take_kernel(own, place, source, after, taken, came):
+    local = taken.shape[0]
+    copies = half_copies(source, taken, (place[0] if own else 1 - place[0]) * local, came)
     for c in copies:
         c.start()
     for c in copies:
@@ -122,17 +122,12 @@
     return [(wanted == codes[e : e + 1, :]).astype(F32) for e in range(count)]
 
 
-def first_kernel(units, picks, load, place, *refs):
+def first_kernel(units, picks, place, *refs):
     feeds, refs = refs[:units], refs[units:]
-    source, other, _, part, code, gate = refs[:6]
-    own, (packed, *came) = (refs[6], refs[7:]) if load else (source, refs[6:])
+    own, other, _, part, code, gate, packed = refs
     local, rows, half = packed.shape
     slots = rows // (2 * units)
     tokens = feeds[0].shape[0] // 2 - META
-    if load:
-        for c in half_copies(source, own, place[0] * local, came[0]):
-            c.start()
-
     before = (
         lax.broadcasted_iota(jnp.int32, (tokens, tokens), 0)
         < lax.broadcasted_iota(jnp.int32, (tokens, tokens), 1)
@@ -173,11 +168,8 @@
     @pl.loop(0, local // 2)
     def _(pair):
         for e in (2 * pair, 2 * pair + 1):
-            total = dot(packed[e, :, pl.ds(there, quarter)], other[e])
-            if load:
-                base = place[0] * local
-                pltpu.make_async_copy(source.at[base + e], own.at[e], came[0].at[e]).wait()
-            total += dot(packed[e, :, pl.ds(here, quarter)], own[e])
+            total = dot(packed[e, :, pl.ds(here, quarter)], own[e])
+            total += dot(packed[e, :, pl.ds(there, quarter)], other[e])
             part[e] = total.astype(BF16)
 
 
@@ -234,8 +226,7 @@
 ANY = pl.BlockSpec(memory_space=pl.ANY)
 HBM = pl.BlockSpec(memory_space=pltpu.HBM)
 GRANT = 24 << 20
-GIVE_GRANTS = (46 << 20, 42 << 20)
-FIRST_GRANT = 40 << 20
+GIVE_GRANTS = (46 << 20, 42 << 20, 44 << 20)
 SECOND_GRANT = 36 << 20
 
 
@@ -243,7 +234,7 @@
     return pltpu.CompilerParams(vmem_limit_bytes=size)
 
 
-def first_stage(feeds, place, own, other, after, picks, load):
+def first_stage(feeds, place, own, other, after, picks):
     units = len(feeds)
     local, quarter, hidden = other.shape
     half = 2 * quarter
@@ -251,14 +242,12 @@
     rows = 2 * units * CAP
     table = jax.ShapeDtypeStruct((local, 2 * units * tokens), F32)
     return pl.pallas_call(
-        functools.partial(first_kernel, units, picks, load),
-        in_specs=[SMEM] + [VMEM] * units + [HBM if load else VMEM, VMEM, ANY],
-        out_specs=[VMEM] * (3 + load),
-        scratch_shapes=[pltpu.VMEM((local, rows, half), BF16)]
-        + [pltpu.SemaphoreType.DMA((local,))] * load,
-        out_shape=[jax.ShapeDtypeStruct((local, rows, hidden), BF16), table, table]
-        + [jax.ShapeDtypeStruct(other.shape, BF16)] * load,
-        compiler_params=granted(FIRST_GRANT if load else GRANT),
+        functools.partial(first_kernel, units, picks),
+        in_specs=[SMEM] + [VMEM] * (units + 2) + [ANY],
+        out_specs=[VMEM] * 3,
+        scratch_shapes=[pltpu.VMEM((local, rows, half), BF16)],
+        out_shape=[jax.ShapeDtypeStruct((local, rows, hidden), BF16), table, table],
+        compiler_params=granted(),
         cost_estimate=cost(KERNEL_FLOPS, 2 * local * half * hidden),
     )(place, *feeds, own, other, after)
 
@@ -314,10 +303,10 @@
         out[at, pl.ds(there, quarter)] = right[b * rows : (b + 1) * rows]
 
 
-def give_stage(place, source, after, grant):
+def take_stage(place, source, own, after, grant):
     shape = (source.shape[0] // 2, *source.shape[1:])
     return pl.pallas_call(
-        give_kernel,
+        functools.partial(take_kernel, own),
         in_specs=[SMEM, HBM, ANY],
         out_specs=VMEM,
         out_shape=jax.ShapeDtypeStruct(shape, BF16),
@@ -360,7 +349,10 @@
     def share(value):
         return swap(value, SIDE, 1)
 
-    give_in = give_stage(place, expert_in, place, GIVE_GRANTS[0])
+    def take(source, own, after, grant):
+        return take_stage(place, source, own, after, grant)
+
+    give_in = take(expert_in, False, place, GIVE_GRANTS[0])
     other_in = share(give_in)
     block = jax.ShapeDtypeStruct((rows + META, half), BF16)
     mine, theirs = kernel(
@@ -368,11 +360,7 @@
         place, tokens, expert_ids.T, gate_weights.T,
     )
     peer = cross(theirs)
-    give_out = give_stage(place, expert_out, mine, GIVE_GRANTS[1])
-    other_shared_in = share(shared_in)
-    other_out = share(give_out)
-    other_shared_out = share(shared_out)
-
+    own_in = take(expert_in, True, mine, GIVE_GRANTS[1])
     unit = jnp.concatenate([mine[:rows], peer[:rows], mine[rows:], peer[rows:]], axis=0)
     far = far_groups(groups)
     near = swap(unit, GROUP, 1)
@@ -385,18 +373,13 @@
         feeds[str(g)] = [got, share(got)]
 
     firsts, kept, sums = {}, {}, []
-    last, own_in, own_out = give_out, None, None
+    last, own_out = own_in, None
 
     def first(g):
-        nonlocal last, own_in
-        load = own_in is None
-        part, code, gate, *held = first_stage(
-            feeds[g], place, expert_in if load else own_in, other_in, last, picks,
-            load,
-        )
+        nonlocal last
+        part, code, gate = first_stage(feeds[g], place, own_in, other_in, last, picks)
         firsts[g] = (part, code, gate, cross(part))
         last = code
-        own_in = held[0] if load else own_in
 
     def second(g):
         nonlocal last, own_out
@@ -420,6 +403,20 @@
         sums.append(came)
 
     first("o")
+    last = give_out = take(expert_out, False, last, GIVE_GRANTS[2])
+    other_out = share(give_out)
+    other_shared_in = share(shared_in)
+    other_shared_out = share(shared_out)
+    first("n")
+    first("l")
+    second("o")
+    for g in far[:1]:
+        first(str(g))
+    second("n")
+    second("l")
+    for g in far[1:]:
+        first(str(g))
+    first("t")
     (shared_part,) = kernel(
         shared_first_kernel, last,
         [jax.ShapeDtypeStruct((2 * rows, hidden), BF16)],
@@ -427,23 +424,13 @@
     )
     last = shared_part
     shared_far = cross(shared_part)
-    first("n")
-    second("o")
-    for g in far[:1]:
-        first(str(g))
+    for g in [*map(str, far), "t"]:
+        second(g)
     (shared,) = kernel(
         shared_second_kernel, last,
         [jax.ShapeDtypeStruct((2 * rows, half), F32)],
         place, shared_part, shared_far, shared_out, other_shared_out,
     )
-    last = shared
-    second("n")
-    for g in far[1:]:
-        first(str(g))
-    first("l")
-    first("t")
-    for g in [*map(str, far), "l", "t"]:
-        second(g)
 
     total = sum(sums, shared + kept["o"])
     crossed = cross(total[rows:].astype(BF16)).astype(F32)

time: 194 us -> 163 us (0.84)
  waiting for transfers between devices: 107 us -> 78.5 us
  starting transfers between devices: 31.5 us -> 27.8 us
    ppermute x27, waiting for transfers between devices: 107 us -> 78.5 us  [swap(): lax.ppermute(value, axis, [(i, i ^ mask) for i in range(lax.axis_size(axi...]
    ppermute x27, starting transfers between devices: 31.5 us -> 27.8 us  [swap(): lax.ppermute(value, axis, [(i, i ^ mask) for i in range(lax.axis_size(axi...]
    pallas_call x8 -> x9, Pallas kernels: 27.9 us -> 29.5 us  [the longest x6 20.7 us: first_stage(): pl.pallas_call(functools.partial(first_kernel, units, picks), in_specs=[S...]
  transfers between devices with their start and end apart: 27 -> 27, of which waited for: 12 -> 14; matrix products, arithmetic and copies ran while one was open for 0% -> 0% of each run, Pallas kernels for 22% -> 26%
where the time goes in v5:
time: 163 us; the launch traced here: 162 us
  waiting for transfers between devices  78.5 us (48%)
  Pallas kernels  54.1 us (33%)
  starting transfers between devices  27.8 us (17%)
    ppermute x27, waiting for transfers between devices, swap(): lax.ppermute(value, axis, [(i, i ^ mask) for i in range(lax.axis_size(axi...  78.5 us
    ppermute x27, starting transfers between devices, swap(): lax.ppermute(value, axis, [(i, i ^ mask) for i in range(lax.axis_size(axi...  27.8 us
    pallas_call x6, Pallas kernels, second_stage(): pl.pallas_call(functools.partial(second_kernel, units, keep, send, load),...  21.5 us
    pallas_call x6, Pallas kernels, first_stage(): pl.pallas_call(functools.partial(first_kernel, units, picks), in_specs=[S...  20.7 us
    pallas_call x3, Pallas kernels, take_stage(): pl.pallas_call(functools.partial(take_kernel, own), in_specs=[SMEM, HBM,...  8.77 us
  transfers between devices with their start and end apart: 27, of which 14 were waited for; matrix products, arithmetic and copies ran while one was open for 0% of the time, Pallas kernels for 26%

profile of v5, /device:TPU:0, one launch (start us, length us, event | category | flops | bytes accessed | tf_op | source)
XLA Modules:
  0.0 162.4 jit_solution(17138521818633229813)
XLA Ops:
  0.1 2.9 %shard_map.73._ = bf16[8,384,768]{2,1,0:T(8,128)(2,1)S(1)} custom-call(s32[3]{0:T(128)S(1)} %pad_add_fusion.place.after, bf16[16,384,768]{2,1,0:T(8,128)(2,1)} %source.4, s32[3]{0:T(128)S(1)} %pad_add_fusion.place.after), custom_call_target="tpu_custom_call" | custom-call | flops 10000000 | bytes 9437184 | tf_op jit(solution)/shard_map/pallas_call | solution.py:308
  4.4 2.6 %collective-permute-start = (bf16[144,768]{1,0:T(8,128)(2,1)S(1)}, bf16[144,768]{1,0:T(8,128)(2,1)S(1)}, u32[]{:S(2)}, u32[]{:S(2)}) collective-permute-start(bf16[144,768]{1,0:T(8,128)(2,1)S(1)} %get-tuple-element.32), channel_id=1, source_target_pairs={{0,2},{1,3},{2,0},{3,1},{4,6},{5,7},{6,4},{7,5},{8,10},{9,11},{10,... | collective-permute-start | bytes 663560 | tf_op jit(solution)/shard_map/ppermute | solution.py:344
  7.0 2.9 %shard_map.75.refs_1_.refs_3_.refs_2_ = bf16[8,384,768]{2,1,0:T(8,128)(2,1)S(1)} custom-call(s32[3]{0:T(128)S(1)} %pad_add_fusion.place.after, bf16[16,384,768]{2,1,0:T(8,128)(2,1)} %source.4, bf16[144,768]{1,0:T(8,128)(2,1)S(1)} %get-tuple-element.31.after), custom_call_target="tpu_custom_call" | custom-call | flops 10000000 | bytes 9437184 | tf_op jit(solution)/shard_map/pallas_call | solution.py:308
  10.0 3.1 %collective-permute-done = bf16[144,768]{1,0:T(8,128)(2,1)S(1)} collective-permute-done((bf16[144,768]{1,0:T(8,128)(2,1)S(1)}, bf16[144,768]{1,0:T(8,128)(2,1)S(1)}, u32[]{:S(2)}, u32[]{:S(2)}) %collective-permute-start) | collective-permute-done | bytes 221216 | tf_op jit(solution)/shard_map/ppermute | solution.py:344
  13.2 3.1 %shard_map.76 = (bf16[8,40,768]{2,1,0:T(8,128)(2,1)S(1)}, f32[8,256]{1,0:T(8,128)S(1)}, f32[8,256]{1,0:T(8,128)S(1)}) custom-call(s32[3]{0:T(128)S(1)} %pad_add_fusion.place.after, bf16[288,768]{1,0:T(8,128)(2,1)S(1)} %pad_maximum_fusion.refs_0_.feed, bf16[8,384,768]{2,1,0:T(8,128)(2,1)S(1)} %shard_map.75.refs_1_.refs_3_.refs_2_, ...), custom_call_target="tpu_custom_call" | custom-call | flops 10000000 | bytes 9437184 | tf_op jit(solution)/shard_map/pallas_call | solution.py:244
  16.2 2.9 %shard_map.77.refs_3_ = bf16[8,768,384]{2,1,0:T(8,128)(2,1)S(1)} custom-call(s32[3]{0:T(128)S(1)} %pad_add_fusion.place.after, bf16[16,768,384]{2,1,0:T(8,128)(2,1)} %refs_4_.1, f32[8,256]{1,0:T(8,128)S(1)} %get-tuple-element.33.after.refs_0_), custom_call_target="tpu_custom_call" | custom-call | flops 10000000 | bytes 9437184 | tf_op jit(solution)/shard_map/pallas_call | solution.py:308
  19.2 1.9 %collective-permute-start.7 = (bf16[288,768]{1,0:T(8,128)(2,1)S(1)}, bf16[288,768]{1,0:T(8,128)(2,1)S(1)}, u32[]{:S(2)}, u32[]{:S(2)}) collective-permute-start(bf16[288,768]{1,0:T(8,128)(2,1)S(1)} %pad_maximum_fusion.refs_0_.feed), channel_id=1, source_target_pairs={{0,4},{4,0},{8,12},{12,8},{1,5},{5,1},{9,13},{13,9},{2,6},{6,2},{1... | collective-permute-start | bytes 1327112 | tf_op jit(solution)/shard_map/ppermute | solution.py:344
  21.1 10.8 %collective-permute-done.7.refs_0_ = bf16[288,768]{1,0:T(8,128)(2,1)S(1)} collective-permute-done((bf16[288,768]{1,0:T(8,128)(2,1)S(1)}, bf16[288,768]{1,0:T(8,128)(2,1)S(1)}, u32[]{:S(2)}, u32[]{:S(2)}) %collective-permute-start.7) | collective-permute-done | bytes 442400 | tf_op jit(solution)/shard_map/ppermute | solution.py:344
  31.9 3.8 %collective-permute-start.4 = (bf16[288,768]{1,0:T(8,128)(2,1)S(1)}, bf16[288,768]{1,0:T(8,128)(2,1)S(1)}, u32[]{:S(2)}, u32[]{:S(2)}) collective-permute-start(bf16[288,768]{1,0:T(8,128)(2,1)S(1)} %pad_maximum_fusion.refs_0_.feed), channel_id=1, source_target_pairs={{0,12},{4,8},{8,4},{12,0},{1,13},{5,9},{9,5},{13,1},{2,14},{6,10},... | collective-permute-start | bytes 1327112 | tf_op jit(solution)/shard_map/ppermute | solution.py:344
  37.2 3.1 %shard_map.78 = (bf16[8,40,768]{2,1,0:T(8,128)(2,1)S(1)}, f32[8,256]{1,0:T(8,128)S(1)}, f32[8,256]{1,0:T(8,128)S(1)}) custom-call(s32[3]{0:T(128)S(1)} %pad_add_fusion.place.after, bf16[288,768]{1,0:T(8,128)(2,1)S(1)} %collective-permute-done.7.refs_0_, bf16[8,384,768]{2,1,0:T(8,128)(2,1)S(1)} %shard_map.75.refs_1_.refs_3_.refs_2_, ...), custom_call_target="tpu_custom_call" | custom-call | flops 10000000 | bytes 9437184 | tf_op jit(solution)/shard_map/pallas_call | solution.py:244
  40.8 3.8 %shard_map.79 = (bf16[8,40,768]{2,1,0:T(8,128)(2,1)}, f32[8,256]{1,0:T(8,128)S(1)}, f32[8,256]{1,0:T(8,128)S(1)}) custom-call(s32[3]{0:T(128)S(1)} %pad_add_fusion.place.after, bf16[288,768]{1,0:T(8,128)(2,1)S(1)} %collective-permute-done.11.refs_0_, bf16[8,384,768]{2,1,0:T(8,128)(2,1)S(1)} %shard_map.75.refs_1_.refs_3_.refs_2_, ...), custom_call_target="tpu_custom_call" | custom-call | flops 10000000 | bytes 9437184 | tf_op jit(solution)/shard_map/pallas_call | solution.py:244
  46.6 3.2 %collective-permute-done.9.refs_3_ = bf16[8,40,768]{2,1,0:T(8,128)(2,1)S(1)} collective-permute-done((bf16[8,40,768]{2,1,0:T(8,128)(2,1)S(1)}, bf16[8,40,768]{2,1,0:T(8,128)(2,1)S(1)}, u32[]{:S(2)}, u32[]{:S(2)}) %collective-permute-start.9) | collective-permute-done | bytes 491552 | tf_op jit(solution)/shard_map/ppermute | solution.py:344
  49.7 6.0 %collective-permute-start.5 = (bf16[288,768]{1,0:T(8,128)(2,1)S(1)}, bf16[288,768]{1,0:T(8,128)(2,1)}, u32[]{:S(2)}, u32[]{:S(2)}) collective-permute-start(bf16[288,768]{1,0:T(8,128)(2,1)S(1)} %collective-permute-done.4.refs_0_), channel_id=1, source_target_pairs={{0,4},{4,0},{8,12},{12,8},{1,5},{5,1},{9,13},{13,9},{2,6},{6,2},{1... | collective-permute-start | bytes 1327112 | tf_op jit(solution)/shard_map/ppermute | solution.py:344
  55.7 4.9 %shard_map.80 = (f32[256,768]{1,0:T(8,128)S(1)}, bf16[8,768,384]{2,1,0:T(8,128)(2,1)S(1)}) custom-call(s32[3]{0:T(128)S(1)} %pad_add_fusion.place.after, f32[8,256]{1,0:T(8,128)S(1)} %get-tuple-element.33.after.refs_0_, f32[8,256]{1,0:T(8,128)S(1)} %get-tuple-element.37.refs_1_, bf16[8,40,768]{2,1,0:T(8,128)(2,1)S(1)} %get-tuple-element.38.refs_2_, ...), custom_call_target="tpu_custom_call" | custom-call | flops 10000000 | bytes 9437184 | tf_op jit(solution)/shard_map/pallas_call | solution.py:267
  60.6 3.6 %shard_map.81 = (bf16[8,80,768]{2,1,0:T(8,128)(2,1)S(1)}, f32[8,512]{1,0:T(8,128)S(1)}, f32[8,512]{1,0:T(8,128)S(1)}) custom-call(s32[3]{0:T(128)S(1)} %pad_add_fusion.place.after, bf16[288,768]{1,0:T(8,128)(2,1)S(1)} %collective-permute-done.4.refs_0_, bf16[288,768]{1,0:T(8,128)(2,1)S(1)} %collective-permute-done.12.refs_1_, ...), custom_call_target="tpu_custom_call" | custom-call | flops 10000000 | bytes 9437184 | tf_op jit(solution)/shard_map/pallas_call | solution.py:244
  65.7 2.9 %shard_map.82.refs_6_ = f32[256,768]{1,0:T(8,128)S(1)} custom-call(s32[3]{0:T(128)S(1)} %pad_add_fusion.place.after, f32[8,256]{1,0:T(8,128)S(1)} %get-tuple-element.34.refs_3_.refs_0_, f32[8,256]{1,0:T(8,128)S(1)} %get-tuple-element.35.refs_1_, bf16[8,40,768]{2,1,0:T(8,128)(2,1)S(1)} %get-tuple-element.36.refs_2_, ...), custom_call_target="tpu_custom_call" | custom-call | flops 10000000 | bytes 9437184 | tf_op jit(solution)/shard_map/pallas_call | solution.py:267
  68.6 2.3 %collective-permute-done.13.refs_3_ = bf16[8,40,768]{2,1,0:T(8,128)(2,1)} collective-permute-done((bf16[8,40,768]{2,1,0:T(8,128)(2,1)}, bf16[8,40,768]{2,1,0:T(8,128)(2,1)}, u32[]{:S(2)}, u32[]{:S(2)}) %collective-permute-start.13) | collective-permute-done | bytes 491552 | tf_op jit(solution)/shard_map/ppermute | solution.py:344
  70.9 3.6 %shard_map.83 = bf16[256,768]{1,0:T(8,128)(2,1)S(1)} custom-call(s32[3]{0:T(128)S(1)} %pad_add_fusion.place.after, f32[8,256]{1,0:T(8,128)S(1)} %get-tuple-element.39.refs_6_.refs_0_, f32[8,256]{1,0:T(8,128)S(1)} %get-tuple-element.43.refs_1_, bf16[8,40,768]{2,1,0:T(8,128)(2,1)} %get-tuple-element.44.refs_2_, ...), custom_call_target="tpu_custom_call" | custom-call | flops 10000000 | bytes 9437184 | tf_op jit(solution)/shard_map/pallas_call | solution.py:267
  77.0 4.1 %shard_map.84 = (bf16[8,80,768]{2,1,0:T(8,128)(2,1)S(1)}, f32[8,512]{1,0:T(8,128)S(1)}, f32[8,512]{1,0:T(8,128)S(1)}) custom-call(s32[3]{0:T(128)S(1)} %pad_add_fusion.place.after, bf16[288,768]{1,0:T(8,128)(2,1)} %collective-permute-done.5.refs_0_, bf16[288,768]{1,0:T(8,128)(2,1)S(1)} %collective-permute-done.6.refs_1_, ...), custom_call_target="tpu_custom_call" | custom-call | flops 10000000 | bytes 9437184 | tf_op jit(solution)/shard_map/pallas_call | solution.py:244
  81.0 1.6 collective-permute-start.18
  82.6 3.1 %shard_map.85 = (bf16[8,40,768]{2,1,0:T(8,128)(2,1)S(1)}, f32[8,256]{1,0:T(8,128)S(1)}, f32[8,256]{1,0:T(8,128)S(1)}) custom-call(s32[3]{0:T(128)S(1)} %pad_add_fusion.place.after, bf16[288,768]{1,0:T(8,128)(2,1)S(1)} %collective-permute-done.2.refs_0_, bf16[8,384,768]{2,1,0:T(8,128)(2,1)S(1)} %shard_map.75.refs_1_.refs_3_.refs_2_, ...), custom_call_target="tpu_custom_call" | custom-call | flops 10000000 | bytes 9437184 | tf_op jit(solution)/shard_map/pallas_call | solution.py:244
  86.8 5.1 %collective-permute-done.19.refs_3_ = bf16[8,80,768]{2,1,0:T(8,128)(2,1)S(1)} collective-permute-done((bf16[8,80,768]{2,1,0:T(8,128)(2,1)S(1)}, bf16[8,80,768]{2,1,0:T(8,128)(2,1)S(1)}, u32[]{:S(2)}, u32[]{:S(2)}) %collective-permute-start.19) | collective-permute-done | bytes 983072 | tf_op jit(solution)/shard_map/ppermute | solution.py:344
  91.9 3.6 %shard_map.87 = (f32[256,768]{1,0:T(8,128)S(1)}, bf16[256,768]{1,0:T(8,128)(2,1)S(1)}) custom-call(s32[3]{0:T(128)S(1)} %pad_add_fusion.place.after, f32[8,512]{1,0:T(8,128)S(1)} %get-tuple-element.42.refs_6_.refs_0_, f32[8,512]{1,0:T(8,128)S(1)} %get-tuple-element.51.refs_1_, bf16[8,80,768]{2,1,0:T(8,128)(2,1)S(1)} %get-tuple-element.52.refs_2_, ...), custom_call_target="tpu_custom_call" | custom-call | flops 10000000 | bytes 9437184 | tf_op jit(solution)/shard_map/pallas_call | solution.py:267
  95.6 1.7 %collective-permute-done.20 = bf16[256,768]{1,0:T(8,128)(2,1)S(1)} collective-permute-done((bf16[256,768]{1,0:T(8,128)(2,1)S(1)}, bf16[256,768]{1,0:T(8,128)(2,1)S(1)}, u32[]{:S(2)}, u32[]{:S(2)}) %collective-permute-start.20) | collective-permute-done | bytes 393248 | tf_op jit(solution)/shard_map/ppermute | solution.py:344
  97.4 14.8 %collective-permute-done.18.refs_3_ = bf16[8,80,768]{2,1,0:T(8,128)(2,1)S(1)} collective-permute-done((bf16[8,80,768]{2,1,0:T(8,128)(2,1)S(1)}, bf16[8,80,768]{2,1,0:T(8,128)(2,1)S(1)}, u32[]{:S(2)}, u32[]{:S(2)}) %collective-permute-start.18) | collective-permute-done | bytes 983072 | tf_op jit(solution)/shard_map/ppermute | solution.py:344
  112.2 3.6 %shard_map.88 = (f32[256,768]{1,0:T(8,128)S(1)}, bf16[256,768]{1,0:T(8,128)(2,1)S(1)}) custom-call(s32[3]{0:T(128)S(1)} %pad_add_fusion.place.after, f32[8,512]{1,0:T(8,128)S(1)} %get-tuple-element.45.refs_3_.refs_0_, f32[8,512]{1,0:T(8,128)S(1)} %get-tuple-element.49.refs_1_, bf16[8,80,768]{2,1,0:T(8,128)(2,1)S(1)} %get-tuple-element.50.refs_2_, ...), custom_call_target="tpu_custom_call" | custom-call | flops 10000000 | bytes 9437184 | tf_op jit(solution)/shard_map/pallas_call | solution.py:267
  119.4 11.1 %collective-permute-done.17.refs_3_ = bf16[8,40,768]{2,1,0:T(8,128)(2,1)S(1)} collective-permute-done((bf16[8,40,768]{2,1,0:T(8,128)(2,1)S(1)}, bf16[8,40,768]{2,1,0:T(8,128)(2,1)S(1)}, u32[]{:S(2)}, u32[]{:S(2)}) %collective-permute-start.17) | collective-permute-done | bytes 491552 | tf_op jit(solution)/shard_map/ppermute | solution.py:344
  130.5 2.9 %shard_map.89._ = bf16[256,768]{1,0:T(8,128)(2,1)S(1)} custom-call(s32[3]{0:T(128)S(1)} %pad_add_fusion.place.after, f32[8,256]{1,0:T(8,128)S(1)} %get-tuple-element.46._.refs_0_, f32[8,256]{1,0:T(8,128)S(1)} %get-tuple-element.47.refs_1_, bf16[8,40,768]{2,1,0:T(8,128)(2,1)S(1)} %get-tuple-element.48.refs_2_, ...), custom_call_target="tpu_custom_call" | custom-call | flops 10000000 | bytes 9437184 | tf_op jit(solution)/shard_map/pallas_call | solution.py:267
  133.6 4.5 %collective-permute-done.15.far = bf16[256,768]{1,0:T(8,128)(2,1)S(1)} collective-permute-done((bf16[256,768]{1,0:T(8,128)(2,1)S(1)}, bf16[256,768]{1,0:T(8,128)(2,1)S(1)}, u32[]{:S(2)}, u32[]{:S(2)}) %collective-permute-start.15) | collective-permute-done | bytes 393248 | tf_op jit(solution)/shard_map/ppermute | solution.py:344
  139.3 16.1 %collective-permute-done.24 = bf16[256,768]{1,0:T(8,128)(2,1)S(1)} collective-permute-done((bf16[256,768]{1,0:T(8,128)(2,1)S(1)}, bf16[256,768]{1,0:T(8,128)(2,1)S(1)}, u32[]{:S(2)}, u32[]{:S(2)}) %collective-permute-start.24) | collective-permute-done | bytes 393248 | tf_op jit(solution)/shard_map/ppermute | solution.py:344
  155.8 1.6 collective-permute-start.26
  157.4 4.2 %collective-permute-done.26 = bf16[128,768]{1,0:T(8,128)(2,1)S(1)} collective-permute-done((bf16[128,768]{1,0:T(8,128)(2,1)S(1)}, bf16[128,768]{1,0:T(8,128)(2,1)S(1)}, u32[]{:S(2)}, u32[]{:S(2)}) %collective-permute-start.26) | collective-permute-done | bytes 196640 | tf_op jit(solution)/shard_map/ppermute | solution.py:344
  (63 shorter events, 17.1 us)
Async XLA Ops:
  0.1 3.5 %copy-start = (bf16[128,1536]{1,0:T(8,128)(2,1)S(1)}, bf16[128,1536]{1,0:T(8,128)(2,1)}, u32[]{:S(2)}) copy-start(bf16[128,1536]{1,0:T(8,128)(2,1)} %tokens.1) | copy-start | bytes 1179652
  0.1 3.5 %copy-start.3 = (s32[128,8]{0,1:T(8,128)S(1)}, s32[128,8]{0,1:T(8,128)}, u32[]{:S(2)}) copy-start(s32[128,8]{0,1:T(8,128)} %param.8) | copy-start | bytes 12292
  0.1 3.5 %copy-start.4 = (f32[128,8]{0,1:T(8,128)S(1)}, f32[128,8]{0,1:T(8,128)}, u32[]{:S(2)}) copy-start(f32[128,8]{0,1:T(8,128)} %param.9) | copy-start | bytes 12292
  3.0 10.1 %collective-permute-start.3 = (bf16[8,384,768]{2,1,0:T(8,128)(2,1)S(1)}, bf16[8,384,768]{2,1,0:T(8,128)(2,1)S(1)}, u32[]{:S(2)}, u32[]{:S(2)}) collective-permute-start(bf16[8,384,768]{2,1,0:T(8,128)(2,1)S(1)} %shard_map.73._), channel_id=1, source_target_pairs={{0,1},{1,0},{2,3},{3,2},{4,5},{5,4},{6,7},{7,6},{8,9},{9,8},{10,11... | collective-permute-start | bytes 14155784 | tf_op jit(solution)/shard_map/ppermute | solution.py:344
  4.4 8.6 %collective-permute-start = (bf16[144,768]{1,0:T(8,128)(2,1)S(1)}, bf16[144,768]{1,0:T(8,128)(2,1)S(1)}, u32[]{:S(2)}, u32[]{:S(2)}) collective-permute-start(bf16[144,768]{1,0:T(8,128)(2,1)S(1)} %get-tuple-element.32), channel_id=1, source_target_pairs={{0,2},{1,3},{2,0},{3,1},{4,6},{5,7},{6,4},{7,5},{8,10},{9,11},{10,... | collective-permute-start | bytes 663560 | tf_op jit(solution)/shard_map/ppermute | solution.py:344
  19.2 36.6 %collective-permute-start.10 = (bf16[8,768,384]{2,1,0:T(8,128)(2,1)S(1)}, bf16[8,768,384]{2,1,0:T(8,128)(2,1)S(1)}, u32[]{:S(2)}, u32[]{:S(2)}) collective-permute-start(bf16[8,768,384]{2,1,0:T(8,128)(2,1)S(1)} %shard_map.77.refs_3_), channel_id=1, source_target_pairs={{0,1},{1,0},{2,3},{3,2},{4,5},{5,4},{6,7},{7,6},{8,9},{9,8},{10,11... | collective-permute-start | bytes 14155784 | tf_op jit(solution)/shard_map/ppermute | solution.py:344
  19.2 12.7 %collective-permute-start.7 = (bf16[288,768]{1,0:T(8,128)(2,1)S(1)}, bf16[288,768]{1,0:T(8,128)(2,1)S(1)}, u32[]{:S(2)}, u32[]{:S(2)}) collective-permute-start(bf16[288,768]{1,0:T(8,128)(2,1)S(1)} %pad_maximum_fusion.refs_0_.feed), channel_id=1, source_target_pairs={{0,4},{4,0},{8,12},{12,8},{1,5},{5,1},{9,13},{13,9},{2,6},{6,2},{1... | collective-permute-start | bytes 1327112 | tf_op jit(solution)/shard_map/ppermute | solution.py:344
  31.9 8.9 %collective-permute-start.11 = (bf16[288,768]{1,0:T(8,128)(2,1)S(1)}, bf16[288,768]{1,0:T(8,128)(2,1)S(1)}, u32[]{:S(2)}, u32[]{:S(2)}) collective-permute-start(bf16[288,768]{1,0:T(8,128)(2,1)S(1)} %collective-permute-done.7.refs_0_), channel_id=1, source_target_pairs={{0,1},{1,0},{2,3},{3,2},{4,5},{5,4},{6,7},{7,6},{8,9},{9,8},{10,11... | collective-permute-start | bytes 1327112 | tf_op jit(solution)/shard_map/ppermute | solution.py:344
  31.9 14.7 %collective-permute-start.4 = (bf16[288,768]{1,0:T(8,128)(2,1)S(1)}, bf16[288,768]{1,0:T(8,128)(2,1)S(1)}, u32[]{:S(2)}, u32[]{:S(2)}) collective-permute-start(bf16[288,768]{1,0:T(8,128)(2,1)S(1)} %pad_maximum_fusion.refs_0_.feed), channel_id=1, source_target_pairs={{0,12},{4,8},{8,4},{12,0},{1,13},{5,9},{9,5},{13,1},{2,14},{6,10},... | collective-permute-start | bytes 1327112 | tf_op jit(solution)/shard_map/ppermute | solution.py:344
  35.7 14.1 %collective-permute-start.9 = (bf16[8,40,768]{2,1,0:T(8,128)(2,1)S(1)}, bf16[8,40,768]{2,1,0:T(8,128)(2,1)S(1)}, u32[]{:S(2)}, u32[]{:S(2)}) collective-permute-start(bf16[8,40,768]{2,1,0:T(8,128)(2,1)S(1)} %get-tuple-element.38.refs_2_), channel_id=1, source_target_pairs={{0,2},{1,3},{2,0},{3,1},{4,6},{5,7},{6,4},{7,5},{8,10},{9,11},{10,... | collective-permute-start | bytes 1474568 | tf_op jit(solution)/shard_map/ppermute | solution.py:344
  40.2 25.5 %collective-permute-start.8 = (bf16[8,40,768]{2,1,0:T(8,128)(2,1)S(1)}, bf16[8,40,768]{2,1,0:T(8,128)(2,1)S(1)}, u32[]{:S(2)}, u32[]{:S(2)}) collective-permute-start(bf16[8,40,768]{2,1,0:T(8,128)(2,1)S(1)} %get-tuple-element.36.refs_2_), channel_id=1, source_target_pairs={{0,2},{1,3},{2,0},{3,1},{4,6},{5,7},{6,4},{7,5},{8,10},{9,11},{10,... | collective-permute-start | bytes 1474568 | tf_op jit(solution)/shard_map/ppermute | solution.py:344
  44.7 26.3 %collective-permute-start.13 = (bf16[8,40,768]{2,1,0:T(8,128)(2,1)}, bf16[8,40,768]{2,1,0:T(8,128)(2,1)}, u32[]{:S(2)}, u32[]{:S(2)}) collective-permute-start(bf16[8,40,768]{2,1,0:T(8,128)(2,1)} %get-tuple-element.44.refs_2_), channel_id=1, source_target_pairs={{0,2},{1,3},{2,0},{3,1},{4,6},{5,7},{6,4},{7,5},{8,10},{9,11},{10,... | collective-permute-start | bytes 1474568 | tf_op jit(solution)/shard_map/ppermute | solution.py:344
  46.6 14.0 %collective-permute-start.12 = (bf16[288,768]{1,0:T(8,128)(2,1)S(1)}, bf16[288,768]{1,0:T(8,128)(2,1)S(1)}, u32[]{:S(2)}, u32[]{:S(2)}) collective-permute-start(bf16[288,768]{1,0:T(8,128)(2,1)S(1)} %collective-permute-done.4.refs_0_), channel_id=1, source_target_pairs={{0,1},{1,0},{2,3},{3,2},{4,5},{5,4},{6,7},{7,6},{8,9},{9,8},{10,11... | collective-permute-start | bytes 1327112 | tf_op jit(solution)/shard_map/ppermute | solution.py:344
  49.7 24.9 %collective-permute-start.5 = (bf16[288,768]{1,0:T(8,128)(2,1)S(1)}, bf16[288,768]{1,0:T(8,128)(2,1)}, u32[]{:S(2)}, u32[]{:S(2)}) collective-permute-start(bf16[288,768]{1,0:T(8,128)(2,1)S(1)} %collective-permute-done.4.refs_0_), channel_id=1, source_target_pairs={{0,4},{4,0},{8,12},{12,8},{1,5},{5,1},{9,13},{13,9},{2,6},{6,2},{1... | collective-permute-start | bytes 1327112 | tf_op jit(solution)/shard_map/ppermute | solution.py:344
  64.2 27.7 %collective-permute-start.19 = (bf16[8,80,768]{2,1,0:T(8,128)(2,1)S(1)}, bf16[8,80,768]{2,1,0:T(8,128)(2,1)S(1)}, u32[]{:S(2)}, u32[]{:S(2)}) collective-permute-start(bf16[8,80,768]{2,1,0:T(8,128)(2,1)S(1)} %get-tuple-element.52.refs_2_), channel_id=1, source_target_pairs={{0,2},{1,3},{2,0},{3,1},{4,6},{5,7},{6,4},{7,5},{8,10},{9,11},{10,... | collective-permute-start | bytes 2949128 | tf_op jit(solution)/shard_map/ppermute | solution.py:344
  70.9 4.2 %copy-start.1 = (bf16[384,768]{1,0:T(8,128)(2,1)S(1)}, bf16[384,768]{1,0:T(8,128)(2,1)}, u32[]{:S(2)}) copy-start(bf16[384,768]{1,0:T(8,128)(2,1)} %own.2) | copy-start | bytes 1769476
  74.5 1.8 %collective-permute-start.14 = (bf16[256,768]{1,0:T(8,128)(2,1)S(1)}, bf16[256,768]{1,0:T(8,128)(2,1)S(1)}, u32[]{:S(2)}, u32[]{:S(2)}) collective-permute-start(bf16[256,768]{1,0:T(8,128)(2,1)S(1)} %shard_map.83), channel_id=1, source_target_pairs={{0,1},{1,0},{2,3},{3,2},{4,5},{5,4},{6,7},{7,6},{8,9},{9,8},{10,11... | collective-permute-start | bytes 1179656 | tf_op jit(solution)/shard_map/ppermute | solution.py:344
  74.6 2.3 %collective-permute-start.6 = (bf16[288,768]{1,0:T(8,128)(2,1)}, bf16[288,768]{1,0:T(8,128)(2,1)S(1)}, u32[]{:S(2)}, u32[]{:S(2)}) collective-permute-start(bf16[288,768]{1,0:T(8,128)(2,1)} %collective-permute-done.5.refs_0_), channel_id=1, source_target_pairs={{0,1},{1,0},{2,3},{3,2},{4,5},{5,4},{6,7},{7,6},{8,9},{9,8},{10,11... | collective-permute-start | bytes 1327112 | tf_op jit(solution)/shard_map/ppermute | solution.py:344
  75.1 10.5 %collective-permute-start.1 = (bf16[384,768]{1,0:T(8,128)(2,1)S(1)}, bf16[384,768]{1,0:T(8,128)(2,1)S(1)}, u32[]{:S(2)}, u32[]{:S(2)}) collective-permute-start(bf16[384,768]{1,0:T(8,128)(2,1)S(1)} %copy-done.1), channel_id=1, source_target_pairs={{0,1},{1,0},{2,3},{3,2},{4,5},{5,4},{6,7},{7,6},{8,9},{9,8},{10,11... | collective-permute-start | bytes 1769480 | tf_op jit(solution)/shard_map/ppermute | solution.py:344
  75.2 7.4 %collective-permute-start.2 = (bf16[288,768]{1,0:T(8,128)(2,1)S(1)}, bf16[288,768]{1,0:T(8,128)(2,1)S(1)}, u32[]{:S(2)}, u32[]{:S(2)}) collective-permute-start(bf16[288,768]{1,0:T(8,128)(2,1)S(1)} %pad_maximum_fusion.refs_0_.feed), channel_id=1, source_target_pairs={{0,1},{1,0},{2,3},{3,2},{4,5},{5,4},{6,7},{7,6},{8,9},{9,8},{10,11... | collective-permute-start | bytes 1327112 | tf_op jit(solution)/shard_map/ppermute | solution.py:344
  81.0 31.2 %collective-permute-start.18 = (bf16[8,80,768]{2,1,0:T(8,128)(2,1)S(1)}, bf16[8,80,768]{2,1,0:T(8,128)(2,1)S(1)}, u32[]{:S(2)}, u32[]{:S(2)}) collective-permute-start(bf16[8,80,768]{2,1,0:T(8,128)(2,1)S(1)} %get-tuple-element.50.refs_2_), channel_id=1, source_target_pairs={{0,2},{1,3},{2,0},{3,1},{4,6},{5,7},{6,4},{7,5},{8,10},{9,11},{10,... | collective-permute-start | bytes 2949128 | tf_op jit(solution)/shard_map/ppermute | solution.py:344
  95.5 1.8 %collective-permute-start.20 = (bf16[256,768]{1,0:T(8,128)(2,1)S(1)}, bf16[256,768]{1,0:T(8,128)(2,1)S(1)}, u32[]{:S(2)}, u32[]{:S(2)}) collective-permute-start(bf16[256,768]{1,0:T(8,128)(2,1)S(1)} %get-tuple-element.54), channel_id=1, source_target_pairs={{0,1},{1,0},{2,3},{3,2},{4,5},{5,4},{6,7},{7,6},{8,9},{9,8},{10,11... | collective-permute-start | bytes 1179656 | tf_op jit(solution)/shard_map/ppermute | solution.py:344
  112.2 3.7 %copy-start.2 = (bf16[768,384]{1,0:T(8,128)(2,1)S(1)}, bf16[768,384]{1,0:T(8,128)(2,1)}, u32[]{:S(2)}) copy-start(bf16[768,384]{1,0:T(8,128)(2,1)} %own.3) | copy-start | bytes 1769476
  115.8 2.6 %collective-permute-start.21 = (bf16[256,768]{1,0:T(8,128)(2,1)S(1)}, bf16[256,768]{1,0:T(8,128)(2,1)S(1)}, u32[]{:S(2)}, u32[]{:S(2)}) collective-permute-start(bf16[256,768]{1,0:T(8,128)(2,1)S(1)} %get-tuple-element.56), channel_id=1, source_target_pairs={{0,1},{1,0},{2,3},{3,2},{4,5},{5,4},{6,7},{7,6},{8,9},{9,8},{10,11... | collective-permute-start | bytes 1179656 | tf_op jit(solution)/shard_map/ppermute | solution.py:344
  115.9 17.6 %collective-permute-start.16 = (bf16[768,384]{1,0:T(8,128)(2,1)S(1)}, bf16[768,384]{1,0:T(8,128)(2,1)S(1)}, u32[]{:S(2)}, u32[]{:S(2)}) collective-permute-start(bf16[768,384]{1,0:T(8,128)(2,1)S(1)} %copy-done.2), channel_id=1, source_target_pairs={{0,1},{1,0},{2,3},{3,2},{4,5},{5,4},{6,7},{7,6},{8,9},{9,8},{10,11... | collective-permute-start | bytes 1769480 | tf_op jit(solution)/shard_map/ppermute | solution.py:344
  116.4 14.1 %collective-permute-start.17 = (bf16[8,40,768]{2,1,0:T(8,128)(2,1)S(1)}, bf16[8,40,768]{2,1,0:T(8,128)(2,1)S(1)}, u32[]{:S(2)}, u32[]{:S(2)}) collective-permute-start(bf16[8,40,768]{2,1,0:T(8,128)(2,1)S(1)} %get-tuple-element.48.refs_2_), channel_id=1, source_target_pairs={{0,2},{1,3},{2,0},{3,1},{4,6},{5,7},{6,4},{7,5},{8,10},{9,11},{10,... | collective-permute-start | bytes 1474568 | tf_op jit(solution)/shard_map/ppermute | solution.py:344
  117.9 20.1 %collective-permute-start.15 = (bf16[256,768]{1,0:T(8,128)(2,1)S(1)}, bf16[256,768]{1,0:T(8,128)(2,1)S(1)}, u32[]{:S(2)}, u32[]{:S(2)}) collective-permute-start(bf16[256,768]{1,0:T(8,128)(2,1)S(1)} %shard_map.86.refs_6_.near), channel_id=1, source_target_pairs={{0,2},{1,3},{2,0},{3,1},{4,6},{5,7},{6,4},{7,5},{8,10},{9,11},{10,... | collective-permute-start | bytes 1179656 | tf_op jit(solution)/shard_map/ppermute | solution.py:344
  118.4 20.9 %collective-permute-start.22 = (bf16[256,768]{1,0:T(8,128)(2,1)S(1)}, bf16[256,768]{1,0:T(8,128)(2,1)S(1)}, u32[]{:S(2)}, u32[]{:S(2)}) collective-permute-start(bf16[256,768]{1,0:T(8,128)(2,1)S(1)} %add_convert_fusion.2.refs_4_), channel_id=1, source_target_pairs={{0,4},{4,0},{8,12},{12,8},{1,5},{5,1},{9,13},{13,9},{2,6},{6,2},{1... | collective-permute-start | bytes 1179656 | tf_op jit(solution)/shard_map/ppermute | solution.py:344
  118.4 20.9 %collective-permute-start.23 = (bf16[256,768]{1,0:T(8,128)(2,1)S(1)}, bf16[256,768]{1,0:T(8,128)(2,1)S(1)}, u32[]{:S(2)}, u32[]{:S(2)}) collective-permute-start(bf16[256,768]{1,0:T(8,128)(2,1)S(1)} %add_convert_fusion.1.refs_6_), channel_id=1, source_target_pairs={{0,12},{4,8},{8,4},{12,0},{1,13},{5,9},{9,5},{13,1},{2,14},{6,10},... | collective-permute-start | bytes 1179656 | tf_op jit(solution)/shard_map/ppermute | solution.py:344
  133.4 5.9 %collective-permute-start.25 = (bf16[256,768]{1,0:T(8,128)(2,1)S(1)}, bf16[256,768]{1,0:T(8,128)(2,1)S(1)}, u32[]{:S(2)}, u32[]{:S(2)}) collective-permute-start(bf16[256,768]{1,0:T(8,128)(2,1)S(1)} %shard_map.89._), channel_id=1, source_target_pairs={{0,1},{1,0},{2,3},{3,2},{4,5},{5,4},{6,7},{7,6},{8,9},{9,8},{10,11... | collective-permute-start | bytes 1179656 | tf_op jit(solution)/shard_map/ppermute | solution.py:344
  133.5 22.0 %collective-permute-start.24 = (bf16[256,768]{1,0:T(8,128)(2,1)S(1)}, bf16[256,768]{1,0:T(8,128)(2,1)S(1)}, u32[]{:S(2)}, u32[]{:S(2)}) collective-permute-start(bf16[256,768]{1,0:T(8,128)(2,1)S(1)} %add_convert_fusion.refs_6_), channel_id=1, source_target_pairs={{0,8},{4,12},{8,0},{12,4},{1,9},{5,13},{9,1},{13,5},{2,10},{6,14},... | collective-permute-start | bytes 1179656 | tf_op jit(solution)/shard_map/ppermute | solution.py:344
  155.8 5.7 %collective-permute-start.26 = (bf16[128,768]{1,0:T(8,128)(2,1)S(1)}, bf16[128,768]{1,0:T(8,128)(2,1)S(1)}, u32[]{:S(2)}, u32[]{:S(2)}) collective-permute-start(bf16[128,768]{1,0:T(8,128)(2,1)S(1)} %slice.32), channel_id=1, source_target_pairs={{0,2},{1,3},{2,0},{3,1},{4,6},{5,7},{6,4},{7,5},{8,10},{9,11},{10,... | collective-permute-start | bytes 589832 | tf_op jit(solution)/shard_map/ppermute | solution.py:344

commit v6 on v5

--- a/solution.py
+++ b/solution.py
@@ -13,7 +13,7 @@
 F32 = jnp.float32
 BF16 = jnp.bfloat16
 KERNEL_FLOPS = 10_000_000
-META = 16
+META = 8
 
 
 def layer_norm(tokens):
@@ -102,7 +102,9 @@
     picks = ids.shape[0]
     spare = jnp.zeros((picks, half - 3 * rows), F32)
     table = jnp.concatenate([ids[...].astype(F32), high, rest, spare], axis=1)
-    table = jnp.concatenate([table, jnp.zeros((META - picks, half), F32)], axis=0).astype(BF16)
+    if picks < META:
+        table = jnp.concatenate([table, jnp.zeros((META - picks, half), F32)], axis=0)
+    table = table.astype(BF16)
     mine[rows : rows + META, :] = table
     theirs[rows : rows + META, :] = table
 
@@ -173,9 +175,9 @@
             part[e] = total.astype(BF16)
 
 
-def second_kernel(units, keep, send, load, place, *refs):
-    code, gate, near, far, source, other, _ = refs[:7]
-    shown = keep + send
+def second_kernel(units, keep, send, join, load, place, *refs):
+    code, gate, near, far, source, other, after = refs[:7]
+    shown = keep + send + join
     outs, refs = refs[7 : 7 + shown], refs[7 + shown :]
     own, (total, *came) = (refs[0], refs[1:]) if load else (source, refs)
     local = code.shape[0]
@@ -219,6 +221,8 @@
             slot += 1
         if send:
             outs[slot][:, columns] = summed[(units - 1) * count :].astype(BF16)
+        if join:
+            outs[slot][:, columns] = (summed + after[:, columns].astype(F32)).astype(BF16)
 
 
 SMEM = pl.BlockSpec(memory_space=pltpu.SMEM)
@@ -226,7 +230,7 @@
 ANY = pl.BlockSpec(memory_space=pl.ANY)
 HBM = pl.BlockSpec(memory_space=pltpu.HBM)
 GRANT = 24 << 20
-GIVE_GRANTS = (46 << 20, 42 << 20, 44 << 20)
+GIVE_GRANTS = (46 << 20, 42 << 20, 42 << 20)
 SECOND_GRANT = 36 << 20
 
 
@@ -252,7 +256,7 @@
     )(place, *feeds, own, other, after)
 
 
-def second_stage(units, code, gate, near, far, place, own, other, after, keep, send, load):
+def second_stage(units, code, gate, near, far, place, own, other, after, keep, send, join, load):
     local, hidden, quarter = other.shape
     half = 2 * quarter
     rows = near.shape[1]
@@ -260,13 +264,13 @@
     shapes = []
     if keep:
         shapes.append(jax.ShapeDtypeStruct((count, half), F32))
-    if send:
+    if send or join:
         shapes.append(jax.ShapeDtypeStruct((count, half), BF16))
     if load:
         shapes.append(jax.ShapeDtypeStruct(other.shape, BF16))
     return pl.pallas_call(
-        functools.partial(second_kernel, units, keep, send, load),
-        in_specs=[SMEM] + [VMEM] * 4 + [HBM if load else VMEM, VMEM, ANY],
+        functools.partial(second_kernel, units, keep, send, join, load),
+        in_specs=[SMEM] + [VMEM] * 4 + [HBM if load else VMEM, VMEM, VMEM if join else ANY],
         out_specs=[VMEM] * len(shapes),
         scratch_shapes=[pltpu.VMEM((local * rows, half), F32)]
         + [pltpu.SemaphoreType.DMA((local,))] * load,
@@ -361,16 +365,19 @@
     )
     peer = cross(theirs)
     own_in = take(expert_in, True, mine, GIVE_GRANTS[1])
-    unit = jnp.concatenate([mine[:rows], peer[:rows], mine[rows:], peer[rows:]], axis=0)
     far = far_groups(groups)
-    near = swap(unit, GROUP, 1)
+    unit = pair_up(mine, peer, rows)
+    near = pair_up(swap(mine, GROUP, 1), swap(peer, GROUP, 1), rows)
     feeds = {"o": [unit], "n": [near], "l": [share(near)], "t": [share(unit)]}
     for g in far:
         if g % 2:
-            got = swap(unit, GROUP, g)
+            early = swap(mine, GROUP, g)
+            got = pair_up(early, swap(peer, GROUP, g), rows)
         else:
             got = swap(feeds[str(g + 1)][0], GROUP, 1)
         feeds[str(g)] = [got, share(got)]
+    if far:
+        feeds["m"] = [feeds["2"].pop()]
 
     firsts, kept, sums = {}, {}, []
     last, own_out = own_in, None
@@ -385,18 +392,24 @@
         nonlocal last, own_out
         part, code, gate, across = firsts[g]
         load = own_out is None
-        keep, send = g not in "lt", g not in "on"
+        keep, send, join = g not in "ltm2", g not in "on2", g == "2"
         outs = second_stage(
             len(feeds[g]), code, gate, part, across, place, expert_out if load else own_out,
-            other_out, last, keep, send, load,
+            other_out, kept["m"] if join else last, keep, send, join, load,
         )
         last = outs[0]
         own_out = outs[-1] if load else own_out
         if keep:
             kept[g] = outs[0]
+        if join:
+            sums.append(swap(last, GROUP, 2).astype(F32))
         if not send:
             return
-        came = share(outs[keep]).astype(F32)
+        came = share(outs[keep])
+        if g == "m":
+            kept[g] = came
+            return
+        came = came.astype(F32)
         if g != "t":
             last = (kept.pop("n" if g == "l" else g) + came).astype(BF16)
             came = swap(last, GROUP, 1 if g == "l" else int(g)).astype(F32)
@@ -407,15 +420,16 @@
     other_out = share(give_out)
     other_shared_in = share(shared_in)
     other_shared_out = share(shared_out)
+    tail = [str(g) for g in far[:-1]] + ["m", "2"] * bool(far)
     first("n")
     first("l")
     second("o")
-    for g in far[:1]:
-        first(str(g))
+    for g in tail[:1]:
+        first(g)
     second("n")
     second("l")
-    for g in far[1:]:
-        first(str(g))
+    for g in tail[1:]:
+        first(g)
     first("t")
     (shared_part,) = kernel(
         shared_first_kernel, last,
@@ -424,7 +438,7 @@
     )
     last = shared_part
     shared_far = cross(shared_part)
-    for g in [*map(str, far), "t"]:
+    for g in [*tail, "t"]:
         second(g)
     (shared,) = kernel(
         shared_second_kernel, last,
@@ -447,13 +461,17 @@
     return (
         sides == 4
         and expert_in.shape[0] % (blocks * 16) == 0
-        and groups in (2, 4, 8)
+        and groups in (4, 8)
         and rows % 128 == 0
         and width % 512 == 0
         and width // 2 >= 3 * rows
-        and expert_ids.shape[1] <= 8
+        and expert_ids.shape[1] <= META
         and expert_in.shape[2] % 128 == 0
     )
+
+
+def pair_up(first, second, rows):
+    return jnp.concatenate([first[:rows], second[:rows], first[rows:], second[rows:]], axis=0)
 
 
 def far_groups(groups):

time: 163 us -> 170 us (1.043)
  waiting for transfers between devices: 78.5 us -> 83.2 us
  Pallas kernels: 54.1 us -> 56.9 us
    ppermute x27 -> x30, waiting for transfers between devices: 78.5 us -> 83.2 us  [swap(): lax.ppermute(value, axis, [(i, i ^ mask) for i in range(lax.axis_size(axi...]
    pallas_call x6 -> x7, Pallas kernels: 21.5 us -> 22.9 us  [second_stage(): pl.pallas_call(functools.partial(second_kernel, units, keep, send, join,...]
    pallas_call x6 -> x7, Pallas kernels: 20.7 us -> 22 us  [first_stage(): pl.pallas_call(functools.partial(first_kernel, units, picks), in_specs=[S...]
    ppermute x27 -> x30, starting transfers between devices: 27.8 us -> 28 us  [swap(): lax.ppermute(value, axis, [(i, i ^ mask) for i in range(lax.axis_size(axi...]
  transfers between devices with their start and end apart: 27 -> 30, of which waited for: 14 -> 17; matrix products, arithmetic and copies ran while one was open for 0% -> 0% of each run, Pallas kernels for 26% -> 26%
where the time goes in v6:
time: 170 us
  waiting for transfers between devices  83.2 us (49%)
  Pallas kernels  56.9 us (33%)
  starting transfers between devices  28 us (16%)
    ppermute x30, waiting for transfers between devices, swap(): lax.ppermute(value, axis, [(i, i ^ mask) for i in range(lax.axis_size(axi...  83.2 us
    ppermute x30, starting transfers between devices, swap(): lax.ppermute(value, axis, [(i, i ^ mask) for i in range(lax.axis_size(axi...  28 us
    pallas_call x7, Pallas kernels, second_stage(): pl.pallas_call(functools.partial(second_kernel, units, keep, send, join,...  22.9 us
    pallas_call x7, Pallas kernels, first_stage(): pl.pallas_call(functools.partial(first_kernel, units, picks), in_specs=[S...  22 us
    pallas_call x3, Pallas kernels, take_stage(): pl.pallas_call(functools.partial(take_kernel, own), in_specs=[SMEM, HBM,...  8.77 us
  transfers between devices with their start and end apart: 30, of which 17 were waited for; matrix products, arithmetic and copies ran while one was open for 0% of the time, Pallas kernels for 26%

profile of v6, /device:TPU:0, one launch (start us, length us, event | category | flops | bytes accessed | tf_op | source)
XLA Modules:
  0.0 170.2 jit_solution(7726058923345135152)
XLA Ops:
  0.1 2.9 %shard_map.73._ = bf16[8,384,768]{2,1,0:T(8,128)(2,1)S(1)} custom-call(s32[3]{0:T(128)S(1)} %pad_add_fusion.place.after, bf16[16,384,768]{2,1,0:T(8,128)(2,1)} %source.4, s32[3]{0:T(128)S(1)} %pad_add_fusion.place.after), custom_call_target="tpu_custom_call" | custom-call | flops 10000000 | bytes 9437184 | tf_op jit(solution)/shard_map/pallas_call | solution.py:312
  7.0 2.9 %shard_map.75.refs_1_.refs_3_.refs_2_ = bf16[8,384,768]{2,1,0:T(8,128)(2,1)S(1)} custom-call(s32[3]{0:T(128)S(1)} %pad_add_fusion.place.after, bf16[16,384,768]{2,1,0:T(8,128)(2,1)} %source.4, bf16[136,768]{1,0:T(8,128)(2,1)S(1)} %get-tuple-element.32.after), custom_call_target="tpu_custom_call" | custom-call | flops 10000000 | bytes 9437184 | tf_op jit(solution)/shard_map/pallas_call | solution.py:312
  10.0 2.8 %collective-permute-done = bf16[136,768]{1,0:T(8,128)(2,1)S(1)} collective-permute-done((bf16[136,768]{1,0:T(8,128)(2,1)S(1)}, bf16[136,768]{1,0:T(8,128)(2,1)S(1)}, u32[]{:S(2)}, u32[]{:S(2)}) %collective-permute-start) | collective-permute-done | bytes 208928 | tf_op jit(solution)/shard_map/ppermute | solution.py:348
  12.9 3.1 %shard_map.76 = (bf16[8,40,768]{2,1,0:T(8,128)(2,1)S(1)}, f32[8,256]{1,0:T(8,128)S(1)}, f32[8,256]{1,0:T(8,128)S(1)}) custom-call(s32[3]{0:T(128)S(1)} %pad_add_fusion.place.after, bf16[272,768]{1,0:T(8,128)(2,1)S(1)} %pad_maximum_fusion.refs_0_.feed, bf16[8,384,768]{2,1,0:T(8,128)(2,1)S(1)} %shard_map.75.refs_1_.refs_3_.refs_2_, ...), custom_call_target="tpu_custom_call" | custom-call | flops 10000000 | bytes 9437184 | tf_op jit(solution)/shard_map/pallas_call | solution.py:248
  16.0 2.9 %shard_map.77.refs_3_ = bf16[8,768,384]{2,1,0:T(8,128)(2,1)S(1)} custom-call(s32[3]{0:T(128)S(1)} %pad_add_fusion.place.after, bf16[16,768,384]{2,1,0:T(8,128)(2,1)} %refs_4_.1, f32[8,256]{1,0:T(8,128)S(1)} %get-tuple-element.34.after.refs_0_), custom_call_target="tpu_custom_call" | custom-call | flops 10000000 | bytes 9437184 | tf_op jit(solution)/shard_map/pallas_call | solution.py:312
  21.1 3.8 %collective-permute-start.4 = (bf16[136,768]{1,0:T(8,128)(2,1)S(1)}, bf16[136,768]{1,0:T(8,128)(2,1)S(1)}, u32[]{:S(2)}, u32[]{:S(2)}) collective-permute-start(bf16[136,768]{1,0:T(8,128)(2,1)S(1)} %get-tuple-element.32.after), channel_id=1, source_target_pairs={{0,12},{4,8},{8,4},{12,0},{1,13},{5,9},{9,5},{13,1},{2,14},{6,10},... | collective-permute-start | bytes 626696 | tf_op jit(solution)/shard_map/ppermute | solution.py:348
  27.1 4.0 %collective-permute-done.9 = bf16[136,768]{1,0:T(8,128)(2,1)S(1)} collective-permute-done((bf16[136,768]{1,0:T(8,128)(2,1)S(1)}, bf16[136,768]{1,0:T(8,128)(2,1)S(1)}, u32[]{:S(2)}, u32[]{:S(2)}) %collective-permute-start.9) | collective-permute-done | bytes 208928 | tf_op jit(solution)/shard_map/ppermute | solution.py:348
  31.2 7.2 %collective-permute-done.4 = bf16[136,768]{1,0:T(8,128)(2,1)S(1)} collective-permute-done((bf16[136,768]{1,0:T(8,128)(2,1)S(1)}, bf16[136,768]{1,0:T(8,128)(2,1)S(1)}, u32[]{:S(2)}, u32[]{:S(2)}) %collective-permute-start.4) | collective-permute-done | bytes 208928 | tf_op jit(solution)/shard_map/ppermute | solution.py:348
  38.4 3.9 %collective-permute-done.5 = bf16[136,768]{1,0:T(8,128)(2,1)S(1)} collective-permute-done((bf16[136,768]{1,0:T(8,128)(2,1)S(1)}, bf16[136,768]{1,0:T(8,128)(2,1)S(1)}, u32[]{:S(2)}, u32[]{:S(2)}) %collective-permute-start.5) | collective-permute-done | bytes 208928 | tf_op jit(solution)/shard_map/ppermute | solution.py:348
  44.0 3.1 %shard_map.78 = (bf16[8,40,768]{2,1,0:T(8,128)(2,1)S(1)}, f32[8,256]{1,0:T(8,128)S(1)}, f32[8,256]{1,0:T(8,128)S(1)}) custom-call(s32[3]{0:T(128)S(1)} %pad_add_fusion.place.after, bf16[272,768]{1,0:T(8,128)(2,1)S(1)} %pad_maximum_fusion.2.refs_0_, bf16[8,384,768]{2,1,0:T(8,128)(2,1)S(1)} %shard_map.75.refs_1_.refs_3_.refs_2_, ...), custom_call_target="tpu_custom_call" | custom-call | flops 10000000 | bytes 9437184 | tf_op jit(solution)/shard_map/pallas_call | solution.py:248
  47.7 3.1 %shard_map.79 = (bf16[8,40,768]{2,1,0:T(8,128)(2,1)S(1)}, f32[8,256]{1,0:T(8,128)S(1)}, f32[8,256]{1,0:T(8,128)S(1)}) custom-call(s32[3]{0:T(128)S(1)} %pad_add_fusion.place.after, bf16[272,768]{1,0:T(8,128)(2,1)S(1)} %collective-permute-done.13.refs_0_, bf16[8,384,768]{2,1,0:T(8,128)(2,1)S(1)} %shard_map.75.refs_1_.refs_3_.refs_2_, ...), custom_call_target="tpu_custom_call" | custom-call | flops 10000000 | bytes 9437184 | tf_op jit(solution)/shard_map/pallas_call | solution.py:248
  52.3 4.2 %collective-permute-done.11.refs_3_ = bf16[8,40,768]{2,1,0:T(8,128)(2,1)S(1)} collective-permute-done((bf16[8,40,768]{2,1,0:T(8,128)(2,1)S(1)}, bf16[8,40,768]{2,1,0:T(8,128)(2,1)S(1)}, u32[]{:S(2)}, u32[]{:S(2)}) %collective-permute-start.11) | collective-permute-done | bytes 491552 | tf_op jit(solution)/shard_map/ppermute | solution.py:348
  56.5 4.9 %shard_map.80 = (f32[256,768]{1,0:T(8,128)S(1)}, bf16[8,768,384]{2,1,0:T(8,128)(2,1)S(1)}) custom-call(s32[3]{0:T(128)S(1)} %pad_add_fusion.place.after, f32[8,256]{1,0:T(8,128)S(1)} %get-tuple-element.34.after.refs_0_, f32[8,256]{1,0:T(8,128)S(1)} %get-tuple-element.38.refs_1_, bf16[8,40,768]{2,1,0:T(8,128)(2,1)S(1)} %get-tuple-element.39.refs_2_, ...), custom_call_target="tpu_custom_call" | custom-call | flops 10000000 | bytes 9437184 | tf_op jit(solution)/shard_map/pallas_call | solution.py:271
  61.4 3.6 %shard_map.81 = (bf16[8,80,768]{2,1,0:T(8,128)(2,1)S(1)}, f32[8,512]{1,0:T(8,128)S(1)}, f32[8,512]{1,0:T(8,128)S(1)}) custom-call(s32[3]{0:T(128)S(1)} %pad_add_fusion.place.after, bf16[272,768]{1,0:T(8,128)(2,1)S(1)} %pad_maximum_fusion.1.refs_0_, bf16[272,768]{1,0:T(8,128)(2,1)S(1)} %collective-permute-done.14.refs_1_, ...), custom_call_target="tpu_custom_call" | custom-call | flops 10000000 | bytes 9437184 | tf_op jit(solution)/shard_map/pallas_call | solution.py:248
  67.5 2.9 %shard_map.82.refs_6_ = f32[256,768]{1,0:T(8,128)S(1)} custom-call(s32[3]{0:T(128)S(1)} %pad_add_fusion.place.after, f32[8,256]{1,0:T(8,128)S(1)} %get-tuple-element.35.refs_3_.refs_0_, f32[8,256]{1,0:T(8,128)S(1)} %get-tuple-element.36.refs_1_, bf16[8,40,768]{2,1,0:T(8,128)(2,1)S(1)} %get-tuple-element.37.refs_2_, ...), custom_call_target="tpu_custom_call" | custom-call | flops 10000000 | bytes 9437184 | tf_op jit(solution)/shard_map/pallas_call | solution.py:271
  70.4 7.2 %collective-permute-done.15.refs_3_ = bf16[8,40,768]{2,1,0:T(8,128)(2,1)S(1)} collective-permute-done((bf16[8,40,768]{2,1,0:T(8,128)(2,1)S(1)}, bf16[8,40,768]{2,1,0:T(8,128)(2,1)S(1)}, u32[]{:S(2)}, u32[]{:S(2)}) %collective-permute-start.15) | collective-permute-done | bytes 491552 | tf_op jit(solution)/shard_map/ppermute | solution.py:348
  77.6 2.9 %shard_map.83 = bf16[256,768]{1,0:T(8,128)(2,1)S(1)} custom-call(s32[3]{0:T(128)S(1)} %pad_add_fusion.place.after, f32[8,256]{1,0:T(8,128)S(1)} %get-tuple-element.40.refs_6_.refs_0_, f32[8,256]{1,0:T(8,128)S(1)} %get-tuple-element.44.refs_1_, bf16[8,40,768]{2,1,0:T(8,128)(2,1)S(1)} %get-tuple-element.45.refs_2_, ...), custom_call_target="tpu_custom_call" | custom-call | flops 10000000 | bytes 9437184 | tf_op jit(solution)/shard_map/pallas_call | solution.py:271
  83.7 3.1 %shard_map.84 = (bf16[8,40,768]{2,1,0:T(8,128)(2,1)S(1)}, f32[8,256]{1,0:T(8,128)S(1)}, f32[8,256]{1,0:T(8,128)S(1)}) custom-call(s32[3]{0:T(128)S(1)} %pad_add_fusion.place.after, bf16[272,768]{1,0:T(8,128)(2,1)S(1)} %collective-permute-done.7.refs_0_, bf16[8,384,768]{2,1,0:T(8,128)(2,1)S(1)} %shard_map.75.refs_1_.refs_3_.refs_2_, ...), custom_call_target="tpu_custom_call" | custom-call | flops 10000000 | bytes 9437184 | tf_op jit(solution)/shard_map/pallas_call | solution.py:248
  86.8 3.1 %shard_map.85 = (bf16[8,40,768]{2,1,0:T(8,128)(2,1)S(1)}, f32[8,256]{1,0:T(8,128)S(1)}, f32[8,256]{1,0:T(8,128)S(1)}) custom-call(s32[3]{0:T(128)S(1)} %pad_add_fusion.place.after, bf16[272,768]{1,0:T(8,128)(2,1)S(1)} %collective-permute-done.6.refs_0_, bf16[8,384,768]{2,1,0:T(8,128)(2,1)S(1)} %shard_map.75.refs_1_.refs_3_.refs_2_, ...), custom_call_target="tpu_custom_call" | custom-call | flops 10000000 | bytes 9437184 | tf_op jit(solution)/shard_map/pallas_call | solution.py:248
  89.9 3.1 %shard_map.86 = (bf16[8,40,768]{2,1,0:T(8,128)(2,1)S(1)}, f32[8,256]{1,0:T(8,128)S(1)}, f32[8,256]{1,0:T(8,128)S(1)}) custom-call(s32[3]{0:T(128)S(1)} %pad_add_fusion.place.after, bf16[272,768]{1,0:T(8,128)(2,1)S(1)} %collective-permute-done.2.refs_0_, bf16[8,384,768]{2,1,0:T(8,128)(2,1)S(1)} %shard_map.75.refs_1_.refs_3_.refs_2_, ...), custom_call_target="tpu_custom_call" | custom-call | flops 10000000 | bytes 9437184 | tf_op jit(solution)/shard_map/pallas_call | solution.py:248
  94.1 3.1 %collective-permute-done.22.refs_3_ = bf16[8,80,768]{2,1,0:T(8,128)(2,1)S(1)} collective-permute-done((bf16[8,80,768]{2,1,0:T(8,128)(2,1)S(1)}, bf16[8,80,768]{2,1,0:T(8,128)(2,1)S(1)}, u32[]{:S(2)}, u32[]{:S(2)}) %collective-permute-start.22) | collective-permute-done | bytes 983072 | tf_op jit(solution)/shard_map/ppermute | solution.py:348
  97.2 3.6 %shard_map.88 = (f32[256,768]{1,0:T(8,128)S(1)}, bf16[256,768]{1,0:T(8,128)(2,1)S(1)}) custom-call(s32[3]{0:T(128)S(1)} %pad_add_fusion.place.after, f32[8,512]{1,0:T(8,128)S(1)} %get-tuple-element.43.refs_6_.refs_0_, f32[8,512]{1,0:T(8,128)S(1)} %get-tuple-element.55.refs_1_, bf16[8,80,768]{2,1,0:T(8,128)(2,1)S(1)} %get-tuple-element.56.refs_2_, ...), custom_call_target="tpu_custom_call" | custom-call | flops 10000000 | bytes 9437184 | tf_op jit(solution)/shard_map/pallas_call | solution.py:271
  104.7 10.3 %collective-permute-done.21.refs_3_ = bf16[8,40,768]{2,1,0:T(8,128)(2,1)S(1)} collective-permute-done((bf16[8,40,768]{2,1,0:T(8,128)(2,1)S(1)}, bf16[8,40,768]{2,1,0:T(8,128)(2,1)S(1)}, u32[]{:S(2)}, u32[]{:S(2)}) %collective-permute-start.21) | collective-permute-done | bytes 491552 | tf_op jit(solution)/shard_map/ppermute | solution.py:348
  115.1 2.9 %shard_map.89 = bf16[256,768]{1,0:T(8,128)(2,1)S(1)} custom-call(s32[3]{0:T(128)S(1)} %pad_add_fusion.place.after, f32[8,256]{1,0:T(8,128)S(1)} %get-tuple-element.46.refs_3_.refs_0_, f32[8,256]{1,0:T(8,128)S(1)} %get-tuple-element.53.refs_1_, bf16[8,40,768]{2,1,0:T(8,128)(2,1)S(1)} %get-tuple-element.54.refs_2_, ...), custom_call_target="tpu_custom_call" | custom-call | flops 10000000 | bytes 9437184 | tf_op jit(solution)/shard_map/pallas_call | solution.py:271
  119.6 6.0 %collective-permute-done.20.refs_3_ = bf16[8,40,768]{2,1,0:T(8,128)(2,1)S(1)} collective-permute-done((bf16[8,40,768]{2,1,0:T(8,128)(2,1)S(1)}, bf16[8,40,768]{2,1,0:T(8,128)(2,1)S(1)}, u32[]{:S(2)}, u32[]{:S(2)}) %collective-permute-start.20) | collective-permute-done | bytes 491552 | tf_op jit(solution)/shard_map/ppermute | solution.py:348
  125.6 2.9 %collective-permute-start.26 = (bf16[256,768]{1,0:T(8,128)(2,1)S(1)}, bf16[256,768]{1,0:T(8,128)(2,1)S(1)}, u32[]{:S(2)}, u32[]{:S(2)}) collective-permute-start(bf16[256,768]{1,0:T(8,128)(2,1)S(1)} %add_convert_fusion.refs_6_), channel_id=1, source_target_pairs={{0,12},{4,8},{8,4},{12,0},{1,13},{5,9},{9,5},{13,1},{2,14},{6,10},... | collective-permute-start | bytes 1179656 | tf_op jit(solution)/shard_map/ppermute | solution.py:348
  128.5 2.9 %shard_map.90.refs_6_ = bf16[256,768]{1,0:T(8,128)(2,1)S(1)} custom-call(s32[3]{0:T(128)S(1)} %pad_add_fusion.place.after, f32[8,256]{1,0:T(8,128)S(1)} %get-tuple-element.47.refs_3_.refs_0_, f32[8,256]{1,0:T(8,128)S(1)} %get-tuple-element.51.refs_1_, bf16[8,40,768]{2,1,0:T(8,128)(2,1)S(1)} %get-tuple-element.52.refs_2_, ...), custom_call_target="tpu_custom_call" | custom-call | flops 10000000 | bytes 9437184 | tf_op jit(solution)/shard_map/pallas_call | solution.py:271
  131.4 4.8 %collective-permute-done.19.refs_3_ = bf16[8,40,768]{2,1,0:T(8,128)(2,1)S(1)} collective-permute-done((bf16[8,40,768]{2,1,0:T(8,128)(2,1)S(1)}, bf16[8,40,768]{2,1,0:T(8,128)(2,1)S(1)}, u32[]{:S(2)}, u32[]{:S(2)}) %collective-permute-start.19) | collective-permute-done | bytes 491552 | tf_op jit(solution)/shard_map/ppermute | solution.py:348
  136.1 2.9 %shard_map.91._ = bf16[256,768]{1,0:T(8,128)(2,1)S(1)} custom-call(s32[3]{0:T(128)S(1)} %pad_add_fusion.place.after, f32[8,256]{1,0:T(8,128)S(1)} %get-tuple-element.48._.refs_0_, f32[8,256]{1,0:T(8,128)S(1)} %get-tuple-element.49.refs_1_, bf16[8,40,768]{2,1,0:T(8,128)(2,1)S(1)} %get-tuple-element.50.refs_2_, ...), custom_call_target="tpu_custom_call" | custom-call | flops 10000000 | bytes 9437184 | tf_op jit(solution)/shard_map/pallas_call | solution.py:271
  140.6 3.4 %collective-permute-done.17.far = bf16[256,768]{1,0:T(8,128)(2,1)S(1)} collective-permute-done((bf16[256,768]{1,0:T(8,128)(2,1)S(1)}, bf16[256,768]{1,0:T(8,128)(2,1)S(1)}, u32[]{:S(2)}, u32[]{:S(2)}) %collective-permute-start.17) | collective-permute-done | bytes 393248 | tf_op jit(solution)/shard_map/ppermute | solution.py:348
  147.0 15.1 %collective-permute-done.27 = bf16[256,768]{1,0:T(8,128)(2,1)S(1)} collective-permute-done((bf16[256,768]{1,0:T(8,128)(2,1)S(1)}, bf16[256,768]{1,0:T(8,128)(2,1)S(1)}, u32[]{:S(2)}, u32[]{:S(2)}) %collective-permute-start.27) | collective-permute-done | bytes 393248 | tf_op jit(solution)/shard_map/ppermute | solution.py:348
  164.0 5.2 %collective-permute-done.29 = bf16[128,768]{1,0:T(8,128)(2,1)S(1)} collective-permute-done((bf16[128,768]{1,0:T(8,128)(2,1)S(1)}, bf16[128,768]{1,0:T(8,128)(2,1)S(1)}, u32[]{:S(2)}, u32[]{:S(2)}) %collective-permute-start.29) | collective-permute-done | bytes 196640 | tf_op jit(solution)/shard_map/ppermute | solution.py:348
  (80 shorter events, 32.1 us)
Async XLA Ops:
  0.1 3.5 %copy-start.4 = (f32[128,8]{0,1:T(8,128)S(1)}, f32[128,8]{0,1:T(8,128)}, u32[]{:S(2)}) copy-start(f32[128,8]{0,1:T(8,128)} %param.9) | copy-start | bytes 12292
  3.0 9.9 %collective-permute-start.3 = (bf16[8,384,768]{2,1,0:T(8,128)(2,1)S(1)}, bf16[8,384,768]{2,1,0:T(8,128)(2,1)S(1)}, u32[]{:S(2)}, u32[]{:S(2)}) collective-permute-start(bf16[8,384,768]{2,1,0:T(8,128)(2,1)S(1)} %shard_map.73._), channel_id=1, source_target_pairs={{0,1},{1,0},{2,3},{3,2},{4,5},{5,4},{6,7},{7,6},{8,9},{9,8},{10,11... | collective-permute-start | bytes 14155784 | tf_op jit(solution)/shard_map/ppermute | solution.py:348
  4.4 8.4 %collective-permute-start = (bf16[136,768]{1,0:T(8,128)(2,1)S(1)}, bf16[136,768]{1,0:T(8,128)(2,1)S(1)}, u32[]{:S(2)}, u32[]{:S(2)}) collective-permute-start(bf16[136,768]{1,0:T(8,128)(2,1)S(1)} %get-tuple-element.33), channel_id=1, source_target_pairs={{0,2},{1,3},{2,0},{3,1},{4,6},{5,7},{6,4},{7,5},{8,10},{9,11},{10,... | collective-permute-start | bytes 626696 | tf_op jit(solution)/shard_map/ppermute | solution.py:348
  18.9 37.6 %collective-permute-start.12 = (bf16[8,768,384]{2,1,0:T(8,128)(2,1)S(1)}, bf16[8,768,384]{2,1,0:T(8,128)(2,1)S(1)}, u32[]{:S(2)}, u32[]{:S(2)}) collective-permute-start(bf16[8,768,384]{2,1,0:T(8,128)(2,1)S(1)} %shard_map.77.refs_3_), channel_id=1, source_target_pairs={{0,1},{1,0},{2,3},{3,2},{4,5},{5,4},{6,7},{7,6},{8,9},{9,8},{10,11... | collective-permute-start | bytes 14155784 | tf_op jit(solution)/shard_map/ppermute | solution.py:348
  19.0 8.1 %collective-permute-start.8 = (bf16[136,768]{1,0:T(8,128)(2,1)S(1)}, bf16[136,768]{1,0:T(8,128)(2,1)S(1)}, u32[]{:S(2)}, u32[]{:S(2)}) collective-permute-start(bf16[136,768]{1,0:T(8,128)(2,1)S(1)} %get-tuple-element.32.after), channel_id=1, source_target_pairs={{0,4},{4,0},{8,12},{12,8},{1,5},{5,1},{9,13},{13,9},{2,6},{6,2},{1... | collective-permute-start | bytes 626696 | tf_op jit(solution)/shard_map/ppermute | solution.py:348
  20.9 10.2 %collective-permute-start.9 = (bf16[136,768]{1,0:T(8,128)(2,1)S(1)}, bf16[136,768]{1,0:T(8,128)(2,1)S(1)}, u32[]{:S(2)}, u32[]{:S(2)}) collective-permute-start(bf16[136,768]{1,0:T(8,128)(2,1)S(1)} %collective-permute-done), channel_id=1, source_target_pairs={{0,4},{4,0},{8,12},{12,8},{1,5},{5,1},{9,13},{13,9},{2,6},{6,2},{1... | collective-permute-start | bytes 626696 | tf_op jit(solution)/shard_map/ppermute | solution.py:348
  21.1 17.3 %collective-permute-start.4 = (bf16[136,768]{1,0:T(8,128)(2,1)S(1)}, bf16[136,768]{1,0:T(8,128)(2,1)S(1)}, u32[]{:S(2)}, u32[]{:S(2)}) collective-permute-start(bf16[136,768]{1,0:T(8,128)(2,1)S(1)} %get-tuple-element.32.after), channel_id=1, source_target_pairs={{0,12},{4,8},{8,4},{12,0},{1,13},{5,9},{9,5},{13,1},{2,14},{6,10},... | collective-permute-start | bytes 626696 | tf_op jit(solution)/shard_map/ppermute | solution.py:348
  24.9 17.4 %collective-permute-start.5 = (bf16[136,768]{1,0:T(8,128)(2,1)S(1)}, bf16[136,768]{1,0:T(8,128)(2,1)S(1)}, u32[]{:S(2)}, u32[]{:S(2)}) collective-permute-start(bf16[136,768]{1,0:T(8,128)(2,1)S(1)} %collective-permute-done), channel_id=1, source_target_pairs={{0,12},{4,8},{8,4},{12,0},{1,13},{5,9},{9,5},{13,1},{2,14},{6,10},... | collective-permute-start | bytes 626696 | tf_op jit(solution)/shard_map/ppermute | solution.py:348
  31.2 16.6 %collective-permute-start.13 = (bf16[272,768]{1,0:T(8,128)(2,1)S(1)}, bf16[272,768]{1,0:T(8,128)(2,1)S(1)}, u32[]{:S(2)}, u32[]{:S(2)}) collective-permute-start(bf16[272,768]{1,0:T(8,128)(2,1)S(1)} %pad_maximum_fusion.2.refs_0_), channel_id=1, source_target_pairs={{0,1},{1,0},{2,3},{3,2},{4,5},{5,4},{6,7},{7,6},{8,9},{9,8},{10,11... | collective-permute-start | bytes 1253384 | tf_op jit(solution)/shard_map/ppermute | solution.py:348
  42.4 14.2 %collective-permute-start.11 = (bf16[8,40,768]{2,1,0:T(8,128)(2,1)S(1)}, bf16[8,40,768]{2,1,0:T(8,128)(2,1)S(1)}, u32[]{:S(2)}, u32[]{:S(2)}) collective-permute-start(bf16[8,40,768]{2,1,0:T(8,128)(2,1)S(1)} %get-tuple-element.39.refs_2_), channel_id=1, source_target_pairs={{0,2},{1,3},{2,0},{3,1},{4,6},{5,7},{6,4},{7,5},{8,10},{9,11},{10,... | collective-permute-start | bytes 1474568 | tf_op jit(solution)/shard_map/ppermute | solution.py:348
  44.0 17.5 %collective-permute-start.14 = (bf16[272,768]{1,0:T(8,128)(2,1)S(1)}, bf16[272,768]{1,0:T(8,128)(2,1)S(1)}, u32[]{:S(2)}, u32[]{:S(2)}) collective-permute-start(bf16[272,768]{1,0:T(8,128)(2,1)S(1)} %pad_maximum_fusion.1.refs_0_), channel_id=1, source_target_pairs={{0,1},{1,0},{2,3},{3,2},{4,5},{5,4},{6,7},{7,6},{8,9},{9,8},{10,11... | collective-permute-start | bytes 1253384 | tf_op jit(solution)/shard_map/ppermute | solution.py:348
  47.1 20.4 %collective-permute-start.10 = (bf16[8,40,768]{2,1,0:T(8,128)(2,1)S(1)}, bf16[8,40,768]{2,1,0:T(8,128)(2,1)S(1)}, u32[]{:S(2)}, u32[]{:S(2)}) collective-permute-start(bf16[8,40,768]{2,1,0:T(8,128)(2,1)S(1)} %get-tuple-element.37.refs_2_), channel_id=1, source_target_pairs={{0,2},{1,3},{2,0},{3,1},{4,6},{5,7},{6,4},{7,5},{8,10},{9,11},{10,... | collective-permute-start | bytes 1474568 | tf_op jit(solution)/shard_map/ppermute | solution.py:348
  50.8 26.8 %collective-permute-start.15 = (bf16[8,40,768]{2,1,0:T(8,128)(2,1)S(1)}, bf16[8,40,768]{2,1,0:T(8,128)(2,1)S(1)}, u32[]{:S(2)}, u32[]{:S(2)}) collective-permute-start(bf16[8,40,768]{2,1,0:T(8,128)(2,1)S(1)} %get-tuple-element.45.refs_2_), channel_id=1, source_target_pairs={{0,2},{1,3},{2,0},{3,1},{4,6},{5,7},{6,4},{7,5},{8,10},{9,11},{10,... | collective-permute-start | bytes 1474568 | tf_op jit(solution)/shard_map/ppermute | solution.py:348
  65.0 32.2 %collective-permute-start.22 = (bf16[8,80,768]{2,1,0:T(8,128)(2,1)S(1)}, bf16[8,80,768]{2,1,0:T(8,128)(2,1)S(1)}, u32[]{:S(2)}, u32[]{:S(2)}) collective-permute-start(bf16[8,80,768]{2,1,0:T(8,128)(2,1)S(1)} %get-tuple-element.56.refs_2_), channel_id=1, source_target_pairs={{0,2},{1,3},{2,0},{3,1},{4,6},{5,7},{6,4},{7,5},{8,10},{9,11},{10,... | collective-permute-start | bytes 2949128 | tf_op jit(solution)/shard_map/ppermute | solution.py:348
  66.6 14.5 %collective-permute-start.6 = (bf16[272,768]{1,0:T(8,128)(2,1)S(1)}, bf16[272,768]{1,0:T(8,128)(2,1)S(1)}, u32[]{:S(2)}, u32[]{:S(2)}) collective-permute-start(bf16[272,768]{1,0:T(8,128)(2,1)S(1)} %pad_maximum_fusion.1.refs_0_), channel_id=1, source_target_pairs={{0,4},{4,0},{8,12},{12,8},{1,5},{5,1},{9,13},{13,9},{2,6},{6,2},{1... | collective-permute-start | bytes 1253384 | tf_op jit(solution)/shard_map/ppermute | solution.py:348
  80.5 1.8 %collective-permute-start.16 = (bf16[256,768]{1,0:T(8,128)(2,1)S(1)}, bf16[256,768]{1,0:T(8,128)(2,1)S(1)}, u32[]{:S(2)}, u32[]{:S(2)}) collective-permute-start(bf16[256,768]{1,0:T(8,128)(2,1)S(1)} %shard_map.83), channel_id=1, source_target_pairs={{0,1},{1,0},{2,3},{3,2},{4,5},{5,4},{6,7},{7,6},{8,9},{9,8},{10,11... | collective-permute-start | bytes 1179656 | tf_op jit(solution)/shard_map/ppermute | solution.py:348
  80.6 12.4 %collective-permute-start.1 = (bf16[384,768]{1,0:T(8,128)(2,1)S(1)}, bf16[384,768]{1,0:T(8,128)(2,1)S(1)}, u32[]{:S(2)}, u32[]{:S(2)}) collective-permute-start(bf16[384,768]{1,0:T(8,128)(2,1)S(1)} %copy-done.1), channel_id=1, source_target_pairs={{0,1},{1,0},{2,3},{3,2},{4,5},{5,4},{6,7},{7,6},{8,9},{9,8},{10,11... | collective-permute-start | bytes 1769480 | tf_op jit(solution)/shard_map/ppermute | solution.py:348
  81.1 2.6 %collective-permute-start.7 = (bf16[272,768]{1,0:T(8,128)(2,1)S(1)}, bf16[272,768]{1,0:T(8,128)(2,1)S(1)}, u32[]{:S(2)}, u32[]{:S(2)}) collective-permute-start(bf16[272,768]{1,0:T(8,128)(2,1)S(1)} %collective-permute-done.6.refs_0_), channel_id=1, source_target_pairs={{0,1},{1,0},{2,3},{3,2},{4,5},{5,4},{6,7},{7,6},{8,9},{9,8},{10,11... | collective-permute-start | bytes 1253384 | tf_op jit(solution)/shard_map/ppermute | solution.py:348
  81.2 8.7 %collective-permute-start.2 = (bf16[272,768]{1,0:T(8,128)(2,1)S(1)}, bf16[272,768]{1,0:T(8,128)(2,1)S(1)}, u32[]{:S(2)}, u32[]{:S(2)}) collective-permute-start(bf16[272,768]{1,0:T(8,128)(2,1)S(1)} %pad_maximum_fusion.refs_0_.feed), channel_id=1, source_target_pairs={{0,1},{1,0},{2,3},{3,2},{4,5},{5,4},{6,7},{7,6},{8,9},{9,8},{10,11... | collective-permute-start | bytes 1253384 | tf_op jit(solution)/shard_map/ppermute | solution.py:348
  97.2 5.3 %copy-start.2 = (bf16[768,384]{1,0:T(8,128)(2,1)S(1)}, bf16[768,384]{1,0:T(8,128)(2,1)}, u32[]{:S(2)}) copy-start(bf16[768,384]{1,0:T(8,128)(2,1)} %own.3) | copy-start | bytes 1769476
  100.8 3.8 %collective-permute-start.23 = (bf16[256,768]{1,0:T(8,128)(2,1)S(1)}, bf16[256,768]{1,0:T(8,128)(2,1)S(1)}, u32[]{:S(2)}, u32[]{:S(2)}) collective-permute-start(bf16[256,768]{1,0:T(8,128)(2,1)S(1)} %get-tuple-element.58), channel_id=1, source_target_pairs={{0,1},{1,0},{2,3},{3,2},{4,5},{5,4},{6,7},{7,6},{8,9},{9,8},{10,11... | collective-permute-start | bytes 1179656 | tf_op jit(solution)/shard_map/ppermute | solution.py:348
  100.9 14.2 %collective-permute-start.21 = (bf16[8,40,768]{2,1,0:T(8,128)(2,1)S(1)}, bf16[8,40,768]{2,1,0:T(8,128)(2,1)S(1)}, u32[]{:S(2)}, u32[]{:S(2)}) collective-permute-start(bf16[8,40,768]{2,1,0:T(8,128)(2,1)S(1)} %get-tuple-element.54.refs_2_), channel_id=1, source_target_pairs={{0,2},{1,3},{2,0},{3,1},{4,6},{5,7},{6,4},{7,5},{8,10},{9,11},{10,... | collective-permute-start | bytes 1474568 | tf_op jit(solution)/shard_map/ppermute | solution.py:348
  102.5 36.6 %collective-permute-start.18 = (bf16[768,384]{1,0:T(8,128)(2,1)S(1)}, bf16[768,384]{1,0:T(8,128)(2,1)S(1)}, u32[]{:S(2)}, u32[]{:S(2)}) collective-permute-start(bf16[768,384]{1,0:T(8,128)(2,1)S(1)} %copy-done.2), channel_id=1, source_target_pairs={{0,1},{1,0},{2,3},{3,2},{4,5},{5,4},{6,7},{7,6},{8,9},{9,8},{10,11... | collective-permute-start | bytes 1769480 | tf_op jit(solution)/shard_map/ppermute | solution.py:348
  102.6 23.0 %collective-permute-start.20 = (bf16[8,40,768]{2,1,0:T(8,128)(2,1)S(1)}, bf16[8,40,768]{2,1,0:T(8,128)(2,1)S(1)}, u32[]{:S(2)}, u32[]{:S(2)}) collective-permute-start(bf16[8,40,768]{2,1,0:T(8,128)(2,1)S(1)} %get-tuple-element.52.refs_2_), channel_id=1, source_target_pairs={{0,2},{1,3},{2,0},{3,1},{4,6},{5,7},{6,4},{7,5},{8,10},{9,11},{10,... | collective-permute-start | bytes 1474568 | tf_op jit(solution)/shard_map/ppermute | solution.py:348
  103.2 33.0 %collective-permute-start.19 = (bf16[8,40,768]{2,1,0:T(8,128)(2,1)S(1)}, bf16[8,40,768]{2,1,0:T(8,128)(2,1)S(1)}, u32[]{:S(2)}, u32[]{:S(2)}) collective-permute-start(bf16[8,40,768]{2,1,0:T(8,128)(2,1)S(1)} %get-tuple-element.50.refs_2_), channel_id=1, source_target_pairs={{0,2},{1,3},{2,0},{3,1},{4,6},{5,7},{6,4},{7,5},{8,10},{9,11},{10,... | collective-permute-start | bytes 1474568 | tf_op jit(solution)/shard_map/ppermute | solution.py:348
  118.0 7.6 %collective-permute-start.24 = (bf16[256,768]{1,0:T(8,128)(2,1)S(1)}, bf16[256,768]{1,0:T(8,128)(2,1)S(1)}, u32[]{:S(2)}, u32[]{:S(2)}) collective-permute-start(bf16[256,768]{1,0:T(8,128)(2,1)S(1)} %shard_map.89), channel_id=1, source_target_pairs={{0,1},{1,0},{2,3},{3,2},{4,5},{5,4},{6,7},{7,6},{8,9},{9,8},{10,11... | collective-permute-start | bytes 1179656 | tf_op jit(solution)/shard_map/ppermute | solution.py:348
  118.0 26.0 %collective-permute-start.17 = (bf16[256,768]{1,0:T(8,128)(2,1)S(1)}, bf16[256,768]{1,0:T(8,128)(2,1)S(1)}, u32[]{:S(2)}, u32[]{:S(2)}) collective-permute-start(bf16[256,768]{1,0:T(8,128)(2,1)S(1)} %shard_map.87.refs_6_.near), channel_id=1, source_target_pairs={{0,2},{1,3},{2,0},{3,1},{4,6},{5,7},{6,4},{7,5},{8,10},{9,11},{10,... | collective-permute-start | bytes 1179656 | tf_op jit(solution)/shard_map/ppermute | solution.py:348
  125.6 19.7 %collective-permute-start.25 = (bf16[256,768]{1,0:T(8,128)(2,1)S(1)}, bf16[256,768]{1,0:T(8,128)(2,1)S(1)}, u32[]{:S(2)}, u32[]{:S(2)}) collective-permute-start(bf16[256,768]{1,0:T(8,128)(2,1)S(1)} %add_convert_fusion.1.refs_3_), channel_id=1, source_target_pairs={{0,4},{4,0},{8,12},{12,8},{1,5},{5,1},{9,13},{13,9},{2,6},{6,2},{1... | collective-permute-start | bytes 1179656 | tf_op jit(solution)/shard_map/ppermute | solution.py:348
  125.6 21.4 %collective-permute-start.26 = (bf16[256,768]{1,0:T(8,128)(2,1)S(1)}, bf16[256,768]{1,0:T(8,128)(2,1)S(1)}, u32[]{:S(2)}, u32[]{:S(2)}) collective-permute-start(bf16[256,768]{1,0:T(8,128)(2,1)S(1)} %add_convert_fusion.refs_6_), channel_id=1, source_target_pairs={{0,12},{4,8},{8,4},{12,0},{1,13},{5,9},{9,5},{13,1},{2,14},{6,10},... | collective-permute-start | bytes 1179656 | tf_op jit(solution)/shard_map/ppermute | solution.py:348
  139.0 8.0 %collective-permute-start.28 = (bf16[256,768]{1,0:T(8,128)(2,1)S(1)}, bf16[256,768]{1,0:T(8,128)(2,1)S(1)}, u32[]{:S(2)}, u32[]{:S(2)}) collective-permute-start(bf16[256,768]{1,0:T(8,128)(2,1)S(1)} %shard_map.91._), channel_id=1, source_target_pairs={{0,1},{1,0},{2,3},{3,2},{4,5},{5,4},{6,7},{7,6},{8,9},{9,8},{10,11... | collective-permute-start | bytes 1179656 | tf_op jit(solution)/shard_map/ppermute | solution.py:348
  139.1 23.0 %collective-permute-start.27 = (bf16[256,768]{1,0:T(8,128)(2,1)S(1)}, bf16[256,768]{1,0:T(8,128)(2,1)S(1)}, u32[]{:S(2)}, u32[]{:S(2)}) collective-permute-start(bf16[256,768]{1,0:T(8,128)(2,1)S(1)} %shard_map.90.refs_6_), channel_id=1, source_target_pairs={{0,8},{4,12},{8,0},{12,4},{1,9},{5,13},{9,1},{13,5},{2,10},{6,14},... | collective-permute-start | bytes 1179656 | tf_op jit(solution)/shard_map/ppermute | solution.py:348
  162.5 6.8 %collective-permute-start.29 = (bf16[128,768]{1,0:T(8,128)(2,1)S(1)}, bf16[128,768]{1,0:T(8,128)(2,1)S(1)}, u32[]{:S(2)}, u32[]{:S(2)}) collective-permute-start(bf16[128,768]{1,0:T(8,128)(2,1)S(1)} %slice.72), channel_id=1, source_target_pairs={{0,2},{1,3},{2,0},{3,1},{4,6},{5,7},{6,4},{7,5},{8,10},{9,11},{10,... | collective-permute-start | bytes 589832 | tf_op jit(solution)/shard_map/ppermute | solution.py:348
  (3 other events, 10.0 us)

commit v7 on v6

--- a/solution.py
+++ b/solution.py
@@ -124,42 +124,51 @@
     return [(wanted == codes[e : e + 1, :]).astype(F32) for e in range(count)]
 
 
-def first_kernel(units, picks, place, *refs):
-    feeds, refs = refs[:units], refs[units:]
-    own, other, _, part, code, gate, packed = refs
+def first_kernel(feed_count, tokens, picks, place, *refs):
+    feeds, refs = refs[:feed_count], refs[feed_count:]
+    own, other, _, part, code, gate, *pair, packed = refs
     local, rows, half = packed.shape
-    slots = rows // (2 * units)
-    tokens = feeds[0].shape[0] // 2 - META
+    block_counts = [feed.shape[0] // (tokens + META) for feed in feeds]
+    for unit in pair:
+        for b, feed in enumerate(feeds):
+            at = len(feeds) * tokens + b * META
+            unit[b * tokens : (b + 1) * tokens, :] = feed[0:tokens, :]
+            unit[at : at + META, :] = feed[tokens:, :]
+    slots = rows // sum(block_counts)
     before = (
         lax.broadcasted_iota(jnp.int32, (tokens, tokens), 0)
         < lax.broadcasted_iota(jnp.int32, (tokens, tokens), 1)
     ).astype(F32).astype(BF16)
     expert = (lax.broadcasted_iota(jnp.int32, (local, tokens), 0) + place[2]).astype(F32)
-    for u in range(units):
-        for b in range(2):
-            at = 2 * tokens + b * META
-            table = feeds[u][at : at + META, 0 : 3 * tokens].astype(F32)
-            named = jnp.zeros((local, tokens), F32)
-            weight = jnp.zeros((local, tokens), F32)
-            for k in range(picks):
-                same = table[k : k + 1, 0:tokens] == expert
-                value = table[k : k + 1, tokens : 2 * tokens] + table[k : k + 1, 2 * tokens :]
-                named = jnp.where(same, 1.0, named)
-                weight = jnp.where(same, value, weight)
-            rank = dot(named.astype(BF16), before)
-            turn = place[1] if b == 0 else 1 - place[1]
-            base = ((2 * u + turn) * slots).astype(F32)
-            column = (2 * u + b) * tokens
-            code[:, column : column + tokens] = jnp.where(named > 0, rank + base, -1.0)
-            gate[:, column : column + tokens] = weight
+    tables = [
+        feed[count * tokens + b * META : count * tokens + (b + 1) * META, 0 : 3 * tokens]
+        for feed, count in zip(feeds, block_counts)
+        for b in range(count)
+    ]
+    for i, table in enumerate(tables):
+        table = table.astype(F32)
+        named = jnp.zeros((local, tokens), F32)
+        weight = jnp.zeros((local, tokens), F32)
+        for k in range(picks):
+            same = table[k : k + 1, 0:tokens] == expert
+            value = table[k : k + 1, tokens : 2 * tokens] + table[k : k + 1, 2 * tokens :]
+            named = jnp.where(same, 1.0, named)
+            weight = jnp.where(same, value, weight)
+        rank = dot(named.astype(BF16), before)
+        turn = 1 - place[1] if i % 2 else place[1]
+        base = ((i - i % 2 + turn) * slots).astype(F32)
+        column = i * tokens
+        code[:, column : column + tokens] = jnp.where(named > 0, rank + base, -1.0)
+        gate[:, column : column + tokens] = weight
     pick = jnp.concatenate(selection(code[...], rows), axis=0).astype(BF16)
     wide = half // 3 if half % 384 == 0 else half
     for n in range(half // wide):
         columns = slice(n * wide, (n + 1) * wide)
-        chosen = sum(
-            dot(pick[:, 2 * u * tokens : 2 * (u + 1) * tokens], feeds[u][0 : 2 * tokens, columns])
-            for u in range(units)
-        )
+        chosen, column = 0.0, 0
+        for feed, count in zip(feeds, block_counts):
+            held = slice(column, column + count * tokens)
+            chosen += dot(pick[:, held], feed[0 : count * tokens, columns])
+            column += count * tokens
         for e in range(local):
             packed[e, :, columns] = chosen[e * rows : (e + 1) * rows].astype(BF16)
 
@@ -231,26 +240,26 @@
 HBM = pl.BlockSpec(memory_space=pltpu.HBM)
 GRANT = 24 << 20
 GIVE_GRANTS = (46 << 20, 42 << 20, 42 << 20)
-SECOND_GRANT = 36 << 20
+SECOND_GRANT = 35 << 20
 
 
 def granted(size=GRANT):
     return pltpu.CompilerParams(vmem_limit_bytes=size)
 
 
-def first_stage(feeds, place, own, other, after, picks):
-    units = len(feeds)
+def first_stage(feeds, tokens, place, own, other, after, picks):
     local, quarter, hidden = other.shape
     half = 2 * quarter
-    tokens = feeds[0].shape[0] // 2 - META
-    rows = 2 * units * CAP
-    table = jax.ShapeDtypeStruct((local, 2 * units * tokens), F32)
+    blocks = sum(feed.shape[0] for feed in feeds) // (tokens + META)
+    rows = blocks * CAP
+    pair = [jax.ShapeDtypeStruct((blocks * (tokens + META), half), BF16)] * (len(feeds) == blocks)
+    table = jax.ShapeDtypeStruct((local, blocks * tokens), F32)
     return pl.pallas_call(
-        functools.partial(first_kernel, units, picks),
-        in_specs=[SMEM] + [VMEM] * (units + 2) + [ANY],
-        out_specs=[VMEM] * 3,
+        functools.partial(first_kernel, len(feeds), tokens, picks),
+        in_specs=[SMEM] + [VMEM] * (len(feeds) + 2) + [ANY],
+        out_specs=[VMEM] * (3 + len(pair)),
         scratch_shapes=[pltpu.VMEM((local, rows, half), BF16)],
-        out_shape=[jax.ShapeDtypeStruct((local, rows, hidden), BF16), table, table],
+        out_shape=[jax.ShapeDtypeStruct((local, rows, hidden), BF16), table, table, *pair],
         compiler_params=granted(),
         cost_estimate=cost(KERNEL_FLOPS, 2 * local * half * hidden),
     )(place, *feeds, own, other, after)
@@ -366,9 +375,8 @@
     peer = cross(theirs)
     own_in = take(expert_in, True, mine, GIVE_GRANTS[1])
     far = far_groups(groups)
-    unit = pair_up(mine, peer, rows)
-    near = pair_up(swap(mine, GROUP, 1), swap(peer, GROUP, 1), rows)
-    feeds = {"o": [unit], "n": [near], "l": [share(near)], "t": [share(unit)]}
+    feeds = {"o": [mine, peer]}
+    feeds["n"] = [swap(mine, GROUP, 1), swap(peer, GROUP, 1)]
     for g in far:
         if g % 2:
             early = swap(mine, GROUP, g)
@@ -384,9 +392,10 @@
 
     def first(g):
         nonlocal last
-        part, code, gate = first_stage(feeds[g], place, own_in, other_in, last, picks)
+        part, code, gate, *pair = first_stage(feeds[g], rows, place, own_in, other_in, last, picks)
         firsts[g] = (part, code, gate, cross(part))
         last = code
+        return pair
 
     def second(g):
         nonlocal last, own_out
@@ -394,7 +403,7 @@
         load = own_out is None
         keep, send, join = g not in "ltm2", g not in "on2", g == "2"
         outs = second_stage(
-            len(feeds[g]), code, gate, part, across, place, expert_out if load else own_out,
+            code.shape[1] // (2 * rows), code, gate, part, across, place, expert_out if load else own_out,
             other_out, kept["m"] if join else last, keep, send, join, load,
         )
         last = outs[0]
@@ -415,13 +424,15 @@
             came = swap(last, GROUP, 1 if g == "l" else int(g)).astype(F32)
         sums.append(came)
 
-    first("o")
+    (unit,) = first("o")
+    feeds["t"] = [share(unit)]
     last = give_out = take(expert_out, False, last, GIVE_GRANTS[2])
     other_out = share(give_out)
     other_shared_in = share(shared_in)
     other_shared_out = share(shared_out)
     tail = [str(g) for g in far[:-1]] + ["m", "2"] * bool(far)
-    first("n")
+    (near,) = first("n")
+    feeds["l"] = [share(near)]
     first("l")
     second("o")
     for g in tail[:1]:

time: 170 us -> 173 us (1.018)
  starting transfers between devices: 28 us -> 31 us
    ppermute x30, starting transfers between devices: 28 us -> 31 us  [swap(): lax.ppermute(value, axis, [(i, i ^ mask) for i in range(lax.axis_size(axi...]
where the time goes in v7:
time: 173 us
  waiting for transfers between devices  83.3 us (48%)
  Pallas kernels  57.3 us (33%)
  starting transfers between devices  31 us (18%)
    ppermute x30, waiting for transfers between devices, swap(): lax.ppermute(value, axis, [(i, i ^ mask) for i in range(lax.axis_size(axi...  83.3 us
    ppermute x30, starting transfers between devices, swap(): lax.ppermute(value, axis, [(i, i ^ mask) for i in range(lax.axis_size(axi...  31 us
    pallas_call x7, Pallas kernels, second_stage(): pl.pallas_call(functools.partial(second_kernel, units, keep, send, join,...  23 us
    pallas_call x7, Pallas kernels, first_stage(): pl.pallas_call(functools.partial(first_kernel, len(feeds), tokens, picks)...  22.3 us
    pallas_call x3, Pallas kernels, take_stage(): pl.pallas_call(functools.partial(take_kernel, own), in_specs=[SMEM, HBM,...  8.77 us
  transfers between devices with their start and end apart: 30, of which 17 were waited for; matrix products, arithmetic and copies ran while one was open for 0% of the time, Pallas kernels for 26%

profile of v7, /device:TPU:0, one launch (start us, length us, event | category | flops | bytes accessed | tf_op | source)
XLA Modules:
  0.0 173.3 jit_solution(6505852873669149864)
XLA Ops:
  0.1 2.9 %shard_map.73._ = bf16[8,384,768]{2,1,0:T(8,128)(2,1)S(1)} custom-call(s32[3]{0:T(128)S(1)} %pad_add_fusion.place.after, bf16[16,384,768]{2,1,0:T(8,128)(2,1)} %source.4, s32[3]{0:T(128)S(1)} %pad_add_fusion.place.after), custom_call_target="tpu_custom_call" | custom-call | flops 10000000 | bytes 9437184 | tf_op jit(solution)/shard_map/pallas_call | solution.py:321
  7.0 2.9 %shard_map.75.refs_2_.refs_4_.refs_1_ = bf16[8,384,768]{2,1,0:T(8,128)(2,1)S(1)} custom-call(s32[3]{0:T(128)S(1)} %pad_add_fusion.place.after, bf16[16,384,768]{2,1,0:T(8,128)(2,1)} %source.4, bf16[136,768]{1,0:T(8,128)(2,1)S(1)} %get-tuple-element.34.after.refs_0_), custom_call_target="tpu_custom_call" | custom-call | flops 10000000 | bytes 9437184 | tf_op jit(solution)/shard_map/pallas_call | solution.py:321
  9.9 2.9 %collective-permute-done.refs_1_ = bf16[136,768]{1,0:T(8,128)(2,1)S(1)} collective-permute-done((bf16[136,768]{1,0:T(8,128)(2,1)S(1)}, bf16[136,768]{1,0:T(8,128)(2,1)S(1)}, u32[]{:S(2)}, u32[]{:S(2)}) %collective-permute-start) | collective-permute-done | bytes 208928 | tf_op jit(solution)/shard_map/ppermute | solution.py:357
  12.8 3.2 %shard_map.76 = (bf16[8,40,768]{2,1,0:T(8,128)(2,1)S(1)}, f32[8,256]{1,0:T(8,128)S(1)}, f32[8,256]{1,0:T(8,128)S(1)}, bf16[272,768]{1,0:T(8,128)(2,1)S(1)}) custom-call(s32[3]{0:T(128)S(1)} %pad_add_fusion.place.after, bf16[136,768]{1,0:T(8,128)(2,1)S(1)} %get-tuple-element.34.after.refs_0_, bf16[136,768]{1,0:T(8,128)(2,1)S(1)} %collective-permute-done.refs_1_, ...), custom_call_target="tpu_custom_call" | custom-call | flops 10000000 | bytes 9437184 | tf_op jit(solution)/shard_map/pallas_call | solution.py:257
  16.0 2.9 %shard_map.77.refs_4_ = bf16[8,768,384]{2,1,0:T(8,128)(2,1)S(1)} custom-call(s32[3]{0:T(128)S(1)} %pad_add_fusion.place.after, bf16[16,768,384]{2,1,0:T(8,128)(2,1)} %refs_4_.1, f32[8,256]{1,0:T(8,128)S(1)} %get-tuple-element.37.after.refs_0_), custom_call_target="tpu_custom_call" | custom-call | flops 10000000 | bytes 9437184 | tf_op jit(solution)/shard_map/pallas_call | solution.py:321
  21.1 3.8 %collective-permute-start.4 = (bf16[136,768]{1,0:T(8,128)(2,1)S(1)}, bf16[136,768]{1,0:T(8,128)(2,1)S(1)}, u32[]{:S(2)}, u32[]{:S(2)}) collective-permute-start(bf16[136,768]{1,0:T(8,128)(2,1)S(1)} %get-tuple-element.34.after.refs_0_), channel_id=1, source_target_pairs={{0,12},{4,8},{8,4},{12,0},{1,13},{5,9},{9,5},{13,1},{2,14},{6,10},... | collective-permute-start | bytes 626696 | tf_op jit(solution)/shard_map/ppermute | solution.py:357
  27.1 4.0 %collective-permute-done.9.refs_1_ = bf16[136,768]{1,0:T(8,128)(2,1)S(1)} collective-permute-done((bf16[136,768]{1,0:T(8,128)(2,1)S(1)}, bf16[136,768]{1,0:T(8,128)(2,1)S(1)}, u32[]{:S(2)}, u32[]{:S(2)}) %collective-permute-start.9) | collective-permute-done | bytes 208928 | tf_op jit(solution)/shard_map/ppermute | solution.py:357
  31.2 3.2 %shard_map.78 = (bf16[8,40,768]{2,1,0:T(8,128)(2,1)S(1)}, f32[8,256]{1,0:T(8,128)S(1)}, f32[8,256]{1,0:T(8,128)S(1)}, bf16[272,768]{1,0:T(8,128)(2,1)S(1)}) custom-call(s32[3]{0:T(128)S(1)} %pad_add_fusion.place.after, bf16[136,768]{1,0:T(8,128)(2,1)S(1)} %collective-permute-done.8.refs_0_, bf16[136,768]{1,0:T(8,128)(2,1)S(1)} %collective-permute-done.9.refs_1_, ...), custom_call_target="tpu_custom_call" | custom-call | flops 10000000 | bytes 9437184 | tf_op jit(solution)/shard_map/pallas_call | solution.py:257
  34.5 4.0 %collective-permute-done.4 = bf16[136,768]{1,0:T(8,128)(2,1)S(1)} collective-permute-done((bf16[136,768]{1,0:T(8,128)(2,1)S(1)}, bf16[136,768]{1,0:T(8,128)(2,1)S(1)}, u32[]{:S(2)}, u32[]{:S(2)}) %collective-permute-start.4) | collective-permute-done | bytes 208928 | tf_op jit(solution)/shard_map/ppermute | solution.py:357
  38.5 3.9 %collective-permute-done.5 = bf16[136,768]{1,0:T(8,128)(2,1)S(1)} collective-permute-done((bf16[136,768]{1,0:T(8,128)(2,1)S(1)}, bf16[136,768]{1,0:T(8,128)(2,1)S(1)}, u32[]{:S(2)}, u32[]{:S(2)}) %collective-permute-start.5) | collective-permute-done | bytes 208928 | tf_op jit(solution)/shard_map/ppermute | solution.py:357
  44.7 3.1 %shard_map.79 = (bf16[8,40,768]{2,1,0:T(8,128)(2,1)S(1)}, f32[8,256]{1,0:T(8,128)S(1)}, f32[8,256]{1,0:T(8,128)S(1)}) custom-call(s32[3]{0:T(128)S(1)} %pad_add_fusion.place.after, bf16[272,768]{1,0:T(8,128)(2,1)S(1)} %collective-permute-done.13.refs_0_, bf16[8,384,768]{2,1,0:T(8,128)(2,1)S(1)} %shard_map.75.refs_2_.refs_4_.refs_1_, ...), custom_call_target="tpu_custom_call" | custom-call | flops 10000000 | bytes 9437184 | tf_op jit(solution)/shard_map/pallas_call | solution.py:257
  49.3 7.3 %collective-permute-done.11.refs_3_ = bf16[8,40,768]{2,1,0:T(8,128)(2,1)S(1)} collective-permute-done((bf16[8,40,768]{2,1,0:T(8,128)(2,1)S(1)}, bf16[8,40,768]{2,1,0:T(8,128)(2,1)S(1)}, u32[]{:S(2)}, u32[]{:S(2)}) %collective-permute-start.11) | collective-permute-done | bytes 491552 | tf_op jit(solution)/shard_map/ppermute | solution.py:357
  56.6 4.9 %shard_map.80 = (f32[256,768]{1,0:T(8,128)S(1)}, bf16[8,768,384]{2,1,0:T(8,128)(2,1)S(1)}) custom-call(s32[3]{0:T(128)S(1)} %pad_add_fusion.place.after, f32[8,256]{1,0:T(8,128)S(1)} %get-tuple-element.37.after.refs_0_, f32[8,256]{1,0:T(8,128)S(1)} %get-tuple-element.41.refs_1_, bf16[8,40,768]{2,1,0:T(8,128)(2,1)S(1)} %get-tuple-element.42.refs_2_, ...), custom_call_target="tpu_custom_call" | custom-call | flops 10000000 | bytes 9437184 | tf_op jit(solution)/shard_map/pallas_call | solution.py:280
  61.5 3.6 %shard_map.81 = (bf16[8,80,768]{2,1,0:T(8,128)(2,1)S(1)}, f32[8,512]{1,0:T(8,128)S(1)}, f32[8,512]{1,0:T(8,128)S(1)}) custom-call(s32[3]{0:T(128)S(1)} %pad_add_fusion.place.after, bf16[272,768]{1,0:T(8,128)(2,1)S(1)} %pad_maximum_fusion.refs_0_, bf16[272,768]{1,0:T(8,128)(2,1)S(1)} %collective-permute-done.14.refs_1_, ...), custom_call_target="tpu_custom_call" | custom-call | flops 10000000 | bytes 9437184 | tf_op jit(solution)/shard_map/pallas_call | solution.py:257
  67.6 2.9 %shard_map.82.refs_6_ = f32[256,768]{1,0:T(8,128)S(1)} custom-call(s32[3]{0:T(128)S(1)} %pad_add_fusion.place.after, f32[8,256]{1,0:T(8,128)S(1)} %get-tuple-element.38.refs_3_.refs_0_, f32[8,256]{1,0:T(8,128)S(1)} %get-tuple-element.39.refs_1_, bf16[8,40,768]{2,1,0:T(8,128)(2,1)S(1)} %get-tuple-element.40.refs_2_, ...), custom_call_target="tpu_custom_call" | custom-call | flops 10000000 | bytes 9437184 | tf_op jit(solution)/shard_map/pallas_call | solution.py:280
  70.5 7.2 %collective-permute-done.15.refs_3_ = bf16[8,40,768]{2,1,0:T(8,128)(2,1)S(1)} collective-permute-done((bf16[8,40,768]{2,1,0:T(8,128)(2,1)S(1)}, bf16[8,40,768]{2,1,0:T(8,128)(2,1)S(1)}, u32[]{:S(2)}, u32[]{:S(2)}) %collective-permute-start.15) | collective-permute-done | bytes 491552 | tf_op jit(solution)/shard_map/ppermute | solution.py:357
  77.7 2.9 %shard_map.83 = bf16[256,768]{1,0:T(8,128)(2,1)S(1)} custom-call(s32[3]{0:T(128)S(1)} %pad_add_fusion.place.after, f32[8,256]{1,0:T(8,128)S(1)} %get-tuple-element.44.refs_6_.refs_0_, f32[8,256]{1,0:T(8,128)S(1)} %get-tuple-element.48.refs_1_, bf16[8,40,768]{2,1,0:T(8,128)(2,1)S(1)} %get-tuple-element.49.refs_2_, ...), custom_call_target="tpu_custom_call" | custom-call | flops 10000000 | bytes 9437184 | tf_op jit(solution)/shard_map/pallas_call | solution.py:280
  83.8 3.1 %shard_map.84 = (bf16[8,40,768]{2,1,0:T(8,128)(2,1)S(1)}, f32[8,256]{1,0:T(8,128)S(1)}, f32[8,256]{1,0:T(8,128)S(1)}) custom-call(s32[3]{0:T(128)S(1)} %pad_add_fusion.place.after, bf16[272,768]{1,0:T(8,128)(2,1)S(1)} %collective-permute-done.7.refs_0_, bf16[8,384,768]{2,1,0:T(8,128)(2,1)S(1)} %shard_map.75.refs_2_.refs_4_.refs_1_, ...), custom_call_target="tpu_custom_call" | custom-call | flops 10000000 | bytes 9437184 | tf_op jit(solution)/shard_map/pallas_call | solution.py:257
  86.9 3.1 %shard_map.85 = (bf16[8,40,768]{2,1,0:T(8,128)(2,1)S(1)}, f32[8,256]{1,0:T(8,128)S(1)}, f32[8,256]{1,0:T(8,128)S(1)}) custom-call(s32[3]{0:T(128)S(1)} %pad_add_fusion.place.after, bf16[272,768]{1,0:T(8,128)(2,1)S(1)} %collective-permute-done.6.refs_0_, bf16[8,384,768]{2,1,0:T(8,128)(2,1)S(1)} %shard_map.75.refs_2_.refs_4_.refs_1_, ...), custom_call_target="tpu_custom_call" | custom-call | flops 10000000 | bytes 9437184 | tf_op jit(solution)/shard_map/pallas_call | solution.py:257
  89.9 3.1 %shard_map.86 = (bf16[8,40,768]{2,1,0:T(8,128)(2,1)S(1)}, f32[8,256]{1,0:T(8,128)S(1)}, f32[8,256]{1,0:T(8,128)S(1)}) custom-call(s32[3]{0:T(128)S(1)} %pad_add_fusion.place.after, bf16[272,768]{1,0:T(8,128)(2,1)S(1)} %collective-permute-done.3.refs_0_, bf16[8,384,768]{2,1,0:T(8,128)(2,1)S(1)} %shard_map.75.refs_2_.refs_4_.refs_1_, ...), custom_call_target="tpu_custom_call" | custom-call | flops 10000000 | bytes 9437184 | tf_op jit(solution)/shard_map/pallas_call | solution.py:257
  94.2 3.1 %collective-permute-done.22.refs_3_ = bf16[8,80,768]{2,1,0:T(8,128)(2,1)S(1)} collective-permute-done((bf16[8,80,768]{2,1,0:T(8,128)(2,1)S(1)}, bf16[8,80,768]{2,1,0:T(8,128)(2,1)S(1)}, u32[]{:S(2)}, u32[]{:S(2)}) %collective-permute-start.22) | collective-permute-done | bytes 983072 | tf_op jit(solution)/shard_map/ppermute | solution.py:357
  97.3 3.6 %shard_map.88 = (f32[256,768]{1,0:T(8,128)S(1)}, bf16[256,768]{1,0:T(8,128)(2,1)S(1)}) custom-call(s32[3]{0:T(128)S(1)} %pad_add_fusion.place.after, f32[8,512]{1,0:T(8,128)S(1)} %get-tuple-element.47.refs_6_.refs_0_, f32[8,512]{1,0:T(8,128)S(1)} %get-tuple-element.59.refs_1_, bf16[8,80,768]{2,1,0:T(8,128)(2,1)S(1)} %get-tuple-element.60.refs_2_, ...), custom_call_target="tpu_custom_call" | custom-call | flops 10000000 | bytes 9437184 | tf_op jit(solution)/shard_map/pallas_call | solution.py:280
  104.8 10.3 %collective-permute-done.21.refs_3_ = bf16[8,40,768]{2,1,0:T(8,128)(2,1)S(1)} collective-permute-done((bf16[8,40,768]{2,1,0:T(8,128)(2,1)S(1)}, bf16[8,40,768]{2,1,0:T(8,128)(2,1)S(1)}, u32[]{:S(2)}, u32[]{:S(2)}) %collective-permute-start.21) | collective-permute-done | bytes 491552 | tf_op jit(solution)/shard_map/ppermute | solution.py:357
  115.2 2.9 %shard_map.89 = bf16[256,768]{1,0:T(8,128)(2,1)S(1)} custom-call(s32[3]{0:T(128)S(1)} %pad_add_fusion.place.after, f32[8,256]{1,0:T(8,128)S(1)} %get-tuple-element.50.refs_3_.refs_0_, f32[8,256]{1,0:T(8,128)S(1)} %get-tuple-element.57.refs_1_, bf16[8,40,768]{2,1,0:T(8,128)(2,1)S(1)} %get-tuple-element.58.refs_2_, ...), custom_call_target="tpu_custom_call" | custom-call | flops 10000000 | bytes 9437184 | tf_op jit(solution)/shard_map/pallas_call | solution.py:280
  119.7 6.0 %collective-permute-done.20.refs_3_ = bf16[8,40,768]{2,1,0:T(8,128)(2,1)S(1)} collective-permute-done((bf16[8,40,768]{2,1,0:T(8,128)(2,1)S(1)}, bf16[8,40,768]{2,1,0:T(8,128)(2,1)S(1)}, u32[]{:S(2)}, u32[]{:S(2)}) %collective-permute-start.20) | collective-permute-done | bytes 491552 | tf_op jit(solution)/shard_map/ppermute | solution.py:357
  125.7 5.8 %collective-permute-start.26 = (bf16[256,768]{1,0:T(8,128)(2,1)S(1)}, bf16[256,768]{1,0:T(8,128)(2,1)S(1)}, u32[]{:S(2)}, u32[]{:S(2)}) collective-permute-start(bf16[256,768]{1,0:T(8,128)(2,1)S(1)} %add_convert_fusion.refs_6_), channel_id=1, source_target_pairs={{0,12},{4,8},{8,4},{12,0},{1,13},{5,9},{9,5},{13,1},{2,14},{6,10},... | collective-permute-start | bytes 1179656 | tf_op jit(solution)/shard_map/ppermute | solution.py:357
  131.5 2.9 %shard_map.90.refs_6_ = bf16[256,768]{1,0:T(8,128)(2,1)S(1)} custom-call(s32[3]{0:T(128)S(1)} %pad_add_fusion.place.after, f32[8,256]{1,0:T(8,128)S(1)} %get-tuple-element.51.refs_3_.refs_0_, f32[8,256]{1,0:T(8,128)S(1)} %get-tuple-element.55.refs_1_, bf16[8,40,768]{2,1,0:T(8,128)(2,1)S(1)} %get-tuple-element.56.refs_2_, ...), custom_call_target="tpu_custom_call" | custom-call | flops 10000000 | bytes 9437184 | tf_op jit(solution)/shard_map/pallas_call | solution.py:280
  136.2 2.9 %shard_map.91._ = bf16[256,768]{1,0:T(8,128)(2,1)S(1)} custom-call(s32[3]{0:T(128)S(1)} %pad_add_fusion.place.after, f32[8,256]{1,0:T(8,128)S(1)} %get-tuple-element.52._.refs_0_, f32[8,256]{1,0:T(8,128)S(1)} %get-tuple-element.53.refs_1_, bf16[8,40,768]{2,1,0:T(8,128)(2,1)S(1)} %get-tuple-element.54.refs_2_, ...), custom_call_target="tpu_custom_call" | custom-call | flops 10000000 | bytes 9437184 | tf_op jit(solution)/shard_map/pallas_call | solution.py:280
  140.7 3.4 %collective-permute-done.17.far = bf16[256,768]{1,0:T(8,128)(2,1)S(1)} collective-permute-done((bf16[256,768]{1,0:T(8,128)(2,1)S(1)}, bf16[256,768]{1,0:T(8,128)(2,1)S(1)}, u32[]{:S(2)}, u32[]{:S(2)}) %collective-permute-start.17) | collective-permute-done | bytes 393248 | tf_op jit(solution)/shard_map/ppermute | solution.py:357
  145.4 4.6 %collective-permute-done.26 = bf16[256,768]{1,0:T(8,128)(2,1)S(1)} collective-permute-done((bf16[256,768]{1,0:T(8,128)(2,1)S(1)}, bf16[256,768]{1,0:T(8,128)(2,1)S(1)}, u32[]{:S(2)}, u32[]{:S(2)}) %collective-permute-start.26) | collective-permute-done | bytes 393248 | tf_op jit(solution)/shard_map/ppermute | solution.py:357
  150.0 15.4 %collective-permute-done.27 = bf16[256,768]{1,0:T(8,128)(2,1)S(1)} collective-permute-done((bf16[256,768]{1,0:T(8,128)(2,1)S(1)}, bf16[256,768]{1,0:T(8,128)(2,1)S(1)}, u32[]{:S(2)}, u32[]{:S(2)}) %collective-permute-start.27) | collective-permute-done | bytes 393248 | tf_op jit(solution)/shard_map/ppermute | solution.py:357
  167.2 5.2 %collective-permute-done.29 = bf16[128,768]{1,0:T(8,128)(2,1)S(1)} collective-permute-done((bf16[128,768]{1,0:T(8,128)(2,1)S(1)}, bf16[128,768]{1,0:T(8,128)(2,1)S(1)}, u32[]{:S(2)}, u32[]{:S(2)}) %collective-permute-start.29) | collective-permute-done | bytes 196640 | tf_op jit(solution)/shard_map/ppermute | solution.py:357
  (70 shorter events, 32.0 us)
Async XLA Ops:
  0.1 3.5 %copy-start.4 = (f32[128,8]{0,1:T(8,128)S(1)}, f32[128,8]{0,1:T(8,128)}, u32[]{:S(2)}) copy-start(f32[128,8]{0,1:T(8,128)} %param.9) | copy-start | bytes 12292
  3.0 9.8 %collective-permute-start.1 = (bf16[8,384,768]{2,1,0:T(8,128)(2,1)S(1)}, bf16[8,384,768]{2,1,0:T(8,128)(2,1)S(1)}, u32[]{:S(2)}, u32[]{:S(2)}) collective-permute-start(bf16[8,384,768]{2,1,0:T(8,128)(2,1)S(1)} %shard_map.73._), channel_id=1, source_target_pairs={{0,1},{1,0},{2,3},{3,2},{4,5},{5,4},{6,7},{7,6},{8,9},{9,8},{10,11... | collective-permute-start | bytes 14155784 | tf_op jit(solution)/shard_map/ppermute | solution.py:357
  4.4 8.4 %collective-permute-start = (bf16[136,768]{1,0:T(8,128)(2,1)S(1)}, bf16[136,768]{1,0:T(8,128)(2,1)S(1)}, u32[]{:S(2)}, u32[]{:S(2)}) collective-permute-start(bf16[136,768]{1,0:T(8,128)(2,1)S(1)} %get-tuple-element.35), channel_id=1, source_target_pairs={{0,2},{1,3},{2,0},{3,1},{4,6},{5,7},{6,4},{7,5},{8,10},{9,11},{10,... | collective-permute-start | bytes 626696 | tf_op jit(solution)/shard_map/ppermute | solution.py:357
  19.0 37.6 %collective-permute-start.12 = (bf16[8,768,384]{2,1,0:T(8,128)(2,1)S(1)}, bf16[8,768,384]{2,1,0:T(8,128)(2,1)S(1)}, u32[]{:S(2)}, u32[]{:S(2)}) collective-permute-start(bf16[8,768,384]{2,1,0:T(8,128)(2,1)S(1)} %shard_map.77.refs_4_), channel_id=1, source_target_pairs={{0,1},{1,0},{2,3},{3,2},{4,5},{5,4},{6,7},{7,6},{8,9},{9,8},{10,11... | collective-permute-start | bytes 14155784 | tf_op jit(solution)/shard_map/ppermute | solution.py:357
  19.0 8.1 %collective-permute-start.8 = (bf16[136,768]{1,0:T(8,128)(2,1)S(1)}, bf16[136,768]{1,0:T(8,128)(2,1)S(1)}, u32[]{:S(2)}, u32[]{:S(2)}) collective-permute-start(bf16[136,768]{1,0:T(8,128)(2,1)S(1)} %get-tuple-element.34.after.refs_0_), channel_id=1, source_target_pairs={{0,4},{4,0},{8,12},{12,8},{1,5},{5,1},{9,13},{13,9},{2,6},{6,2},{1... | collective-permute-start | bytes 626696 | tf_op jit(solution)/shard_map/ppermute | solution.py:357
  20.9 10.2 %collective-permute-start.9 = (bf16[136,768]{1,0:T(8,128)(2,1)S(1)}, bf16[136,768]{1,0:T(8,128)(2,1)S(1)}, u32[]{:S(2)}, u32[]{:S(2)}) collective-permute-start(bf16[136,768]{1,0:T(8,128)(2,1)S(1)} %collective-permute-done.refs_1_), channel_id=1, source_target_pairs={{0,4},{4,0},{8,12},{12,8},{1,5},{5,1},{9,13},{13,9},{2,6},{6,2},{1... | collective-permute-start | bytes 626696 | tf_op jit(solution)/shard_map/ppermute | solution.py:357
  21.1 17.3 %collective-permute-start.4 = (bf16[136,768]{1,0:T(8,128)(2,1)S(1)}, bf16[136,768]{1,0:T(8,128)(2,1)S(1)}, u32[]{:S(2)}, u32[]{:S(2)}) collective-permute-start(bf16[136,768]{1,0:T(8,128)(2,1)S(1)} %get-tuple-element.34.after.refs_0_), channel_id=1, source_target_pairs={{0,12},{4,8},{8,4},{12,0},{1,13},{5,9},{9,5},{13,1},{2,14},{6,10},... | collective-permute-start | bytes 626696 | tf_op jit(solution)/shard_map/ppermute | solution.py:357
  25.0 17.4 %collective-permute-start.5 = (bf16[136,768]{1,0:T(8,128)(2,1)S(1)}, bf16[136,768]{1,0:T(8,128)(2,1)S(1)}, u32[]{:S(2)}, u32[]{:S(2)}) collective-permute-start(bf16[136,768]{1,0:T(8,128)(2,1)S(1)} %collective-permute-done.refs_1_), channel_id=1, source_target_pairs={{0,12},{4,8},{8,4},{12,0},{1,13},{5,9},{9,5},{13,1},{2,14},{6,10},... | collective-permute-start | bytes 626696 | tf_op jit(solution)/shard_map/ppermute | solution.py:357
  34.4 10.3 %collective-permute-start.13 = (bf16[272,768]{1,0:T(8,128)(2,1)S(1)}, bf16[272,768]{1,0:T(8,128)(2,1)S(1)}, u32[]{:S(2)}, u32[]{:S(2)}) collective-permute-start(bf16[272,768]{1,0:T(8,128)(2,1)S(1)} %get-tuple-element.43), channel_id=1, source_target_pairs={{0,1},{1,0},{2,3},{3,2},{4,5},{5,4},{6,7},{7,6},{8,9},{9,8},{10,11... | collective-permute-start | bytes 1253384 | tf_op jit(solution)/shard_map/ppermute | solution.py:357
  42.4 14.2 %collective-permute-start.11 = (bf16[8,40,768]{2,1,0:T(8,128)(2,1)S(1)}, bf16[8,40,768]{2,1,0:T(8,128)(2,1)S(1)}, u32[]{:S(2)}, u32[]{:S(2)}) collective-permute-start(bf16[8,40,768]{2,1,0:T(8,128)(2,1)S(1)} %get-tuple-element.42.refs_2_), channel_id=1, source_target_pairs={{0,2},{1,3},{2,0},{3,1},{4,6},{5,7},{6,4},{7,5},{8,10},{9,11},{10,... | collective-permute-start | bytes 1474568 | tf_op jit(solution)/shard_map/ppermute | solution.py:357
  44.0 17.5 %collective-permute-start.14 = (bf16[272,768]{1,0:T(8,128)(2,1)S(1)}, bf16[272,768]{1,0:T(8,128)(2,1)S(1)}, u32[]{:S(2)}, u32[]{:S(2)}) collective-permute-start(bf16[272,768]{1,0:T(8,128)(2,1)S(1)} %pad_maximum_fusion.refs_0_), channel_id=1, source_target_pairs={{0,1},{1,0},{2,3},{3,2},{4,5},{5,4},{6,7},{7,6},{8,9},{9,8},{10,11... | collective-permute-start | bytes 1253384 | tf_op jit(solution)/shard_map/ppermute | solution.py:357
  44.1 23.5 %collective-permute-start.10 = (bf16[8,40,768]{2,1,0:T(8,128)(2,1)S(1)}, bf16[8,40,768]{2,1,0:T(8,128)(2,1)S(1)}, u32[]{:S(2)}, u32[]{:S(2)}) collective-permute-start(bf16[8,40,768]{2,1,0:T(8,128)(2,1)S(1)} %get-tuple-element.40.refs_2_), channel_id=1, source_target_pairs={{0,2},{1,3},{2,0},{3,1},{4,6},{5,7},{6,4},{7,5},{8,10},{9,11},{10,... | collective-permute-start | bytes 1474568 | tf_op jit(solution)/shard_map/ppermute | solution.py:357
  47.8 29.9 %collective-permute-start.15 = (bf16[8,40,768]{2,1,0:T(8,128)(2,1)S(1)}, bf16[8,40,768]{2,1,0:T(8,128)(2,1)S(1)}, u32[]{:S(2)}, u32[]{:S(2)}) collective-permute-start(bf16[8,40,768]{2,1,0:T(8,128)(2,1)S(1)} %get-tuple-element.49.refs_2_), channel_id=1, source_target_pairs={{0,2},{1,3},{2,0},{3,1},{4,6},{5,7},{6,4},{7,5},{8,10},{9,11},{10,... | collective-permute-start | bytes 1474568 | tf_op jit(solution)/shard_map/ppermute | solution.py:357
  65.1 32.2 %collective-permute-start.22 = (bf16[8,80,768]{2,1,0:T(8,128)(2,1)S(1)}, bf16[8,80,768]{2,1,0:T(8,128)(2,1)S(1)}, u32[]{:S(2)}, u32[]{:S(2)}) collective-permute-start(bf16[8,80,768]{2,1,0:T(8,128)(2,1)S(1)} %get-tuple-element.60.refs_2_), channel_id=1, source_target_pairs={{0,2},{1,3},{2,0},{3,1},{4,6},{5,7},{6,4},{7,5},{8,10},{9,11},{10,... | collective-permute-start | bytes 2949128 | tf_op jit(solution)/shard_map/ppermute | solution.py:357
  66.7 14.5 %collective-permute-start.6 = (bf16[272,768]{1,0:T(8,128)(2,1)S(1)}, bf16[272,768]{1,0:T(8,128)(2,1)S(1)}, u32[]{:S(2)}, u32[]{:S(2)}) collective-permute-start(bf16[272,768]{1,0:T(8,128)(2,1)S(1)} %pad_maximum_fusion.refs_0_), channel_id=1, source_target_pairs={{0,4},{4,0},{8,12},{12,8},{1,5},{5,1},{9,13},{13,9},{2,6},{6,2},{1... | collective-permute-start | bytes 1253384 | tf_op jit(solution)/shard_map/ppermute | solution.py:357
  80.6 1.8 %collective-permute-start.16 = (bf16[256,768]{1,0:T(8,128)(2,1)S(1)}, bf16[256,768]{1,0:T(8,128)(2,1)S(1)}, u32[]{:S(2)}, u32[]{:S(2)}) collective-permute-start(bf16[256,768]{1,0:T(8,128)(2,1)S(1)} %shard_map.83), channel_id=1, source_target_pairs={{0,1},{1,0},{2,3},{3,2},{4,5},{5,4},{6,7},{7,6},{8,9},{9,8},{10,11... | collective-permute-start | bytes 1179656 | tf_op jit(solution)/shard_map/ppermute | solution.py:357
  80.7 12.4 %collective-permute-start.2 = (bf16[384,768]{1,0:T(8,128)(2,1)S(1)}, bf16[384,768]{1,0:T(8,128)(2,1)S(1)}, u32[]{:S(2)}, u32[]{:S(2)}) collective-permute-start(bf16[384,768]{1,0:T(8,128)(2,1)S(1)} %copy-done.1), channel_id=1, source_target_pairs={{0,1},{1,0},{2,3},{3,2},{4,5},{5,4},{6,7},{7,6},{8,9},{9,8},{10,11... | collective-permute-start | bytes 1769480 | tf_op jit(solution)/shard_map/ppermute | solution.py:357
  81.1 2.6 %collective-permute-start.7 = (bf16[272,768]{1,0:T(8,128)(2,1)S(1)}, bf16[272,768]{1,0:T(8,128)(2,1)S(1)}, u32[]{:S(2)}, u32[]{:S(2)}) collective-permute-start(bf16[272,768]{1,0:T(8,128)(2,1)S(1)} %collective-permute-done.6.refs_0_), channel_id=1, source_target_pairs={{0,1},{1,0},{2,3},{3,2},{4,5},{5,4},{6,7},{7,6},{8,9},{9,8},{10,11... | collective-permute-start | bytes 1253384 | tf_op jit(solution)/shard_map/ppermute | solution.py:357
  81.2 8.7 %collective-permute-start.3 = (bf16[272,768]{1,0:T(8,128)(2,1)S(1)}, bf16[272,768]{1,0:T(8,128)(2,1)S(1)}, u32[]{:S(2)}, u32[]{:S(2)}) collective-permute-start(bf16[272,768]{1,0:T(8,128)(2,1)S(1)} %get-tuple-element.36.feed), channel_id=1, source_target_pairs={{0,1},{1,0},{2,3},{3,2},{4,5},{5,4},{6,7},{7,6},{8,9},{9,8},{10,11... | collective-permute-start | bytes 1253384 | tf_op jit(solution)/shard_map/ppermute | solution.py:357
  97.3 5.3 %copy-start.2 = (bf16[768,384]{1,0:T(8,128)(2,1)S(1)}, bf16[768,384]{1,0:T(8,128)(2,1)}, u32[]{:S(2)}) copy-start(bf16[768,384]{1,0:T(8,128)(2,1)} %own.3) | copy-start | bytes 1769476
  100.9 3.8 %collective-permute-start.23 = (bf16[256,768]{1,0:T(8,128)(2,1)S(1)}, bf16[256,768]{1,0:T(8,128)(2,1)S(1)}, u32[]{:S(2)}, u32[]{:S(2)}) collective-permute-start(bf16[256,768]{1,0:T(8,128)(2,1)S(1)} %get-tuple-element.62), channel_id=1, source_target_pairs={{0,1},{1,0},{2,3},{3,2},{4,5},{5,4},{6,7},{7,6},{8,9},{9,8},{10,11... | collective-permute-start | bytes 1179656 | tf_op jit(solution)/shard_map/ppermute | solution.py:357
  101.0 14.2 %collective-permute-start.21 = (bf16[8,40,768]{2,1,0:T(8,128)(2,1)S(1)}, bf16[8,40,768]{2,1,0:T(8,128)(2,1)S(1)}, u32[]{:S(2)}, u32[]{:S(2)}) collective-permute-start(bf16[8,40,768]{2,1,0:T(8,128)(2,1)S(1)} %get-tuple-element.58.refs_2_), channel_id=1, source_target_pairs={{0,2},{1,3},{2,0},{3,1},{4,6},{5,7},{6,4},{7,5},{8,10},{9,11},{10,... | collective-permute-start | bytes 1474568 | tf_op jit(solution)/shard_map/ppermute | solution.py:357
  102.6 36.6 %collective-permute-start.18 = (bf16[768,384]{1,0:T(8,128)(2,1)S(1)}, bf16[768,384]{1,0:T(8,128)(2,1)S(1)}, u32[]{:S(2)}, u32[]{:S(2)}) collective-permute-start(bf16[768,384]{1,0:T(8,128)(2,1)S(1)} %copy-done.2), channel_id=1, source_target_pairs={{0,1},{1,0},{2,3},{3,2},{4,5},{5,4},{6,7},{7,6},{8,9},{9,8},{10,11... | collective-permute-start | bytes 1769480 | tf_op jit(solution)/shard_map/ppermute | solution.py:357
  102.7 23.0 %collective-permute-start.20 = (bf16[8,40,768]{2,1,0:T(8,128)(2,1)S(1)}, bf16[8,40,768]{2,1,0:T(8,128)(2,1)S(1)}, u32[]{:S(2)}, u32[]{:S(2)}) collective-permute-start(bf16[8,40,768]{2,1,0:T(8,128)(2,1)S(1)} %get-tuple-element.56.refs_2_), channel_id=1, source_target_pairs={{0,2},{1,3},{2,0},{3,1},{4,6},{5,7},{6,4},{7,5},{8,10},{9,11},{10,... | collective-permute-start | bytes 1474568 | tf_op jit(solution)/shard_map/ppermute | solution.py:357
  103.3 33.0 %collective-permute-start.19 = (bf16[8,40,768]{2,1,0:T(8,128)(2,1)S(1)}, bf16[8,40,768]{2,1,0:T(8,128)(2,1)S(1)}, u32[]{:S(2)}, u32[]{:S(2)}) collective-permute-start(bf16[8,40,768]{2,1,0:T(8,128)(2,1)S(1)} %get-tuple-element.54.refs_2_), channel_id=1, source_target_pairs={{0,2},{1,3},{2,0},{3,1},{4,6},{5,7},{6,4},{7,5},{8,10},{9,11},{10,... | collective-permute-start | bytes 1474568 | tf_op jit(solution)/shard_map/ppermute | solution.py:357
  118.1 7.6 %collective-permute-start.24 = (bf16[256,768]{1,0:T(8,128)(2,1)S(1)}, bf16[256,768]{1,0:T(8,128)(2,1)S(1)}, u32[]{:S(2)}, u32[]{:S(2)}) collective-permute-start(bf16[256,768]{1,0:T(8,128)(2,1)S(1)} %shard_map.89), channel_id=1, source_target_pairs={{0,1},{1,0},{2,3},{3,2},{4,5},{5,4},{6,7},{7,6},{8,9},{9,8},{10,11... | collective-permute-start | bytes 1179656 | tf_op jit(solution)/shard_map/ppermute | solution.py:357
  118.2 26.0 %collective-permute-start.17 = (bf16[256,768]{1,0:T(8,128)(2,1)S(1)}, bf16[256,768]{1,0:T(8,128)(2,1)S(1)}, u32[]{:S(2)}, u32[]{:S(2)}) collective-permute-start(bf16[256,768]{1,0:T(8,128)(2,1)S(1)} %shard_map.87.refs_6_.near), channel_id=1, source_target_pairs={{0,2},{1,3},{2,0},{3,1},{4,6},{5,7},{6,4},{7,5},{8,10},{9,11},{10,... | collective-permute-start | bytes 1179656 | tf_op jit(solution)/shard_map/ppermute | solution.py:357
  125.7 19.7 %collective-permute-start.25 = (bf16[256,768]{1,0:T(8,128)(2,1)S(1)}, bf16[256,768]{1,0:T(8,128)(2,1)S(1)}, u32[]{:S(2)}, u32[]{:S(2)}) collective-permute-start(bf16[256,768]{1,0:T(8,128)(2,1)S(1)} %add_convert_fusion.1.refs_3_), channel_id=1, source_target_pairs={{0,4},{4,0},{8,12},{12,8},{1,5},{5,1},{9,13},{13,9},{2,6},{6,2},{1... | collective-permute-start | bytes 1179656 | tf_op jit(solution)/shard_map/ppermute | solution.py:357
  125.7 24.3 %collective-permute-start.26 = (bf16[256,768]{1,0:T(8,128)(2,1)S(1)}, bf16[256,768]{1,0:T(8,128)(2,1)S(1)}, u32[]{:S(2)}, u32[]{:S(2)}) collective-permute-start(bf16[256,768]{1,0:T(8,128)(2,1)S(1)} %add_convert_fusion.refs_6_), channel_id=1, source_target_pairs={{0,12},{4,8},{8,4},{12,0},{1,13},{5,9},{9,5},{13,1},{2,14},{6,10},... | collective-permute-start | bytes 1179656 | tf_op jit(solution)/shard_map/ppermute | solution.py:357
  139.1 10.9 %collective-permute-start.28 = (bf16[256,768]{1,0:T(8,128)(2,1)S(1)}, bf16[256,768]{1,0:T(8,128)(2,1)S(1)}, u32[]{:S(2)}, u32[]{:S(2)}) collective-permute-start(bf16[256,768]{1,0:T(8,128)(2,1)S(1)} %shard_map.91._), channel_id=1, source_target_pairs={{0,1},{1,0},{2,3},{3,2},{4,5},{5,4},{6,7},{7,6},{8,9},{9,8},{10,11... | collective-permute-start | bytes 1179656 | tf_op jit(solution)/shard_map/ppermute | solution.py:357
  139.2 26.2 %collective-permute-start.27 = (bf16[256,768]{1,0:T(8,128)(2,1)S(1)}, bf16[256,768]{1,0:T(8,128)(2,1)S(1)}, u32[]{:S(2)}, u32[]{:S(2)}) collective-permute-start(bf16[256,768]{1,0:T(8,128)(2,1)S(1)} %shard_map.90.refs_6_), channel_id=1, source_target_pairs={{0,8},{4,12},{8,0},{12,4},{1,9},{5,13},{9,1},{13,5},{2,10},{6,14},... | collective-permute-start | bytes 1179656 | tf_op jit(solution)/shard_map/ppermute | solution.py:357
  165.7 6.8 %collective-permute-start.29 = (bf16[128,768]{1,0:T(8,128)(2,1)S(1)}, bf16[128,768]{1,0:T(8,128)(2,1)S(1)}, u32[]{:S(2)}, u32[]{:S(2)}) collective-permute-start(bf16[128,768]{1,0:T(8,128)(2,1)S(1)} %slice.34), channel_id=1, source_target_pairs={{0,2},{1,3},{2,0},{3,1},{4,6},{5,7},{6,4},{7,5},{8,10},{9,11},{10,... | collective-permute-start | bytes 589832 | tf_op jit(solution)/shard_map/ppermute | solution.py:357
  (3 other events, 10.0 us)

commit v8 on v7

--- a/solution.py
+++ b/solution.py
@@ -9,6 +9,7 @@
 
 
 CAP = 20
+STEP = 4
 SWEEP, GROUP, SIDE = "sweep", "expert", "dp"
 F32 = jnp.float32
 BF16 = jnp.bfloat16
@@ -176,9 +177,9 @@
     here = pl.multiple_of(place[0] * quarter, quarter)
     there = pl.multiple_of((1 - place[0]) * quarter, quarter)
 
-    @pl.loop(0, local // 2)
-    def _(pair):
-        for e in (2 * pair, 2 * pair + 1):
+    @pl.loop(0, local // STEP)
+    def _(turn):
+        for e in [STEP * turn + i for i in range(STEP)]:
             total = dot(packed[e, :, pl.ds(here, quarter)], own[e])
             total += dot(packed[e, :, pl.ds(there, quarter)], other[e])
             part[e] = total.astype(BF16)
@@ -200,9 +201,9 @@
     there = pl.multiple_of((1 - place[0]) * quarter, quarter)
     wanted = lax.broadcasted_iota(jnp.int32, (rows, code.shape[1]), 0).astype(F32)
 
-    @pl.loop(0, local // 2)
-    def _(pair):
-        for e in (2 * pair, 2 * pair + 1):
+    @pl.loop(0, local // STEP)
+    def _(turn):
+        for e in [STEP * turn + i for i in range(STEP)]:
             same = wanted == code[pl.ds(e, 1), :]
             scale = jnp.sum(jnp.where(same, gate[pl.ds(e, 1), :], 0.0), axis=1, keepdims=True)
             hidden = jax.nn.gelu(near[e].astype(F32) + far[e].astype(F32)).astype(BF16)
@@ -239,7 +240,7 @@
 ANY = pl.BlockSpec(memory_space=pl.ANY)
 HBM = pl.BlockSpec(memory_space=pltpu.HBM)
 GRANT = 24 << 20
-GIVE_GRANTS = (46 << 20, 42 << 20, 42 << 20)
+GIVE_GRANTS = (46 << 20, 41 << 20, 41 << 20)
 SECOND_GRANT = 35 << 20
 
 

time: 173 us -> 173 us (level)
  Pallas kernels: 57.3 us -> 53.6 us
  waiting for transfers between devices: 83.3 us -> 86.6 us
    ppermute x30, waiting for transfers between devices: 83.3 us -> 86.6 us  [swap(): lax.ppermute(value, axis, [(i, i ^ mask) for i in range(lax.axis_size(axi...]
    pallas_call x7, Pallas kernels: 23 us -> 21.1 us  [second_stage(): pl.pallas_call(functools.partial(second_kernel, units, keep, send, join,...]
  transfers between devices with their start and end apart: 30 -> 30, of which waited for: 17 -> 18; matrix products, arithmetic and copies ran while one was open for 0% -> 0% of each run, Pallas kernels for 26% -> 24%
where the time goes in v8:
time: 173 us
  waiting for transfers between devices  86.6 us (50%)
  Pallas kernels  53.6 us (31%)
  starting transfers between devices  30.7 us (18%)
    ppermute x30, waiting for transfers between devices, swap(): lax.ppermute(value, axis, [(i, i ^ mask) for i in range(lax.axis_size(axi...  86.6 us
    ppermute x30, starting transfers between devices, swap(): lax.ppermute(value, axis, [(i, i ^ mask) for i in range(lax.axis_size(axi...  30.7 us
    pallas_call x7, Pallas kernels, second_stage(): pl.pallas_call(functools.partial(second_kernel, units, keep, send, join,...  21.1 us
    pallas_call x7, Pallas kernels, first_stage(): pl.pallas_call(functools.partial(first_kernel, len(feeds), tokens, picks)...  20.6 us
    pallas_call x3, Pallas kernels, take_stage(): pl.pallas_call(functools.partial(take_kernel, own), in_specs=[SMEM, HBM,...  8.77 us
  transfers between devices with their start and end apart: 30, of which 18 were waited for; matrix products, arithmetic and copies ran while one was open for 0% of the time, Pallas kernels for 24%

profile of v8, /device:TPU:0, one launch (start us, length us, event | category | flops | bytes accessed | tf_op | source)
XLA Modules:
  0.0 172.7 jit_solution(15976894764363851390)
XLA Ops:
  0.1 2.9 %shard_map.73._ = bf16[8,384,768]{2,1,0:T(8,128)(2,1)S(1)} custom-call(s32[3]{0:T(128)S(1)} %pad_add_fusion.place.after, bf16[16,384,768]{2,1,0:T(8,128)(2,1)} %source.4, s32[3]{0:T(128)S(1)} %pad_add_fusion.place.after), custom_call_target="tpu_custom_call" | custom-call | flops 10000000 | bytes 9437184 | tf_op jit(solution)/shard_map/pallas_call | solution.py:322
  7.0 2.9 %shard_map.75.refs_2_.refs_4_.refs_1_ = bf16[8,384,768]{2,1,0:T(8,128)(2,1)S(1)} custom-call(s32[3]{0:T(128)S(1)} %pad_add_fusion.place.after, bf16[16,384,768]{2,1,0:T(8,128)(2,1)} %source.4, bf16[136,768]{1,0:T(8,128)(2,1)S(1)} %get-tuple-element.34.after.refs_0_), custom_call_target="tpu_custom_call" | custom-call | flops 10000000 | bytes 9437184 | tf_op jit(solution)/shard_map/pallas_call | solution.py:322
  9.9 2.9 %collective-permute-done.refs_1_ = bf16[136,768]{1,0:T(8,128)(2,1)S(1)} collective-permute-done((bf16[136,768]{1,0:T(8,128)(2,1)S(1)}, bf16[136,768]{1,0:T(8,128)(2,1)S(1)}, u32[]{:S(2)}, u32[]{:S(2)}) %collective-permute-start) | collective-permute-done | bytes 208928 | tf_op jit(solution)/shard_map/ppermute | solution.py:358
  12.8 3.0 %shard_map.76 = (bf16[8,40,768]{2,1,0:T(8,128)(2,1)S(1)}, f32[8,256]{1,0:T(8,128)S(1)}, f32[8,256]{1,0:T(8,128)S(1)}, bf16[272,768]{1,0:T(8,128)(2,1)S(1)}) custom-call(s32[3]{0:T(128)S(1)} %pad_add_fusion.place.after, bf16[136,768]{1,0:T(8,128)(2,1)S(1)} %get-tuple-element.34.after.refs_0_, bf16[136,768]{1,0:T(8,128)(2,1)S(1)} %collective-permute-done.refs_1_, ...), custom_call_target="tpu_custom_call" | custom-call | flops 10000000 | bytes 9437184 | tf_op jit(solution)/shard_map/pallas_call | solution.py:258
  15.8 2.9 %shard_map.77.refs_4_ = bf16[8,768,384]{2,1,0:T(8,128)(2,1)S(1)} custom-call(s32[3]{0:T(128)S(1)} %pad_add_fusion.place.after, bf16[16,768,384]{2,1,0:T(8,128)(2,1)} %refs_4_.1, f32[8,256]{1,0:T(8,128)S(1)} %get-tuple-element.37.after.refs_0_), custom_call_target="tpu_custom_call" | custom-call | flops 10000000 | bytes 9437184 | tf_op jit(solution)/shard_map/pallas_call | solution.py:322
  20.9 3.8 %collective-permute-start.4 = (bf16[136,768]{1,0:T(8,128)(2,1)S(1)}, bf16[136,768]{1,0:T(8,128)(2,1)S(1)}, u32[]{:S(2)}, u32[]{:S(2)}) collective-permute-start(bf16[136,768]{1,0:T(8,128)(2,1)S(1)} %get-tuple-element.34.after.refs_0_), channel_id=1, source_target_pairs={{0,12},{4,8},{8,4},{12,0},{1,13},{5,9},{9,5},{13,1},{2,14},{6,10},... | collective-permute-start | bytes 626696 | tf_op jit(solution)/shard_map/ppermute | solution.py:358
  26.9 4.0 %collective-permute-done.9.refs_1_ = bf16[136,768]{1,0:T(8,128)(2,1)S(1)} collective-permute-done((bf16[136,768]{1,0:T(8,128)(2,1)S(1)}, bf16[136,768]{1,0:T(8,128)(2,1)S(1)}, u32[]{:S(2)}, u32[]{:S(2)}) %collective-permute-start.9) | collective-permute-done | bytes 208928 | tf_op jit(solution)/shard_map/ppermute | solution.py:358
  30.9 3.0 %shard_map.78 = (bf16[8,40,768]{2,1,0:T(8,128)(2,1)S(1)}, f32[8,256]{1,0:T(8,128)S(1)}, f32[8,256]{1,0:T(8,128)S(1)}, bf16[272,768]{1,0:T(8,128)(2,1)S(1)}) custom-call(s32[3]{0:T(128)S(1)} %pad_add_fusion.place.after, bf16[136,768]{1,0:T(8,128)(2,1)S(1)} %collective-permute-done.8.refs_0_, bf16[136,768]{1,0:T(8,128)(2,1)S(1)} %collective-permute-done.9.refs_1_, ...), custom_call_target="tpu_custom_call" | custom-call | flops 10000000 | bytes 9437184 | tf_op jit(solution)/shard_map/pallas_call | solution.py:258
  34.0 4.2 %collective-permute-done.4 = bf16[136,768]{1,0:T(8,128)(2,1)S(1)} collective-permute-done((bf16[136,768]{1,0:T(8,128)(2,1)S(1)}, bf16[136,768]{1,0:T(8,128)(2,1)S(1)}, u32[]{:S(2)}, u32[]{:S(2)}) %collective-permute-start.4) | collective-permute-done | bytes 208928 | tf_op jit(solution)/shard_map/ppermute | solution.py:358
  38.3 3.9 %collective-permute-done.5 = bf16[136,768]{1,0:T(8,128)(2,1)S(1)} collective-permute-done((bf16[136,768]{1,0:T(8,128)(2,1)S(1)}, bf16[136,768]{1,0:T(8,128)(2,1)S(1)}, u32[]{:S(2)}, u32[]{:S(2)}) %collective-permute-start.5) | collective-permute-done | bytes 208928 | tf_op jit(solution)/shard_map/ppermute | solution.py:358
  44.5 2.8 %shard_map.79 = (bf16[8,40,768]{2,1,0:T(8,128)(2,1)S(1)}, f32[8,256]{1,0:T(8,128)S(1)}, f32[8,256]{1,0:T(8,128)S(1)}) custom-call(s32[3]{0:T(128)S(1)} %pad_add_fusion.place.after, bf16[272,768]{1,0:T(8,128)(2,1)S(1)} %collective-permute-done.13.refs_0_, bf16[8,384,768]{2,1,0:T(8,128)(2,1)S(1)} %shard_map.75.refs_2_.refs_4_.refs_1_, ...), custom_call_target="tpu_custom_call" | custom-call | flops 10000000 | bytes 9437184 | tf_op jit(solution)/shard_map/pallas_call | solution.py:258
  48.9 7.5 %collective-permute-done.11.refs_3_ = bf16[8,40,768]{2,1,0:T(8,128)(2,1)S(1)} collective-permute-done((bf16[8,40,768]{2,1,0:T(8,128)(2,1)S(1)}, bf16[8,40,768]{2,1,0:T(8,128)(2,1)S(1)}, u32[]{:S(2)}, u32[]{:S(2)}) %collective-permute-start.11) | collective-permute-done | bytes 491552 | tf_op jit(solution)/shard_map/ppermute | solution.py:358
  56.4 4.5 %shard_map.80 = (f32[256,768]{1,0:T(8,128)S(1)}, bf16[8,768,384]{2,1,0:T(8,128)(2,1)S(1)}) custom-call(s32[3]{0:T(128)S(1)} %pad_add_fusion.place.after, f32[8,256]{1,0:T(8,128)S(1)} %get-tuple-element.37.after.refs_0_, f32[8,256]{1,0:T(8,128)S(1)} %get-tuple-element.41.refs_1_, bf16[8,40,768]{2,1,0:T(8,128)(2,1)S(1)} %get-tuple-element.42.refs_2_, ...), custom_call_target="tpu_custom_call" | custom-call | flops 10000000 | bytes 9437184 | tf_op jit(solution)/shard_map/pallas_call | solution.py:281
  60.9 3.4 %shard_map.81 = (bf16[8,80,768]{2,1,0:T(8,128)(2,1)S(1)}, f32[8,512]{1,0:T(8,128)S(1)}, f32[8,512]{1,0:T(8,128)S(1)}) custom-call(s32[3]{0:T(128)S(1)} %pad_add_fusion.place.after, bf16[272,768]{1,0:T(8,128)(2,1)S(1)} %pad_maximum_fusion.refs_0_, bf16[272,768]{1,0:T(8,128)(2,1)S(1)} %collective-permute-done.14.refs_1_, ...), custom_call_target="tpu_custom_call" | custom-call | flops 10000000 | bytes 9437184 | tf_op jit(solution)/shard_map/pallas_call | solution.py:258
  66.9 2.6 %shard_map.82.refs_6_ = f32[256,768]{1,0:T(8,128)S(1)} custom-call(s32[3]{0:T(128)S(1)} %pad_add_fusion.place.after, f32[8,256]{1,0:T(8,128)S(1)} %get-tuple-element.38.refs_3_.refs_0_, f32[8,256]{1,0:T(8,128)S(1)} %get-tuple-element.39.refs_1_, bf16[8,40,768]{2,1,0:T(8,128)(2,1)S(1)} %get-tuple-element.40.refs_2_, ...), custom_call_target="tpu_custom_call" | custom-call | flops 10000000 | bytes 9437184 | tf_op jit(solution)/shard_map/pallas_call | solution.py:281
  69.5 7.9 %collective-permute-done.15.refs_3_ = bf16[8,40,768]{2,1,0:T(8,128)(2,1)S(1)} collective-permute-done((bf16[8,40,768]{2,1,0:T(8,128)(2,1)S(1)}, bf16[8,40,768]{2,1,0:T(8,128)(2,1)S(1)}, u32[]{:S(2)}, u32[]{:S(2)}) %collective-permute-start.15) | collective-permute-done | bytes 491552 | tf_op jit(solution)/shard_map/ppermute | solution.py:358
  77.4 2.6 %shard_map.83 = bf16[256,768]{1,0:T(8,128)(2,1)S(1)} custom-call(s32[3]{0:T(128)S(1)} %pad_add_fusion.place.after, f32[8,256]{1,0:T(8,128)S(1)} %get-tuple-element.44.refs_6_.refs_0_, f32[8,256]{1,0:T(8,128)S(1)} %get-tuple-element.48.refs_1_, bf16[8,40,768]{2,1,0:T(8,128)(2,1)S(1)} %get-tuple-element.49.refs_2_, ...), custom_call_target="tpu_custom_call" | custom-call | flops 10000000 | bytes 9437184 | tf_op jit(solution)/shard_map/pallas_call | solution.py:281
  83.3 2.8 %shard_map.84 = (bf16[8,40,768]{2,1,0:T(8,128)(2,1)S(1)}, f32[8,256]{1,0:T(8,128)S(1)}, f32[8,256]{1,0:T(8,128)S(1)}) custom-call(s32[3]{0:T(128)S(1)} %pad_add_fusion.place.after, bf16[272,768]{1,0:T(8,128)(2,1)S(1)} %collective-permute-done.7.refs_0_, bf16[8,384,768]{2,1,0:T(8,128)(2,1)S(1)} %shard_map.75.refs_2_.refs_4_.refs_1_, ...), custom_call_target="tpu_custom_call" | custom-call | flops 10000000 | bytes 9437184 | tf_op jit(solution)/shard_map/pallas_call | solution.py:258
  86.1 2.8 %shard_map.85 = (bf16[8,40,768]{2,1,0:T(8,128)(2,1)S(1)}, f32[8,256]{1,0:T(8,128)S(1)}, f32[8,256]{1,0:T(8,128)S(1)}) custom-call(s32[3]{0:T(128)S(1)} %pad_add_fusion.place.after, bf16[272,768]{1,0:T(8,128)(2,1)S(1)} %collective-permute-done.6.refs_0_, bf16[8,384,768]{2,1,0:T(8,128)(2,1)S(1)} %shard_map.75.refs_2_.refs_4_.refs_1_, ...), custom_call_target="tpu_custom_call" | custom-call | flops 10000000 | bytes 9437184 | tf_op jit(solution)/shard_map/pallas_call | solution.py:258
  89.0 2.8 %shard_map.86 = (bf16[8,40,768]{2,1,0:T(8,128)(2,1)S(1)}, f32[8,256]{1,0:T(8,128)S(1)}, f32[8,256]{1,0:T(8,128)S(1)}) custom-call(s32[3]{0:T(128)S(1)} %pad_add_fusion.place.after, bf16[272,768]{1,0:T(8,128)(2,1)S(1)} %collective-permute-done.3.refs_0_, bf16[8,384,768]{2,1,0:T(8,128)(2,1)S(1)} %shard_map.75.refs_2_.refs_4_.refs_1_, ...), custom_call_target="tpu_custom_call" | custom-call | flops 10000000 | bytes 9437184 | tf_op jit(solution)/shard_map/pallas_call | solution.py:258
  92.9 4.1 %collective-permute-done.22.refs_3_ = bf16[8,80,768]{2,1,0:T(8,128)(2,1)S(1)} collective-permute-done((bf16[8,80,768]{2,1,0:T(8,128)(2,1)S(1)}, bf16[8,80,768]{2,1,0:T(8,128)(2,1)S(1)}, u32[]{:S(2)}, u32[]{:S(2)}) %collective-permute-start.22) | collective-permute-done | bytes 983072 | tf_op jit(solution)/shard_map/ppermute | solution.py:358
  97.1 3.5 %shard_map.88 = (f32[256,768]{1,0:T(8,128)S(1)}, bf16[256,768]{1,0:T(8,128)(2,1)S(1)}) custom-call(s32[3]{0:T(128)S(1)} %pad_add_fusion.place.after, f32[8,512]{1,0:T(8,128)S(1)} %get-tuple-element.47.refs_6_.refs_0_, f32[8,512]{1,0:T(8,128)S(1)} %get-tuple-element.59.refs_1_, bf16[8,80,768]{2,1,0:T(8,128)(2,1)S(1)} %get-tuple-element.60.refs_2_, ...), custom_call_target="tpu_custom_call" | custom-call | flops 10000000 | bytes 9437184 | tf_op jit(solution)/shard_map/pallas_call | solution.py:281
  104.4 10.3 %collective-permute-done.21.refs_3_ = bf16[8,40,768]{2,1,0:T(8,128)(2,1)S(1)} collective-permute-done((bf16[8,40,768]{2,1,0:T(8,128)(2,1)S(1)}, bf16[8,40,768]{2,1,0:T(8,128)(2,1)S(1)}, u32[]{:S(2)}, u32[]{:S(2)}) %collective-permute-start.21) | collective-permute-done | bytes 491552 | tf_op jit(solution)/shard_map/ppermute | solution.py:358
  114.8 2.6 %shard_map.89 = bf16[256,768]{1,0:T(8,128)(2,1)S(1)} custom-call(s32[3]{0:T(128)S(1)} %pad_add_fusion.place.after, f32[8,256]{1,0:T(8,128)S(1)} %get-tuple-element.50.refs_3_.refs_0_, f32[8,256]{1,0:T(8,128)S(1)} %get-tuple-element.57.refs_1_, bf16[8,40,768]{2,1,0:T(8,128)(2,1)S(1)} %get-tuple-element.58.refs_2_, ...), custom_call_target="tpu_custom_call" | custom-call | flops 10000000 | bytes 9437184 | tf_op jit(solution)/shard_map/pallas_call | solution.py:281
  119.0 6.3 %collective-permute-done.20.refs_3_ = bf16[8,40,768]{2,1,0:T(8,128)(2,1)S(1)} collective-permute-done((bf16[8,40,768]{2,1,0:T(8,128)(2,1)S(1)}, bf16[8,40,768]{2,1,0:T(8,128)(2,1)S(1)}, u32[]{:S(2)}, u32[]{:S(2)}) %collective-permute-start.20) | collective-permute-done | bytes 491552 | tf_op jit(solution)/shard_map/ppermute | solution.py:358
  125.3 5.6 %collective-permute-start.26 = (bf16[256,768]{1,0:T(8,128)(2,1)S(1)}, bf16[256,768]{1,0:T(8,128)(2,1)S(1)}, u32[]{:S(2)}, u32[]{:S(2)}) collective-permute-start(bf16[256,768]{1,0:T(8,128)(2,1)S(1)} %add_convert_fusion.refs_6_), channel_id=1, source_target_pairs={{0,12},{4,8},{8,4},{12,0},{1,13},{5,9},{9,5},{13,1},{2,14},{6,10},... | collective-permute-start | bytes 1179656 | tf_op jit(solution)/shard_map/ppermute | solution.py:358
  130.9 2.6 %shard_map.90.refs_6_ = bf16[256,768]{1,0:T(8,128)(2,1)S(1)} custom-call(s32[3]{0:T(128)S(1)} %pad_add_fusion.place.after, f32[8,256]{1,0:T(8,128)S(1)} %get-tuple-element.51.refs_3_.refs_0_, f32[8,256]{1,0:T(8,128)S(1)} %get-tuple-element.55.refs_1_, bf16[8,40,768]{2,1,0:T(8,128)(2,1)S(1)} %get-tuple-element.56.refs_2_, ...), custom_call_target="tpu_custom_call" | custom-call | flops 10000000 | bytes 9437184 | tf_op jit(solution)/shard_map/pallas_call | solution.py:281
  135.9 2.6 %shard_map.91._ = bf16[256,768]{1,0:T(8,128)(2,1)S(1)} custom-call(s32[3]{0:T(128)S(1)} %pad_add_fusion.place.after, f32[8,256]{1,0:T(8,128)S(1)} %get-tuple-element.52._.refs_0_, f32[8,256]{1,0:T(8,128)S(1)} %get-tuple-element.53.refs_1_, bf16[8,40,768]{2,1,0:T(8,128)(2,1)S(1)} %get-tuple-element.54.refs_2_, ...), custom_call_target="tpu_custom_call" | custom-call | flops 10000000 | bytes 9437184 | tf_op jit(solution)/shard_map/pallas_call | solution.py:281
  140.1 3.7 %collective-permute-done.17.far = bf16[256,768]{1,0:T(8,128)(2,1)S(1)} collective-permute-done((bf16[256,768]{1,0:T(8,128)(2,1)S(1)}, bf16[256,768]{1,0:T(8,128)(2,1)S(1)}, u32[]{:S(2)}, u32[]{:S(2)}) %collective-permute-start.17) | collective-permute-done | bytes 393248 | tf_op jit(solution)/shard_map/ppermute | solution.py:358
  145.0 4.3 %collective-permute-done.26 = bf16[256,768]{1,0:T(8,128)(2,1)S(1)} collective-permute-done((bf16[256,768]{1,0:T(8,128)(2,1)S(1)}, bf16[256,768]{1,0:T(8,128)(2,1)S(1)}, u32[]{:S(2)}, u32[]{:S(2)}) %collective-permute-start.26) | collective-permute-done | bytes 393248 | tf_op jit(solution)/shard_map/ppermute | solution.py:358
  149.4 15.4 %collective-permute-done.27 = bf16[256,768]{1,0:T(8,128)(2,1)S(1)} collective-permute-done((bf16[256,768]{1,0:T(8,128)(2,1)S(1)}, bf16[256,768]{1,0:T(8,128)(2,1)S(1)}, u32[]{:S(2)}, u32[]{:S(2)}) %collective-permute-start.27) | collective-permute-done | bytes 393248 | tf_op jit(solution)/shard_map/ppermute | solution.py:358
  166.6 5.2 %collective-permute-done.29 = bf16[128,768]{1,0:T(8,128)(2,1)S(1)} collective-permute-done((bf16[128,768]{1,0:T(8,128)(2,1)S(1)}, bf16[128,768]{1,0:T(8,128)(2,1)S(1)}, u32[]{:S(2)}, u32[]{:S(2)}) %collective-permute-start.29) | collective-permute-done | bytes 196640 | tf_op jit(solution)/shard_map/ppermute | solution.py:358
  (70 shorter events, 32.7 us)
Async XLA Ops:
  0.1 3.5 %copy-start.4 = (f32[128,8]{0,1:T(8,128)S(1)}, f32[128,8]{0,1:T(8,128)}, u32[]{:S(2)}) copy-start(f32[128,8]{0,1:T(8,128)} %param.9) | copy-start | bytes 12292
  3.0 9.8 %collective-permute-start.1 = (bf16[8,384,768]{2,1,0:T(8,128)(2,1)S(1)}, bf16[8,384,768]{2,1,0:T(8,128)(2,1)S(1)}, u32[]{:S(2)}, u32[]{:S(2)}) collective-permute-start(bf16[8,384,768]{2,1,0:T(8,128)(2,1)S(1)} %shard_map.73._), channel_id=1, source_target_pairs={{0,1},{1,0},{2,3},{3,2},{4,5},{5,4},{6,7},{7,6},{8,9},{9,8},{10,11... | collective-permute-start | bytes 14155784 | tf_op jit(solution)/shard_map/ppermute | solution.py:358
  4.4 8.4 %collective-permute-start = (bf16[136,768]{1,0:T(8,128)(2,1)S(1)}, bf16[136,768]{1,0:T(8,128)(2,1)S(1)}, u32[]{:S(2)}, u32[]{:S(2)}) collective-permute-start(bf16[136,768]{1,0:T(8,128)(2,1)S(1)} %get-tuple-element.35), channel_id=1, source_target_pairs={{0,2},{1,3},{2,0},{3,1},{4,6},{5,7},{6,4},{7,5},{8,10},{9,11},{10,... | collective-permute-start | bytes 626696 | tf_op jit(solution)/shard_map/ppermute | solution.py:358
  18.7 37.6 %collective-permute-start.12 = (bf16[8,768,384]{2,1,0:T(8,128)(2,1)S(1)}, bf16[8,768,384]{2,1,0:T(8,128)(2,1)S(1)}, u32[]{:S(2)}, u32[]{:S(2)}) collective-permute-start(bf16[8,768,384]{2,1,0:T(8,128)(2,1)S(1)} %shard_map.77.refs_4_), channel_id=1, source_target_pairs={{0,1},{1,0},{2,3},{3,2},{4,5},{5,4},{6,7},{7,6},{8,9},{9,8},{10,11... | collective-permute-start | bytes 14155784 | tf_op jit(solution)/shard_map/ppermute | solution.py:358
  18.8 8.1 %collective-permute-start.8 = (bf16[136,768]{1,0:T(8,128)(2,1)S(1)}, bf16[136,768]{1,0:T(8,128)(2,1)S(1)}, u32[]{:S(2)}, u32[]{:S(2)}) collective-permute-start(bf16[136,768]{1,0:T(8,128)(2,1)S(1)} %get-tuple-element.34.after.refs_0_), channel_id=1, source_target_pairs={{0,4},{4,0},{8,12},{12,8},{1,5},{5,1},{9,13},{13,9},{2,6},{6,2},{1... | collective-permute-start | bytes 626696 | tf_op jit(solution)/shard_map/ppermute | solution.py:358
  20.7 10.2 %collective-permute-start.9 = (bf16[136,768]{1,0:T(8,128)(2,1)S(1)}, bf16[136,768]{1,0:T(8,128)(2,1)S(1)}, u32[]{:S(2)}, u32[]{:S(2)}) collective-permute-start(bf16[136,768]{1,0:T(8,128)(2,1)S(1)} %collective-permute-done.refs_1_), channel_id=1, source_target_pairs={{0,4},{4,0},{8,12},{12,8},{1,5},{5,1},{9,13},{13,9},{2,6},{6,2},{1... | collective-permute-start | bytes 626696 | tf_op jit(solution)/shard_map/ppermute | solution.py:358
  20.9 17.3 %collective-permute-start.4 = (bf16[136,768]{1,0:T(8,128)(2,1)S(1)}, bf16[136,768]{1,0:T(8,128)(2,1)S(1)}, u32[]{:S(2)}, u32[]{:S(2)}) collective-permute-start(bf16[136,768]{1,0:T(8,128)(2,1)S(1)} %get-tuple-element.34.after.refs_0_), channel_id=1, source_target_pairs={{0,12},{4,8},{8,4},{12,0},{1,13},{5,9},{9,5},{13,1},{2,14},{6,10},... | collective-permute-start | bytes 626696 | tf_op jit(solution)/shard_map/ppermute | solution.py:358
  24.7 17.4 %collective-permute-start.5 = (bf16[136,768]{1,0:T(8,128)(2,1)S(1)}, bf16[136,768]{1,0:T(8,128)(2,1)S(1)}, u32[]{:S(2)}, u32[]{:S(2)}) collective-permute-start(bf16[136,768]{1,0:T(8,128)(2,1)S(1)} %collective-permute-done.refs_1_), channel_id=1, source_target_pairs={{0,12},{4,8},{8,4},{12,0},{1,13},{5,9},{9,5},{13,1},{2,14},{6,10},... | collective-permute-start | bytes 626696 | tf_op jit(solution)/shard_map/ppermute | solution.py:358
  33.9 10.6 %collective-permute-start.13 = (bf16[272,768]{1,0:T(8,128)(2,1)S(1)}, bf16[272,768]{1,0:T(8,128)(2,1)S(1)}, u32[]{:S(2)}, u32[]{:S(2)}) collective-permute-start(bf16[272,768]{1,0:T(8,128)(2,1)S(1)} %get-tuple-element.43), channel_id=1, source_target_pairs={{0,1},{1,0},{2,3},{3,2},{4,5},{5,4},{6,7},{7,6},{8,9},{9,8},{10,11... | collective-permute-start | bytes 1253384 | tf_op jit(solution)/shard_map/ppermute | solution.py:358
  42.2 14.2 %collective-permute-start.11 = (bf16[8,40,768]{2,1,0:T(8,128)(2,1)S(1)}, bf16[8,40,768]{2,1,0:T(8,128)(2,1)S(1)}, u32[]{:S(2)}, u32[]{:S(2)}) collective-permute-start(bf16[8,40,768]{2,1,0:T(8,128)(2,1)S(1)} %get-tuple-element.42.refs_2_), channel_id=1, source_target_pairs={{0,2},{1,3},{2,0},{3,1},{4,6},{5,7},{6,4},{7,5},{8,10},{9,11},{10,... | collective-permute-start | bytes 1474568 | tf_op jit(solution)/shard_map/ppermute | solution.py:358
  43.8 17.1 %collective-permute-start.14 = (bf16[272,768]{1,0:T(8,128)(2,1)S(1)}, bf16[272,768]{1,0:T(8,128)(2,1)S(1)}, u32[]{:S(2)}, u32[]{:S(2)}) collective-permute-start(bf16[272,768]{1,0:T(8,128)(2,1)S(1)} %pad_maximum_fusion.refs_0_), channel_id=1, source_target_pairs={{0,1},{1,0},{2,3},{3,2},{4,5},{5,4},{6,7},{7,6},{8,9},{9,8},{10,11... | collective-permute-start | bytes 1253384 | tf_op jit(solution)/shard_map/ppermute | solution.py:358
  43.9 23.0 %collective-permute-start.10 = (bf16[8,40,768]{2,1,0:T(8,128)(2,1)S(1)}, bf16[8,40,768]{2,1,0:T(8,128)(2,1)S(1)}, u32[]{:S(2)}, u32[]{:S(2)}) collective-permute-start(bf16[8,40,768]{2,1,0:T(8,128)(2,1)S(1)} %get-tuple-element.40.refs_2_), channel_id=1, source_target_pairs={{0,2},{1,3},{2,0},{3,1},{4,6},{5,7},{6,4},{7,5},{8,10},{9,11},{10,... | collective-permute-start | bytes 1474568 | tf_op jit(solution)/shard_map/ppermute | solution.py:358
  47.3 30.1 %collective-permute-start.15 = (bf16[8,40,768]{2,1,0:T(8,128)(2,1)S(1)}, bf16[8,40,768]{2,1,0:T(8,128)(2,1)S(1)}, u32[]{:S(2)}, u32[]{:S(2)}) collective-permute-start(bf16[8,40,768]{2,1,0:T(8,128)(2,1)S(1)} %get-tuple-element.49.refs_2_), channel_id=1, source_target_pairs={{0,2},{1,3},{2,0},{3,1},{4,6},{5,7},{6,4},{7,5},{8,10},{9,11},{10,... | collective-permute-start | bytes 1474568 | tf_op jit(solution)/shard_map/ppermute | solution.py:358
  64.3 32.8 %collective-permute-start.22 = (bf16[8,80,768]{2,1,0:T(8,128)(2,1)S(1)}, bf16[8,80,768]{2,1,0:T(8,128)(2,1)S(1)}, u32[]{:S(2)}, u32[]{:S(2)}) collective-permute-start(bf16[8,80,768]{2,1,0:T(8,128)(2,1)S(1)} %get-tuple-element.60.refs_2_), channel_id=1, source_target_pairs={{0,2},{1,3},{2,0},{3,1},{4,6},{5,7},{6,4},{7,5},{8,10},{9,11},{10,... | collective-permute-start | bytes 2949128 | tf_op jit(solution)/shard_map/ppermute | solution.py:358
  65.8 14.8 %collective-permute-start.6 = (bf16[272,768]{1,0:T(8,128)(2,1)S(1)}, bf16[272,768]{1,0:T(8,128)(2,1)S(1)}, u32[]{:S(2)}, u32[]{:S(2)}) collective-permute-start(bf16[272,768]{1,0:T(8,128)(2,1)S(1)} %pad_maximum_fusion.refs_0_), channel_id=1, source_target_pairs={{0,4},{4,0},{8,12},{12,8},{1,5},{5,1},{9,13},{13,9},{2,6},{6,2},{1... | collective-permute-start | bytes 1253384 | tf_op jit(solution)/shard_map/ppermute | solution.py:358
  80.1 1.8 %collective-permute-start.16 = (bf16[256,768]{1,0:T(8,128)(2,1)S(1)}, bf16[256,768]{1,0:T(8,128)(2,1)S(1)}, u32[]{:S(2)}, u32[]{:S(2)}) collective-permute-start(bf16[256,768]{1,0:T(8,128)(2,1)S(1)} %shard_map.83), channel_id=1, source_target_pairs={{0,1},{1,0},{2,3},{3,2},{4,5},{5,4},{6,7},{7,6},{8,9},{9,8},{10,11... | collective-permute-start | bytes 1179656 | tf_op jit(solution)/shard_map/ppermute | solution.py:358
  80.1 11.6 %collective-permute-start.2 = (bf16[384,768]{1,0:T(8,128)(2,1)S(1)}, bf16[384,768]{1,0:T(8,128)(2,1)S(1)}, u32[]{:S(2)}, u32[]{:S(2)}) collective-permute-start(bf16[384,768]{1,0:T(8,128)(2,1)S(1)} %copy-done.1), channel_id=1, source_target_pairs={{0,1},{1,0},{2,3},{3,2},{4,5},{5,4},{6,7},{7,6},{8,9},{9,8},{10,11... | collective-permute-start | bytes 1769480 | tf_op jit(solution)/shard_map/ppermute | solution.py:358
  80.6 2.6 %collective-permute-start.7 = (bf16[272,768]{1,0:T(8,128)(2,1)S(1)}, bf16[272,768]{1,0:T(8,128)(2,1)S(1)}, u32[]{:S(2)}, u32[]{:S(2)}) collective-permute-start(bf16[272,768]{1,0:T(8,128)(2,1)S(1)} %collective-permute-done.6.refs_0_), channel_id=1, source_target_pairs={{0,1},{1,0},{2,3},{3,2},{4,5},{5,4},{6,7},{7,6},{8,9},{9,8},{10,11... | collective-permute-start | bytes 1253384 | tf_op jit(solution)/shard_map/ppermute | solution.py:358
  80.7 8.2 %collective-permute-start.3 = (bf16[272,768]{1,0:T(8,128)(2,1)S(1)}, bf16[272,768]{1,0:T(8,128)(2,1)S(1)}, u32[]{:S(2)}, u32[]{:S(2)}) collective-permute-start(bf16[272,768]{1,0:T(8,128)(2,1)S(1)} %get-tuple-element.36.feed), channel_id=1, source_target_pairs={{0,1},{1,0},{2,3},{3,2},{4,5},{5,4},{6,7},{7,6},{8,9},{9,8},{10,11... | collective-permute-start | bytes 1253384 | tf_op jit(solution)/shard_map/ppermute | solution.py:358
  97.1 5.1 %copy-start.2 = (bf16[768,384]{1,0:T(8,128)(2,1)S(1)}, bf16[768,384]{1,0:T(8,128)(2,1)}, u32[]{:S(2)}) copy-start(bf16[768,384]{1,0:T(8,128)(2,1)} %own.3) | copy-start | bytes 1769476
  100.6 3.8 %collective-permute-start.23 = (bf16[256,768]{1,0:T(8,128)(2,1)S(1)}, bf16[256,768]{1,0:T(8,128)(2,1)S(1)}, u32[]{:S(2)}, u32[]{:S(2)}) collective-permute-start(bf16[256,768]{1,0:T(8,128)(2,1)S(1)} %get-tuple-element.62), channel_id=1, source_target_pairs={{0,1},{1,0},{2,3},{3,2},{4,5},{5,4},{6,7},{7,6},{8,9},{9,8},{10,11... | collective-permute-start | bytes 1179656 | tf_op jit(solution)/shard_map/ppermute | solution.py:358
  100.6 14.2 %collective-permute-start.21 = (bf16[8,40,768]{2,1,0:T(8,128)(2,1)S(1)}, bf16[8,40,768]{2,1,0:T(8,128)(2,1)S(1)}, u32[]{:S(2)}, u32[]{:S(2)}) collective-permute-start(bf16[8,40,768]{2,1,0:T(8,128)(2,1)S(1)} %get-tuple-element.58.refs_2_), channel_id=1, source_target_pairs={{0,2},{1,3},{2,0},{3,1},{4,6},{5,7},{6,4},{7,5},{8,10},{9,11},{10,... | collective-permute-start | bytes 1474568 | tf_op jit(solution)/shard_map/ppermute | solution.py:358
  102.2 36.4 %collective-permute-start.18 = (bf16[768,384]{1,0:T(8,128)(2,1)S(1)}, bf16[768,384]{1,0:T(8,128)(2,1)S(1)}, u32[]{:S(2)}, u32[]{:S(2)}) collective-permute-start(bf16[768,384]{1,0:T(8,128)(2,1)S(1)} %copy-done.2), channel_id=1, source_target_pairs={{0,1},{1,0},{2,3},{3,2},{4,5},{5,4},{6,7},{7,6},{8,9},{9,8},{10,11... | collective-permute-start | bytes 1769480 | tf_op jit(solution)/shard_map/ppermute | solution.py:358
  102.3 23.0 %collective-permute-start.20 = (bf16[8,40,768]{2,1,0:T(8,128)(2,1)S(1)}, bf16[8,40,768]{2,1,0:T(8,128)(2,1)S(1)}, u32[]{:S(2)}, u32[]{:S(2)}) collective-permute-start(bf16[8,40,768]{2,1,0:T(8,128)(2,1)S(1)} %get-tuple-element.56.refs_2_), channel_id=1, source_target_pairs={{0,2},{1,3},{2,0},{3,1},{4,6},{5,7},{6,4},{7,5},{8,10},{9,11},{10,... | collective-permute-start | bytes 1474568 | tf_op jit(solution)/shard_map/ppermute | solution.py:358
  102.9 33.0 %collective-permute-start.19 = (bf16[8,40,768]{2,1,0:T(8,128)(2,1)S(1)}, bf16[8,40,768]{2,1,0:T(8,128)(2,1)S(1)}, u32[]{:S(2)}, u32[]{:S(2)}) collective-permute-start(bf16[8,40,768]{2,1,0:T(8,128)(2,1)S(1)} %get-tuple-element.54.refs_2_), channel_id=1, source_target_pairs={{0,2},{1,3},{2,0},{3,1},{4,6},{5,7},{6,4},{7,5},{8,10},{9,11},{10,... | collective-permute-start | bytes 1474568 | tf_op jit(solution)/shard_map/ppermute | solution.py:358
  117.4 7.9 %collective-permute-start.24 = (bf16[256,768]{1,0:T(8,128)(2,1)S(1)}, bf16[256,768]{1,0:T(8,128)(2,1)S(1)}, u32[]{:S(2)}, u32[]{:S(2)}) collective-permute-start(bf16[256,768]{1,0:T(8,128)(2,1)S(1)} %shard_map.89), channel_id=1, source_target_pairs={{0,1},{1,0},{2,3},{3,2},{4,5},{5,4},{6,7},{7,6},{8,9},{9,8},{10,11... | collective-permute-start | bytes 1179656 | tf_op jit(solution)/shard_map/ppermute | solution.py:358
  117.5 26.3 %collective-permute-start.17 = (bf16[256,768]{1,0:T(8,128)(2,1)S(1)}, bf16[256,768]{1,0:T(8,128)(2,1)S(1)}, u32[]{:S(2)}, u32[]{:S(2)}) collective-permute-start(bf16[256,768]{1,0:T(8,128)(2,1)S(1)} %shard_map.87.refs_6_.near), channel_id=1, source_target_pairs={{0,2},{1,3},{2,0},{3,1},{4,6},{5,7},{6,4},{7,5},{8,10},{9,11},{10,... | collective-permute-start | bytes 1179656 | tf_op jit(solution)/shard_map/ppermute | solution.py:358
  125.3 19.7 %collective-permute-start.25 = (bf16[256,768]{1,0:T(8,128)(2,1)S(1)}, bf16[256,768]{1,0:T(8,128)(2,1)S(1)}, u32[]{:S(2)}, u32[]{:S(2)}) collective-permute-start(bf16[256,768]{1,0:T(8,128)(2,1)S(1)} %add_convert_fusion.1.refs_3_), channel_id=1, source_target_pairs={{0,4},{4,0},{8,12},{12,8},{1,5},{5,1},{9,13},{13,9},{2,6},{6,2},{1... | collective-permute-start | bytes 1179656 | tf_op jit(solution)/shard_map/ppermute | solution.py:358
  125.3 24.0 %collective-permute-start.26 = (bf16[256,768]{1,0:T(8,128)(2,1)S(1)}, bf16[256,768]{1,0:T(8,128)(2,1)S(1)}, u32[]{:S(2)}, u32[]{:S(2)}) collective-permute-start(bf16[256,768]{1,0:T(8,128)(2,1)S(1)} %add_convert_fusion.refs_6_), channel_id=1, source_target_pairs={{0,12},{4,8},{8,4},{12,0},{1,13},{5,9},{9,5},{13,1},{2,14},{6,10},... | collective-permute-start | bytes 1179656 | tf_op jit(solution)/shard_map/ppermute | solution.py:358
  138.5 10.9 %collective-permute-start.28 = (bf16[256,768]{1,0:T(8,128)(2,1)S(1)}, bf16[256,768]{1,0:T(8,128)(2,1)S(1)}, u32[]{:S(2)}, u32[]{:S(2)}) collective-permute-start(bf16[256,768]{1,0:T(8,128)(2,1)S(1)} %shard_map.91._), channel_id=1, source_target_pairs={{0,1},{1,0},{2,3},{3,2},{4,5},{5,4},{6,7},{7,6},{8,9},{9,8},{10,11... | collective-permute-start | bytes 1179656 | tf_op jit(solution)/shard_map/ppermute | solution.py:358
  138.6 26.2 %collective-permute-start.27 = (bf16[256,768]{1,0:T(8,128)(2,1)S(1)}, bf16[256,768]{1,0:T(8,128)(2,1)S(1)}, u32[]{:S(2)}, u32[]{:S(2)}) collective-permute-start(bf16[256,768]{1,0:T(8,128)(2,1)S(1)} %shard_map.90.refs_6_), channel_id=1, source_target_pairs={{0,8},{4,12},{8,0},{12,4},{1,9},{5,13},{9,1},{13,5},{2,10},{6,14},... | collective-permute-start | bytes 1179656 | tf_op jit(solution)/shard_map/ppermute | solution.py:358
  165.1 6.8 %collective-permute-start.29 = (bf16[128,768]{1,0:T(8,128)(2,1)S(1)}, bf16[128,768]{1,0:T(8,128)(2,1)S(1)}, u32[]{:S(2)}, u32[]{:S(2)}) collective-permute-start(bf16[128,768]{1,0:T(8,128)(2,1)S(1)} %slice.34), channel_id=1, source_target_pairs={{0,2},{1,3},{2,0},{3,1},{4,6},{5,7},{6,4},{7,5},{8,10},{9,11},{10,... | collective-permute-start | bytes 589832 | tf_op jit(solution)/shard_map/ppermute | solution.py:358
  (3 other events, 9.7 us)

commit v9 on v8

--- a/solution.py
+++ b/solution.py
@@ -110,9 +110,9 @@
     theirs[rows : rows + META, :] = table
 
 
-def take_kernel(own, place, source, after, taken, came):
-    local = taken.shape[0]
-    copies = half_copies(source, taken, (place[0] if own else 1 - place[0]) * local, came)
+def take_kernel(own, lead, place, source, after, taken, came):
+    local = source.shape[0] // 2
+    copies = half_copies(source, taken, (place[0] if own else 1 - place[0]) * local + lead, came)
     for c in copies:
         c.start()
     for c in copies:
@@ -127,7 +127,7 @@
 
 def first_kernel(feed_count, tokens, picks, place, *refs):
     feeds, refs = refs[:feed_count], refs[feed_count:]
-    own, other, _, part, code, gate, *pair, packed = refs
+    own, low, high, _, part, code, gate, *pair, packed = refs
     local, rows, half = packed.shape
     block_counts = [feed.shape[0] // (tokens + META) for feed in feeds]
     for unit in pair:
@@ -177,12 +177,11 @@
     here = pl.multiple_of(place[0] * quarter, quarter)
     there = pl.multiple_of((1 - place[0]) * quarter, quarter)
 
-    @pl.loop(0, local // STEP)
-    def _(turn):
-        for e in [STEP * turn + i for i in range(STEP)]:
-            total = dot(packed[e, :, pl.ds(here, quarter)], own[e])
-            total += dot(packed[e, :, pl.ds(there, quarter)], other[e])
-            part[e] = total.astype(BF16)
+    for e in range(local):
+        other = low if e < local // 2 else high
+        total = dot(packed[e, :, pl.ds(here, quarter)], own[e])
+        total += dot(packed[e, :, pl.ds(there, quarter)], other[e % (local // 2)])
+        part[e] = total.astype(BF16)
 
 
 def second_kernel(units, keep, send, join, load, place, *refs):
@@ -240,7 +239,7 @@
 ANY = pl.BlockSpec(memory_space=pl.ANY)
 HBM = pl.BlockSpec(memory_space=pltpu.HBM)
 GRANT = 24 << 20
-GIVE_GRANTS = (46 << 20, 41 << 20, 41 << 20)
+GIVE_GRANTS = (46 << 20, 42 << 20, 41 << 20)
 SECOND_GRANT = 35 << 20
 
 
@@ -249,7 +248,7 @@
 
 
 def first_stage(feeds, tokens, place, own, other, after, picks):
-    local, quarter, hidden = other.shape
+    local, quarter, hidden = own.shape
     half = 2 * quarter
     blocks = sum(feed.shape[0] for feed in feeds) // (tokens + META)
     rows = blocks * CAP
@@ -257,13 +256,13 @@
     table = jax.ShapeDtypeStruct((local, blocks * tokens), F32)
     return pl.pallas_call(
         functools.partial(first_kernel, len(feeds), tokens, picks),
-        in_specs=[SMEM] + [VMEM] * (len(feeds) + 2) + [ANY],
+        in_specs=[SMEM] + [VMEM] * (len(feeds) + 3) + [ANY],
         out_specs=[VMEM] * (3 + len(pair)),
         scratch_shapes=[pltpu.VMEM((local, rows, half), BF16)],
         out_shape=[jax.ShapeDtypeStruct((local, rows, hidden), BF16), table, table, *pair],
         compiler_params=granted(),
         cost_estimate=cost(KERNEL_FLOPS, 2 * local * half * hidden),
-    )(place, *feeds, own, other, after)
+    )(place, *feeds, own, *other, after)
 
 
 def second_stage(units, code, gate, near, far, place, own, other, after, keep, send, join, load):
@@ -317,10 +316,10 @@
         out[at, pl.ds(there, quarter)] = right[b * rows : (b + 1) * rows]
 
 
-def take_stage(place, source, own, after, grant):
-    shape = (source.shape[0] // 2, *source.shape[1:])
+def take_stage(place, source, own, after, grant, lead, count):
+    shape = (count, *source.shape[1:])
     return pl.pallas_call(
-        functools.partial(take_kernel, own),
+        functools.partial(take_kernel, own, lead),
         in_specs=[SMEM, HBM, ANY],
         out_specs=VMEM,
         out_shape=jax.ShapeDtypeStruct(shape, BF16),
@@ -363,18 +362,20 @@
     def share(value):
         return swap(value, SIDE, 1)
 
-    def take(source, own, after, grant):
-        return take_stage(place, source, own, after, grant)
-
-    give_in = take(expert_in, False, place, GIVE_GRANTS[0])
-    other_in = share(give_in)
+    def take(source, own, after, grant, lead=0, count=local):
+        return take_stage(place, source, own, after, grant, lead, count)
+
+    give_in = take(expert_in, False, place, GIVE_GRANTS[0], 0, local // 2)
+    other_in = [share(give_in)]
     block = jax.ShapeDtypeStruct((rows + META, half), BF16)
     mine, theirs = kernel(
         norm_kernel, give_in, [block] * 2,
         place, tokens, expert_ids.T, gate_weights.T,
     )
     peer = cross(theirs)
-    own_in = take(expert_in, True, mine, GIVE_GRANTS[1])
+    give_in = take(expert_in, False, mine, GIVE_GRANTS[0], local // 2, local // 2)
+    other_in.append(share(give_in))
+    own_in = take(expert_in, True, give_in, GIVE_GRANTS[1])
     far = far_groups(groups)
     feeds = {"o": [mine, peer]}
     feeds["n"] = [swap(mine, GROUP, 1), swap(peer, GROUP, 1)]

time: 173 us -> 174 us (level)
    pallas_call x3 -> x4, Pallas kernels: 8.77 us -> 10.2 us  [take_stage(): pl.pallas_call(functools.partial(take_kernel, own, lead), in_specs=[SMEM,...]
    ppermute x30 -> x31, starting transfers between devices: 30.7 us -> 31.2 us  [swap(): lax.ppermute(value, axis, [(i, i ^ mask) for i in range(lax.axis_size(axi...]
    ppermute x30 -> x31, waiting for transfers between devices: 86.6 us -> 86.6 us  [swap(): lax.ppermute(value, axis, [(i, i ^ mask) for i in range(lax.axis_size(axi...]
  transfers between devices with their start and end apart: 30 -> 31, of which waited for: 18 -> 18; matrix products, arithmetic and copies ran while one was open for 0% -> 0% of each run, Pallas kernels for 24% -> 23%
where the time goes in v9:
time: 174 us
  waiting for transfers between devices  86.6 us (50%)
  Pallas kernels  54.7 us (31%)
  starting transfers between devices  31.2 us (18%)
    ppermute x31, waiting for transfers between devices, swap(): lax.ppermute(value, axis, [(i, i ^ mask) for i in range(lax.axis_size(axi...  86.6 us
    ppermute x31, starting transfers between devices, swap(): lax.ppermute(value, axis, [(i, i ^ mask) for i in range(lax.axis_size(axi...  31.2 us
    pallas_call x7, Pallas kernels, second_stage(): pl.pallas_call(functools.partial(second_kernel, units, keep, send, join,...  21.1 us
    pallas_call x7, Pallas kernels, first_stage(): pl.pallas_call(functools.partial(first_kernel, len(feeds), tokens, picks)...  20.1 us
    pallas_call x4, Pallas kernels, take_stage(): pl.pallas_call(functools.partial(take_kernel, own, lead), in_specs=[SMEM,...  10.2 us
  transfers between devices with their start and end apart: 31, of which 18 were waited for; matrix products, arithmetic and copies ran while one was open for 0% of the time, Pallas kernels for 23%

profile of v9, /device:TPU:0, one launch (start us, length us, event | category | flops | bytes accessed | tf_op | source)
XLA Modules:
  0.0 174.3 jit_solution(11628614258249668173)
XLA Ops:
  6.0 2.9 %collective-permute-start = (bf16[136,768]{1,0:T(8,128)(2,1)S(1)}, bf16[136,768]{1,0:T(8,128)(2,1)S(1)}, u32[]{:S(2)}, u32[]{:S(2)}) collective-permute-start(bf16[136,768]{1,0:T(8,128)(2,1)S(1)} %get-tuple-element.35), channel_id=1, source_target_pairs={{0,2},{1,3},{2,0},{3,1},{4,6},{5,7},{6,4},{7,5},{8,10},{9,11},{10,... | collective-permute-start | bytes 626696 | tf_op jit(solution)/shard_map/ppermute | solution.py:357
  8.9 2.9 %shard_map.76.refs_2_.refs_5_.refs_1_ = bf16[8,384,768]{2,1,0:T(8,128)(2,1)S(1)} custom-call(s32[3]{0:T(128)S(1)} %pad_add_fusion.place.after, bf16[16,384,768]{2,1,0:T(8,128)(2,1)} %source.6, bf16[4,384,768]{2,1,0:T(8,128)(2,1)S(1)} %shard_map.75.after), custom_call_target="tpu_custom_call" | custom-call | flops 10000000 | bytes 9437184 | tf_op jit(solution)/shard_map/pallas_call | solution.py:321
  11.8 2.5 %collective-permute-done.refs_1_ = bf16[136,768]{1,0:T(8,128)(2,1)S(1)} collective-permute-done((bf16[136,768]{1,0:T(8,128)(2,1)S(1)}, bf16[136,768]{1,0:T(8,128)(2,1)S(1)}, u32[]{:S(2)}, u32[]{:S(2)}) %collective-permute-start) | collective-permute-done | bytes 208928 | tf_op jit(solution)/shard_map/ppermute | solution.py:357
  14.3 2.9 %shard_map.77 = (bf16[8,40,768]{2,1,0:T(8,128)(2,1)S(1)}, f32[8,256]{1,0:T(8,128)S(1)}, f32[8,256]{1,0:T(8,128)S(1)}, bf16[272,768]{1,0:T(8,128)(2,1)S(1)}) custom-call(s32[3]{0:T(128)S(1)} %pad_add_fusion.place.after, bf16[136,768]{1,0:T(8,128)(2,1)S(1)} %get-tuple-element.34.after.refs_0_, bf16[136,768]{1,0:T(8,128)(2,1)S(1)} %collective-permute-done.refs_1_, ...), custom_call_target="tpu_custom_call" | custom-call | flops 10000000 | bytes 9437184 | tf_op jit(solution)/shard_map/pallas_call | solution.py:257
  17.2 2.9 %shard_map.78.refs_5_ = bf16[8,768,384]{2,1,0:T(8,128)(2,1)S(1)} custom-call(s32[3]{0:T(128)S(1)} %pad_add_fusion.place.after, bf16[16,768,384]{2,1,0:T(8,128)(2,1)} %refs_4_.1, f32[8,256]{1,0:T(8,128)S(1)} %get-tuple-element.37.after.refs_0_), custom_call_target="tpu_custom_call" | custom-call | flops 10000000 | bytes 9437184 | tf_op jit(solution)/shard_map/pallas_call | solution.py:321
  22.4 4.0 %collective-permute-start.5 = (bf16[136,768]{1,0:T(8,128)(2,1)S(1)}, bf16[136,768]{1,0:T(8,128)(2,1)S(1)}, u32[]{:S(2)}, u32[]{:S(2)}) collective-permute-start(bf16[136,768]{1,0:T(8,128)(2,1)S(1)} %get-tuple-element.34.after.refs_0_), channel_id=1, source_target_pairs={{0,12},{4,8},{8,4},{12,0},{1,13},{5,9},{9,5},{13,1},{2,14},{6,10},... | collective-permute-start | bytes 626696 | tf_op jit(solution)/shard_map/ppermute | solution.py:357
  28.4 4.2 %collective-permute-done.10.refs_1_ = bf16[136,768]{1,0:T(8,128)(2,1)S(1)} collective-permute-done((bf16[136,768]{1,0:T(8,128)(2,1)S(1)}, bf16[136,768]{1,0:T(8,128)(2,1)S(1)}, u32[]{:S(2)}, u32[]{:S(2)}) %collective-permute-start.10) | collective-permute-done | bytes 208928 | tf_op jit(solution)/shard_map/ppermute | solution.py:357
  32.5 2.9 %shard_map.79 = (bf16[8,40,768]{2,1,0:T(8,128)(2,1)S(1)}, f32[8,256]{1,0:T(8,128)S(1)}, f32[8,256]{1,0:T(8,128)S(1)}, bf16[272,768]{1,0:T(8,128)(2,1)S(1)}) custom-call(s32[3]{0:T(128)S(1)} %pad_add_fusion.place.after, bf16[136,768]{1,0:T(8,128)(2,1)S(1)} %collective-permute-done.9.refs_0_, bf16[136,768]{1,0:T(8,128)(2,1)S(1)} %collective-permute-done.10.refs_1_, ...), custom_call_target="tpu_custom_call" | custom-call | flops 10000000 | bytes 9437184 | tf_op jit(solution)/shard_map/pallas_call | solution.py:257
  35.5 4.4 %collective-permute-done.5 = bf16[136,768]{1,0:T(8,128)(2,1)S(1)} collective-permute-done((bf16[136,768]{1,0:T(8,128)(2,1)S(1)}, bf16[136,768]{1,0:T(8,128)(2,1)S(1)}, u32[]{:S(2)}, u32[]{:S(2)}) %collective-permute-start.5) | collective-permute-done | bytes 208928 | tf_op jit(solution)/shard_map/ppermute | solution.py:357
  39.9 3.9 %collective-permute-done.6 = bf16[136,768]{1,0:T(8,128)(2,1)S(1)} collective-permute-done((bf16[136,768]{1,0:T(8,128)(2,1)S(1)}, bf16[136,768]{1,0:T(8,128)(2,1)S(1)}, u32[]{:S(2)}, u32[]{:S(2)}) %collective-permute-start.6) | collective-permute-done | bytes 208928 | tf_op jit(solution)/shard_map/ppermute | solution.py:357
  46.1 2.7 %shard_map.80 = (bf16[8,40,768]{2,1,0:T(8,128)(2,1)S(1)}, f32[8,256]{1,0:T(8,128)S(1)}, f32[8,256]{1,0:T(8,128)S(1)}) custom-call(s32[3]{0:T(128)S(1)} %pad_add_fusion.place.after, bf16[272,768]{1,0:T(8,128)(2,1)S(1)} %collective-permute-done.14.refs_0_, bf16[8,384,768]{2,1,0:T(8,128)(2,1)S(1)} %shard_map.76.refs_2_.refs_5_.refs_1_, ...), custom_call_target="tpu_custom_call" | custom-call | flops 10000000 | bytes 9437184 | tf_op jit(solution)/shard_map/pallas_call | solution.py:257
  50.3 7.6 %collective-permute-done.12.refs_3_ = bf16[8,40,768]{2,1,0:T(8,128)(2,1)S(1)} collective-permute-done((bf16[8,40,768]{2,1,0:T(8,128)(2,1)S(1)}, bf16[8,40,768]{2,1,0:T(8,128)(2,1)S(1)}, u32[]{:S(2)}, u32[]{:S(2)}) %collective-permute-start.12) | collective-permute-done | bytes 491552 | tf_op jit(solution)/shard_map/ppermute | solution.py:357
  58.0 4.5 %shard_map.81 = (f32[256,768]{1,0:T(8,128)S(1)}, bf16[8,768,384]{2,1,0:T(8,128)(2,1)S(1)}) custom-call(s32[3]{0:T(128)S(1)} %pad_add_fusion.place.after, f32[8,256]{1,0:T(8,128)S(1)} %get-tuple-element.37.after.refs_0_, f32[8,256]{1,0:T(8,128)S(1)} %get-tuple-element.41.refs_1_, bf16[8,40,768]{2,1,0:T(8,128)(2,1)S(1)} %get-tuple-element.42.refs_2_, ...), custom_call_target="tpu_custom_call" | custom-call | flops 10000000 | bytes 9437184 | tf_op jit(solution)/shard_map/pallas_call | solution.py:280
  62.5 3.6 %shard_map.82 = (bf16[8,80,768]{2,1,0:T(8,128)(2,1)S(1)}, f32[8,512]{1,0:T(8,128)S(1)}, f32[8,512]{1,0:T(8,128)S(1)}) custom-call(s32[3]{0:T(128)S(1)} %pad_add_fusion.place.after, bf16[272,768]{1,0:T(8,128)(2,1)S(1)} %pad_maximum_fusion.refs_0_, bf16[272,768]{1,0:T(8,128)(2,1)S(1)} %collective-permute-done.15.refs_1_, ...), custom_call_target="tpu_custom_call" | custom-call | flops 10000000 | bytes 9437184 | tf_op jit(solution)/shard_map/pallas_call | solution.py:257
  68.5 2.6 %shard_map.83.refs_6_ = f32[256,768]{1,0:T(8,128)S(1)} custom-call(s32[3]{0:T(128)S(1)} %pad_add_fusion.place.after, f32[8,256]{1,0:T(8,128)S(1)} %get-tuple-element.38.refs_4_.refs_0_, f32[8,256]{1,0:T(8,128)S(1)} %get-tuple-element.39.refs_1_, bf16[8,40,768]{2,1,0:T(8,128)(2,1)S(1)} %get-tuple-element.40.refs_2_, ...), custom_call_target="tpu_custom_call" | custom-call | flops 10000000 | bytes 9437184 | tf_op jit(solution)/shard_map/pallas_call | solution.py:280
  71.1 7.9 %collective-permute-done.16.refs_3_ = bf16[8,40,768]{2,1,0:T(8,128)(2,1)S(1)} collective-permute-done((bf16[8,40,768]{2,1,0:T(8,128)(2,1)S(1)}, bf16[8,40,768]{2,1,0:T(8,128)(2,1)S(1)}, u32[]{:S(2)}, u32[]{:S(2)}) %collective-permute-start.16) | collective-permute-done | bytes 491552 | tf_op jit(solution)/shard_map/ppermute | solution.py:357
  79.0 2.6 %shard_map.84 = bf16[256,768]{1,0:T(8,128)(2,1)S(1)} custom-call(s32[3]{0:T(128)S(1)} %pad_add_fusion.place.after, f32[8,256]{1,0:T(8,128)S(1)} %get-tuple-element.44.refs_6_.refs_0_, f32[8,256]{1,0:T(8,128)S(1)} %get-tuple-element.48.refs_1_, bf16[8,40,768]{2,1,0:T(8,128)(2,1)S(1)} %get-tuple-element.49.refs_2_, ...), custom_call_target="tpu_custom_call" | custom-call | flops 10000000 | bytes 9437184 | tf_op jit(solution)/shard_map/pallas_call | solution.py:280
  84.9 2.7 %shard_map.85 = (bf16[8,40,768]{2,1,0:T(8,128)(2,1)S(1)}, f32[8,256]{1,0:T(8,128)S(1)}, f32[8,256]{1,0:T(8,128)S(1)}) custom-call(s32[3]{0:T(128)S(1)} %pad_add_fusion.place.after, bf16[272,768]{1,0:T(8,128)(2,1)S(1)} %collective-permute-done.8.refs_0_, bf16[8,384,768]{2,1,0:T(8,128)(2,1)S(1)} %shard_map.76.refs_2_.refs_5_.refs_1_, ...), custom_call_target="tpu_custom_call" | custom-call | flops 10000000 | bytes 9437184 | tf_op jit(solution)/shard_map/pallas_call | solution.py:257
  87.6 2.7 %shard_map.86 = (bf16[8,40,768]{2,1,0:T(8,128)(2,1)S(1)}, f32[8,256]{1,0:T(8,128)S(1)}, f32[8,256]{1,0:T(8,128)S(1)}) custom-call(s32[3]{0:T(128)S(1)} %pad_add_fusion.place.after, bf16[272,768]{1,0:T(8,128)(2,1)S(1)} %collective-permute-done.7.refs_0_, bf16[8,384,768]{2,1,0:T(8,128)(2,1)S(1)} %shard_map.76.refs_2_.refs_5_.refs_1_, ...), custom_call_target="tpu_custom_call" | custom-call | flops 10000000 | bytes 9437184 | tf_op jit(solution)/shard_map/pallas_call | solution.py:257
  90.3 2.7 %shard_map.87 = (bf16[8,40,768]{2,1,0:T(8,128)(2,1)S(1)}, f32[8,256]{1,0:T(8,128)S(1)}, f32[8,256]{1,0:T(8,128)S(1)}) custom-call(s32[3]{0:T(128)S(1)} %pad_add_fusion.place.after, bf16[272,768]{1,0:T(8,128)(2,1)S(1)} %collective-permute-done.4.refs_0_, bf16[8,384,768]{2,1,0:T(8,128)(2,1)S(1)} %shard_map.76.refs_2_.refs_5_.refs_1_, ...), custom_call_target="tpu_custom_call" | custom-call | flops 10000000 | bytes 9437184 | tf_op jit(solution)/shard_map/pallas_call | solution.py:257
  94.2 4.4 %collective-permute-done.23.refs_3_ = bf16[8,80,768]{2,1,0:T(8,128)(2,1)S(1)} collective-permute-done((bf16[8,80,768]{2,1,0:T(8,128)(2,1)S(1)}, bf16[8,80,768]{2,1,0:T(8,128)(2,1)S(1)}, u32[]{:S(2)}, u32[]{:S(2)}) %collective-permute-start.23) | collective-permute-done | bytes 983072 | tf_op jit(solution)/shard_map/ppermute | solution.py:357
  98.6 3.5 %shard_map.89 = (f32[256,768]{1,0:T(8,128)S(1)}, bf16[256,768]{1,0:T(8,128)(2,1)S(1)}) custom-call(s32[3]{0:T(128)S(1)} %pad_add_fusion.place.after, f32[8,512]{1,0:T(8,128)S(1)} %get-tuple-element.47.refs_6_.refs_0_, f32[8,512]{1,0:T(8,128)S(1)} %get-tuple-element.59.refs_1_, bf16[8,80,768]{2,1,0:T(8,128)(2,1)S(1)} %get-tuple-element.60.refs_2_, ...), custom_call_target="tpu_custom_call" | custom-call | flops 10000000 | bytes 9437184 | tf_op jit(solution)/shard_map/pallas_call | solution.py:280
  106.0 10.3 %collective-permute-done.22.refs_3_ = bf16[8,40,768]{2,1,0:T(8,128)(2,1)S(1)} collective-permute-done((bf16[8,40,768]{2,1,0:T(8,128)(2,1)S(1)}, bf16[8,40,768]{2,1,0:T(8,128)(2,1)S(1)}, u32[]{:S(2)}, u32[]{:S(2)}) %collective-permute-start.22) | collective-permute-done | bytes 491552 | tf_op jit(solution)/shard_map/ppermute | solution.py:357
  116.4 2.6 %shard_map.90 = bf16[256,768]{1,0:T(8,128)(2,1)S(1)} custom-call(s32[3]{0:T(128)S(1)} %pad_add_fusion.place.after, f32[8,256]{1,0:T(8,128)S(1)} %get-tuple-element.50.refs_4_.refs_0_, f32[8,256]{1,0:T(8,128)S(1)} %get-tuple-element.57.refs_1_, bf16[8,40,768]{2,1,0:T(8,128)(2,1)S(1)} %get-tuple-element.58.refs_2_, ...), custom_call_target="tpu_custom_call" | custom-call | flops 10000000 | bytes 9437184 | tf_op jit(solution)/shard_map/pallas_call | solution.py:280
  120.6 6.3 %collective-permute-done.21.refs_3_ = bf16[8,40,768]{2,1,0:T(8,128)(2,1)S(1)} collective-permute-done((bf16[8,40,768]{2,1,0:T(8,128)(2,1)S(1)}, bf16[8,40,768]{2,1,0:T(8,128)(2,1)S(1)}, u32[]{:S(2)}, u32[]{:S(2)}) %collective-permute-start.21) | collective-permute-done | bytes 491552 | tf_op jit(solution)/shard_map/ppermute | solution.py:357
  126.9 5.5 %collective-permute-start.27 = (bf16[256,768]{1,0:T(8,128)(2,1)S(1)}, bf16[256,768]{1,0:T(8,128)(2,1)S(1)}, u32[]{:S(2)}, u32[]{:S(2)}) collective-permute-start(bf16[256,768]{1,0:T(8,128)(2,1)S(1)} %add_convert_fusion.refs_6_), channel_id=1, source_target_pairs={{0,12},{4,8},{8,4},{12,0},{1,13},{5,9},{9,5},{13,1},{2,14},{6,10},... | collective-permute-start | bytes 1179656 | tf_op jit(solution)/shard_map/ppermute | solution.py:357
  132.4 2.6 %shard_map.91.refs_6_ = bf16[256,768]{1,0:T(8,128)(2,1)S(1)} custom-call(s32[3]{0:T(128)S(1)} %pad_add_fusion.place.after, f32[8,256]{1,0:T(8,128)S(1)} %get-tuple-element.51.refs_4_.refs_0_, f32[8,256]{1,0:T(8,128)S(1)} %get-tuple-element.55.refs_1_, bf16[8,40,768]{2,1,0:T(8,128)(2,1)S(1)} %get-tuple-element.56.refs_2_, ...), custom_call_target="tpu_custom_call" | custom-call | flops 10000000 | bytes 9437184 | tf_op jit(solution)/shard_map/pallas_call | solution.py:280
  137.4 2.6 %shard_map.92._ = bf16[256,768]{1,0:T(8,128)(2,1)S(1)} custom-call(s32[3]{0:T(128)S(1)} %pad_add_fusion.place.after, f32[8,256]{1,0:T(8,128)S(1)} %get-tuple-element.52._.refs_0_, f32[8,256]{1,0:T(8,128)S(1)} %get-tuple-element.53.refs_1_, bf16[8,40,768]{2,1,0:T(8,128)(2,1)S(1)} %get-tuple-element.54.refs_2_, ...), custom_call_target="tpu_custom_call" | custom-call | flops 10000000 | bytes 9437184 | tf_op jit(solution)/shard_map/pallas_call | solution.py:280
  141.6 3.7 %collective-permute-done.18.far = bf16[256,768]{1,0:T(8,128)(2,1)S(1)} collective-permute-done((bf16[256,768]{1,0:T(8,128)(2,1)S(1)}, bf16[256,768]{1,0:T(8,128)(2,1)S(1)}, u32[]{:S(2)}, u32[]{:S(2)}) %collective-permute-start.18) | collective-permute-done | bytes 393248 | tf_op jit(solution)/shard_map/ppermute | solution.py:357
  146.6 4.3 %collective-permute-done.27 = bf16[256,768]{1,0:T(8,128)(2,1)S(1)} collective-permute-done((bf16[256,768]{1,0:T(8,128)(2,1)S(1)}, bf16[256,768]{1,0:T(8,128)(2,1)S(1)}, u32[]{:S(2)}, u32[]{:S(2)}) %collective-permute-start.27) | collective-permute-done | bytes 393248 | tf_op jit(solution)/shard_map/ppermute | solution.py:357
  150.9 15.4 %collective-permute-done.28 = bf16[256,768]{1,0:T(8,128)(2,1)S(1)} collective-permute-done((bf16[256,768]{1,0:T(8,128)(2,1)S(1)}, bf16[256,768]{1,0:T(8,128)(2,1)S(1)}, u32[]{:S(2)}, u32[]{:S(2)}) %collective-permute-start.28) | collective-permute-done | bytes 393248 | tf_op jit(solution)/shard_map/ppermute | solution.py:357
  168.1 5.2 %collective-permute-done.30 = bf16[128,768]{1,0:T(8,128)(2,1)S(1)} collective-permute-done((bf16[128,768]{1,0:T(8,128)(2,1)S(1)}, bf16[128,768]{1,0:T(8,128)(2,1)S(1)}, u32[]{:S(2)}, u32[]{:S(2)}) %collective-permute-start.30) | collective-permute-done | bytes 196640 | tf_op jit(solution)/shard_map/ppermute | solution.py:357
  (73 shorter events, 34.3 us)
Async XLA Ops:
  5.3 9.0 %collective-permute-start.2 = (bf16[4,384,768]{2,1,0:T(8,128)(2,1)S(1)}, bf16[4,384,768]{2,1,0:T(8,128)(2,1)S(1)}, u32[]{:S(2)}, u32[]{:S(2)}) collective-permute-start(bf16[4,384,768]{2,1,0:T(8,128)(2,1)S(1)} %shard_map.75.after), channel_id=1, source_target_pairs={{0,1},{1,0},{2,3},{3,2},{4,5},{5,4},{6,7},{7,6},{8,9},{9,8},{10,11... | collective-permute-start | bytes 7077896 | tf_op jit(solution)/shard_map/ppermute | solution.py:357
  5.9 8.4 %collective-permute-start.1 = (bf16[4,384,768]{2,1,0:T(8,128)(2,1)S(1)}, bf16[4,384,768]{2,1,0:T(8,128)(2,1)S(1)}, u32[]{:S(2)}, u32[]{:S(2)}) collective-permute-start(bf16[4,384,768]{2,1,0:T(8,128)(2,1)S(1)} %shard_map.73._), channel_id=1, source_target_pairs={{0,1},{1,0},{2,3},{3,2},{4,5},{5,4},{6,7},{7,6},{8,9},{9,8},{10,11... | collective-permute-start | bytes 7077896 | tf_op jit(solution)/shard_map/ppermute | solution.py:357
  6.0 8.3 %collective-permute-start = (bf16[136,768]{1,0:T(8,128)(2,1)S(1)}, bf16[136,768]{1,0:T(8,128)(2,1)S(1)}, u32[]{:S(2)}, u32[]{:S(2)}) collective-permute-start(bf16[136,768]{1,0:T(8,128)(2,1)S(1)} %get-tuple-element.35), channel_id=1, source_target_pairs={{0,2},{1,3},{2,0},{3,1},{4,6},{5,7},{6,4},{7,5},{8,10},{9,11},{10,... | collective-permute-start | bytes 626696 | tf_op jit(solution)/shard_map/ppermute | solution.py:357
  20.1 37.9 %collective-permute-start.13 = (bf16[8,768,384]{2,1,0:T(8,128)(2,1)S(1)}, bf16[8,768,384]{2,1,0:T(8,128)(2,1)S(1)}, u32[]{:S(2)}, u32[]{:S(2)}) collective-permute-start(bf16[8,768,384]{2,1,0:T(8,128)(2,1)S(1)} %shard_map.78.refs_5_), channel_id=1, source_target_pairs={{0,1},{1,0},{2,3},{3,2},{4,5},{5,4},{6,7},{7,6},{8,9},{9,8},{10,11... | collective-permute-start | bytes 14155784 | tf_op jit(solution)/shard_map/ppermute | solution.py:357
  20.2 8.2 %collective-permute-start.9 = (bf16[136,768]{1,0:T(8,128)(2,1)S(1)}, bf16[136,768]{1,0:T(8,128)(2,1)S(1)}, u32[]{:S(2)}, u32[]{:S(2)}) collective-permute-start(bf16[136,768]{1,0:T(8,128)(2,1)S(1)} %get-tuple-element.34.after.refs_0_), channel_id=1, source_target_pairs={{0,4},{4,0},{8,12},{12,8},{1,5},{5,1},{9,13},{13,9},{2,6},{6,2},{1... | collective-permute-start | bytes 626696 | tf_op jit(solution)/shard_map/ppermute | solution.py:357
  22.3 10.2 %collective-permute-start.10 = (bf16[136,768]{1,0:T(8,128)(2,1)S(1)}, bf16[136,768]{1,0:T(8,128)(2,1)S(1)}, u32[]{:S(2)}, u32[]{:S(2)}) collective-permute-start(bf16[136,768]{1,0:T(8,128)(2,1)S(1)} %collective-permute-done.refs_1_), channel_id=1, source_target_pairs={{0,4},{4,0},{8,12},{12,8},{1,5},{5,1},{9,13},{13,9},{2,6},{6,2},{1... | collective-permute-start | bytes 626696 | tf_op jit(solution)/shard_map/ppermute | solution.py:357
  22.4 17.5 %collective-permute-start.5 = (bf16[136,768]{1,0:T(8,128)(2,1)S(1)}, bf16[136,768]{1,0:T(8,128)(2,1)S(1)}, u32[]{:S(2)}, u32[]{:S(2)}) collective-permute-start(bf16[136,768]{1,0:T(8,128)(2,1)S(1)} %get-tuple-element.34.after.refs_0_), channel_id=1, source_target_pairs={{0,12},{4,8},{8,4},{12,0},{1,13},{5,9},{9,5},{13,1},{2,14},{6,10},... | collective-permute-start | bytes 626696 | tf_op jit(solution)/shard_map/ppermute | solution.py:357
  26.4 17.4 %collective-permute-start.6 = (bf16[136,768]{1,0:T(8,128)(2,1)S(1)}, bf16[136,768]{1,0:T(8,128)(2,1)S(1)}, u32[]{:S(2)}, u32[]{:S(2)}) collective-permute-start(bf16[136,768]{1,0:T(8,128)(2,1)S(1)} %collective-permute-done.refs_1_), channel_id=1, source_target_pairs={{0,12},{4,8},{8,4},{12,0},{1,13},{5,9},{9,5},{13,1},{2,14},{6,10},... | collective-permute-start | bytes 626696 | tf_op jit(solution)/shard_map/ppermute | solution.py:357
  35.4 10.7 %collective-permute-start.14 = (bf16[272,768]{1,0:T(8,128)(2,1)S(1)}, bf16[272,768]{1,0:T(8,128)(2,1)S(1)}, u32[]{:S(2)}, u32[]{:S(2)}) collective-permute-start(bf16[272,768]{1,0:T(8,128)(2,1)S(1)} %get-tuple-element.43), channel_id=1, source_target_pairs={{0,1},{1,0},{2,3},{3,2},{4,5},{5,4},{6,7},{7,6},{8,9},{9,8},{10,11... | collective-permute-start | bytes 1253384 | tf_op jit(solution)/shard_map/ppermute | solution.py:357
  43.8 14.2 %collective-permute-start.12 = (bf16[8,40,768]{2,1,0:T(8,128)(2,1)S(1)}, bf16[8,40,768]{2,1,0:T(8,128)(2,1)S(1)}, u32[]{:S(2)}, u32[]{:S(2)}) collective-permute-start(bf16[8,40,768]{2,1,0:T(8,128)(2,1)S(1)} %get-tuple-element.42.refs_2_), channel_id=1, source_target_pairs={{0,2},{1,3},{2,0},{3,1},{4,6},{5,7},{6,4},{7,5},{8,10},{9,11},{10,... | collective-permute-start | bytes 1474568 | tf_op jit(solution)/shard_map/ppermute | solution.py:357
  45.4 17.1 %collective-permute-start.15 = (bf16[272,768]{1,0:T(8,128)(2,1)S(1)}, bf16[272,768]{1,0:T(8,128)(2,1)S(1)}, u32[]{:S(2)}, u32[]{:S(2)}) collective-permute-start(bf16[272,768]{1,0:T(8,128)(2,1)S(1)} %pad_maximum_fusion.refs_0_), channel_id=1, source_target_pairs={{0,1},{1,0},{2,3},{3,2},{4,5},{5,4},{6,7},{7,6},{8,9},{9,8},{10,11... | collective-permute-start | bytes 1253384 | tf_op jit(solution)/shard_map/ppermute | solution.py:357
  45.5 23.0 %collective-permute-start.11 = (bf16[8,40,768]{2,1,0:T(8,128)(2,1)S(1)}, bf16[8,40,768]{2,1,0:T(8,128)(2,1)S(1)}, u32[]{:S(2)}, u32[]{:S(2)}) collective-permute-start(bf16[8,40,768]{2,1,0:T(8,128)(2,1)S(1)} %get-tuple-element.40.refs_2_), channel_id=1, source_target_pairs={{0,2},{1,3},{2,0},{3,1},{4,6},{5,7},{6,4},{7,5},{8,10},{9,11},{10,... | collective-permute-start | bytes 1474568 | tf_op jit(solution)/shard_map/ppermute | solution.py:357
  48.8 30.2 %collective-permute-start.16 = (bf16[8,40,768]{2,1,0:T(8,128)(2,1)S(1)}, bf16[8,40,768]{2,1,0:T(8,128)(2,1)S(1)}, u32[]{:S(2)}, u32[]{:S(2)}) collective-permute-start(bf16[8,40,768]{2,1,0:T(8,128)(2,1)S(1)} %get-tuple-element.49.refs_2_), channel_id=1, source_target_pairs={{0,2},{1,3},{2,0},{3,1},{4,6},{5,7},{6,4},{7,5},{8,10},{9,11},{10,... | collective-permute-start | bytes 1474568 | tf_op jit(solution)/shard_map/ppermute | solution.py:357
  66.1 32.5 %collective-permute-start.23 = (bf16[8,80,768]{2,1,0:T(8,128)(2,1)S(1)}, bf16[8,80,768]{2,1,0:T(8,128)(2,1)S(1)}, u32[]{:S(2)}, u32[]{:S(2)}) collective-permute-start(bf16[8,80,768]{2,1,0:T(8,128)(2,1)S(1)} %get-tuple-element.60.refs_2_), channel_id=1, source_target_pairs={{0,2},{1,3},{2,0},{3,1},{4,6},{5,7},{6,4},{7,5},{8,10},{9,11},{10,... | collective-permute-start | bytes 2949128 | tf_op jit(solution)/shard_map/ppermute | solution.py:357
  67.7 14.6 %collective-permute-start.7 = (bf16[272,768]{1,0:T(8,128)(2,1)S(1)}, bf16[272,768]{1,0:T(8,128)(2,1)S(1)}, u32[]{:S(2)}, u32[]{:S(2)}) collective-permute-start(bf16[272,768]{1,0:T(8,128)(2,1)S(1)} %pad_maximum_fusion.refs_0_), channel_id=1, source_target_pairs={{0,4},{4,0},{8,12},{12,8},{1,5},{5,1},{9,13},{13,9},{2,6},{6,2},{1... | collective-permute-start | bytes 1253384 | tf_op jit(solution)/shard_map/ppermute | solution.py:357
  81.7 1.8 %collective-permute-start.17 = (bf16[256,768]{1,0:T(8,128)(2,1)S(1)}, bf16[256,768]{1,0:T(8,128)(2,1)S(1)}, u32[]{:S(2)}, u32[]{:S(2)}) collective-permute-start(bf16[256,768]{1,0:T(8,128)(2,1)S(1)} %shard_map.84), channel_id=1, source_target_pairs={{0,1},{1,0},{2,3},{3,2},{4,5},{5,4},{6,7},{7,6},{8,9},{9,8},{10,11... | collective-permute-start | bytes 1179656 | tf_op jit(solution)/shard_map/ppermute | solution.py:357
  81.7 11.3 %collective-permute-start.3 = (bf16[384,768]{1,0:T(8,128)(2,1)S(1)}, bf16[384,768]{1,0:T(8,128)(2,1)S(1)}, u32[]{:S(2)}, u32[]{:S(2)}) collective-permute-start(bf16[384,768]{1,0:T(8,128)(2,1)S(1)} %copy-done.1), channel_id=1, source_target_pairs={{0,1},{1,0},{2,3},{3,2},{4,5},{5,4},{6,7},{7,6},{8,9},{9,8},{10,11... | collective-permute-start | bytes 1769480 | tf_op jit(solution)/shard_map/ppermute | solution.py:357
  82.2 2.6 %collective-permute-start.8 = (bf16[272,768]{1,0:T(8,128)(2,1)S(1)}, bf16[272,768]{1,0:T(8,128)(2,1)S(1)}, u32[]{:S(2)}, u32[]{:S(2)}) collective-permute-start(bf16[272,768]{1,0:T(8,128)(2,1)S(1)} %collective-permute-done.7.refs_0_), channel_id=1, source_target_pairs={{0,1},{1,0},{2,3},{3,2},{4,5},{5,4},{6,7},{7,6},{8,9},{9,8},{10,11... | collective-permute-start | bytes 1253384 | tf_op jit(solution)/shard_map/ppermute | solution.py:357
  82.3 8.0 %collective-permute-start.4 = (bf16[272,768]{1,0:T(8,128)(2,1)S(1)}, bf16[272,768]{1,0:T(8,128)(2,1)S(1)}, u32[]{:S(2)}, u32[]{:S(2)}) collective-permute-start(bf16[272,768]{1,0:T(8,128)(2,1)S(1)} %get-tuple-element.36.feed), channel_id=1, source_target_pairs={{0,1},{1,0},{2,3},{3,2},{4,5},{5,4},{6,7},{7,6},{8,9},{9,8},{10,11... | collective-permute-start | bytes 1253384 | tf_op jit(solution)/shard_map/ppermute | solution.py:357
  98.6 5.2 %copy-start.2 = (bf16[768,384]{1,0:T(8,128)(2,1)S(1)}, bf16[768,384]{1,0:T(8,128)(2,1)}, u32[]{:S(2)}) copy-start(bf16[768,384]{1,0:T(8,128)(2,1)} %own.3) | copy-start | bytes 1769476
  102.1 3.8 %collective-permute-start.24 = (bf16[256,768]{1,0:T(8,128)(2,1)S(1)}, bf16[256,768]{1,0:T(8,128)(2,1)S(1)}, u32[]{:S(2)}, u32[]{:S(2)}) collective-permute-start(bf16[256,768]{1,0:T(8,128)(2,1)S(1)} %get-tuple-element.62), channel_id=1, source_target_pairs={{0,1},{1,0},{2,3},{3,2},{4,5},{5,4},{6,7},{7,6},{8,9},{9,8},{10,11... | collective-permute-start | bytes 1179656 | tf_op jit(solution)/shard_map/ppermute | solution.py:357
  102.2 14.2 %collective-permute-start.22 = (bf16[8,40,768]{2,1,0:T(8,128)(2,1)S(1)}, bf16[8,40,768]{2,1,0:T(8,128)(2,1)S(1)}, u32[]{:S(2)}, u32[]{:S(2)}) collective-permute-start(bf16[8,40,768]{2,1,0:T(8,128)(2,1)S(1)} %get-tuple-element.58.refs_2_), channel_id=1, source_target_pairs={{0,2},{1,3},{2,0},{3,1},{4,6},{5,7},{6,4},{7,5},{8,10},{9,11},{10,... | collective-permute-start | bytes 1474568 | tf_op jit(solution)/shard_map/ppermute | solution.py:357
  103.8 36.4 %collective-permute-start.19 = (bf16[768,384]{1,0:T(8,128)(2,1)S(1)}, bf16[768,384]{1,0:T(8,128)(2,1)S(1)}, u32[]{:S(2)}, u32[]{:S(2)}) collective-permute-start(bf16[768,384]{1,0:T(8,128)(2,1)S(1)} %copy-done.2), channel_id=1, source_target_pairs={{0,1},{1,0},{2,3},{3,2},{4,5},{5,4},{6,7},{7,6},{8,9},{9,8},{10,11... | collective-permute-start | bytes 1769480 | tf_op jit(solution)/shard_map/ppermute | solution.py:357
  103.9 23.0 %collective-permute-start.21 = (bf16[8,40,768]{2,1,0:T(8,128)(2,1)S(1)}, bf16[8,40,768]{2,1,0:T(8,128)(2,1)S(1)}, u32[]{:S(2)}, u32[]{:S(2)}) collective-permute-start(bf16[8,40,768]{2,1,0:T(8,128)(2,1)S(1)} %get-tuple-element.56.refs_2_), channel_id=1, source_target_pairs={{0,2},{1,3},{2,0},{3,1},{4,6},{5,7},{6,4},{7,5},{8,10},{9,11},{10,... | collective-permute-start | bytes 1474568 | tf_op jit(solution)/shard_map/ppermute | solution.py:357
  104.5 33.0 %collective-permute-start.20 = (bf16[8,40,768]{2,1,0:T(8,128)(2,1)S(1)}, bf16[8,40,768]{2,1,0:T(8,128)(2,1)S(1)}, u32[]{:S(2)}, u32[]{:S(2)}) collective-permute-start(bf16[8,40,768]{2,1,0:T(8,128)(2,1)S(1)} %get-tuple-element.54.refs_2_), channel_id=1, source_target_pairs={{0,2},{1,3},{2,0},{3,1},{4,6},{5,7},{6,4},{7,5},{8,10},{9,11},{10,... | collective-permute-start | bytes 1474568 | tf_op jit(solution)/shard_map/ppermute | solution.py:357
  119.0 7.9 %collective-permute-start.25 = (bf16[256,768]{1,0:T(8,128)(2,1)S(1)}, bf16[256,768]{1,0:T(8,128)(2,1)S(1)}, u32[]{:S(2)}, u32[]{:S(2)}) collective-permute-start(bf16[256,768]{1,0:T(8,128)(2,1)S(1)} %shard_map.90), channel_id=1, source_target_pairs={{0,1},{1,0},{2,3},{3,2},{4,5},{5,4},{6,7},{7,6},{8,9},{9,8},{10,11... | collective-permute-start | bytes 1179656 | tf_op jit(solution)/shard_map/ppermute | solution.py:357
  119.1 26.3 %collective-permute-start.18 = (bf16[256,768]{1,0:T(8,128)(2,1)S(1)}, bf16[256,768]{1,0:T(8,128)(2,1)S(1)}, u32[]{:S(2)}, u32[]{:S(2)}) collective-permute-start(bf16[256,768]{1,0:T(8,128)(2,1)S(1)} %shard_map.88.refs_6_.near), channel_id=1, source_target_pairs={{0,2},{1,3},{2,0},{3,1},{4,6},{5,7},{6,4},{7,5},{8,10},{9,11},{10,... | collective-permute-start | bytes 1179656 | tf_op jit(solution)/shard_map/ppermute | solution.py:357
  126.9 19.7 %collective-permute-start.26 = (bf16[256,768]{1,0:T(8,128)(2,1)S(1)}, bf16[256,768]{1,0:T(8,128)(2,1)S(1)}, u32[]{:S(2)}, u32[]{:S(2)}) collective-permute-start(bf16[256,768]{1,0:T(8,128)(2,1)S(1)} %add_convert_fusion.1.refs_4_), channel_id=1, source_target_pairs={{0,4},{4,0},{8,12},{12,8},{1,5},{5,1},{9,13},{13,9},{2,6},{6,2},{1... | collective-permute-start | bytes 1179656 | tf_op jit(solution)/shard_map/ppermute | solution.py:357
  126.9 24.0 %collective-permute-start.27 = (bf16[256,768]{1,0:T(8,128)(2,1)S(1)}, bf16[256,768]{1,0:T(8,128)(2,1)S(1)}, u32[]{:S(2)}, u32[]{:S(2)}) collective-permute-start(bf16[256,768]{1,0:T(8,128)(2,1)S(1)} %add_convert_fusion.refs_6_), channel_id=1, source_target_pairs={{0,12},{4,8},{8,4},{12,0},{1,13},{5,9},{9,5},{13,1},{2,14},{6,10},... | collective-permute-start | bytes 1179656 | tf_op jit(solution)/shard_map/ppermute | solution.py:357
  140.0 10.8 %collective-permute-start.29 = (bf16[256,768]{1,0:T(8,128)(2,1)S(1)}, bf16[256,768]{1,0:T(8,128)(2,1)S(1)}, u32[]{:S(2)}, u32[]{:S(2)}) collective-permute-start(bf16[256,768]{1,0:T(8,128)(2,1)S(1)} %shard_map.92._), channel_id=1, source_target_pairs={{0,1},{1,0},{2,3},{3,2},{4,5},{5,4},{6,7},{7,6},{8,9},{9,8},{10,11... | collective-permute-start | bytes 1179656 | tf_op jit(solution)/shard_map/ppermute | solution.py:357
  140.1 26.1 %collective-permute-start.28 = (bf16[256,768]{1,0:T(8,128)(2,1)S(1)}, bf16[256,768]{1,0:T(8,128)(2,1)S(1)}, u32[]{:S(2)}, u32[]{:S(2)}) collective-permute-start(bf16[256,768]{1,0:T(8,128)(2,1)S(1)} %shard_map.91.refs_6_), channel_id=1, source_target_pairs={{0,8},{4,12},{8,0},{12,4},{1,9},{5,13},{9,1},{13,5},{2,10},{6,14},... | collective-permute-start | bytes 1179656 | tf_op jit(solution)/shard_map/ppermute | solution.py:357
  166.6 6.8 %collective-permute-start.30 = (bf16[128,768]{1,0:T(8,128)(2,1)S(1)}, bf16[128,768]{1,0:T(8,128)(2,1)S(1)}, u32[]{:S(2)}, u32[]{:S(2)}) collective-permute-start(bf16[128,768]{1,0:T(8,128)(2,1)S(1)} %slice.34), channel_id=1, source_target_pairs={{0,2},{1,3},{2,0},{3,1},{4,6},{5,7},{6,4},{7,5},{8,10},{9,11},{10,... | collective-permute-start | bytes 589832 | tf_op jit(solution)/shard_map/ppermute | solution.py:357
  (4 other events, 9.3 us)
